TPU v7x, 32 devices: a whole 2x2x4 slice. The times are simulated.
32 devices in a mesh: row: 8 (over z, y), col: 4 (over x, core).
Axes of the slice: x: 2, y: 2, z: 4, core: 2. Of those that a mesh axis runs over, the one named last changes fastest.
Arguments:
- rhs: float32 [2, 8, 64, 512], P(None, 'row'), may hold values from -6 to 6
- inverse_t: float32 [2, 8, 512, 512], P(None, 'row', None, 'col'), may hold values from -1 to 2, as said below
- u_factors: bfloat16 [2, 8, 4, 4, 32, 512], P(None, 'row', None, 'col'), may hold values from -0.14941406 to 0.14941406
- v_factors: bfloat16 [2, 8, 4, 4, 32, 512], P(None, 'row', None, 'col'), may hold values from -0.14941406 to 0.14941406
- tile_ranks: int32 [2, 8, 4, 4], P(None, 'row', None, 'col'), may hold values from 8 to 32
Outputs:
- solved: float32 [2, 8, 64, 512], P(None, 'row')
Inputs may be any that keep to these rules, and one draw needn't show every extreme that they name: `inverse_t`: each transposed inverse is nonsingular and of order one.
All inputs are finite; a program needn't handle non-finite values.
Results may differ from a plain program's by a relative error of at most 0.004.
Values may be sent and summed in bfloat16 or wider, within the bound.
No kernel may reach another device: no remote copies, remote signals or barrier semaphores. Data moves between devices by JAX's collectives and lax.ppermute only.
A program may use at most 64 MiB of HBM per device.

v0:
```python
import jax
import jax.numpy as jnp
from jax import lax
from jax.sharding import PartitionSpec as P


def broadcast(block, axis, source):
    block = jnp.where(lax.axis_index(axis) == source, block, jnp.zeros_like(block))
    return lax.psum(block, axis)


def pick(array, index, axis):
    return lax.dynamic_index_in_dim(array, index, axis, keepdims=False)


def on_device(rhs, inverse_t, u_factors, v_factors, tile_ranks):
    rhs_here = rhs[:, 0]
    slots = rhs_here.shape[0]
    rank_width = u_factors.shape[4]
    n_row = lax.axis_size("row")
    n_col = lax.axis_size("col")
    blocks = slots * n_row
    my_row = lax.axis_index("row")
    my_col = lax.axis_index("col")
    global_rows = jnp.arange(slots, dtype=jnp.int32) * n_row + my_row
    rank_cols = lax.broadcasted_iota(jnp.int32, (1, 1, rank_width), 2)
    start = jnp.zeros(rhs_here.shape, jnp.float32)

    def apply_update(totals, full, u_col, v_col, ranks, active):
        seg_b = full.astype(jnp.bfloat16)
        proj = jnp.einsum("rb,akb->ark", seg_b, v_col, preferred_element_type=jnp.float32)
        keep = (rank_cols < ranks[:, None, None]) & active[:, None, None]
        proj_b = jnp.where(keep, proj, 0.0).astype(jnp.bfloat16)
        update = jnp.einsum("ark,akb->arb", proj_b, u_col, preferred_element_type=jnp.float32)
        return totals + update

    inverse_here = inverse_t[:, 0]
    u_here = u_factors[:, 0, :, 0]
    v_here = v_factors[:, 0, :, 0]
    ranks_here = tile_ranks[:, 0, :, 0]

    def step(k, carry):
        totals, solved = carry
        k_slot = k // n_row
        k_row = k % n_row
        c_slot = k // n_col
        c_dev = k % n_col
        summed = lax.psum(pick(totals, k_slot, 0).astype(jnp.bfloat16), "col").astype(jnp.float32)
        segment = pick(rhs_here, k_slot, 0) - summed
        piece = jnp.dot(
            segment,
            pick(inverse_here, k_slot, 0),
            precision=lax.Precision.HIGHEST,
            preferred_element_type=jnp.float32,
        )
        spread = broadcast(piece, "row", k_row)
        full = lax.all_gather(spread, "col", axis=1, tiled=True)
        previous = pick(solved, k_slot, 0)
        solved = lax.dynamic_update_index_in_dim(
            solved, jnp.where(my_row == k_row, full, previous), k_slot, 0
        )
        u_col = pick(u_here, c_slot, 1)
        v_col = pick(v_here, c_slot, 1)
        ranks = pick(ranks_here, c_slot, 1)
        active = (global_rows > k) & (my_col == c_dev)
        totals = apply_update(totals, full, u_col, v_col, ranks, active)
        return (totals, solved)

    totals, solved = lax.fori_loop(0, blocks, step, (start, start))
    return solved[:, None]


def solution(mesh):
    in_specs = (
        P(None, "row", None, None),
        P(None, "row", None, "col"),
        P(None, "row", None, "col", None, None),
        P(None, "row", None, "col", None, None),
        P(None, "row", None, "col"),
    )
    out_specs = P(None, "row", None, None)
    return jax.shard_map(
        on_device, mesh=mesh, in_specs=in_specs, out_specs=out_specs, check_vma=False
    )
```

profile of v0, /device:TPU:0, one launch (start us, length us, event | category | flops | bytes accessed | tf_op | source)
XLA Modules:
  0.0 1234.3 jit_solution(4183829090954470033)
XLA Ops:
  9.3 1217.8 %while.21 = (s32[]{:T(128)}, f32[2,64,512]{2,1,0:T(8,128)S(1)}, f32[2,64,512]{2,1,0:T(8,128)S(1)}, s32[2,4]{0,1:T(4,128)S(1)}, s32[]{:T(128)}, /*index=5*/bf16[2...) while((s32[]{:T(128)}, f32[2,64,512]{2,1,0:T(8,128)S(1)}, ...), condition=%wide.region_3.4_spmd.clone.clone.clone, body=%wide.region_0.3_spmd.clone.clone.clone.sunk | while | flops 59039912 | bytes 3215025 | solution.py:69
  10.2 36.5 %all-reduce.2.cloned.1.call-done = bf16[64,512]{1,0:T(8,128)(2,1)} async-done(((bf16[64,512]{1,0:T(8,128)(2,1)}), bf16[64,512]{1,0:T(8,128)(2,1)}) %all-reduce.2.cloned.1.call-update) | async-done | bytes 65552 | tf_op jit(solution)/shard_map/while/body/eval_jaxpr/psum | solution.py:48
  47.8 37.1 %psum.39 = f32[64,128]{1,0:T(8,128)S(1)} all-reduce(f32[64,128]{1,0:T(8,128)S(1)} %convolution_select_fusion.3), channel_id=1, replica_groups=mesh['row'=8,'col'=4] {'row'}, use_global_device_ids=true, to_apply=%region_2.2 | all-reduce | flops 8192 | bytes 65536 | tf_op jit(solution)/shard_map/while/body/eval_jaxpr/psum | solution.py:9
  92.5 30.0 %all-reduce.2.cloned.1.call-done = bf16[64,512]{1,0:T(8,128)(2,1)} async-done(((bf16[64,512]{1,0:T(8,128)(2,1)}), bf16[64,512]{1,0:T(8,128)(2,1)}) %all-reduce.2.cloned.1.call-update) | async-done | bytes 65552 | tf_op jit(solution)/shard_map/while/body/eval_jaxpr/psum | solution.py:48
  123.7 37.1 %psum.39 = f32[64,128]{1,0:T(8,128)S(1)} all-reduce(f32[64,128]{1,0:T(8,128)S(1)} %convolution_select_fusion.3), channel_id=1, replica_groups=mesh['row'=8,'col'=4] {'row'}, use_global_device_ids=true, to_apply=%region_2.2 | all-reduce | flops 8192 | bytes 65536 | tf_op jit(solution)/shard_map/while/body/eval_jaxpr/psum | solution.py:9
  168.4 30.0 %all-reduce.2.cloned.1.call-done = bf16[64,512]{1,0:T(8,128)(2,1)} async-done(((bf16[64,512]{1,0:T(8,128)(2,1)}), bf16[64,512]{1,0:T(8,128)(2,1)}) %all-reduce.2.cloned.1.call-update) | async-done | bytes 65552 | tf_op jit(solution)/shard_map/while/body/eval_jaxpr/psum | solution.py:48
  199.5 37.1 %psum.39 = f32[64,128]{1,0:T(8,128)S(1)} all-reduce(f32[64,128]{1,0:T(8,128)S(1)} %convolution_select_fusion.3), channel_id=1, replica_groups=mesh['row'=8,'col'=4] {'row'}, use_global_device_ids=true, to_apply=%region_2.2 | all-reduce | flops 8192 | bytes 65536 | tf_op jit(solution)/shard_map/while/body/eval_jaxpr/psum | solution.py:9
  244.2 29.7 %all-reduce.2.cloned.1.call-done = bf16[64,512]{1,0:T(8,128)(2,1)} async-done(((bf16[64,512]{1,0:T(8,128)(2,1)}), bf16[64,512]{1,0:T(8,128)(2,1)}) %all-reduce.2.cloned.1.call-update) | async-done | bytes 65552 | tf_op jit(solution)/shard_map/while/body/eval_jaxpr/psum | solution.py:48
  275.1 37.1 %psum.39 = f32[64,128]{1,0:T(8,128)S(1)} all-reduce(f32[64,128]{1,0:T(8,128)S(1)} %convolution_select_fusion.3), channel_id=1, replica_groups=mesh['row'=8,'col'=4] {'row'}, use_global_device_ids=true, to_apply=%region_2.2 | all-reduce | flops 8192 | bytes 65536 | tf_op jit(solution)/shard_map/while/body/eval_jaxpr/psum | solution.py:9
  319.8 29.7 %all-reduce.2.cloned.1.call-done = bf16[64,512]{1,0:T(8,128)(2,1)} async-done(((bf16[64,512]{1,0:T(8,128)(2,1)}), bf16[64,512]{1,0:T(8,128)(2,1)}) %all-reduce.2.cloned.1.call-update) | async-done | bytes 65552 | tf_op jit(solution)/shard_map/while/body/eval_jaxpr/psum | solution.py:48
  350.6 37.1 %psum.39 = f32[64,128]{1,0:T(8,128)S(1)} all-reduce(f32[64,128]{1,0:T(8,128)S(1)} %convolution_select_fusion.3), channel_id=1, replica_groups=mesh['row'=8,'col'=4] {'row'}, use_global_device_ids=true, to_apply=%region_2.2 | all-reduce | flops 8192 | bytes 65536 | tf_op jit(solution)/shard_map/while/body/eval_jaxpr/psum | solution.py:9
  395.4 29.7 %all-reduce.2.cloned.1.call-done = bf16[64,512]{1,0:T(8,128)(2,1)} async-done(((bf16[64,512]{1,0:T(8,128)(2,1)}), bf16[64,512]{1,0:T(8,128)(2,1)}) %all-reduce.2.cloned.1.call-update) | async-done | bytes 65552 | tf_op jit(solution)/shard_map/while/body/eval_jaxpr/psum | solution.py:48
  426.2 37.1 %psum.39 = f32[64,128]{1,0:T(8,128)S(1)} all-reduce(f32[64,128]{1,0:T(8,128)S(1)} %convolution_select_fusion.3), channel_id=1, replica_groups=mesh['row'=8,'col'=4] {'row'}, use_global_device_ids=true, to_apply=%region_2.2 | all-reduce | flops 8192 | bytes 65536 | tf_op jit(solution)/shard_map/while/body/eval_jaxpr/psum | solution.py:9
  470.9 30.0 %all-reduce.2.cloned.1.call-done = bf16[64,512]{1,0:T(8,128)(2,1)} async-done(((bf16[64,512]{1,0:T(8,128)(2,1)}), bf16[64,512]{1,0:T(8,128)(2,1)}) %all-reduce.2.cloned.1.call-update) | async-done | bytes 65552 | tf_op jit(solution)/shard_map/while/body/eval_jaxpr/psum | solution.py:48
  502.1 37.1 %psum.39 = f32[64,128]{1,0:T(8,128)S(1)} all-reduce(f32[64,128]{1,0:T(8,128)S(1)} %convolution_select_fusion.3), channel_id=1, replica_groups=mesh['row'=8,'col'=4] {'row'}, use_global_device_ids=true, to_apply=%region_2.2 | all-reduce | flops 8192 | bytes 65536 | tf_op jit(solution)/shard_map/while/body/eval_jaxpr/psum | solution.py:9
  546.8 30.0 %all-reduce.2.cloned.1.call-done = bf16[64,512]{1,0:T(8,128)(2,1)} async-done(((bf16[64,512]{1,0:T(8,128)(2,1)}), bf16[64,512]{1,0:T(8,128)(2,1)}) %all-reduce.2.cloned.1.call-update) | async-done | bytes 65552 | tf_op jit(solution)/shard_map/while/body/eval_jaxpr/psum | solution.py:48
  577.9 37.1 %psum.39 = f32[64,128]{1,0:T(8,128)S(1)} all-reduce(f32[64,128]{1,0:T(8,128)S(1)} %convolution_select_fusion.3), channel_id=1, replica_groups=mesh['row'=8,'col'=4] {'row'}, use_global_device_ids=true, to_apply=%region_2.2 | all-reduce | flops 8192 | bytes 65536 | tf_op jit(solution)/shard_map/while/body/eval_jaxpr/psum | solution.py:9
  622.6 30.0 %all-reduce.2.cloned.1.call-done = bf16[64,512]{1,0:T(8,128)(2,1)} async-done(((bf16[64,512]{1,0:T(8,128)(2,1)}), bf16[64,512]{1,0:T(8,128)(2,1)}) %all-reduce.2.cloned.1.call-update) | async-done | bytes 65552 | tf_op jit(solution)/shard_map/while/body/eval_jaxpr/psum | solution.py:48
  653.8 37.1 %psum.39 = f32[64,128]{1,0:T(8,128)S(1)} all-reduce(f32[64,128]{1,0:T(8,128)S(1)} %convolution_select_fusion.3), channel_id=1, replica_groups=mesh['row'=8,'col'=4] {'row'}, use_global_device_ids=true, to_apply=%region_2.2 | all-reduce | flops 8192 | bytes 65536 | tf_op jit(solution)/shard_map/while/body/eval_jaxpr/psum | solution.py:9
  698.5 29.7 %all-reduce.2.cloned.1.call-done = bf16[64,512]{1,0:T(8,128)(2,1)} async-done(((bf16[64,512]{1,0:T(8,128)(2,1)}), bf16[64,512]{1,0:T(8,128)(2,1)}) %all-reduce.2.cloned.1.call-update) | async-done | bytes 65552 | tf_op jit(solution)/shard_map/while/body/eval_jaxpr/psum | solution.py:48
  729.4 37.1 %psum.39 = f32[64,128]{1,0:T(8,128)S(1)} all-reduce(f32[64,128]{1,0:T(8,128)S(1)} %convolution_select_fusion.3), channel_id=1, replica_groups=mesh['row'=8,'col'=4] {'row'}, use_global_device_ids=true, to_apply=%region_2.2 | all-reduce | flops 8192 | bytes 65536 | tf_op jit(solution)/shard_map/while/body/eval_jaxpr/psum | solution.py:9
  774.1 30.0 %all-reduce.2.cloned.1.call-done = bf16[64,512]{1,0:T(8,128)(2,1)} async-done(((bf16[64,512]{1,0:T(8,128)(2,1)}), bf16[64,512]{1,0:T(8,128)(2,1)}) %all-reduce.2.cloned.1.call-update) | async-done | bytes 65552 | tf_op jit(solution)/shard_map/while/body/eval_jaxpr/psum | solution.py:48
  805.2 37.1 %psum.39 = f32[64,128]{1,0:T(8,128)S(1)} all-reduce(f32[64,128]{1,0:T(8,128)S(1)} %convolution_select_fusion.3), channel_id=1, replica_groups=mesh['row'=8,'col'=4] {'row'}, use_global_device_ids=true, to_apply=%region_2.2 | all-reduce | flops 8192 | bytes 65536 | tf_op jit(solution)/shard_map/while/body/eval_jaxpr/psum | solution.py:9
  849.9 29.7 %all-reduce.2.cloned.1.call-done = bf16[64,512]{1,0:T(8,128)(2,1)} async-done(((bf16[64,512]{1,0:T(8,128)(2,1)}), bf16[64,512]{1,0:T(8,128)(2,1)}) %all-reduce.2.cloned.1.call-update) | async-done | bytes 65552 | tf_op jit(solution)/shard_map/while/body/eval_jaxpr/psum | solution.py:48
  880.8 37.1 %psum.39 = f32[64,128]{1,0:T(8,128)S(1)} all-reduce(f32[64,128]{1,0:T(8,128)S(1)} %convolution_select_fusion.3), channel_id=1, replica_groups=mesh['row'=8,'col'=4] {'row'}, use_global_device_ids=true, to_apply=%region_2.2 | all-reduce | flops 8192 | bytes 65536 | tf_op jit(solution)/shard_map/while/body/eval_jaxpr/psum | solution.py:9
  925.5 30.0 %all-reduce.2.cloned.1.call-done = bf16[64,512]{1,0:T(8,128)(2,1)} async-done(((bf16[64,512]{1,0:T(8,128)(2,1)}), bf16[64,512]{1,0:T(8,128)(2,1)}) %all-reduce.2.cloned.1.call-update) | async-done | bytes 65552 | tf_op jit(solution)/shard_map/while/body/eval_jaxpr/psum | solution.py:48
  956.6 37.1 %psum.39 = f32[64,128]{1,0:T(8,128)S(1)} all-reduce(f32[64,128]{1,0:T(8,128)S(1)} %convolution_select_fusion.3), channel_id=1, replica_groups=mesh['row'=8,'col'=4] {'row'}, use_global_device_ids=true, to_apply=%region_2.2 | all-reduce | flops 8192 | bytes 65536 | tf_op jit(solution)/shard_map/while/body/eval_jaxpr/psum | solution.py:9
  1001.4 29.7 %all-reduce.2.cloned.1.call-done = bf16[64,512]{1,0:T(8,128)(2,1)} async-done(((bf16[64,512]{1,0:T(8,128)(2,1)}), bf16[64,512]{1,0:T(8,128)(2,1)}) %all-reduce.2.cloned.1.call-update) | async-done | bytes 65552 | tf_op jit(solution)/shard_map/while/body/eval_jaxpr/psum | solution.py:48
  1032.2 37.1 %psum.39 = f32[64,128]{1,0:T(8,128)S(1)} all-reduce(f32[64,128]{1,0:T(8,128)S(1)} %convolution_select_fusion.3), channel_id=1, replica_groups=mesh['row'=8,'col'=4] {'row'}, use_global_device_ids=true, to_apply=%region_2.2 | all-reduce | flops 8192 | bytes 65536 | tf_op jit(solution)/shard_map/while/body/eval_jaxpr/psum | solution.py:9
  1076.9 29.7 %all-reduce.2.cloned.1.call-done = bf16[64,512]{1,0:T(8,128)(2,1)} async-done(((bf16[64,512]{1,0:T(8,128)(2,1)}), bf16[64,512]{1,0:T(8,128)(2,1)}) %all-reduce.2.cloned.1.call-update) | async-done | bytes 65552 | tf_op jit(solution)/shard_map/while/body/eval_jaxpr/psum | solution.py:48
  1107.7 37.1 %psum.39 = f32[64,128]{1,0:T(8,128)S(1)} all-reduce(f32[64,128]{1,0:T(8,128)S(1)} %convolution_select_fusion.3), channel_id=1, replica_groups=mesh['row'=8,'col'=4] {'row'}, use_global_device_ids=true, to_apply=%region_2.2 | all-reduce | flops 8192 | bytes 65536 | tf_op jit(solution)/shard_map/while/body/eval_jaxpr/psum | solution.py:9
  1183.3 37.1 %psum.39 = f32[64,128]{1,0:T(8,128)S(1)} all-reduce(f32[64,128]{1,0:T(8,128)S(1)} %convolution_select_fusion.3), channel_id=1, replica_groups=mesh['row'=8,'col'=4] {'row'}, use_global_device_ids=true, to_apply=%region_2.2 | all-reduce | flops 8192 | bytes 65536 | tf_op jit(solution)/shard_map/while/body/eval_jaxpr/psum | solution.py:9
  (203 shorter events, 171.1 us)
Async XLA Ops:
  6.5 1.8 copy-start
  8.3 1.0 copy-start.2
  9.3 37.4 %all-reduce.2.cloned.1.call-start = ((), (), s32[]{:S(2)}) async-start(), calls=%async_computation | async-start | bytes 131072 | tf_op jit(solution)/shard_map/while/body/eval_jaxpr/psum | solution.py:48
  91.6 30.9 %all-reduce.2.cloned.1.call-start = ((), (), s32[]{:S(2)}) async-start(), calls=%async_computation | async-start | bytes 131072 | tf_op jit(solution)/shard_map/while/body/eval_jaxpr/psum | solution.py:48
  167.5 30.9 %all-reduce.2.cloned.1.call-start = ((), (), s32[]{:S(2)}) async-start(), calls=%async_computation | async-start | bytes 131072 | tf_op jit(solution)/shard_map/while/body/eval_jaxpr/psum | solution.py:48
  243.3 30.6 %all-reduce.2.cloned.1.call-start = ((), (), s32[]{:S(2)}) async-start(), calls=%async_computation | async-start | bytes 131072 | tf_op jit(solution)/shard_map/while/body/eval_jaxpr/psum | solution.py:48
  318.9 30.6 %all-reduce.2.cloned.1.call-start = ((), (), s32[]{:S(2)}) async-start(), calls=%async_computation | async-start | bytes 131072 | tf_op jit(solution)/shard_map/while/body/eval_jaxpr/psum | solution.py:48
  394.4 30.6 %all-reduce.2.cloned.1.call-start = ((), (), s32[]{:S(2)}) async-start(), calls=%async_computation | async-start | bytes 131072 | tf_op jit(solution)/shard_map/while/body/eval_jaxpr/psum | solution.py:48
  470.0 30.9 %all-reduce.2.cloned.1.call-start = ((), (), s32[]{:S(2)}) async-start(), calls=%async_computation | async-start | bytes 131072 | tf_op jit(solution)/shard_map/while/body/eval_jaxpr/psum | solution.py:48
  545.8 30.9 %all-reduce.2.cloned.1.call-start = ((), (), s32[]{:S(2)}) async-start(), calls=%async_computation | async-start | bytes 131072 | tf_op jit(solution)/shard_map/while/body/eval_jaxpr/psum | solution.py:48
  621.7 30.9 %all-reduce.2.cloned.1.call-start = ((), (), s32[]{:S(2)}) async-start(), calls=%async_computation | async-start | bytes 131072 | tf_op jit(solution)/shard_map/while/body/eval_jaxpr/psum | solution.py:48
  697.6 30.6 %all-reduce.2.cloned.1.call-start = ((), (), s32[]{:S(2)}) async-start(), calls=%async_computation | async-start | bytes 131072 | tf_op jit(solution)/shard_map/while/body/eval_jaxpr/psum | solution.py:48
  773.1 30.9 %all-reduce.2.cloned.1.call-start = ((), (), s32[]{:S(2)}) async-start(), calls=%async_computation | async-start | bytes 131072 | tf_op jit(solution)/shard_map/while/body/eval_jaxpr/psum | solution.py:48
  849.0 30.6 %all-reduce.2.cloned.1.call-start = ((), (), s32[]{:S(2)}) async-start(), calls=%async_computation | async-start | bytes 131072 | tf_op jit(solution)/shard_map/while/body/eval_jaxpr/psum | solution.py:48
  924.6 30.9 %all-reduce.2.cloned.1.call-start = ((), (), s32[]{:S(2)}) async-start(), calls=%async_computation | async-start | bytes 131072 | tf_op jit(solution)/shard_map/while/body/eval_jaxpr/psum | solution.py:48
  1000.4 30.6 %all-reduce.2.cloned.1.call-start = ((), (), s32[]{:S(2)}) async-start(), calls=%async_computation | async-start | bytes 131072 | tf_op jit(solution)/shard_map/while/body/eval_jaxpr/psum | solution.py:48
  1076.0 30.6 %all-reduce.2.cloned.1.call-start = ((), (), s32[]{:S(2)}) async-start(), calls=%async_computation | async-start | bytes 131072 | tf_op jit(solution)/shard_map/while/body/eval_jaxpr/psum | solution.py:48
  1151.5 30.6 %all-reduce.2.cloned.1.call-start = ((), (), s32[]{:S(2)}) async-start(), calls=%async_computation | async-start | bytes 131072 | tf_op jit(solution)/shard_map/while/body/eval_jaxpr/psum | solution.py:48
  1227.1 0.7 copy-start.1
Sparse Core Ops, SparseCore 0:
  12.4 34.2 all-reduce.1
  94.7 27.7 all-reduce.1
  170.6 27.7 all-reduce.1
  246.1 27.7 all-reduce.1
  321.7 27.7 all-reduce.1
  397.2 27.7 all-reduce.1
  473.1 27.7 all-reduce.1
  549.0 27.7 all-reduce.1
  624.8 27.7 all-reduce.1
  700.4 27.7 all-reduce.1
  776.3 27.7 all-reduce.1
  851.8 27.7 all-reduce.1
  927.7 27.7 all-reduce.1
  1003.2 27.7 all-reduce.1
  1078.8 27.7 all-reduce.1
  1154.3 27.7 all-reduce.1
where the time goes:
time: 1240 us; the launch traced here: 1230 us
  blocking collectives  680 us (55%)
  waiting for transfers between devices  484 us (39%)
  matrix products  38 us (3%)
  local copies, waits for them, and re-layouts  14 us (1%)
  between operations  13.1 us (1%)
    psum x16, blocking collectives, broadcast(): return lax.psum(block, axis)  593 us
    psum x16, waiting for transfers between devices, step(): lax.psum(pick(totals, k_slot, 0).astype(jnp.bfloat16), 'col')  484 us
    all_gather x16, blocking collectives, step(): full = lax.all_gather(spread, 'col', axis=1, tiled=True)  86.4 us
  transfers between devices with their start and end apart: 16, of which 16 were waited for; matrix products, arithmetic and copies ran while one was open for 0% of the time, Pallas kernels for 0%

commit v1 on v0

v1 whole, which is shorter than its diff:
```python
import functools

import jax
import jax.numpy as jnp
from jax import lax
from jax.experimental import pallas as pl
from jax.experimental.pallas import tpu as pltpu
from jax.sharding import PartitionSpec as P

BF = jnp.bfloat16
F32 = jnp.float32
NT = (((1,), (1,)), ((), ()))
TN = (((0,), (0,)), ((), ()))


def mm(a, b):
    return jnp.dot(a, b, preferred_element_type=F32)


def split_mm(a, b):
    high = a.astype(BF)
    low = (a - high.astype(F32)).astype(BF)
    return mm(high, b) + mm(low, b)


def pack(low, high, both, half):
    return jnp.concatenate([high[:, :half], jnp.where(both, low[:, :half], high[:, half:])], axis=1)


def first_kernel(dims, here_ref, rhs_ref, inv_ref, u_ref, v_ref, msg_ref, far_ref):
    n_row, n_col, r_cols, rank, width, half = dims
    row, col = here_ref[0], here_ref[1]
    turn = row // n_col
    inv = inv_ref[...]
    z = split_mm(rhs_ref[...], inv)
    w = mm(u_ref[: (n_row - 1) * rank, :], inv)
    x = jnp.concatenate([z.astype(BF), w.astype(BF)], axis=0)
    near = []
    for t in range(2):
        s = lax.rem(turn - t + 2, 2)
        v = jnp.concatenate([v_ref[s, 0], v_ref[s, 1]], axis=0)
        tile = lax.dot_general(v, x, NT, preferred_element_type=F32).astype(BF)
        near.append(tile[:rank, :width])
        far_ref[t] = tile[rank:]
    msg_ref[...] = pack(near[0], near[1], col > row, half)


def start_solve(q_ref, n_row, r_cols):
    q_ref[...] = jnp.zeros(q_ref.shape, BF)
    eye = (
        lax.broadcasted_iota(jnp.int32, (r_cols, r_cols), 0)
        == lax.broadcasted_iota(jnp.int32, (r_cols, r_cols), 1)
    ).astype(BF)
    for k in range(n_row):
        q_ref[k, :r_cols, :] = eye


def solve(dims, g_ref, q_ref, extra):
    n_row, n_col, r_cols, rank, width, half = dims
    start_solve(q_ref, n_row, r_cols)
    extras = []
    for k in range(n_row):
        parts = []
        w = half if k <= n_col - 2 else width
        for i in range(k + 1, n_row):
            c, t = i % n_col, i // n_col
            at = half if t == 0 else 0
            parts.append(g_ref[k * n_col + c, :, at : at + w])
        if extra is not None:
            if k == n_row - 1:
                w = width + rank
            parts.append(extra(k)[:, :w])
        if not parts:
            break
        a = parts[0] if len(parts) == 1 else jnp.concatenate(parts, axis=0)
        new = mm(a, q_ref[k, :w, :])
        for i in range(k + 1, n_row):
            at = (i - k - 1) * rank
            q_ref[i, r_cols + k * rank : r_cols + (k + 1) * rank, :] = (-new[at : at + rank]).astype(BF)
        if extra is not None:
            extras.append(new[(n_row - 1 - k) * rank :].astype(BF))
    return extras


def middle_kernel(dims, here_ref, g_ref, far_ref, rhs_ref, inv_ref, u_low_ref, u_ref, v_ref, z0_ref, inv0_ref, u0_ref,
                  msg_ref, minus_ref, y_ref, q_ref):
    n_row, n_col, r_cols, rank, width, half = dims
    row, col = here_ref[0], here_ref[1]
    turn = row // n_col
    base = turn * n_col + col
    inv = inv_ref[...]
    w = mm(u_ref[: (n_row - 2) * rank, :], inv)
    p = solve(dims, g_ref, q_ref, lambda k: far_ref[lax.rem(base - k + n_row, n_row)])
    total = lax.dot_general(jnp.concatenate(p, axis=0), u_low_ref[...], TN, preferred_element_type=F32)
    z = split_mm(rhs_ref[...] - total, inv)
    minus_ref[...] = -total
    x = jnp.concatenate([z.astype(BF), w.astype(BF)], axis=0)
    near = []
    for t in range(2):
        s = lax.rem(turn - t + 2, 2)
        near.append(lax.dot_general(v_ref[s, 2], x, NT, preferred_element_type=F32).astype(BF))
    msg_ref[...] = pack(near[0], near[1], col > row, half)
    own = q_ref[row][r_cols:, :]
    minus = lax.dot_general(own, u0_ref[: (n_row - 1) * rank, :], TN, preferred_element_type=F32)
    y_ref[...] = z0_ref[...] + split_mm(minus, inv0_ref[...])


def last_kernel(dims, here_ref, g_ref, minus_ref, inv_ref, u_ref, z_ref, y_ref, q_ref):
    n_row, n_col, r_cols, rank, width, half = dims
    row = here_ref[0]
    solve(dims, g_ref, q_ref, None)
    own = q_ref[row][r_cols:, :]
    minus = minus_ref[...] + lax.dot_general(own, u_ref[: (n_row - 1) * rank, :], TN, preferred_element_type=F32)
    y_ref[...] = z_ref[...] + split_mm(minus, inv_ref[...])


def call(kernel, outs, scratch, *args):
    vmem = pl.BlockSpec(memory_space=pltpu.VMEM)
    return pl.pallas_call(
        kernel,
        out_shape=outs,
        in_specs=[pl.BlockSpec(memory_space=pltpu.SMEM)] + [vmem] * (len(args) - 1),
        out_specs=[vmem] * len(outs),
        scratch_shapes=scratch,
    )(*args)


def on_device(rhs, inverse_t, u_factors, v_factors, tile_ranks):
    slots, _, r_cols, order = rhs.shape
    rank = u_factors.shape[4]
    n_row = lax.axis_size("row")
    n_col = lax.axis_size("col")
    turns = n_row // n_col
    assert slots == 2 and turns == 2 and u_factors.shape[2] == slots * turns
    row = lax.axis_index("row")
    col = lax.axis_index("col")
    here = jnp.stack([row, col]).astype(jnp.int32)
    both = ("row", "col")
    width = r_cols + (n_row - 2) * rank
    half = r_cols + (n_col - 2) * rank
    assert 2 * half == width
    dims = (n_row, n_col, r_cols, rank, width, half)

    rhs_here = rhs[:, 0]
    inv_here = inverse_t[:, 0]
    u_here = u_factors[:, 0, :, 0].reshape(slots, slots, turns, rank, order)
    v_here = v_factors[:, 0, :, 0].reshape(slots, slots, turns, rank, order)
    ranks = tile_ranks[:, 0, :, 0].reshape(slots, slots, turns)
    keep = lax.broadcasted_iota(jnp.int32, v_here.shape, 3) < ranks[..., None, None]
    v_here = jnp.where(keep, v_here, jnp.zeros_like(v_here))

    turn = row // n_col
    v_got = []
    for s in range(turns):
        send = lax.dynamic_index_in_dim(v_here, (turn + s) % turns, 2, keepdims=False)
        send = jnp.stack([send[0, 0], send[1, 0], send[1, 1]])
        pairs = []
        for t in range(turns):
            for c in range(n_col):
                for q in range(n_col):
                    pairs.append(((t * n_col + c) * n_col + q, (((t + s) % turns) * n_col + q) * n_col + c))
        v_got.append(lax.ppermute(send, both, pairs))
    v_got = jnp.stack(v_got)

    def gather_u(part):
        got = lax.all_gather(part, "col", axis=1)
        return got.reshape(n_row * rank, order)

    inv_full = [lax.all_gather(inv_here[a].astype(BF), "col", axis=1, tiled=True) for a in range(slots)]
    u0 = gather_u(u_here[0, 0])
    u_low = gather_u(u_here[1, 0])
    u1 = gather_u(u_here[1, 1])
    z_here = jnp.stack([
        jnp.dot(rhs_here[a], inv_here[a], precision=lax.Precision.HIGHEST, preferred_element_type=F32)
        for a in range(slots)
    ])
    z = lax.all_gather(z_here, "col", axis=2, tiled=True)

    msg, far = call(
        functools.partial(first_kernel, dims),
        [
            jax.ShapeDtypeStruct((rank, width), BF),
            jax.ShapeDtypeStruct((turns, rank, width + rank), BF),
        ],
        [],
        here, rhs_here[0], inv_full[0], u0, v_got,
    )

    far_got = []
    for s in range(n_row):
        send = lax.dynamic_index_in_dim(far, ((row + s) % n_row) // n_col, 0, keepdims=False)
        pairs = []
        for k in range(n_row):
            for q in range(n_col):
                to = (k + s) % n_row
                pairs.append((k * n_col + q, ((to // n_col) * n_col + q) * n_col + to % n_col))
        far_got.append(lax.ppermute(send, both, pairs))
    far_got = jnp.stack(far_got)

    def spread(m):
        copies = jnp.broadcast_to(m[None], (n_row * n_col,) + m.shape)
        return lax.all_to_all(copies, both, split_axis=0, concat_axis=0, tiled=True)

    q_scratch = [pltpu.VMEM((n_row, width + rank, r_cols), BF)]
    msg, minus, y0 = call(
        functools.partial(middle_kernel, dims),
        [
            jax.ShapeDtypeStruct((rank, width), BF),
            jax.ShapeDtypeStruct((r_cols, order), F32),
            jax.ShapeDtypeStruct((r_cols, order), F32),
        ],
        q_scratch,
        here, spread(msg), far_got, rhs_here[1], inv_full[1], u_low, u1, v_got, z[0], inv_full[0], u0,
    )
    (y1,) = call(
        functools.partial(last_kernel, dims),
        [jax.ShapeDtypeStruct((r_cols, order), F32)],
        q_scratch,
        here, spread(msg), minus, inv_full[1], u1, z[1],
    )
    return jnp.stack([y0, y1])[:, None]


def solution(mesh):
    in_specs = (
        P(None, "row", None, None),
        P(None, "row", None, "col"),
        P(None, "row", None, "col", None, None),
        P(None, "row", None, "col", None, None),
        P(None, "row", None, "col"),
    )
    out_specs = P(None, "row", None, None)
    return jax.shard_map(
        on_device, mesh=mesh, in_specs=in_specs, out_specs=out_specs, check_vma=False
    )
```

time: 1240 us -> 122 us (0.10)
  blocking collectives: 680 us -> 66.2 us
  waiting for transfers between devices: 484 us -> 10.5 us
  matrix products: 38 us -> 0.55 us
  starting transfers between devices: 0.63 us -> 21.1 us
  between operations: 13.1 us -> 0.17 us
    psum x16 -> x0, blocking collectives: 593 us -> none  [broadcast(): return lax.psum(block, axis)]
    psum x16 -> x0, waiting for transfers between devices: 484 us -> none  [step(): lax.psum(pick(totals, k_slot, 0).astype(jnp.bfloat16), 'col')]
    all_gather x16 -> x6, blocking collectives: 86.4 us -> 46.9 us  [the longest x3 25.4 us: gather_u(): got = lax.all_gather(part, 'col', axis=1)]
    dot_general x32 -> x2, matrix products: 38 us -> 0.55 us  [on_device(): jnp.dot(rhs_here[a], inv_here[a], precision=lax.Precision.HIGHEST, prefer...]
    all_to_all x0 -> x1, blocking collectives: none -> 19.4 us  [spread(): return lax.all_to_all(copies, both, split_axis=0, concat_axis=0, tiled=True)]
    ppermute x0 -> x10, starting transfers between devices: none -> 17.6 us  [the longest x8 12.7 us: on_device(): far_got.append(lax.ppermute(send, both, pairs))]
  transfers between devices with their start and end apart: 16 -> 11, of which waited for: 16 -> 4; matrix products, arithmetic and copies ran while one was open for 0% -> 3% of each run, Pallas kernels for 0% -> 0%
where the time goes in v1:
time: 122 us
  blocking collectives  66.2 us (54%)
  starting transfers between devices  21.1 us (17%)
  Pallas kernels  10.9 us (9%)
  waiting for transfers between devices  10.5 us (9%)
  local copies, waits for them, and re-layouts  7.46 us (6%)
  other arithmetic  4.67 us (4%)
    all_gather x3, blocking collectives, gather_u(): got = lax.all_gather(part, 'col', axis=1)  25.4 us
    all_to_all x1, blocking collectives, spread(): return lax.all_to_all(copies, both, split_axis=0, concat_axis=0, tiled=True)  19.4 us
    all_gather x2, blocking collectives, on_device(): lax.all_gather(inv_here[a].astype(BF), 'col', axis=1, tiled=True)  15.6 us
    ppermute x8, starting transfers between devices, on_device(): far_got.append(lax.ppermute(send, both, pairs))  12.7 us
    pallas_call x3, Pallas kernels, call(): pl.pallas_call(kernel, out_shape=outs, in_specs=[pl.BlockSpec(memory_spac...  10.9 us
    all_gather x1, blocking collectives, on_device(): z = lax.all_gather(z_here, 'col', axis=2, tiled=True)  5.86 us
    all_to_all x1, waiting for transfers between devices, spread(): return lax.all_to_all(copies, both, split_axis=0, concat_axis=0, tiled=True)  5.31 us
    ppermute x8, waiting for transfers between devices, on_device(): far_got.append(lax.ppermute(send, both, pairs))  5.22 us
  transfers between devices with their start and end apart: 11, of which 4 were waited for; matrix products, arithmetic and copies ran while one was open for 3% of the time, Pallas kernels for 0%

profile of v1, /device:TPU:0, one launch (start us, length us, event | category | flops | bytes accessed | tf_op | source)
XLA Modules:
  0.0 121.6 jit_solution(13812777261176772704)
XLA Ops:
  0.7 0.7 reduce.3
  1.5 1.1 fusion
  2.7 0.8 collective-permute-start
  3.5 4.1 %collective-permute-start.1 = (bf16[3,32,512]{2,1,0:T(8,128)(2,1)S(1)}, bf16[3,32,512]{2,1,0:T(8,128)(2,1)S(1)}, u32[]{:S(2)}, u32[]{:S(2)}) collective-permute-start(bf16[3,32,512]{2,1,0:T(8,128)(2,1)S(1)} %pad_maximum_fusion.2), channel_id=1, source_target_pairs={{0,16},{1,20},{2,24},{3,28},{4,17},{5,21},{6,25},{7,29},{8,18},{9,... | collective-permute-start | bytes 294920 | tf_op jit(solution)/shard_map/ppermute | solution.py:162
  7.7 0.9 copy-done.2
  8.6 0.7 slice_bitcast_fusion.2
  10.6 9.8 %all-gather = bf16[1,1,2,128,512]{4,3,2,1,0:T(8,128)(2,1)} all-gather(bf16[1,1,2,32,512]{4,3,2,1,0:T(8,128)(2,1)S(1)} %get-tuple-element.21), channel_id=2, replica_groups=mesh['row'=8,'col'=4] {'col'}, dimensions={3}, use_global_device_ids=true | all-gather | bytes 327680 | tf_op jit(solution)/shard_map/all_gather | solution.py:166
  20.4 7.8 %all_gather.18.inv_ref.inv0_ref = bf16[512,512]{1,0:T(8,128)(2,1)} all-gather(bf16[512,128]{1,0:T(8,128)(2,1)S(1)} %get-tuple-element.16), channel_id=1, replica_groups=mesh['row'=8,'col'=4] {'col'}, dimensions={1}, use_global_device_ids=true | all-gather | bytes 655360 | tf_op jit(solution)/shard_map/all_gather | solution.py:169
  28.2 7.7 %all_gather.20.inv_ref = bf16[512,512]{1,0:T(8,128)(2,1)} all-gather(bf16[512,128]{1,0:T(8,128)(2,1)S(1)} %get-tuple-element.15), channel_id=1, replica_groups=mesh['row'=8,'col'=4] {'col'}, dimensions={1}, use_global_device_ids=true | all-gather | bytes 655360 | tf_op jit(solution)/shard_map/all_gather | solution.py:169
  36.0 5.9 %all_gather.23 = f32[2,64,512]{2,1,0:T(8,128)S(1)} all-gather(f32[2,64,128]{2,1,0:T(8,128)S(1)} %pad_maximum_fusion.3), channel_id=1, replica_groups=mesh['row'=8,'col'=4] {'col'}, dimensions={2}, use_global_device_ids=true | all-gather | bytes 327680 | tf_op jit(solution)/shard_map/all_gather | solution.py:177
  41.8 0.7 slice_bitcast_fusion
  43.1 6.3 %all-gather.2 = bf16[1,1,2,128,512]{4,3,2,1,0:T(8,128)(2,1)} all-gather(bf16[1,1,2,32,512]{4,3,2,1,0:T(8,128)(2,1)S(1)} %get-tuple-element.19), channel_id=4, replica_groups=mesh['row'=8,'col'=4] {'col'}, dimensions={3}, use_global_device_ids=true | all-gather | bytes 327680 | tf_op jit(solution)/shard_map/all_gather | solution.py:166
  49.4 0.7 pad_maximum_fusion.v_ref
  50.1 2.6 %shard_map.55 = (bf16[32,256]{1,0:T(8,128)(2,1)}, bf16[2,32,288]{2,1,0:T(8,128)(2,1)}) custom-call(s32[2]{0:T(128)} %pad_add_fusion.here_ref, f32[64,512]{1,0:T(8,128)} %get-tuple-element.23.rhs_ref, bf16[512,512]{1,0:T(8,128)(2,1)} %all_gather.18.inv_ref.inv0_ref, bf16[256,512]{1,0:T(8,128)(2,1)} %bitcast.88, bf16[2,3,32,512]{3,2,1,0:T(8,128)(2,1)} %pad_maximum_fusion.v_ref), custom_call_target="tpu_custom_call" | custom-call | tf_op jit(solution)/shard_map/pallas_call | solution.py:119
  52.7 0.9 dynamic-slice_bitcast_fusion.2
  54.3 9.3 %all-gather.1 = bf16[1,1,2,128,512]{4,3,2,1,0:T(8,128)(2,1)} all-gather(bf16[1,1,2,32,512]{4,3,2,1,0:T(8,128)(2,1)S(1)} %get-tuple-element.20), channel_id=3, replica_groups=mesh['row'=8,'col'=4] {'col'}, dimensions={3}, use_global_device_ids=true | all-gather | bytes 327680 | tf_op jit(solution)/shard_map/all_gather | solution.py:166
  64.0 2.4 %collective-permute-start.4 = (bf16[32,288]{1,0:T(8,128)(2,1)S(1)}, bf16[32,288]{1,0:T(8,128)(2,1)S(1)}, u32[]{:S(2)}, u32[]{:S(2)}) collective-permute-start(bf16[32,288]{1,0:T(8,128)(2,1)S(1)} %get-tuple-element.37), channel_id=1, source_target_pairs={{0,2},{1,6},{2,10},{3,14},{4,3},{5,7},{6,11},{7,15},{8,16},{9,20},... | collective-permute-start | bytes 55304 | tf_op jit(solution)/shard_map/ppermute | solution.py:197
  66.4 1.7 %collective-permute-start.5 = (bf16[32,288]{1,0:T(8,128)(2,1)S(1)}, bf16[32,288]{1,0:T(8,128)(2,1)S(1)}, u32[]{:S(2)}, u32[]{:S(2)}) collective-permute-start(bf16[32,288]{1,0:T(8,128)(2,1)S(1)} %get-tuple-element.36), channel_id=1, source_target_pairs={{0,3},{1,7},{2,11},{3,15},{4,16},{5,20},{6,24},{7,28},{8,17},{9,21... | collective-permute-start | bytes 55304 | tf_op jit(solution)/shard_map/ppermute | solution.py:197
  68.1 2.1 %collective-permute-start.6 = (bf16[32,288]{1,0:T(8,128)(2,1)S(1)}, bf16[32,288]{1,0:T(8,128)(2,1)S(1)}, u32[]{:S(2)}, u32[]{:S(2)}) collective-permute-start(bf16[32,288]{1,0:T(8,128)(2,1)S(1)} %get-tuple-element.35), channel_id=1, source_target_pairs={{0,16},{1,20},{2,24},{3,28},{4,17},{5,21},{6,25},{7,29},{8,18},{9,... | collective-permute-start | bytes 55304 | tf_op jit(solution)/shard_map/ppermute | solution.py:197
  70.2 0.9 broadcast_in_dim.9
  71.1 3.5 %all-to-all-start = ((bf16[32,32,256]{2,1,0:T(8,128)(2,1)}), bf16[32,32,256]{2,1,0:T(8,128)(2,1)S(1)}, u32[]{:S(2)}, u32[]{:S(2)}) async-start(bf16[32,32,256]{2,1,0:T(8,128)(2,1)} %broadcast_in_dim.9), calls=%async_computation | async-start | bytes 1048576 | tf_op jit(solution)/shard_map/all_to_all | solution.py:202
  74.7 2.5 %collective-permute-start.7 = (bf16[32,288]{1,0:T(8,128)(2,1)S(1)}, bf16[32,288]{1,0:T(8,128)(2,1)S(1)}, u32[]{:S(2)}, u32[]{:S(2)}) collective-permute-start(bf16[32,288]{1,0:T(8,128)(2,1)S(1)} %get-tuple-element.34), channel_id=1, source_target_pairs={{0,17},{1,21},{2,25},{3,29},{4,18},{5,22},{6,26},{7,30},{8,19},{9,... | collective-permute-start | bytes 55304 | tf_op jit(solution)/shard_map/ppermute | solution.py:197
  77.1 1.5 %collective-permute-start.8 = (bf16[32,288]{1,0:T(8,128)(2,1)S(1)}, bf16[32,288]{1,0:T(8,128)(2,1)S(1)}, u32[]{:S(2)}, u32[]{:S(2)}) collective-permute-start(bf16[32,288]{1,0:T(8,128)(2,1)S(1)} %get-tuple-element.33), channel_id=1, source_target_pairs={{0,18},{1,22},{2,26},{3,30},{4,19},{5,23},{6,27},{7,31},{8,0},{9,4... | collective-permute-start | bytes 55304 | tf_op jit(solution)/shard_map/ppermute | solution.py:197
  78.6 1.5 %collective-permute-start.9 = (bf16[32,288]{1,0:T(8,128)(2,1)S(1)}, bf16[32,288]{1,0:T(8,128)(2,1)S(1)}, u32[]{:S(2)}, u32[]{:S(2)}) collective-permute-start(bf16[32,288]{1,0:T(8,128)(2,1)S(1)} %get-tuple-element.32), channel_id=1, source_target_pairs={{0,19},{1,23},{2,27},{3,31},{4,0},{5,4},{6,8},{7,12},{8,1},{9,5},{... | collective-permute-start | bytes 55304 | tf_op jit(solution)/shard_map/ppermute | solution.py:197
  80.2 4.8 %collective-permute-done.7 = bf16[32,288]{1,0:T(8,128)(2,1)S(1)} collective-permute-done((bf16[32,288]{1,0:T(8,128)(2,1)S(1)}, bf16[32,288]{1,0:T(8,128)(2,1)S(1)}, u32[]{:S(2)}, u32[]{:S(2)}) %collective-permute-start.7) | collective-permute-done | bytes 18464 | tf_op jit(solution)/shard_map/ppermute | solution.py:197
  85.4 5.3 %all-to-all-done.g_ref = bf16[32,32,256]{2,1,0:T(8,128)(2,1)S(1)} async-done(((bf16[32,32,256]{2,1,0:T(8,128)(2,1)}), bf16[32,32,256]{2,1,0:T(8,128)(2,1)S(1)}, u32[]{:S(2)}, u32[]{:S(2)}) %all-to-all-start) | async-done | bytes 524320 | tf_op jit(solution)/shard_map/all_to_all | solution.py:202
  90.7 0.8 copy-done
  91.5 4.7 %shard_map.56 = (bf16[32,256]{1,0:T(8,128)(2,1)}, f32[64,512]{1,0:T(8,128)}, f32[64,512]{1,0:T(8,128)}) custom-call(s32[2]{0:T(128)} %pad_add_fusion.here_ref, bf16[32,32,256]{2,1,0:T(8,128)(2,1)} %copy-done, bf16[8,32,288]{2,1,0:T(8,128)(2,1)} %copy-done.3, f32[64,512]{1,0:T(8,128)} %get-tuple-element.22.rhs_ref, bf16[512,512]{1,0:T(8,128)(2,1)} %all_gather.20.inv_ref, ...), custom_call_target="tpu_custom_call" | custom-call | tf_op jit(solution)/shard_map/pallas_call | solution.py:119
  96.3 0.8 broadcast_in_dim.20
  97.0 19.4 %all_to_all.10.g_ref = bf16[32,32,256]{2,1,0:T(8,128)(2,1)} all-to-all(bf16[32,32,256]{2,1,0:T(8,128)(2,1)S(1)} %broadcast_in_dim.20), channel_id=1, replica_groups=mesh['row'=8,'col'=4] {'row','col'}, dimensions={0} | all-to-all | bytes 1048576 | tf_op jit(solution)/shard_map/all_to_all | solution.py:202
  116.4 3.6 %shard_map.57 = f32[64,512]{1,0:T(8,128)} custom-call(s32[2]{0:T(128)} %pad_add_fusion.here_ref, bf16[32,32,256]{2,1,0:T(8,128)(2,1)} %all_to_all.10.g_ref, f32[64,512]{1,0:T(8,128)} %get-tuple-element.14.minus_ref, bf16[512,512]{1,0:T(8,128)(2,1)} %all_gather.20.inv_ref, bf16[256,512]{1,0:T(8,128)(2,1)} %bitcast.87, f32[64,512]{1,0:T(8,128)} %get-tuple-element.17.z_ref), custom_call_target="tpu_custom_call" | custom-call | tf_op jit(solution)/shard_map/pallas_call | solution.py:119
  120.0 1.6 %maximum_bitcast_fusion = f32[2,1,64,512]{3,2,1,0:T(8,128)} fusion(f32[1,64,512]{2,1,0:T(8,128)} %bitcast.91, f32[1,64,512]{2,1,0:T(8,128)S(1)} %bitcast.94), kind=kLoop, calls=%fused_computation.4 | loop fusion | flops 65536 | bytes 524288 | tf_op jit(solution)/shard_map/broadcast_in_dim | solution.py:221
  (46 shorter events, 4.3 us)
Async XLA Ops:
  0.0 0.7 copy-start.7
  2.7 5.0 %copy-start.1 = (f32[2,1,512,128]{3,2,1,0:T(8,128)S(1)}, f32[2,1,512,128]{3,2,1,0:T(8,128)}, u32[]{:S(2)}) copy-start(f32[2,1,512,128]{3,2,1,0:T(8,128)} %param.6) | copy-start | bytes 1572868
  2.7 46.7 %collective-permute-start = (bf16[3,32,512]{2,1,0:T(8,128)(2,1)S(1)}, bf16[3,32,512]{2,1,0:T(8,128)(2,1)S(1)}, u32[]{:S(2)}, u32[]{:S(2)}) collective-permute-start(bf16[3,32,512]{2,1,0:T(8,128)(2,1)S(1)} %pad_maximum_fusion.1), channel_id=1, source_target_pairs={{0,0},{1,4},{2,8},{3,12},{4,1},{5,5},{6,9},{7,13},{8,2},{9,6},{10,... | collective-permute-start | bytes 294920 | tf_op jit(solution)/shard_map/ppermute | solution.py:162
  3.5 45.9 %collective-permute-start.1 = (bf16[3,32,512]{2,1,0:T(8,128)(2,1)S(1)}, bf16[3,32,512]{2,1,0:T(8,128)(2,1)S(1)}, u32[]{:S(2)}, u32[]{:S(2)}) collective-permute-start(bf16[3,32,512]{2,1,0:T(8,128)(2,1)S(1)} %pad_maximum_fusion.2), channel_id=1, source_target_pairs={{0,16},{1,20},{2,24},{3,28},{4,17},{5,21},{6,25},{7,29},{8,18},{9,... | collective-permute-start | bytes 294920 | tf_op jit(solution)/shard_map/ppermute | solution.py:162
  7.7 1.0 copy-start.2
  9.6 1.0 copy-start.4
  53.6 21.0 %collective-permute-start.2 = (bf16[32,288]{1,0:T(8,128)(2,1)S(1)}, bf16[32,288]{1,0:T(8,128)(2,1)S(1)}, u32[]{:S(2)}, u32[]{:S(2)}) collective-permute-start(bf16[32,288]{1,0:T(8,128)(2,1)S(1)} %get-tuple-element.39), channel_id=1, source_target_pairs={{0,0},{1,4},{2,8},{3,12},{4,1},{5,5},{6,9},{7,13},{8,2},{9,6},{10,... | collective-permute-start | bytes 55304 | tf_op jit(solution)/shard_map/ppermute | solution.py:197
  54.3 15.9 %copy-start.6 = (bf16[32,256]{1,0:T(8,128)(2,1)S(1)}, bf16[32,256]{1,0:T(8,128)(2,1)}, u32[]{:S(2)}) copy-start(bf16[32,256]{1,0:T(8,128)(2,1)} %get-tuple-element.10) | copy-start | bytes 49156
  63.7 13.5 %collective-permute-start.3 = (bf16[32,288]{1,0:T(8,128)(2,1)S(1)}, bf16[32,288]{1,0:T(8,128)(2,1)S(1)}, u32[]{:S(2)}, u32[]{:S(2)}) collective-permute-start(bf16[32,288]{1,0:T(8,128)(2,1)S(1)} %get-tuple-element.38), channel_id=1, source_target_pairs={{0,1},{1,5},{2,9},{3,13},{4,2},{5,6},{6,10},{7,14},{8,3},{9,7},{10... | collective-permute-start | bytes 55304 | tf_op jit(solution)/shard_map/ppermute | solution.py:197
  64.0 14.6 %collective-permute-start.4 = (bf16[32,288]{1,0:T(8,128)(2,1)S(1)}, bf16[32,288]{1,0:T(8,128)(2,1)S(1)}, u32[]{:S(2)}, u32[]{:S(2)}) collective-permute-start(bf16[32,288]{1,0:T(8,128)(2,1)S(1)} %get-tuple-element.37), channel_id=1, source_target_pairs={{0,2},{1,6},{2,10},{3,14},{4,3},{5,7},{6,11},{7,15},{8,16},{9,20},... | collective-permute-start | bytes 55304 | tf_op jit(solution)/shard_map/ppermute | solution.py:197
  66.4 13.7 %collective-permute-start.5 = (bf16[32,288]{1,0:T(8,128)(2,1)S(1)}, bf16[32,288]{1,0:T(8,128)(2,1)S(1)}, u32[]{:S(2)}, u32[]{:S(2)}) collective-permute-start(bf16[32,288]{1,0:T(8,128)(2,1)S(1)} %get-tuple-element.36), channel_id=1, source_target_pairs={{0,3},{1,7},{2,11},{3,15},{4,16},{5,20},{6,24},{7,28},{8,17},{9,21... | collective-permute-start | bytes 55304 | tf_op jit(solution)/shard_map/ppermute | solution.py:197
  68.1 12.0 %collective-permute-start.6 = (bf16[32,288]{1,0:T(8,128)(2,1)S(1)}, bf16[32,288]{1,0:T(8,128)(2,1)S(1)}, u32[]{:S(2)}, u32[]{:S(2)}) collective-permute-start(bf16[32,288]{1,0:T(8,128)(2,1)S(1)} %get-tuple-element.35), channel_id=1, source_target_pairs={{0,16},{1,20},{2,24},{3,28},{4,17},{5,21},{6,25},{7,29},{8,18},{9,... | collective-permute-start | bytes 55304 | tf_op jit(solution)/shard_map/ppermute | solution.py:197
  71.1 19.6 %all-to-all-start = ((bf16[32,32,256]{2,1,0:T(8,128)(2,1)}), bf16[32,32,256]{2,1,0:T(8,128)(2,1)S(1)}, u32[]{:S(2)}, u32[]{:S(2)}) async-start(bf16[32,32,256]{2,1,0:T(8,128)(2,1)} %broadcast_in_dim.9), calls=%async_computation | async-start | bytes 1048576 | tf_op jit(solution)/shard_map/all_to_all | solution.py:202
  74.7 10.3 %collective-permute-start.7 = (bf16[32,288]{1,0:T(8,128)(2,1)S(1)}, bf16[32,288]{1,0:T(8,128)(2,1)S(1)}, u32[]{:S(2)}, u32[]{:S(2)}) collective-permute-start(bf16[32,288]{1,0:T(8,128)(2,1)S(1)} %get-tuple-element.34), channel_id=1, source_target_pairs={{0,17},{1,21},{2,25},{3,29},{4,18},{5,22},{6,26},{7,30},{8,19},{9,... | collective-permute-start | bytes 55304 | tf_op jit(solution)/shard_map/ppermute | solution.py:197
  77.1 8.0 %collective-permute-start.8 = (bf16[32,288]{1,0:T(8,128)(2,1)S(1)}, bf16[32,288]{1,0:T(8,128)(2,1)S(1)}, u32[]{:S(2)}, u32[]{:S(2)}) collective-permute-start(bf16[32,288]{1,0:T(8,128)(2,1)S(1)} %get-tuple-element.33), channel_id=1, source_target_pairs={{0,18},{1,22},{2,26},{3,30},{4,19},{5,23},{6,27},{7,31},{8,0},{9,4... | collective-permute-start | bytes 55304 | tf_op jit(solution)/shard_map/ppermute | solution.py:197
  78.6 6.8 %collective-permute-start.9 = (bf16[32,288]{1,0:T(8,128)(2,1)S(1)}, bf16[32,288]{1,0:T(8,128)(2,1)S(1)}, u32[]{:S(2)}, u32[]{:S(2)}) collective-permute-start(bf16[32,288]{1,0:T(8,128)(2,1)S(1)} %get-tuple-element.32), channel_id=1, source_target_pairs={{0,19},{1,23},{2,27},{3,31},{4,0},{5,4},{6,8},{7,12},{8,1},{9,5},{... | collective-permute-start | bytes 55304 | tf_op jit(solution)/shard_map/ppermute | solution.py:197
  85.4 5.3 %copy-start.3 = (bf16[8,32,288]{2,1,0:T(8,128)(2,1)}, bf16[8,32,288]{2,1,0:T(8,128)(2,1)S(1)}, u32[]{:S(2)}) copy-start(bf16[8,32,288]{2,1,0:T(8,128)(2,1)S(1)} %bitcast_dynamic-update-slice_fusion.far_ref) | copy-start | bytes 442372
  90.7 0.8 copy-start
  116.4 3.6 %copy-start.5 = (f32[64,512]{1,0:T(8,128)S(1)}, f32[64,512]{1,0:T(8,128)}, u32[]{:S(2)}) copy-start(f32[64,512]{1,0:T(8,128)} %get-tuple-element.12) | copy-start | bytes 393220

commit v2 on v1

v2 whole, which is shorter than its diff:
```python
import functools

import jax
import jax.numpy as jnp
from jax import lax
from jax.experimental import pallas as pl
from jax.experimental.pallas import tpu as pltpu
from jax.sharding import PartitionSpec as P

BF = jnp.bfloat16
F32 = jnp.float32
NT = (((1,), (1,)), ((), ()))
TN = (((0,), (0,)), ((), ()))
TURNS = 2


def mm(a, b):
    return jnp.dot(a, b, preferred_element_type=F32)


def split_mm(a, b):
    high = a.astype(BF)
    low = (a - high.astype(F32)).astype(BF)
    return mm(high, b) + mm(low, b)


def pack(low, high, both, half):
    return jnp.concatenate([high[:, :half], jnp.where(both, low[:, :half], high[:, half:])], axis=1)


def place(n_col):
    return lax.axis_index("row"), lax.axis_index("col"), lax.axis_index("row") // n_col


def put_columns(out_ref, at, rows, block):
    lanes = out_ref.shape[1]
    count = block.shape[1] // lanes
    for m in range(count):
        out_ref[at + m * rows : at + (m + 1) * rows, :] = block[:, m * lanes : (m + 1) * lanes]


def columns(ref, source, at, rows, start, stop, count):
    return jnp.concatenate([ref[source, at + m * rows + start : at + m * rows + stop, :] for m in range(count)], axis=1)


def prep_kernel(dims, ranks_ref, inv_ref, u_ref, v_ref, send_ref, near_ref):
    n_row, n_col, r_cols, rank, width, half = dims
    row, col, turn = place(n_col)
    order = inv_ref.shape[1]
    near_ref[:order, :] = inv_ref[0].astype(BF)
    put_columns(near_ref, order, TURNS * rank, u_ref[0, 0].reshape(TURNS * rank, order))
    rank_rows = lax.broadcasted_iota(jnp.int32, v_ref.shape[3:], 0)
    for s in range(TURNS):
        t = lax.rem(turn + s, TURNS)
        for n, (i, k) in enumerate(((0, 0), (1, 0), (1, 1))):
            keep = rank_rows < ranks_ref[(i * 2 + k) * TURNS + t]
            v = v_ref[i, k, t]
            send_ref[s, n] = jnp.where(keep, v, jnp.zeros_like(v))


def gathered_inverse(ref, order):
    return jnp.concatenate([ref[c, :order, :] for c in range(ref.shape[0])], axis=1)


def gathered_u(ref, at, rank, blocks):
    n_col = ref.shape[0]
    return jnp.concatenate(
        [columns(ref, j % n_col, at, TURNS * rank, (j // n_col) * rank, (j // n_col + 1) * rank, n_col)
         for j in range(blocks)], axis=0)


def first_kernel(dims, rhs_ref, near_ref, v_a_ref, v_b_ref, msg_ref, far_ref):
    n_row, n_col, r_cols, rank, width, half = dims
    row, col, turn = place(n_col)
    order = rhs_ref.shape[2]
    inv = gathered_inverse(near_ref, order)
    z = split_mm(rhs_ref[0], inv)
    w = mm(gathered_u(near_ref, order, rank, n_row - 1), inv)
    x = jnp.concatenate([z.astype(BF), w.astype(BF)], axis=0)
    near = []
    for t in range(TURNS):
        straight = turn == t
        v = jnp.where(straight, v_a_ref[:2], v_b_ref[:2]).reshape(2 * rank, order)
        tile = lax.dot_general(v, x, NT, preferred_element_type=F32).astype(BF)
        near.append(tile[:rank, :width])
        to = lax.rem(turn + t, TURNS)
        far_ref[lax.rem(TURNS + t - turn, TURNS)] = tile[rank:]
    msg = pack(near[0], near[1], col > row, half)
    for d in range(msg_ref.shape[0]):
        msg_ref[d] = msg


def start_solve(q_ref, n_row, r_cols):
    q_ref[...] = jnp.zeros(q_ref.shape, BF)
    eye = (
        lax.broadcasted_iota(jnp.int32, (r_cols, r_cols), 0)
        == lax.broadcasted_iota(jnp.int32, (r_cols, r_cols), 1)
    ).astype(BF)
    for k in range(n_row):
        q_ref[k, :r_cols, :] = eye


def solve(dims, g_ref, q_ref, extra):
    n_row, n_col, r_cols, rank, width, half = dims
    start_solve(q_ref, n_row, r_cols)
    extras = []
    for k in range(n_row):
        parts = []
        w = half if k <= n_col - 2 else width
        for i in range(k + 1, n_row):
            c, t = i % n_col, i // n_col
            at = half if t == 0 else 0
            parts.append(g_ref[k * n_col + c, :, at : at + w])
        if extra is not None:
            if k == n_row - 1:
                w = width + rank
            parts.append(extra(k)[:, :w])
        if not parts:
            break
        a = parts[0] if len(parts) == 1 else jnp.concatenate(parts, axis=0)
        new = mm(a, q_ref[k, :w, :])
        for i in range(k + 1, n_row):
            at = (i - k - 1) * rank
            q_ref[i, r_cols + k * rank : r_cols + (k + 1) * rank, :] = (-new[at : at + rank]).astype(BF)
        if extra is not None:
            extras.append(new[(n_row - 1 - k) * rank :].astype(BF))
    return extras


def middle_kernel(dims, g_ref, far_ref, rhs_ref, next_ref, u_ref, v_a_ref, v_b_ref, msg_ref, minus_ref, own_ref, q_ref):
    n_row, n_col, r_cols, rank, width, half = dims
    row, col, turn = place(n_col)
    order = rhs_ref.shape[2]
    inv = gathered_inverse(next_ref, order)
    u = jnp.concatenate([u_ref[j % n_col, j // n_col] for j in range(n_row - 2)], axis=0)
    w = mm(u, inv)
    p = solve(dims, g_ref, q_ref, lambda k: far_ref[k % n_col, lax.rem(turn - k // n_col + TURNS, TURNS)])
    total = lax.dot_general(jnp.concatenate(p, axis=0), gathered_u(next_ref, order, rank, n_row), TN,
                            preferred_element_type=F32)
    z = split_mm(rhs_ref[1] - total, inv)
    minus_ref[...] = -total
    x = jnp.concatenate([z.astype(BF), w.astype(BF)], axis=0)
    near = []
    for t in range(TURNS):
        v = jnp.where(turn == t, v_a_ref[2], v_b_ref[2])
        near.append(lax.dot_general(v, x, NT, preferred_element_type=F32).astype(BF))
    msg = pack(near[0], near[1], col > row, half)
    for d in range(msg_ref.shape[0]):
        msg_ref[d] = msg
    own_ref[...] = q_ref[row][r_cols:, :]


def early_kernel(dims, own_ref, near_ref, z_ref, y_ref):
    n_row, n_col, r_cols, rank, width, half = dims
    order = y_ref.shape[1]
    minus = lax.dot_general(own_ref[...], gathered_u(near_ref, order, rank, n_row - 1), TN, preferred_element_type=F32)
    z = jnp.concatenate([z_ref[c, 0] for c in range(n_col)], axis=1)
    y_ref[...] = z + split_mm(minus, gathered_inverse(near_ref, order))


def last_kernel(dims, g_ref, minus_ref, next_ref, u_ref, z_ref, early_ref, y_ref, q_ref):
    n_row, n_col, r_cols, rank, width, half = dims
    order = minus_ref.shape[1]
    y_ref[0] = early_ref[...]
    solve(dims, g_ref, q_ref, None)
    own = q_ref[lax.axis_index("row")][r_cols:, :]
    u = jnp.concatenate([u_ref[j % n_col, j // n_col] for j in range(n_row - 1)], axis=0)
    minus = minus_ref[...] + lax.dot_general(own, u, TN, preferred_element_type=F32)
    z = jnp.concatenate([z_ref[c, 1] for c in range(n_col)], axis=1)
    y_ref[1] = z + split_mm(minus, gathered_inverse(next_ref, order))


def call(kernel, outs, *args, scratch=(), scalars=0, name=None):
    vmem = pl.BlockSpec(memory_space=pltpu.VMEM)
    return pl.pallas_call(
        kernel,
        out_shape=outs,
        in_specs=[pl.BlockSpec(memory_space=pltpu.SMEM)] * scalars + [vmem] * (len(args) - scalars),
        out_specs=[vmem] * len(outs),
        scratch_shapes=list(scratch),
        name=name,
    )(*args)


def on_device(rhs, inverse_t, u_factors, v_factors, tile_ranks):
    slots, _, r_cols, order = rhs.shape
    rank = u_factors.shape[4]
    n_row = lax.axis_size("row")
    n_col = lax.axis_size("col")
    assert slots == 2 and n_row == TURNS * n_col and u_factors.shape[2] == slots * TURNS
    both = ("row", "col")
    lanes = order // n_col
    width = r_cols + (n_row - 2) * rank
    half = r_cols + (n_col - 2) * rank
    assert 2 * half == width
    dims = (n_row, n_col, r_cols, rank, width, half)
    shape = jax.ShapeDtypeStruct
    devices = n_row * n_col

    rhs_here = rhs[:, 0]
    inv_here = inverse_t[:, 0]
    u_here = u_factors[:, 0, :, 0].reshape(slots, slots, TURNS, rank, order)
    v_here = v_factors[:, 0, :, 0].reshape(slots, slots, TURNS, rank, order)
    ranks = tile_ranks.reshape(-1)

    def turn_rows(parts):
        got = []
        for s in range(TURNS):
            pairs = []
            for t in range(TURNS):
                for c in range(n_col):
                    for q in range(n_col):
                        pairs.append(((t * n_col + c) * n_col + q, (((t + s) % TURNS) * n_col + q) * n_col + c))
            got.append(lax.ppermute(parts[s], both, pairs))
        return got

    def spread(m):
        return lax.all_to_all(m, both, split_axis=0, concat_axis=0, tiled=True)

    def kernel(body):
        return functools.partial(body, dims)

    u_rows = n_col * TURNS * rank
    v_send, near = call(
        kernel(prep_kernel),
        [shape((TURNS, 3, rank, order), BF), shape((order + u_rows, lanes), BF)],
        ranks, inv_here, u_here, v_here, scalars=1, name="prep",
    )
    v_a, v_b = turn_rows(v_send)
    near = lax.all_gather(near, "col")

    msg, far = call(
        kernel(first_kernel),
        [shape((devices, rank, width), BF), shape((TURNS, rank, width + rank), BF)],
        rhs_here, near, v_a, v_b, name="first",
    )

    later_inv, later_u_low, later_u, msg, far = lax.optimization_barrier(
        (inv_here[1], u_here[1, 0], u_here[1, 1], msg, far))
    got = spread(msg)
    far = lax.all_gather(jnp.stack(turn_rows(far)), "col")
    nxt = jnp.concatenate([later_inv.astype(BF)] + [
        later_u_low.reshape(TURNS * rank, order)[:, m * lanes : (m + 1) * lanes] for m in range(n_col)], axis=0)
    nxt = lax.all_gather(nxt, "col")
    u_next = lax.all_gather(later_u, "col")

    q_scratch = [pltpu.VMEM((n_row, width + rank, r_cols), BF)]
    msg, minus, own = call(
        kernel(middle_kernel),
        [shape((devices, rank, width), BF), shape((r_cols, order), F32), shape((width + rank - r_cols, r_cols), BF)],
        got, far, rhs_here, nxt, u_next, v_a, v_b, scratch=q_scratch, name="middle",
    )
    rhs_late, inv_late, msg = lax.optimization_barrier((rhs_here, inv_here, msg))
    got = spread(msg)
    z = lax.dot_general(rhs_late, inv_late, (((2,), (1,)), ((0,), (0,))), precision=lax.Precision.HIGHEST,
                        preferred_element_type=F32)
    z = lax.all_gather(z, "col")
    (early,) = call(kernel(early_kernel), [shape((r_cols, order), F32)], own, near, z, name="early")
    (y,) = call(
        kernel(last_kernel), [shape((slots, r_cols, order), F32)],
        got, minus, nxt, u_next, z, early, scratch=q_scratch, name="last",
    )
    return y[:, None]


def solution(mesh):
    in_specs = (
        P(None, "row", None, None),
        P(None, "row", None, "col"),
        P(None, "row", None, "col", None, None),
        P(None, "row", None, "col", None, None),
        P(None, "row", None, "col"),
    )
    out_specs = P(None, "row", None, None)
    return jax.shard_map(
        on_device, mesh=mesh, in_specs=in_specs, out_specs=out_specs, check_vma=False
    )
```

time: 122 us -> 89.3 us (0.73)
  blocking collectives: 66.2 us -> 47.8 us
  waiting for transfers between devices: 10.5 us -> 3.62 us
  starting transfers between devices: 21.1 us -> 16.1 us
  Pallas kernels: 10.9 us -> 15.3 us
  other arithmetic: 4.67 us -> 0.68 us
  local copies, waits for them, and re-layouts: 7.46 us -> 4.64 us
    all_to_all x1 -> x0, blocking collectives: 19.4 us -> none  [spread(): return lax.all_to_all(copies, both, split_axis=0, concat_axis=0, tiled=True)]
    ppermute x10 -> x4, starting transfers between devices: 17.6 us -> 8.19 us  [turn_rows(): got.append(lax.ppermute(parts[s], both, pairs))]
    ppermute x10 -> x4, waiting for transfers between devices: 5.22 us -> 0.01 us  [turn_rows(): got.append(lax.ppermute(parts[s], both, pairs))]
    all_to_all x1 -> x2, starting transfers between devices: 3.54 us -> 7.94 us  [spread(): return lax.all_to_all(m, both, split_axis=0, concat_axis=0, tiled=True)]
    pallas_call x3 -> x5, Pallas kernels: 10.9 us -> 15.3 us  [call(): pl.pallas_call(kernel, out_shape=outs, in_specs=[pl.BlockSpec(memory_spac...]
    all_to_all x1 -> x2, waiting for transfers between devices: 5.31 us -> 3.61 us  [spread(): return lax.all_to_all(m, both, split_axis=0, concat_axis=0, tiled=True)]
    broadcast_in_dim x2 -> x0, local copies, waits for them, and re-layouts: 1.64 us -> none  [spread(): copies = jnp.broadcast_to(m[None], (n_row * n_col,) + m.shape)]
    broadcast_in_dim x1 -> x0, other arithmetic: 1.62 us -> none  [on_device(): return jnp.stack([y0, y1])[:, None]]
  transfers between devices with their start and end apart: 11 -> 6, of which waited for: 4 -> 1; matrix products, arithmetic and copies ran while one was open for 3% -> 1% of each run, Pallas kernels for 0% -> 3%
where the time goes in v2:
time: 89.3 us; the launch traced here: 88.8 us
  blocking collectives  47.8 us (54%)
  starting transfers between devices  16.1 us (18%)
  Pallas kernels  15.3 us (17%)
  local copies, waits for them, and re-layouts  4.64 us (5%)
  waiting for transfers between devices  3.62 us (4%)
    pallas_call x5, Pallas kernels, call(): pl.pallas_call(kernel, out_shape=outs, in_specs=[pl.BlockSpec(memory_spac...  15.3 us
    all_gather x1, blocking collectives, on_device(): nxt = lax.all_gather(nxt, 'col')  13.9 us
    all_gather x1, blocking collectives, on_device(): near = lax.all_gather(near, 'col')  12 us
    all_gather x1, blocking collectives, on_device(): z = lax.all_gather(z, 'col')  9.25 us
    ppermute x4, starting transfers between devices, turn_rows(): got.append(lax.ppermute(parts[s], both, pairs))  8.19 us
    all_to_all x2, starting transfers between devices, spread(): return lax.all_to_all(m, both, split_axis=0, concat_axis=0, tiled=True)  7.94 us
    all_gather x1, blocking collectives, on_device(): u_next = lax.all_gather(later_u, 'col')  6.61 us
    all_gather x1, blocking collectives, on_device(): far = lax.all_gather(jnp.stack(turn_rows(far)), 'col')  6.05 us
  transfers between devices with their start and end apart: 6, of which 1 were waited for; matrix products, arithmetic and copies ran while one was open for 1% of the time, Pallas kernels for 3%

profile of v2, /device:TPU:0, one launch (start us, length us, event | category | flops | bytes accessed | tf_op | source)
XLA Modules:
  0.0 88.8 jit_solution(18191551442272401987)
XLA Ops:
  0.0 0.5 broadcast.3
  0.5 0.2 copy-done.9
  0.7 0.7 reduce.3
  1.3 0.7 reshape.11.ranks_ref
  2.0 2.0 %prep.1 = (bf16[2,3,32,512]{3,2,1,0:T(8,128)(2,1)}, bf16[768,128]{1,0:T(8,128)(2,1)}) custom-call(s32[8]{0:T(128)} %reshape.11.ranks_ref, f32[2,512,128]{2,1,0:T(8,128)} %bitcast.36, bf16[2,2,2,32,512]{4,3,2,1,0:T(8,128)(2,1)} %bitcast.46, bf16[2,2,2,32,512]{4,3,2,1,0:T(8,128)(2,1)} %bitcast.52), custom_call_target="tpu_custom_call" | custom-call | tf_op jit(solution)/shard_map/prep/pallas_call | solution.py:175
  4.0 1.0 %slice_bitcast_fusion.1 = (bf16[3,32,512]{2,1,0:T(8,128)(2,1)S(1)}, bf16[3,32,512]{2,1,0:T(8,128)(2,1)S(1)}) fusion(bf16[2,3,32,512]{3,2,1,0:T(8,128)(2,1)} %get-tuple-element.21), kind=kLoop, calls=%fused_computation.2 | loop fusion | bytes 393216 | tf_op jit(solution)/shard_map/squeeze | solution.py:214
  5.0 4.1 %collective-permute-start.1 = (bf16[3,32,512]{2,1,0:T(8,128)(2,1)S(1)}, bf16[3,32,512]{2,1,0:T(8,128)(2,1)S(1)}, u32[]{:S(2)}, u32[]{:S(2)}) collective-permute-start(bf16[3,32,512]{2,1,0:T(8,128)(2,1)S(1)} %get-tuple-element.37), channel_id=1, source_target_pairs={{0,16},{1,20},{2,24},{3,28},{4,17},{5,21},{6,25},{7,29},{8,18},{9,... | collective-permute-start | bytes 294920 | tf_op jit(solution)/shard_map/ppermute | solution.py:214
  9.1 0.7 collective-permute-start
  9.8 0.0 copy-start.4
  9.8 12.0 %all-gather = bf16[3072,128]{1,0:T(8,128)(2,1)} all-gather(bf16[768,128]{1,0:T(8,128)(2,1)S(1)} %copy-done.7), channel_id=2, replica_groups=mesh['row'=8,'col'=4] {'col'}, dimensions={0}, use_global_device_ids=true | all-gather | bytes 983040 | tf_op jit(solution)/shard_map/all_gather | solution.py:230
  21.9 0.0 collective-permute-done.1.v_b_ref
  21.9 0.0 copy-start.6
  21.9 0.6 copy-done.5
  22.5 0.0 copy-done.6
  22.5 2.9 %first.1 = (bf16[32,32,256]{2,1,0:T(8,128)(2,1)}, bf16[2,32,288]{2,1,0:T(8,128)(2,1)}) custom-call(f32[2,64,512]{2,1,0:T(8,128)} %bitcast.42, bf16[4,768,128]{2,1,0:T(8,128)(2,1)} %bitcast.32, bf16[3,32,512]{2,1,0:T(8,128)(2,1)} %copy-done.6, bf16[3,32,512]{2,1,0:T(8,128)(2,1)} %copy-done.5), custom_call_target="tpu_custom_call" | custom-call | tf_op jit(solution)/shard_map/first/pallas_call | solution.py:175
  25.4 4.9 %all-to-all-start = ((bf16[32,32,256]{2,1,0:T(8,128)(2,1)}), bf16[32,32,256]{2,1,0:T(8,128)(2,1)S(1)}, u32[]{:S(2)}, u32[]{:S(2)}) async-start(bf16[32,32,256]{2,1,0:T(8,128)(2,1)} %get-tuple-element.24), calls=%async_computation | async-start | bytes 1048576 | tf_op jit(solution)/shard_map/all_to_all | solution.py:218
  30.3 0.7 collective-permute-start.2
  31.0 2.7 %collective-permute-start.3 = (bf16[32,288]{1,0:T(8,128)(2,1)S(1)}, bf16[32,288]{1,0:T(8,128)(2,1)S(1)}, u32[]{:S(2)}, u32[]{:S(2)}) collective-permute-start(bf16[32,288]{1,0:T(8,128)(2,1)S(1)} %get-tuple-element.40), channel_id=1, source_target_pairs={{0,16},{1,20},{2,24},{3,28},{4,17},{5,21},{6,25},{7,29},{8,18},{9,... | collective-permute-start | bytes 55304 | tf_op jit(solution)/shard_map/ppermute | solution.py:214
  33.8 13.9 %all-gather.2 = bf16[3072,128]{1,0:T(8,128)(2,1)} all-gather(bf16[768,128]{1,0:T(8,128)(2,1)S(1)} %slice_dynamic-update-slice_fusion), channel_id=4, replica_groups=mesh['row'=8,'col'=4] {'col'}, dimensions={0}, use_global_device_ids=true | all-gather | bytes 983040 | tf_op jit(solution)/shard_map/all_gather | solution.py:244
  47.7 6.6 %all-gather.3 = bf16[8,32,512]{2,1,0:T(8,128)(2,1)} all-gather(bf16[2,32,512]{2,1,0:T(8,128)(2,1)S(1)} %get-tuple-element.28), channel_id=5, replica_groups=mesh['row'=8,'col'=4] {'col'}, dimensions={0}, use_global_device_ids=true | all-gather | bytes 327680 | tf_op jit(solution)/shard_map/all_gather | solution.py:245
  54.3 0.0 collective-permute-done.2
  54.3 0.0 collective-permute-done.3
  54.4 6.0 %all-gather.1 = bf16[8,32,288]{2,1,0:T(8,128)(2,1)} all-gather(bf16[2,32,288]{2,1,0:T(8,128)(2,1)S(1)} %pad_maximum_fusion), channel_id=3, replica_groups=mesh['row'=8,'col'=4] {'col'}, dimensions={0}, use_global_device_ids=true | all-gather | bytes 184320 | tf_op jit(solution)/shard_map/all_gather | solution.py:241
  60.4 0.8 copy-done.2
  61.2 4.4 %middle.1 = (bf16[32,32,256]{2,1,0:T(8,128)(2,1)}, f32[64,512]{1,0:T(8,128)}, bf16[224,64]{1,0:T(8,128)(2,1)}) custom-call(bf16[32,32,256]{2,1,0:T(8,128)(2,1)} %copy-done.2, bf16[4,2,32,288]{3,2,1,0:T(8,128)(2,1)} %bitcast.45, f32[2,64,512]{2,1,0:T(8,128)} %bitcast.43, bf16[4,768,128]{2,1,0:T(8,128)(2,1)} %bitcast.34, bf16[4,2,32,512]{3,2,1,0:T(8,128)(2,1)} %bitcast.38, ...), custom_call_target="tpu_custom_call" | custom-call | tf_op jit(solution)/shard_map/middle/pallas_call | solution.py:175
  65.6 3.1 %all-to-all-start.1 = ((bf16[32,32,256]{2,1,0:T(8,128)(2,1)}), bf16[32,32,256]{2,1,0:T(8,128)(2,1)S(1)}, u32[]{:S(2)}, u32[]{:S(2)}) async-start(bf16[32,32,256]{2,1,0:T(8,128)(2,1)} %get-tuple-element.30), calls=%async_computation.1 | async-start | bytes 1048576 | tf_op jit(solution)/shard_map/all_to_all | solution.py:218
  68.6 0.4 fusion
  69.1 9.3 %all-gather.4 = f32[8,64,128]{2,1,0:T(8,128)} all-gather(f32[2,64,128]{2,1,0:T(8,128)S(1)} %fusion), channel_id=6, replica_groups=mesh['row'=8,'col'=4] {'col'}, dimensions={0}, use_global_device_ids=true | all-gather | bytes 327680 | tf_op jit(solution)/shard_map/all_gather | solution.py:257
  78.3 2.3 %early.1.early_ref = f32[64,512]{1,0:T(8,128)} custom-call(bf16[224,64]{1,0:T(8,128)(2,1)} %get-tuple-element.34.own_ref, bf16[4,768,128]{2,1,0:T(8,128)(2,1)} %bitcast.33, f32[4,2,64,128]{3,2,1,0:T(8,128)} %bitcast.40), custom_call_target="tpu_custom_call" | custom-call | tf_op jit(solution)/shard_map/early/pallas_call | solution.py:175
  80.6 3.6 %all-to-all-done.1.g_ref = bf16[32,32,256]{2,1,0:T(8,128)(2,1)S(1)} async-done(((bf16[32,32,256]{2,1,0:T(8,128)(2,1)}), bf16[32,32,256]{2,1,0:T(8,128)(2,1)S(1)}, u32[]{:S(2)}, u32[]{:S(2)}) %all-to-all-start.1) | async-done | bytes 524320 | tf_op jit(solution)/shard_map/all_to_all | solution.py:218
  84.3 0.8 copy-done.3
  85.1 3.7 %last.1 = f32[2,64,512]{2,1,0:T(8,128)} custom-call(bf16[32,32,256]{2,1,0:T(8,128)(2,1)} %copy-done.3, f32[64,512]{1,0:T(8,128)} %get-tuple-element.31.minus_ref, bf16[4,768,128]{2,1,0:T(8,128)(2,1)} %bitcast.35, bf16[4,2,32,512]{3,2,1,0:T(8,128)(2,1)} %bitcast.39, f32[4,2,64,128]{3,2,1,0:T(8,128)} %bitcast.41, f32[64,512]{1,0:T(8,128)} %early.1.early_ref), custom_call_target="tpu_custom_call" | custom-call | tf_op jit(solution)/shard_map/last/pallas_call | solution.py:175
  (24 shorter events, 0.1 us)
Async XLA Ops:
  0.0 0.7 copy-start.9
  2.0 7.8 %copy-start = (f32[2,1,512,128]{3,2,1,0:T(8,128)S(1)}, f32[2,1,512,128]{3,2,1,0:T(8,128)}, u32[]{:S(2)}) copy-start(f32[2,1,512,128]{3,2,1,0:T(8,128)} %param.6) | copy-start | bytes 1572868
  5.0 4.8 %copy-start.7 = (bf16[768,128]{1,0:T(8,128)(2,1)S(1)}, bf16[768,128]{1,0:T(8,128)(2,1)}, u32[]{:S(2)}) copy-start(bf16[768,128]{1,0:T(8,128)(2,1)} %get-tuple-element.20) | copy-start | bytes 589828
  5.0 16.9 %collective-permute-start.1 = (bf16[3,32,512]{2,1,0:T(8,128)(2,1)S(1)}, bf16[3,32,512]{2,1,0:T(8,128)(2,1)S(1)}, u32[]{:S(2)}, u32[]{:S(2)}) collective-permute-start(bf16[3,32,512]{2,1,0:T(8,128)(2,1)S(1)} %get-tuple-element.37), channel_id=1, source_target_pairs={{0,16},{1,20},{2,24},{3,28},{4,17},{5,21},{6,25},{7,29},{8,18},{9,... | collective-permute-start | bytes 294920 | tf_op jit(solution)/shard_map/ppermute | solution.py:214
  9.1 12.8 %collective-permute-start = (bf16[3,32,512]{2,1,0:T(8,128)(2,1)S(1)}, bf16[3,32,512]{2,1,0:T(8,128)(2,1)S(1)}, u32[]{:S(2)}, u32[]{:S(2)}) collective-permute-start(bf16[3,32,512]{2,1,0:T(8,128)(2,1)S(1)} %get-tuple-element.38), channel_id=1, source_target_pairs={{0,0},{1,4},{2,8},{3,12},{4,1},{5,5},{6,9},{7,13},{8,2},{9,6},{10,... | collective-permute-start | bytes 294920 | tf_op jit(solution)/shard_map/ppermute | solution.py:214
  9.8 12.0 %copy-start.4 = (bf16[2,1,4,1,32,512]{5,4,3,2,1,0:T(8,128)(2,1)S(1)}, bf16[2,1,4,1,32,512]{5,4,3,2,1,0:T(8,128)(2,1)}, u32[]{:S(2)}) copy-start(bf16[2,1,4,1,32,512]{5,4,3,2,1,0:T(8,128)(2,1)} %param.7) | copy-start | bytes 786436
  21.9 0.6 copy-start.5
  21.9 0.7 copy-start.6
  25.4 4.9 %copy-start.8 = (bf16[2,32,288]{2,1,0:T(8,128)(2,1)S(1)}, bf16[2,32,288]{2,1,0:T(8,128)(2,1)}, u32[]{:S(2)}) copy-start(bf16[2,32,288]{2,1,0:T(8,128)(2,1)} %get-tuple-element.25) | copy-start | bytes 110596
  25.4 35.0 %all-to-all-start = ((bf16[32,32,256]{2,1,0:T(8,128)(2,1)}), bf16[32,32,256]{2,1,0:T(8,128)(2,1)S(1)}, u32[]{:S(2)}, u32[]{:S(2)}) async-start(bf16[32,32,256]{2,1,0:T(8,128)(2,1)} %get-tuple-element.24), calls=%async_computation | async-start | bytes 1048576 | tf_op jit(solution)/shard_map/all_to_all | solution.py:218
  30.3 24.0 %collective-permute-start.2 = (bf16[32,288]{1,0:T(8,128)(2,1)S(1)}, bf16[32,288]{1,0:T(8,128)(2,1)S(1)}, u32[]{:S(2)}, u32[]{:S(2)}) collective-permute-start(bf16[32,288]{1,0:T(8,128)(2,1)S(1)} %get-tuple-element.39), channel_id=1, source_target_pairs={{0,0},{1,4},{2,8},{3,12},{4,1},{5,5},{6,9},{7,13},{8,2},{9,6},{10,... | collective-permute-start | bytes 55304 | tf_op jit(solution)/shard_map/ppermute | solution.py:214
  31.0 23.4 %collective-permute-start.3 = (bf16[32,288]{1,0:T(8,128)(2,1)S(1)}, bf16[32,288]{1,0:T(8,128)(2,1)S(1)}, u32[]{:S(2)}, u32[]{:S(2)}) collective-permute-start(bf16[32,288]{1,0:T(8,128)(2,1)S(1)} %get-tuple-element.40), channel_id=1, source_target_pairs={{0,16},{1,20},{2,24},{3,28},{4,17},{5,21},{6,25},{7,29},{8,18},{9,... | collective-permute-start | bytes 55304 | tf_op jit(solution)/shard_map/ppermute | solution.py:214
  60.4 0.8 copy-start.2
  65.6 3.1 %copy-start.1 = (f32[2,1,64,512]{3,2,1,0:T(8,128)S(1)}, f32[2,1,64,512]{3,2,1,0:T(8,128)}, u32[]{:S(2)}) copy-start(f32[2,1,64,512]{3,2,1,0:T(8,128)} %param.5) | copy-start | bytes 786436
  65.6 18.7 %all-to-all-start.1 = ((bf16[32,32,256]{2,1,0:T(8,128)(2,1)}), bf16[32,32,256]{2,1,0:T(8,128)(2,1)S(1)}, u32[]{:S(2)}, u32[]{:S(2)}) async-start(bf16[32,32,256]{2,1,0:T(8,128)(2,1)} %get-tuple-element.30), calls=%async_computation.1 | async-start | bytes 1048576 | tf_op jit(solution)/shard_map/all_to_all | solution.py:218
  84.2 0.8 copy-start.3

commit v3 on v2

v3 whole, which is shorter than its diff:
```python
import functools

import jax
import jax.numpy as jnp
from jax import lax
from jax.experimental import pallas as pl
from jax.experimental.pallas import tpu as pltpu
from jax.sharding import Mesh
from jax.sharding import PartitionSpec as P

BF = jnp.bfloat16
F32 = jnp.float32
NT = (((1,), (1,)), ((), ()))
TN = (((0,), (0,)), ((), ()))
TURNS = 2


def mm(a, b):
    return jnp.dot(a, b, preferred_element_type=F32)


def split_mm(a, b):
    high = a.astype(BF)
    low = (a - high.astype(F32)).astype(BF)
    return mm(high, b) + mm(low, b)


def pack(low, high, both, half):
    return jnp.concatenate([high[:, :half], jnp.where(both, low[:, :half], high[:, half:])], axis=1)


def place():
    row, x, core = lax.axis_index("row"), lax.axis_index("x"), lax.axis_index("core")
    n_col = lax.axis_size("x") * lax.axis_size("core")
    return row, x * lax.axis_size("core") + core, row // n_col


def join(scratch, pieces):
    x, core, n_x = lax.axis_index("x"), lax.axis_index("core"), lax.axis_size("x")
    for s in range(n_x):
        for other in range(2):
            source = lax.rem(x - s + n_x, n_x) * 2 + (1 - core if other else core)
            scratch[source] = pieces[2 * s + other][...]


def put_columns(out_ref, at, rows, block):
    lanes = out_ref.shape[1]
    count = block.shape[1] // lanes
    for m in range(count):
        out_ref[at + m * rows : at + (m + 1) * rows, :] = block[:, m * lanes : (m + 1) * lanes]


def columns(ref, source, at, rows, start, stop, count):
    return jnp.concatenate([ref[source, at + m * rows + start : at + m * rows + stop, :] for m in range(count)], axis=1)


def prep_kernel(dims, ranks_ref, inv_ref, u_ref, v_ref, send_a_ref, send_b_ref, near_ref):
    n_row, n_col, r_cols, rank, width, half = dims
    row, col, turn = place()
    order = inv_ref.shape[1]
    near_ref[:order, :] = inv_ref[0].astype(BF)
    put_columns(near_ref, order, TURNS * rank, u_ref[0, 0].reshape(TURNS * rank, order))
    rank_rows = lax.broadcasted_iota(jnp.int32, v_ref.shape[3:], 0)
    for s, send_ref in enumerate((send_a_ref, send_b_ref)):
        t = lax.rem(turn + s, TURNS)
        for n, (i, k) in enumerate(((0, 0), (1, 0), (1, 1))):
            keep = rank_rows < ranks_ref[i, 0, 0, k * TURNS + t]
            v = v_ref[i, k, t]
            send_ref[n] = jnp.where(keep, v, jnp.zeros_like(v))


def gathered_inverse(ref, order):
    return jnp.concatenate([ref[c, :order, :] for c in range(ref.shape[0])], axis=1)


def gathered_u(ref, at, rank, blocks):
    n_col = ref.shape[0]
    return jnp.concatenate(
        [columns(ref, j % n_col, at, TURNS * rank, (j // n_col) * rank, (j // n_col + 1) * rank, n_col)
         for j in range(blocks)], axis=0)


def first_kernel(dims, *refs):
    n_row, n_col, r_cols, rank, width, half = dims
    rhs_ref, v_a_ref, v_b_ref = refs[:3]
    msg_ref, far_a_ref, far_b_ref, near_ref = refs[-4:]
    row, col, turn = place()
    order = rhs_ref.shape[2]
    join(near_ref, refs[3:-4])
    inv = gathered_inverse(near_ref, order)
    z = split_mm(rhs_ref[0], inv)
    w = mm(gathered_u(near_ref, order, rank, n_row - 1), inv)
    x = jnp.concatenate([z.astype(BF), w.astype(BF)], axis=0)
    tiles = []
    for v_ref in (v_a_ref, v_b_ref):
        v = v_ref[:2].reshape(2 * rank, order)
        tiles.append(lax.dot_general(v, x, NT, preferred_element_type=F32).astype(BF))
    straight = turn == 0
    low = jnp.where(straight, tiles[0][:rank, :width], tiles[1][:rank, :width])
    high = jnp.where(straight, tiles[1][:rank, :width], tiles[0][:rank, :width])
    far_a_ref[...] = tiles[0][rank:]
    far_b_ref[...] = tiles[1][rank:]
    msg = pack(low, high, col > row, half)
    for d in range(msg_ref.shape[0]):
        msg_ref[d] = msg


def start_solve(q_ref, n_row, r_cols):
    q_ref[...] = jnp.zeros(q_ref.shape, BF)
    eye = (
        lax.broadcasted_iota(jnp.int32, (r_cols, r_cols), 0)
        == lax.broadcasted_iota(jnp.int32, (r_cols, r_cols), 1)
    ).astype(BF)
    for k in range(n_row):
        q_ref[k, :r_cols, :] = eye


def solve(dims, same_ref, other_ref, g_ref, q_ref, extra):
    n_row, n_col, r_cols, rank, width, half = dims
    core = lax.axis_index("core")
    g_ref[core] = same_ref[...]
    g_ref[1 - core] = other_ref[...]
    start_solve(q_ref, n_row, r_cols)
    extras = []
    for k in range(n_row):
        parts = []
        w = half if k <= n_col - 2 else width
        for i in range(k + 1, n_row):
            c, t = i % n_col, i // n_col
            at = half if t == 0 else 0
            parts.append(g_ref[c % 2, k * (n_col // 2) + c // 2, :, at : at + w])
        if extra is not None:
            if k == n_row - 1:
                w = width + rank
            parts.append(extra(k)[:, :w])
        if not parts:
            break
        a = parts[0] if len(parts) == 1 else jnp.concatenate(parts, axis=0)
        new = mm(a, q_ref[k, :w, :])
        for i in range(k + 1, n_row):
            at = (i - k - 1) * rank
            q_ref[i, r_cols + k * rank : r_cols + (k + 1) * rank, :] = (-new[at : at + rank]).astype(BF)
        if extra is not None:
            extras.append(new[(n_row - 1 - k) * rank :].astype(BF))
    return extras


def middle_kernel(dims, *refs):
    n_row, n_col, r_cols, rank, width, half = dims
    same_ref, other_ref, rhs_ref, v_a_ref, v_b_ref = refs[:5]
    fars, nexts = refs[5 : 5 + n_col], refs[5 + n_col : 5 + 2 * n_col]
    msg_ref, minus_ref, own_ref, g_ref, q_ref, far_ref, next_ref = refs[5 + 2 * n_col :]
    row, col, turn = place()
    order = rhs_ref.shape[2]
    rows = n_col * TURNS * rank
    join(next_ref, nexts)
    join(far_ref, fars)
    inv = gathered_inverse(next_ref, order)
    w = mm(gathered_u(next_ref, order + rows, rank, n_row - 2), inv)
    p = solve(dims, same_ref, other_ref, g_ref, q_ref,
              lambda k: far_ref[k % n_col, lax.rem(turn - k // n_col + TURNS, TURNS)])
    total = lax.dot_general(jnp.concatenate(p, axis=0), gathered_u(next_ref, order, rank, n_row), TN,
                            preferred_element_type=F32)
    z = split_mm(rhs_ref[1] - total, inv)
    minus_ref[...] = -total
    x = jnp.concatenate([z.astype(BF), w.astype(BF)], axis=0)
    tiles = [lax.dot_general(v_ref[2], x, NT, preferred_element_type=F32).astype(BF) for v_ref in (v_a_ref, v_b_ref)]
    straight = turn == 0
    low = jnp.where(straight, tiles[0], tiles[1])
    high = jnp.where(straight, tiles[1], tiles[0])
    msg = pack(low, high, col > row, half)
    for d in range(msg_ref.shape[0]):
        msg_ref[d] = msg
    own_ref[...] = q_ref[row][r_cols:, :]


def early_kernel(dims, *refs):
    n_row, n_col, r_cols, rank, width, half = dims
    own_ref = refs[0]
    nears, zs = refs[1 : 1 + n_col], refs[1 + n_col : 1 + 2 * n_col]
    y_ref, z_out_ref, near_ref, z_ref = refs[1 + 2 * n_col :]
    order = y_ref.shape[1]
    join(near_ref, nears)
    join(z_ref, zs)
    minus = lax.dot_general(own_ref[...], gathered_u(near_ref, order, rank, n_row - 1), TN, preferred_element_type=F32)
    z = jnp.concatenate([z_ref[c, 0] for c in range(n_col)], axis=1)
    y_ref[...] = z + split_mm(minus, gathered_inverse(near_ref, order))
    z_out_ref[...] = jnp.concatenate([z_ref[c, 1] for c in range(n_col)], axis=1)


def last_kernel(dims, *refs):
    n_row, n_col, r_cols, rank, width, half = dims
    same_ref, other_ref, minus_ref, z_ref, early_ref = refs[:5]
    y_ref, g_ref, q_ref, next_ref = refs[5 + n_col :]
    order = minus_ref.shape[1]
    y_ref[0] = early_ref[...]
    join(next_ref, refs[5 : 5 + n_col])
    solve(dims, same_ref, other_ref, g_ref, q_ref, None)
    own = q_ref[lax.axis_index("row")][r_cols:, :]
    u = gathered_u(next_ref, order + n_col * TURNS * rank, rank, n_row - 1)
    minus = minus_ref[...] + lax.dot_general(own, u, TN, preferred_element_type=F32)
    y_ref[1] = z_ref[...] + split_mm(minus, gathered_inverse(next_ref, order))


def call(kernel, outs, *args, scratch=(), scalars=0, name=None):
    vmem = pl.BlockSpec(memory_space=pltpu.VMEM)
    return pl.pallas_call(
        kernel,
        out_shape=outs,
        in_specs=[pl.BlockSpec(memory_space=pltpu.SMEM)] * scalars + [vmem] * (len(args) - scalars),
        out_specs=[vmem] * len(outs),
        scratch_shapes=list(scratch),
        compiler_params=pltpu.CompilerParams(vmem_limit_bytes=VMEM_LIMIT),
        name=name,
    )(*args)


VMEM_LIMIT = 24 * 2**20


def on_device(rhs, inverse_t, u_factors, v_factors, tile_ranks):
    slots, _, r_cols, order = rhs.shape
    rank = u_factors.shape[4]
    n_row = lax.axis_size("row")
    n_x = lax.axis_size("x")
    n_col = 2 * n_x
    assert slots == 2 and n_row == TURNS * n_col and u_factors.shape[2] == slots * TURNS
    everywhere = ("row", "x", "core")
    lanes = order // n_col
    width = r_cols + (n_row - 2) * rank
    half = r_cols + (n_col - 2) * rank
    assert 2 * half == width
    dims = (n_row, n_col, r_cols, rank, width, half)
    shape = jax.ShapeDtypeStruct
    swap = [(0, 1), (1, 0)]

    rhs_here = rhs[:, 0]
    inv_here = inverse_t[:, 0]
    u_here = u_factors[:, 0, :, 0].reshape(slots, slots, TURNS, rank, order)
    v_here = v_factors[:, 0, :, 0].reshape(slots, slots, TURNS, rank, order)
    ranks = jnp.swapaxes(tile_ranks, 2, 3)

    def gather(part):
        pieces = []
        for s in range(n_x):
            moved = lax.ppermute(part, "x", [(i, (i + s) % n_x) for i in range(n_x)]) if s else part
            pieces += [moved, lax.ppermute(moved, "core", swap)]
        return pieces

    def turn_rows(parts):
        got = []
        for s in range(TURNS):
            pairs = []
            for t in range(TURNS):
                for c in range(n_col):
                    for q in range(n_col):
                        pairs.append(((t * n_col + c) * n_col + q, (((t + s) % TURNS) * n_col + q) * n_col + c))
            got.append(lax.ppermute(parts[s], everywhere, pairs))
        return got

    def spread(m):
        same = lax.all_to_all(m, ("row", "x"), split_axis=0, concat_axis=0, tiled=True)
        return same, lax.ppermute(same, "core", swap)

    def kernel(body):
        return functools.partial(body, dims)

    u_rows = n_col * TURNS * rank
    messages = shape((n_row * n_x, rank, width), BF)
    far_shape = shape((rank, width + rank), BF)
    near_scratch = pltpu.VMEM((n_col, order + u_rows, lanes), BF)
    next_scratch = pltpu.VMEM((n_col, order + 2 * u_rows, lanes), BF)
    solve_scratch = [
        pltpu.VMEM((2, n_row * n_x, rank, width), BF),
        pltpu.VMEM((n_row, width + rank, r_cols), BF),
    ]

    v_send = shape((3, rank, order), BF)
    v_a, v_b, near = call(
        kernel(prep_kernel),
        [v_send, v_send, shape((order + u_rows, lanes), BF)],
        ranks, inv_here, u_here, v_here, scalars=1, name="prep",
    )
    near = gather(near)
    v_a, v_b = turn_rows([v_a, v_b])

    msg, far_a, far_b = call(
        kernel(first_kernel), [messages, far_shape, far_shape],
        rhs_here, v_a, v_b, *near, scratch=[near_scratch], name="first",
    )

    later_inv, later_u, msg, far_a, far_b = lax.optimization_barrier(
        (inv_here[1], u_here[1], msg, far_a, far_b))
    same, other = spread(msg)
    far = gather(jnp.stack(turn_rows([far_a, far_b])))
    later_u = later_u.reshape(slots, TURNS * rank, order)
    nxt = gather(jnp.concatenate([later_inv.astype(BF)] + [
        later_u[a, :, m * lanes : (m + 1) * lanes] for a in range(slots) for m in range(n_col)], axis=0))

    msg, minus, own = call(
        kernel(middle_kernel),
        [messages, shape((r_cols, order), F32), shape((width + rank - r_cols, r_cols), BF)],
        same, other, rhs_here, v_a, v_b, *far, *nxt,
        scratch=solve_scratch + [pltpu.VMEM((n_col, TURNS, rank, width + rank), BF), next_scratch], name="middle",
    )
    rhs_late, inv_late, msg = lax.optimization_barrier((rhs_here, inv_here, msg))
    same, other = spread(msg)
    z = gather(lax.dot_general(rhs_late, inv_late, (((2,), (1,)), ((0,), (0,))), precision=lax.Precision.HIGHEST,
                               preferred_element_type=F32))
    early, z_last = call(
        kernel(early_kernel), [shape((r_cols, order), F32)] * 2, own, *near, *z,
        scratch=[near_scratch, pltpu.VMEM((n_col, slots, r_cols, lanes), F32)], name="early")
    (y,) = call(
        kernel(last_kernel), [shape((slots, r_cols, order), F32)],
        same, other, minus, z_last, early, *nxt, scratch=solve_scratch + [next_scratch], name="last",
    )
    return y[:, None]


def solution(mesh):
    n_row, n_col = (mesh.shape[name] for name in ("row", "col"))
    fine = Mesh(mesh.devices.reshape(n_row, n_col // 2, 2), ("row", "x", "core"))
    col = ("x", "core")
    in_specs = (
        P(None, "row", None, None),
        P(None, "row", None, col),
        P(None, "row", None, col, None, None),
        P(None, "row", None, col, None, None),
        P(None, "row", None, col),
    )
    out_specs = P(None, "row", None, None)
    return jax.shard_map(
        on_device, mesh=fine, in_specs=in_specs, out_specs=out_specs, check_vma=False
    )
```

time: 89.3 us -> 79.6 us (0.89)
  blocking collectives: 47.8 us -> 16 us
  waiting for transfers between devices: 3.62 us -> 20.1 us
  starting transfers between devices: 16.1 us -> 31.9 us
  Pallas kernels: 15.3 us -> 6.88 us
    all_gather x5 -> x0, blocking collectives: 47.8 us -> none  [the longest x1 13.9 us: on_device(): nxt = lax.all_gather(nxt, 'col')]
    ppermute x4 -> x18, waiting for transfers between devices: 0.01 us -> 20.1 us  [the longest x4 14.5 us: gather(): lax.ppermute(part, 'x', [(i, (i + s) % n_x) for i in range(n_x)])]
    all_to_all x0 -> x1, blocking collectives: none -> 16 us  [spread(): lax.all_to_all(m, ('row', 'x'), split_axis=0, concat_axis=0, tiled=True)]
    ppermute x4 -> x18, starting transfers between devices: 8.19 us -> 21.7 us  [the longest x4 12.1 us: gather(): lax.ppermute(part, 'x', [(i, (i + s) % n_x) for i in range(n_x)])]
    pallas_call x5, Pallas kernels: 15.3 us -> 6.88 us  [call(): pl.pallas_call(kernel, out_shape=outs, in_specs=[pl.BlockSpec(memory_spac...]
    all_to_all x2 -> x1, waiting for transfers between devices: 3.61 us -> 0.01 us  [spread(): lax.all_to_all(m, ('row', 'x'), split_axis=0, concat_axis=0, tiled=True)]
    all_to_all x2 -> x1, starting transfers between devices: 7.94 us -> 10.2 us  [spread(): lax.all_to_all(m, ('row', 'x'), split_axis=0, concat_axis=0, tiled=True)]
    squeeze x3 -> x0, local copies, waits for them, and re-layouts: 0.97 us -> none  [the longest x2 0.96 us: turn_rows(): got.append(lax.ppermute(parts[s], both, pairs))]
  transfers between devices with their start and end apart: 6 -> 19, of which waited for: 1 -> 8; matrix products, arithmetic and copies ran while one was open for 1% -> 1% of each run, Pallas kernels for 3% -> 1%
where the time goes in v3:
time: 79.6 us; the launch traced here: 79.2 us
  starting transfers between devices  31.9 us (40%)
  waiting for transfers between devices  20.1 us (25%)
  blocking collectives  16 us (20%)
  Pallas kernels  6.88 us (9%)
  local copies, waits for them, and re-layouts  3.75 us (5%)
    all_to_all x1, blocking collectives, spread(): lax.all_to_all(m, ('row', 'x'), split_axis=0, concat_axis=0, tiled=True)  16 us
    ppermute x4, waiting for transfers between devices, gather(): lax.ppermute(part, 'x', [(i, (i + s) % n_x) for i in range(n_x)])  14.5 us
    ppermute x4, starting transfers between devices, gather(): lax.ppermute(part, 'x', [(i, (i + s) % n_x) for i in range(n_x)])  12.1 us
    all_to_all x1, starting transfers between devices, spread(): lax.all_to_all(m, ('row', 'x'), split_axis=0, concat_axis=0, tiled=True)  10.2 us
    pallas_call x5, Pallas kernels, call(): pl.pallas_call(kernel, out_shape=outs, in_specs=[pl.BlockSpec(memory_spac...  6.88 us
    ppermute x4, starting transfers between devices, turn_rows(): got.append(lax.ppermute(parts[s], everywhere, pairs))  6.39 us
    unnamed x20, local copies, waits for them, and re-layouts  3.72 us
    ppermute x8, waiting for transfers between devices, gather(): pieces += [moved, lax.ppermute(moved, 'core', swap)]  3.18 us
  transfers between devices with their start and end apart: 19, of which 8 were waited for; matrix products, arithmetic and copies ran while one was open for 1% of the time, Pallas kernels for 1%

profile of v3, /device:TPU:0, one launch (start us, length us, event | category | flops | bytes accessed | tf_op | source)
XLA Modules:
  0.0 79.2 jit_solution(10585613217601896273)
XLA Ops:
  0.0 0.7 copy-done.5
  0.7 1.0 %copy-done = f32[2,1,512,128]{3,2,1,0:T(8,128)S(1)} copy-done((f32[2,1,512,128]{3,2,1,0:T(8,128)S(1)}, f32[2,1,512,128]{3,2,1,0:T(8,128)}, u32[]{:S(2)}) %copy-start) | copy-done | bytes 524312
  1.7 0.9 %copy-done.3 = bf16[2,1,4,1,32,512]{5,4,3,2,1,0:T(8,128)(2,1)S(1)} copy-done((bf16[2,1,4,1,32,512]{5,4,3,2,1,0:T(8,128)(2,1)S(1)}, bf16[2,1,4,1,32,512]{5,4,3,2,1,0:T(8,128)(2,1)}, u32[]{:S(2)}) %copy-start.3) | copy-done | bytes 262168
  2.7 0.9 %copy-done.4 = bf16[2,1,4,1,32,512]{5,4,3,2,1,0:T(8,128)(2,1)S(1)} copy-done((bf16[2,1,4,1,32,512]{5,4,3,2,1,0:T(8,128)(2,1)S(1)}, bf16[2,1,4,1,32,512]{5,4,3,2,1,0:T(8,128)(2,1)}, u32[]{:S(2)}) %copy-start.4) | copy-done | bytes 262168
  3.6 0.6 prep.1
  4.2 3.0 %collective-permute-start.3 = (bf16[768,128]{1,0:T(8,128)(2,1)S(1)}, bf16[768,128]{1,0:T(8,128)(2,1)S(1)}, u32[]{:S(2)}, u32[]{:S(2)}) collective-permute-start(bf16[768,128]{1,0:T(8,128)(2,1)S(1)} %get-tuple-element.26.refs_3_.refs_1_), channel_id=1, source_target_pairs={{0,2},{2,0},{1,3},{3,1},{4,6},{6,4},{5,7},{7,5},{8,10},{10,8},{9,1... | collective-permute-start | bytes 589832 | tf_op jit(solution)/shard_map/ppermute | solution.py:246
  7.3 0.7 collective-permute-start
  7.9 2.7 %collective-permute-start.1 = (bf16[3,32,512]{2,1,0:T(8,128)(2,1)S(1)}, bf16[3,32,512]{2,1,0:T(8,128)(2,1)S(1)}, u32[]{:S(2)}, u32[]{:S(2)}) collective-permute-start(bf16[3,32,512]{2,1,0:T(8,128)(2,1)S(1)} %get-tuple-element.25), channel_id=1, source_target_pairs={{0,16},{1,20},{2,24},{3,28},{4,17},{5,21},{6,25},{7,29},{8,18},{9,... | collective-permute-start | bytes 294920 | tf_op jit(solution)/shard_map/ppermute | solution.py:258
  10.6 1.6 %collective-permute-done.3.refs_5_.refs_3_ = bf16[768,128]{1,0:T(8,128)(2,1)S(1)} collective-permute-done((bf16[768,128]{1,0:T(8,128)(2,1)S(1)}, bf16[768,128]{1,0:T(8,128)(2,1)S(1)}, u32[]{:S(2)}, u32[]{:S(2)}) %collective-permute-start.3) | collective-permute-done | bytes 196640 | tf_op jit(solution)/shard_map/ppermute | solution.py:246
  12.2 1.4 %collective-permute-start.4 = (bf16[768,128]{1,0:T(8,128)(2,1)S(1)}, bf16[768,128]{1,0:T(8,128)(2,1)S(1)}, u32[]{:S(2)}, u32[]{:S(2)}) collective-permute-start(bf16[768,128]{1,0:T(8,128)(2,1)S(1)} %collective-permute-done.3.refs_5_.refs_3_), channel_id=1, source_target_pairs={{0,1},{1,0},{2,3},{3,2},{4,5},{5,4},{6,7},{7,6},{8,9},{9,8},{10,11... | collective-permute-start | bytes 589832 | tf_op jit(solution)/shard_map/ppermute | solution.py:247
  13.6 1.0 %collective-permute-done.4.refs_6_.refs_4_ = bf16[768,128]{1,0:T(8,128)(2,1)S(1)} collective-permute-done((bf16[768,128]{1,0:T(8,128)(2,1)S(1)}, bf16[768,128]{1,0:T(8,128)(2,1)S(1)}, u32[]{:S(2)}, u32[]{:S(2)}) %collective-permute-start.4) | collective-permute-done | bytes 196640 | tf_op jit(solution)/shard_map/ppermute | solution.py:247
  14.6 1.5 %first.1 = (bf16[16,32,256]{2,1,0:T(8,128)(2,1)}, bf16[32,288]{1,0:T(8,128)(2,1)S(1)}, bf16[32,288]{1,0:T(8,128)(2,1)S(1)}) custom-call(f32[2,64,512]{2,1,0:T(8,128)S(1)} %bitcast.52, bf16[3,32,512]{2,1,0:T(8,128)(2,1)S(1)} %collective-permute-done.refs_1_.refs_3_, bf16[3,32,512]{2,1,0:T(8,128)(2,1)S(1)} %collective-permute-done.1.refs_2_.refs_4_, ...), custom_call_target="tpu_custom_call" | custom-call | tf_op jit(solution)/shard_map/first/pallas_call | solution.py:207
  16.1 10.2 %all-to-all-start = ((bf16[16,32,256]{2,1,0:T(8,128)(2,1)}), bf16[16,32,256]{2,1,0:T(8,128)(2,1)S(1)}, u32[]{:S(2)}, u32[]{:S(2)}) async-start(bf16[16,32,256]{2,1,0:T(8,128)(2,1)} %get-tuple-element.30), calls=%async_computation | async-start | bytes 524288 | tf_op jit(solution)/shard_map/all_to_all | solution.py:262
  26.5 2.0 %collective-permute-start.12 = (bf16[1024,128]{1,0:T(8,128)(2,1)S(1)}, bf16[1024,128]{1,0:T(8,128)(2,1)S(1)}, u32[]{:S(2)}, u32[]{:S(2)}) collective-permute-start(bf16[1024,128]{1,0:T(8,128)(2,1)S(1)} %constant_dynamic-update-slice_fusion.refs_9_.refs_5_), channel_id=1, source_target_pairs={{0,2},{2,0},{1,3},{3,1},{4,6},{6,4},{5,7},{7,5},{8,10},{10,8},{9,1... | collective-permute-start | bytes 786440 | tf_op jit(solution)/shard_map/ppermute | solution.py:246
  28.5 8.1 %collective-permute-done.12.refs_11_.refs_7_ = bf16[1024,128]{1,0:T(8,128)(2,1)S(1)} collective-permute-done((bf16[1024,128]{1,0:T(8,128)(2,1)S(1)}, bf16[1024,128]{1,0:T(8,128)(2,1)S(1)}, u32[]{:S(2)}, u32[]{:S(2)}) %collective-permute-start.12) | collective-permute-done | bytes 262176 | tf_op jit(solution)/shard_map/ppermute | solution.py:246
  36.6 0.5 collective-permute-start.5
  37.1 0.7 collective-permute-start.6
  37.8 2.4 %collective-permute-start.7 = (bf16[32,288]{1,0:T(8,128)(2,1)S(1)}, bf16[32,288]{1,0:T(8,128)(2,1)S(1)}, u32[]{:S(2)}, u32[]{:S(2)}) collective-permute-start(bf16[32,288]{1,0:T(8,128)(2,1)S(1)} %get-tuple-element.32), channel_id=1, source_target_pairs={{0,16},{1,20},{2,24},{3,28},{4,17},{5,21},{6,25},{7,29},{8,18},{9,... | collective-permute-start | bytes 55304 | tf_op jit(solution)/shard_map/ppermute | solution.py:258
  40.2 2.4 %collective-permute-done.7 = bf16[32,288]{1,0:T(8,128)(2,1)S(1)} collective-permute-done((bf16[32,288]{1,0:T(8,128)(2,1)S(1)}, bf16[32,288]{1,0:T(8,128)(2,1)S(1)}, u32[]{:S(2)}, u32[]{:S(2)}) %collective-permute-start.7) | collective-permute-done | bytes 18464 | tf_op jit(solution)/shard_map/ppermute | solution.py:258
  42.6 6.2 %collective-permute-start.9 = (bf16[2,32,288]{2,1,0:T(8,128)(2,1)S(1)}, bf16[2,32,288]{2,1,0:T(8,128)(2,1)S(1)}, u32[]{:S(2)}, u32[]{:S(2)}) collective-permute-start(bf16[2,32,288]{2,1,0:T(8,128)(2,1)S(1)} %pad_maximum_fusion.refs_5_), channel_id=1, source_target_pairs={{0,2},{2,0},{1,3},{3,1},{4,6},{6,4},{5,7},{7,5},{8,10},{10,8},{9,1... | collective-permute-start | bytes 110600 | tf_op jit(solution)/shard_map/ppermute | solution.py:246
  48.8 0.9 %collective-permute-start.8 = (bf16[2,32,288]{2,1,0:T(8,128)(2,1)S(1)}, bf16[2,32,288]{2,1,0:T(8,128)(2,1)S(1)}, u32[]{:S(2)}, u32[]{:S(2)}) collective-permute-start(bf16[2,32,288]{2,1,0:T(8,128)(2,1)S(1)} %pad_maximum_fusion.refs_5_), channel_id=1, source_target_pairs={{0,1},{1,0},{2,3},{3,2},{4,5},{5,4},{6,7},{7,6},{8,9},{9,8},{10,11... | collective-permute-start | bytes 110600 | tf_op jit(solution)/shard_map/ppermute | solution.py:247
  49.7 1.3 %collective-permute-done.9.refs_7_ = bf16[2,32,288]{2,1,0:T(8,128)(2,1)S(1)} collective-permute-done((bf16[2,32,288]{2,1,0:T(8,128)(2,1)S(1)}, bf16[2,32,288]{2,1,0:T(8,128)(2,1)S(1)}, u32[]{:S(2)}, u32[]{:S(2)}) %collective-permute-start.9) | collective-permute-done | bytes 36896 | tf_op jit(solution)/shard_map/ppermute | solution.py:246
  50.9 0.3 collective-permute-start.10
  51.2 0.9 %collective-permute-done.10.refs_8_ = bf16[2,32,288]{2,1,0:T(8,128)(2,1)S(1)} collective-permute-done((bf16[2,32,288]{2,1,0:T(8,128)(2,1)S(1)}, bf16[2,32,288]{2,1,0:T(8,128)(2,1)S(1)}, u32[]{:S(2)}, u32[]{:S(2)}) %collective-permute-start.10) | collective-permute-done | bytes 36896 | tf_op jit(solution)/shard_map/ppermute | solution.py:247
  52.2 2.0 %middle.1 = (bf16[16,32,256]{2,1,0:T(8,128)(2,1)S(1)}, f32[64,512]{1,0:T(8,128)S(1)}, bf16[224,64]{1,0:T(8,128)(2,1)S(1)}) custom-call(bf16[16,32,256]{2,1,0:T(8,128)(2,1)S(1)} %all-to-all-done.refs_0_, bf16[16,32,256]{2,1,0:T(8,128)(2,1)S(1)} %collective-permute-done.5.refs_1_, f32[2,64,512]{2,1,0:T(8,128)S(1)} %bitcast.53, ...), custom_call_target="tpu_custom_call" | custom-call | tf_op jit(solution)/shard_map/middle/pallas_call | solution.py:207
  54.2 16.0 %all_to_all.10.refs_0_ = bf16[16,32,256]{2,1,0:T(8,128)(2,1)S(1)} all-to-all(bf16[16,32,256]{2,1,0:T(8,128)(2,1)S(1)} %get-tuple-element.36), channel_id=1, replica_groups=mesh['row'=8,'x'=2,'core'=2] {'row','x'}, dimensions={0} | all-to-all | bytes 524288 | tf_op jit(solution)/shard_map/all_to_all | solution.py:262
  70.2 0.4 fusion.refs_5_
  70.7 0.8 %collective-permute-start.16 = (f32[2,64,128]{2,1,0:T(8,128)S(1)}, f32[2,64,128]{2,1,0:T(8,128)S(1)}, u32[]{:S(2)}, u32[]{:S(2)}) collective-permute-start(f32[2,64,128]{2,1,0:T(8,128)S(1)} %fusion.refs_5_), channel_id=1, source_target_pairs={{0,2},{2,0},{1,3},{3,1},{4,6},{6,4},{5,7},{7,5},{8,10},{10,8},{9,1... | collective-permute-start | bytes 196616 | tf_op jit(solution)/shard_map/ppermute | solution.py:246
  71.7 3.5 %collective-permute-done.16.refs_7_ = f32[2,64,128]{2,1,0:T(8,128)S(1)} collective-permute-done((f32[2,64,128]{2,1,0:T(8,128)S(1)}, f32[2,64,128]{2,1,0:T(8,128)S(1)}, u32[]{:S(2)}, u32[]{:S(2)}) %collective-permute-start.16) | collective-permute-done | bytes 65568 | tf_op jit(solution)/shard_map/ppermute | solution.py:246
  75.2 1.2 %collective-permute-done.17.refs_8_ = f32[2,64,128]{2,1,0:T(8,128)S(1)} collective-permute-done((f32[2,64,128]{2,1,0:T(8,128)S(1)}, f32[2,64,128]{2,1,0:T(8,128)S(1)}, u32[]{:S(2)}, u32[]{:S(2)}) %collective-permute-start.17) | collective-permute-done | bytes 65568 | tf_op jit(solution)/shard_map/ppermute | solution.py:247
  76.5 0.5 early.1
  77.0 2.2 %last.1 = f32[2,64,512]{2,1,0:T(8,128)} custom-call(bf16[16,32,256]{2,1,0:T(8,128)(2,1)S(1)} %all_to_all.10.refs_0_, bf16[16,32,256]{2,1,0:T(8,128)(2,1)S(1)} %collective-permute-done.14.refs_1_, f32[64,512]{1,0:T(8,128)S(1)} %get-tuple-element.37.refs_2_, f32[64,512]{1,0:T(8,128)S(1)} %get-tuple-element.41.refs_3_, ...), custom_call_target="tpu_custom_call" | custom-call | tf_op jit(solution)/shard_map/last/pallas_call | solution.py:207
  (37 shorter events, 0.5 us)
Async XLA Ops:
  0.0 0.7 copy-start.5
  0.7 1.0 %copy-start = (f32[2,1,512,128]{3,2,1,0:T(8,128)S(1)}, f32[2,1,512,128]{3,2,1,0:T(8,128)}, u32[]{:S(2)}) copy-start(f32[2,1,512,128]{3,2,1,0:T(8,128)} %param.6) | copy-start | bytes 1572868
  1.7 0.9 %copy-start.3 = (bf16[2,1,4,1,32,512]{5,4,3,2,1,0:T(8,128)(2,1)S(1)}, bf16[2,1,4,1,32,512]{5,4,3,2,1,0:T(8,128)(2,1)}, u32[]{:S(2)}) copy-start(bf16[2,1,4,1,32,512]{5,4,3,2,1,0:T(8,128)(2,1)} %param.7) | copy-start | bytes 786436
  2.7 0.9 %copy-start.4 = (bf16[2,1,4,1,32,512]{5,4,3,2,1,0:T(8,128)(2,1)S(1)}, bf16[2,1,4,1,32,512]{5,4,3,2,1,0:T(8,128)(2,1)}, u32[]{:S(2)}) copy-start(bf16[2,1,4,1,32,512]{5,4,3,2,1,0:T(8,128)(2,1)} %param.8) | copy-start | bytes 786436
  4.2 7.9 %collective-permute-start.3 = (bf16[768,128]{1,0:T(8,128)(2,1)S(1)}, bf16[768,128]{1,0:T(8,128)(2,1)S(1)}, u32[]{:S(2)}, u32[]{:S(2)}) collective-permute-start(bf16[768,128]{1,0:T(8,128)(2,1)S(1)} %get-tuple-element.26.refs_3_.refs_1_), channel_id=1, source_target_pairs={{0,2},{2,0},{1,3},{3,1},{4,6},{6,4},{5,7},{7,5},{8,10},{10,8},{9,1... | collective-permute-start | bytes 589832 | tf_op jit(solution)/shard_map/ppermute | solution.py:246
  7.3 6.4 %collective-permute-start.2 = (bf16[768,128]{1,0:T(8,128)(2,1)S(1)}, bf16[768,128]{1,0:T(8,128)(2,1)S(1)}, u32[]{:S(2)}, u32[]{:S(2)}) collective-permute-start(bf16[768,128]{1,0:T(8,128)(2,1)S(1)} %get-tuple-element.26.refs_3_.refs_1_), channel_id=1, source_target_pairs={{0,1},{1,0},{2,3},{3,2},{4,5},{5,4},{6,7},{7,6},{8,9},{9,8},{10,11... | collective-permute-start | bytes 589832 | tf_op jit(solution)/shard_map/ppermute | solution.py:247
  7.3 6.3 %collective-permute-start = (bf16[3,32,512]{2,1,0:T(8,128)(2,1)S(1)}, bf16[3,32,512]{2,1,0:T(8,128)(2,1)S(1)}, u32[]{:S(2)}, u32[]{:S(2)}) collective-permute-start(bf16[3,32,512]{2,1,0:T(8,128)(2,1)S(1)} %get-tuple-element.24), channel_id=1, source_target_pairs={{0,0},{1,4},{2,8},{3,12},{4,1},{5,5},{6,9},{7,13},{8,2},{9,6},{10,... | collective-permute-start | bytes 294920 | tf_op jit(solution)/shard_map/ppermute | solution.py:258
  7.9 6.7 %copy-start.2 = (f32[2,1,64,512]{3,2,1,0:T(8,128)S(1)}, f32[2,1,64,512]{3,2,1,0:T(8,128)}, u32[]{:S(2)}) copy-start(f32[2,1,64,512]{3,2,1,0:T(8,128)} %param.5) | copy-start | bytes 786436
  7.9 5.7 %collective-permute-start.1 = (bf16[3,32,512]{2,1,0:T(8,128)(2,1)S(1)}, bf16[3,32,512]{2,1,0:T(8,128)(2,1)S(1)}, u32[]{:S(2)}, u32[]{:S(2)}) collective-permute-start(bf16[3,32,512]{2,1,0:T(8,128)(2,1)S(1)} %get-tuple-element.25), channel_id=1, source_target_pairs={{0,16},{1,20},{2,24},{3,28},{4,17},{5,21},{6,25},{7,29},{8,18},{9,... | collective-permute-start | bytes 294920 | tf_op jit(solution)/shard_map/ppermute | solution.py:258
  12.2 2.4 %collective-permute-start.4 = (bf16[768,128]{1,0:T(8,128)(2,1)S(1)}, bf16[768,128]{1,0:T(8,128)(2,1)S(1)}, u32[]{:S(2)}, u32[]{:S(2)}) collective-permute-start(bf16[768,128]{1,0:T(8,128)(2,1)S(1)} %collective-permute-done.3.refs_5_.refs_3_), channel_id=1, source_target_pairs={{0,1},{1,0},{2,3},{3,2},{4,5},{5,4},{6,7},{7,6},{8,9},{9,8},{10,11... | collective-permute-start | bytes 589832 | tf_op jit(solution)/shard_map/ppermute | solution.py:247
  16.1 20.5 %all-to-all-start = ((bf16[16,32,256]{2,1,0:T(8,128)(2,1)}), bf16[16,32,256]{2,1,0:T(8,128)(2,1)S(1)}, u32[]{:S(2)}, u32[]{:S(2)}) async-start(bf16[16,32,256]{2,1,0:T(8,128)(2,1)} %get-tuple-element.30), calls=%async_computation | async-start | bytes 524288 | tf_op jit(solution)/shard_map/all_to_all | solution.py:262
  26.5 10.1 %collective-permute-start.12 = (bf16[1024,128]{1,0:T(8,128)(2,1)S(1)}, bf16[1024,128]{1,0:T(8,128)(2,1)S(1)}, u32[]{:S(2)}, u32[]{:S(2)}) collective-permute-start(bf16[1024,128]{1,0:T(8,128)(2,1)S(1)} %constant_dynamic-update-slice_fusion.refs_9_.refs_5_), channel_id=1, source_target_pairs={{0,2},{2,0},{1,3},{3,1},{4,6},{6,4},{5,7},{7,5},{8,10},{10,8},{9,1... | collective-permute-start | bytes 786440 | tf_op jit(solution)/shard_map/ppermute | solution.py:246
  28.5 23.7 %collective-permute-start.11 = (bf16[1024,128]{1,0:T(8,128)(2,1)S(1)}, bf16[1024,128]{1,0:T(8,128)(2,1)S(1)}, u32[]{:S(2)}, u32[]{:S(2)}) collective-permute-start(bf16[1024,128]{1,0:T(8,128)(2,1)S(1)} %constant_dynamic-update-slice_fusion.refs_9_.refs_5_), channel_id=1, source_target_pairs={{0,1},{1,0},{2,3},{3,2},{4,5},{5,4},{6,7},{7,6},{8,9},{9,8},{10,11... | collective-permute-start | bytes 786440 | tf_op jit(solution)/shard_map/ppermute | solution.py:247
  36.6 15.6 %collective-permute-start.13 = (bf16[1024,128]{1,0:T(8,128)(2,1)S(1)}, bf16[1024,128]{1,0:T(8,128)(2,1)S(1)}, u32[]{:S(2)}, u32[]{:S(2)}) collective-permute-start(bf16[1024,128]{1,0:T(8,128)(2,1)S(1)} %collective-permute-done.12.refs_11_.refs_7_), channel_id=1, source_target_pairs={{0,1},{1,0},{2,3},{3,2},{4,5},{5,4},{6,7},{7,6},{8,9},{9,8},{10,11... | collective-permute-start | bytes 786440 | tf_op jit(solution)/shard_map/ppermute | solution.py:247
  36.6 15.6 %collective-permute-start.5 = (bf16[16,32,256]{2,1,0:T(8,128)(2,1)S(1)}, bf16[16,32,256]{2,1,0:T(8,128)(2,1)S(1)}, u32[]{:S(2)}, u32[]{:S(2)}) collective-permute-start(bf16[16,32,256]{2,1,0:T(8,128)(2,1)S(1)} %all-to-all-done.refs_0_), channel_id=1, source_target_pairs={{0,1},{1,0},{2,3},{3,2},{4,5},{5,4},{6,7},{7,6},{8,9},{9,8},{10,11... | collective-permute-start | bytes 786440 | tf_op jit(solution)/shard_map/ppermute | solution.py:263
  37.1 3.1 %collective-permute-start.6 = (bf16[32,288]{1,0:T(8,128)(2,1)S(1)}, bf16[32,288]{1,0:T(8,128)(2,1)S(1)}, u32[]{:S(2)}, u32[]{:S(2)}) collective-permute-start(bf16[32,288]{1,0:T(8,128)(2,1)S(1)} %get-tuple-element.31), channel_id=1, source_target_pairs={{0,0},{1,4},{2,8},{3,12},{4,1},{5,5},{6,9},{7,13},{8,2},{9,6},{10,... | collective-permute-start | bytes 55304 | tf_op jit(solution)/shard_map/ppermute | solution.py:258
  37.8 4.8 %collective-permute-start.7 = (bf16[32,288]{1,0:T(8,128)(2,1)S(1)}, bf16[32,288]{1,0:T(8,128)(2,1)S(1)}, u32[]{:S(2)}, u32[]{:S(2)}) collective-permute-start(bf16[32,288]{1,0:T(8,128)(2,1)S(1)} %get-tuple-element.32), channel_id=1, source_target_pairs={{0,16},{1,20},{2,24},{3,28},{4,17},{5,21},{6,25},{7,29},{8,18},{9,... | collective-permute-start | bytes 55304 | tf_op jit(solution)/shard_map/ppermute | solution.py:258
  42.6 8.4 %collective-permute-start.9 = (bf16[2,32,288]{2,1,0:T(8,128)(2,1)S(1)}, bf16[2,32,288]{2,1,0:T(8,128)(2,1)S(1)}, u32[]{:S(2)}, u32[]{:S(2)}) collective-permute-start(bf16[2,32,288]{2,1,0:T(8,128)(2,1)S(1)} %pad_maximum_fusion.refs_5_), channel_id=1, source_target_pairs={{0,2},{2,0},{1,3},{3,1},{4,6},{6,4},{5,7},{7,5},{8,10},{10,8},{9,1... | collective-permute-start | bytes 110600 | tf_op jit(solution)/shard_map/ppermute | solution.py:246
  48.8 2.4 %collective-permute-start.8 = (bf16[2,32,288]{2,1,0:T(8,128)(2,1)S(1)}, bf16[2,32,288]{2,1,0:T(8,128)(2,1)S(1)}, u32[]{:S(2)}, u32[]{:S(2)}) collective-permute-start(bf16[2,32,288]{2,1,0:T(8,128)(2,1)S(1)} %pad_maximum_fusion.refs_5_), channel_id=1, source_target_pairs={{0,1},{1,0},{2,3},{3,2},{4,5},{5,4},{6,7},{7,6},{8,9},{9,8},{10,11... | collective-permute-start | bytes 110600 | tf_op jit(solution)/shard_map/ppermute | solution.py:247
  50.9 1.2 %collective-permute-start.10 = (bf16[2,32,288]{2,1,0:T(8,128)(2,1)S(1)}, bf16[2,32,288]{2,1,0:T(8,128)(2,1)S(1)}, u32[]{:S(2)}, u32[]{:S(2)}) collective-permute-start(bf16[2,32,288]{2,1,0:T(8,128)(2,1)S(1)} %collective-permute-done.9.refs_7_), channel_id=1, source_target_pairs={{0,1},{1,0},{2,3},{3,2},{4,5},{5,4},{6,7},{7,6},{8,9},{9,8},{10,11... | collective-permute-start | bytes 110600 | tf_op jit(solution)/shard_map/ppermute | solution.py:247
  54.2 16.0 %copy-start.1 = (f32[2,1,512,128]{3,2,1,0:T(8,128)S(1)}, f32[2,1,512,128]{3,2,1,0:T(8,128)}, u32[]{:S(2)}) copy-start(f32[2,1,512,128]{3,2,1,0:T(8,128)} %param.6) | copy-start | bytes 1572868
  70.2 6.8 %collective-permute-start.14 = (bf16[16,32,256]{2,1,0:T(8,128)(2,1)S(1)}, bf16[16,32,256]{2,1,0:T(8,128)(2,1)S(1)}, u32[]{:S(2)}, u32[]{:S(2)}) collective-permute-start(bf16[16,32,256]{2,1,0:T(8,128)(2,1)S(1)} %all_to_all.10.refs_0_), channel_id=1, source_target_pairs={{0,1},{1,0},{2,3},{3,2},{4,5},{5,4},{6,7},{7,6},{8,9},{9,8},{10,11... | collective-permute-start | bytes 786440 | tf_op jit(solution)/shard_map/ppermute | solution.py:263
  70.7 4.6 %collective-permute-start.16 = (f32[2,64,128]{2,1,0:T(8,128)S(1)}, f32[2,64,128]{2,1,0:T(8,128)S(1)}, u32[]{:S(2)}, u32[]{:S(2)}) collective-permute-start(f32[2,64,128]{2,1,0:T(8,128)S(1)} %fusion.refs_5_), channel_id=1, source_target_pairs={{0,2},{2,0},{1,3},{3,1},{4,6},{6,4},{5,7},{7,5},{8,10},{10,8},{9,1... | collective-permute-start | bytes 196616 | tf_op jit(solution)/shard_map/ppermute | solution.py:246
  71.5 3.7 %collective-permute-start.15 = (f32[2,64,128]{2,1,0:T(8,128)S(1)}, f32[2,64,128]{2,1,0:T(8,128)S(1)}, u32[]{:S(2)}, u32[]{:S(2)}) collective-permute-start(f32[2,64,128]{2,1,0:T(8,128)S(1)} %fusion.refs_5_), channel_id=1, source_target_pairs={{0,1},{1,0},{2,3},{3,2},{4,5},{5,4},{6,7},{7,6},{8,9},{9,8},{10,11... | collective-permute-start | bytes 196616 | tf_op jit(solution)/shard_map/ppermute | solution.py:247
  75.2 1.3 %collective-permute-start.17 = (f32[2,64,128]{2,1,0:T(8,128)S(1)}, f32[2,64,128]{2,1,0:T(8,128)S(1)}, u32[]{:S(2)}, u32[]{:S(2)}) collective-permute-start(f32[2,64,128]{2,1,0:T(8,128)S(1)} %collective-permute-done.16.refs_7_), channel_id=1, source_target_pairs={{0,1},{1,0},{2,3},{3,2},{4,5},{5,4},{6,7},{7,6},{8,9},{9,8},{10,11... | collective-permute-start | bytes 196616 | tf_op jit(solution)/shard_map/ppermute | solution.py:247

commit v4 on v3

--- a/solution.py
+++ b/solution.py
@@ -54,12 +54,22 @@
     return jnp.concatenate([ref[source, at + m * rows + start : at + m * rows + stop, :] for m in range(count)], axis=1)
 
 
-def prep_kernel(dims, ranks_ref, inv_ref, u_ref, v_ref, send_a_ref, send_b_ref, near_ref):
-    n_row, n_col, r_cols, rank, width, half = dims
-    row, col, turn = place()
-    order = inv_ref.shape[1]
-    near_ref[:order, :] = inv_ref[0].astype(BF)
-    put_columns(near_ref, order, TURNS * rank, u_ref[0, 0].reshape(TURNS * rank, order))
+def prep_kernel(dims, ranks_ref, inv_hbm, u_hbm, v_hbm, send_a_ref, send_b_ref, near_ref, inv_ref, u_ref, v_ref, sems):
+    _, _, _, rank, _, _ = dims
+    _, _, turn = place()
+    order = inv_ref.shape[0]
+    copies = [
+        pltpu.make_async_copy(inv_hbm.at[0], inv_ref, sems.at[0]),
+        pltpu.make_async_copy(u_hbm.at[0, 0], u_ref, sems.at[1]),
+        pltpu.make_async_copy(v_hbm, v_ref, sems.at[2]),
+    ]
+    for copy in copies:
+        copy.start()
+    copies[0].wait()
+    copies[1].wait()
+    near_ref[:order, :] = inv_ref[...].astype(BF)
+    put_columns(near_ref, order, TURNS * rank, u_ref[...].reshape(TURNS * rank, order))
+    copies[2].wait()
     rank_rows = lax.broadcasted_iota(jnp.int32, v_ref.shape[3:], 0)
     for s, send_ref in enumerate((send_a_ref, send_b_ref)):
         t = lax.rem(turn + s, TURNS)
@@ -81,7 +91,7 @@
 
 
 def first_kernel(dims, *refs):
-    n_row, n_col, r_cols, rank, width, half = dims
+    n_row, _, _, rank, width, half = dims
     rhs_ref, v_a_ref, v_b_ref = refs[:3]
     msg_ref, far_a_ref, far_b_ref, near_ref = refs[-4:]
     row, col, turn = place()
@@ -146,7 +156,7 @@
 
 
 def middle_kernel(dims, *refs):
-    n_row, n_col, r_cols, rank, width, half = dims
+    n_row, n_col, r_cols, rank, _, half = dims
     same_ref, other_ref, rhs_ref, v_a_ref, v_b_ref = refs[:5]
     fars, nexts = refs[5 : 5 + n_col], refs[5 + n_col : 5 + 2 * n_col]
     msg_ref, minus_ref, own_ref, g_ref, q_ref, far_ref, next_ref = refs[5 + 2 * n_col :]
@@ -175,7 +185,7 @@
 
 
 def early_kernel(dims, *refs):
-    n_row, n_col, r_cols, rank, width, half = dims
+    n_row, n_col, _, rank, _, _ = dims
     own_ref = refs[0]
     nears, zs = refs[1 : 1 + n_col], refs[1 + n_col : 1 + 2 * n_col]
     y_ref, z_out_ref, near_ref, z_ref = refs[1 + 2 * n_col :]
@@ -189,7 +199,7 @@
 
 
 def last_kernel(dims, *refs):
-    n_row, n_col, r_cols, rank, width, half = dims
+    n_row, n_col, r_cols, rank, _, _ = dims
     same_ref, other_ref, minus_ref, z_ref, early_ref = refs[:5]
     y_ref, g_ref, q_ref, next_ref = refs[5 + n_col :]
     order = minus_ref.shape[1]
@@ -202,20 +212,17 @@
     y_ref[1] = z_ref[...] + split_mm(minus, gathered_inverse(next_ref, order))
 
 
-def call(kernel, outs, *args, scratch=(), scalars=0, name=None):
+def call(kernel, outs, *args, scratch=(), scalars=0, far=False, limit=24 * 2**20):
     vmem = pl.BlockSpec(memory_space=pltpu.VMEM)
+    place_in = pl.BlockSpec(memory_space=pltpu.HBM) if far else vmem
     return pl.pallas_call(
         kernel,
         out_shape=outs,
-        in_specs=[pl.BlockSpec(memory_space=pltpu.SMEM)] * scalars + [vmem] * (len(args) - scalars),
+        in_specs=[pl.BlockSpec(memory_space=pltpu.SMEM)] * scalars + [place_in] * (len(args) - scalars),
         out_specs=[vmem] * len(outs),
         scratch_shapes=list(scratch),
-        compiler_params=pltpu.CompilerParams(vmem_limit_bytes=VMEM_LIMIT),
-        name=name,
+        compiler_params=pltpu.CompilerParams(vmem_limit_bytes=limit),
     )(*args)
-
-
-VMEM_LIMIT = 24 * 2**20
 
 
 def on_device(rhs, inverse_t, u_factors, v_factors, tile_ranks):
@@ -243,7 +250,9 @@
     def gather(part):
         pieces = []
         for s in range(n_x):
-            moved = lax.ppermute(part, "x", [(i, (i + s) % n_x) for i in range(n_x)]) if s else part
+            moved = part
+            if s:
+                moved = lax.ppermute(part, "x", [(i, (i + s) % n_x) for i in range(n_x)])
             pieces += [moved, lax.ppermute(moved, "core", swap)]
         return pieces
 
@@ -279,40 +288,43 @@
     v_a, v_b, near = call(
         kernel(prep_kernel),
         [v_send, v_send, shape((order + u_rows, lanes), BF)],
-        ranks, inv_here, u_here, v_here, scalars=1, name="prep",
+        ranks, inv_here, u_here, v_here, scalars=1, far=True, limit=67043328 - 450 * 1024,
+        scratch=[
+            pltpu.VMEM((order, lanes), F32),
+            pltpu.VMEM((TURNS, rank, order), BF),
+            pltpu.VMEM((slots, slots, TURNS, rank, order), BF),
+            pltpu.SemaphoreType.DMA((3,)),
+        ],
     )
     near = gather(near)
     v_a, v_b = turn_rows([v_a, v_b])
+    later_u = u_here[1].reshape(slots, TURNS * rank, order)
+    nxt = gather(jnp.concatenate([inv_here[1].astype(BF)] + [
+        later_u[a, :, m * lanes : (m + 1) * lanes] for a in range(slots) for m in range(n_col)], axis=0))
+    z = gather(lax.dot_general(rhs_here, inv_here, (((2,), (1,)), ((0,), (0,))), precision=lax.Precision.HIGHEST,
+                               preferred_element_type=F32))
 
     msg, far_a, far_b = call(
         kernel(first_kernel), [messages, far_shape, far_shape],
-        rhs_here, v_a, v_b, *near, scratch=[near_scratch], name="first",
-    )
-
-    later_inv, later_u, msg, far_a, far_b = lax.optimization_barrier(
-        (inv_here[1], u_here[1], msg, far_a, far_b))
+        rhs_here, v_a, v_b, *near, scratch=[near_scratch],
+    )
+
+    far = gather(jnp.stack(turn_rows([far_a, far_b])))
     same, other = spread(msg)
-    far = gather(jnp.stack(turn_rows([far_a, far_b])))
-    later_u = later_u.reshape(slots, TURNS * rank, order)
-    nxt = gather(jnp.concatenate([later_inv.astype(BF)] + [
-        later_u[a, :, m * lanes : (m + 1) * lanes] for a in range(slots) for m in range(n_col)], axis=0))
 
     msg, minus, own = call(
         kernel(middle_kernel),
         [messages, shape((r_cols, order), F32), shape((width + rank - r_cols, r_cols), BF)],
         same, other, rhs_here, v_a, v_b, *far, *nxt,
-        scratch=solve_scratch + [pltpu.VMEM((n_col, TURNS, rank, width + rank), BF), next_scratch], name="middle",
-    )
-    rhs_late, inv_late, msg = lax.optimization_barrier((rhs_here, inv_here, msg))
+        scratch=solve_scratch + [pltpu.VMEM((n_col, TURNS, rank, width + rank), BF), next_scratch],
+    )
     same, other = spread(msg)
-    z = gather(lax.dot_general(rhs_late, inv_late, (((2,), (1,)), ((0,), (0,))), precision=lax.Precision.HIGHEST,
-                               preferred_element_type=F32))
     early, z_last = call(
         kernel(early_kernel), [shape((r_cols, order), F32)] * 2, own, *near, *z,
-        scratch=[near_scratch, pltpu.VMEM((n_col, slots, r_cols, lanes), F32)], name="early")
+        scratch=[near_scratch, pltpu.VMEM((n_col, slots, r_cols, lanes), F32)])
     (y,) = call(
         kernel(last_kernel), [shape((slots, r_cols, order), F32)],
-        same, other, minus, z_last, early, *nxt, scratch=solve_scratch + [next_scratch], name="last",
+        same, other, minus, z_last, early, *nxt, scratch=solve_scratch + [next_scratch],
     )
     return y[:, None]
 
@@ -329,6 +341,4 @@
         P(None, "row", None, col),
     )
     out_specs = P(None, "row", None, None)
-    return jax.shard_map(
-        on_device, mesh=fine, in_specs=in_specs, out_specs=out_specs, check_vma=False
-    )
+    return jax.shard_map(on_device, mesh=fine, in_specs=in_specs, out_specs=out_specs, check_vma=False)

time: 79.6 us -> 79.1 us (level)
  local copies, waits for them, and re-layouts: 3.75 us -> 1.13 us
  Pallas kernels: 6.88 us -> 8.92 us
  starting transfers between devices: 31.9 us -> 33.3 us
  waiting for transfers between devices: 20.1 us -> 18.9 us
    unnamed x20 -> x16, local copies, waits for them, and re-layouts: 3.72 us -> 1.11 us
    pallas_call x5, Pallas kernels: 6.88 us -> 8.92 us  [call(): pl.pallas_call(kernel, out_shape=outs, in_specs=[pl.BlockSpec(memory_spac...]
    ppermute x4, waiting for transfers between devices: 14.5 us -> 13.3 us  [gather(): moved = lax.ppermute(part, 'x', [(i, (i + s) % n_x) for i in range(n_x)])]
    ppermute x4, starting transfers between devices: 6.39 us -> 7.21 us  [turn_rows(): got.append(lax.ppermute(parts[s], everywhere, pairs))]
    ppermute x8, starting transfers between devices: 2.75 us -> 3.57 us  [gather(): pieces += [moved, lax.ppermute(moved, 'core', swap)]]
  transfers between devices with their start and end apart: 19 -> 19, of which waited for: 8 -> 7; matrix products, arithmetic and copies ran while one was open for 1% -> 2% of each run, Pallas kernels for 1% -> 1%
where the time goes in v4:
time: 79.1 us; the launch traced here: 78.7 us
  starting transfers between devices  33.3 us (42%)
  waiting for transfers between devices  18.9 us (24%)
  blocking collectives  15.9 us (20%)
  Pallas kernels  8.92 us (11%)
  local copies, waits for them, and re-layouts  1.13 us (1%)
    all_to_all x1, blocking collectives, spread(): lax.all_to_all(m, ('row', 'x'), split_axis=0, concat_axis=0, tiled=True)  15.9 us
    ppermute x4, waiting for transfers between devices, gather(): moved = lax.ppermute(part, 'x', [(i, (i + s) % n_x) for i in range(n_x)])  13.3 us
    ppermute x4, starting transfers between devices, gather(): moved = lax.ppermute(part, 'x', [(i, (i + s) % n_x) for i in range(n_x)])  12.1 us
    all_to_all x1, starting transfers between devices, spread(): lax.all_to_all(m, ('row', 'x'), split_axis=0, concat_axis=0, tiled=True)  9.89 us
    pallas_call x5, Pallas kernels, call(): pl.pallas_call(kernel, out_shape=outs, in_specs=[pl.BlockSpec(memory_spac...  8.92 us
    ppermute x4, starting transfers between devices, turn_rows(): got.append(lax.ppermute(parts[s], everywhere, pairs))  7.21 us
    ppermute x8, starting transfers between devices, gather(): pieces += [moved, lax.ppermute(moved, 'core', swap)]  3.57 us
    ppermute x8, waiting for transfers between devices, gather(): pieces += [moved, lax.ppermute(moved, 'core', swap)]  3.24 us
  transfers between devices with their start and end apart: 19, of which 7 were waited for; matrix products, arithmetic and copies ran while one was open for 2% of the time, Pallas kernels for 1%

profile of v4, /device:TPU:0, one launch (start us, length us, event | category | flops | bytes accessed | tf_op | source)
XLA Modules:
  0.0 78.7 jit_solution(2692764369641155596)
XLA Ops:
  0.0 2.6 %shard_map.55 = (bf16[3,32,512]{2,1,0:T(8,128)(2,1)}, bf16[3,32,512]{2,1,0:T(8,128)(2,1)}, bf16[768,128]{1,0:T(8,128)(2,1)}) custom-call(s32[2,1,1,4]{3,2,1,0:T(1,128)} %bitcast.68, f32[2,512,128]{2,1,0:T(8,128)} %bitcast.55, bf16[2,2,2,32,512]{4,3,2,1,0:T(8,128)(2,1)} %bitcast.56, bf16[2,2,2,32,512]{4,3,2,1,0:T(8,128)(2,1)} %bitcast.65), custom_call_target="tpu_custom_call" | custom-call | tf_op jit(solution)/shard_map/pallas_call | solution.py:218
  2.7 3.0 %collective-permute-start.3 = (bf16[768,128]{1,0:T(8,128)(2,1)}, bf16[768,128]{1,0:T(8,128)(2,1)S(1)}, u32[]{:S(2)}, u32[]{:S(2)}) collective-permute-start(bf16[768,128]{1,0:T(8,128)(2,1)} %get-tuple-element.18.refs_3_.refs_1_), channel_id=1, source_target_pairs={{0,2},{2,0},{1,3},{3,1},{4,6},{6,4},{5,7},{7,5},{8,10},{10,8},{9,1... | collective-permute-start | bytes 589832 | tf_op jit(solution)/shard_map/ppermute | solution.py:255
  5.7 1.5 %collective-permute-start = (bf16[3,32,512]{2,1,0:T(8,128)(2,1)}, bf16[3,32,512]{2,1,0:T(8,128)(2,1)S(1)}, u32[]{:S(2)}, u32[]{:S(2)}) collective-permute-start(bf16[3,32,512]{2,1,0:T(8,128)(2,1)} %get-tuple-element.16), channel_id=1, source_target_pairs={{0,0},{1,4},{2,8},{3,12},{4,1},{5,5},{6,9},{7,13},{8,2},{9,6},{10,... | collective-permute-start | bytes 294920 | tf_op jit(solution)/shard_map/ppermute | solution.py:267
  7.2 2.6 %collective-permute-start.1 = (bf16[3,32,512]{2,1,0:T(8,128)(2,1)}, bf16[3,32,512]{2,1,0:T(8,128)(2,1)S(1)}, u32[]{:S(2)}, u32[]{:S(2)}) collective-permute-start(bf16[3,32,512]{2,1,0:T(8,128)(2,1)} %get-tuple-element.17), channel_id=1, source_target_pairs={{0,16},{1,20},{2,24},{3,28},{4,17},{5,21},{6,25},{7,29},{8,18},{9,... | collective-permute-start | bytes 294920 | tf_op jit(solution)/shard_map/ppermute | solution.py:267
  9.8 0.0 copy-start
  9.8 0.0 copy-start.1
  9.9 1.0 %fusion.1 = bf16[1024,128]{1,0:T(8,128)(2,1)S(1)} fusion(f32[2,1,512,128]{3,2,1,0:T(8,128)} %param.6), kind=kLoop, calls=%fused_computation.2 | loop fusion | bytes 262144
  11.0 2.2 %collective-permute-start.4 = (bf16[768,128]{1,0:T(8,128)(2,1)S(1)}, bf16[768,128]{1,0:T(8,128)(2,1)S(1)}, u32[]{:S(2)}, u32[]{:S(2)}) collective-permute-start(bf16[768,128]{1,0:T(8,128)(2,1)S(1)} %collective-permute-done.3.refs_5_.refs_3_), channel_id=1, source_target_pairs={{0,1},{1,0},{2,3},{3,2},{4,5},{5,4},{6,7},{7,6},{8,9},{9,8},{10,11... | collective-permute-start | bytes 589832 | tf_op jit(solution)/shard_map/ppermute | solution.py:256
  13.2 1.0 %collective-permute-done.4.refs_6_.refs_4_ = bf16[768,128]{1,0:T(8,128)(2,1)S(1)} collective-permute-done((bf16[768,128]{1,0:T(8,128)(2,1)S(1)}, bf16[768,128]{1,0:T(8,128)(2,1)S(1)}, u32[]{:S(2)}, u32[]{:S(2)}) %collective-permute-start.4) | collective-permute-done | bytes 196640 | tf_op jit(solution)/shard_map/ppermute | solution.py:256
  14.2 1.5 %shard_map.56 = (bf16[16,32,256]{2,1,0:T(8,128)(2,1)}, bf16[32,288]{1,0:T(8,128)(2,1)S(1)}, bf16[32,288]{1,0:T(8,128)(2,1)S(1)}) custom-call(f32[2,64,512]{2,1,0:T(8,128)S(1)} %bitcast.53, bf16[3,32,512]{2,1,0:T(8,128)(2,1)S(1)} %collective-permute-done.refs_1_.refs_3_, bf16[3,32,512]{2,1,0:T(8,128)(2,1)S(1)} %collective-permute-done.1.refs_2_.refs_4_, ...), custom_call_target="tpu_custom_call" | custom-call | tf_op jit(solution)/shard_map/pallas_call | solution.py:218
  15.8 9.9 %all-to-all-start = ((bf16[16,32,256]{2,1,0:T(8,128)(2,1)}), bf16[16,32,256]{2,1,0:T(8,128)(2,1)S(1)}, u32[]{:S(2)}, u32[]{:S(2)}) async-start(bf16[16,32,256]{2,1,0:T(8,128)(2,1)} %get-tuple-element.19), calls=%async_computation | async-start | bytes 524288 | tf_op jit(solution)/shard_map/all_to_all | solution.py:271
  25.7 2.0 %collective-permute-start.12 = (bf16[1024,128]{1,0:T(8,128)(2,1)S(1)}, bf16[1024,128]{1,0:T(8,128)(2,1)S(1)}, u32[]{:S(2)}, u32[]{:S(2)}) collective-permute-start(bf16[1024,128]{1,0:T(8,128)(2,1)S(1)} %constant_dynamic-update-slice_fusion.refs_9_.refs_5_), channel_id=1, source_target_pairs={{0,2},{2,0},{1,3},{3,1},{4,6},{6,4},{5,7},{7,5},{8,10},{10,8},{9,1... | collective-permute-start | bytes 786440 | tf_op jit(solution)/shard_map/ppermute | solution.py:255
  27.7 8.5 %collective-permute-done.12.refs_11_.refs_7_ = bf16[1024,128]{1,0:T(8,128)(2,1)S(1)} collective-permute-done((bf16[1024,128]{1,0:T(8,128)(2,1)S(1)}, bf16[1024,128]{1,0:T(8,128)(2,1)S(1)}, u32[]{:S(2)}, u32[]{:S(2)}) %collective-permute-start.12) | collective-permute-done | bytes 262176 | tf_op jit(solution)/shard_map/ppermute | solution.py:255
  36.2 0.5 collective-permute-start.5
  36.7 0.7 collective-permute-start.6
  37.3 2.4 %collective-permute-start.7 = (bf16[32,288]{1,0:T(8,128)(2,1)S(1)}, bf16[32,288]{1,0:T(8,128)(2,1)S(1)}, u32[]{:S(2)}, u32[]{:S(2)}) collective-permute-start(bf16[32,288]{1,0:T(8,128)(2,1)S(1)} %get-tuple-element.21), channel_id=1, source_target_pairs={{0,16},{1,20},{2,24},{3,28},{4,17},{5,21},{6,25},{7,29},{8,18},{9,... | collective-permute-start | bytes 55304 | tf_op jit(solution)/shard_map/ppermute | solution.py:267
  39.8 2.4 %collective-permute-done.7 = bf16[32,288]{1,0:T(8,128)(2,1)S(1)} collective-permute-done((bf16[32,288]{1,0:T(8,128)(2,1)S(1)}, bf16[32,288]{1,0:T(8,128)(2,1)S(1)}, u32[]{:S(2)}, u32[]{:S(2)}) %collective-permute-start.7) | collective-permute-done | bytes 18464 | tf_op jit(solution)/shard_map/ppermute | solution.py:267
  42.1 6.2 %collective-permute-start.9 = (bf16[2,32,288]{2,1,0:T(8,128)(2,1)S(1)}, bf16[2,32,288]{2,1,0:T(8,128)(2,1)S(1)}, u32[]{:S(2)}, u32[]{:S(2)}) collective-permute-start(bf16[2,32,288]{2,1,0:T(8,128)(2,1)S(1)} %pad_maximum_fusion.refs_5_), channel_id=1, source_target_pairs={{0,2},{2,0},{1,3},{3,1},{4,6},{6,4},{5,7},{7,5},{8,10},{10,8},{9,1... | collective-permute-start | bytes 110600 | tf_op jit(solution)/shard_map/ppermute | solution.py:255
  48.4 0.9 %collective-permute-start.8 = (bf16[2,32,288]{2,1,0:T(8,128)(2,1)S(1)}, bf16[2,32,288]{2,1,0:T(8,128)(2,1)S(1)}, u32[]{:S(2)}, u32[]{:S(2)}) collective-permute-start(bf16[2,32,288]{2,1,0:T(8,128)(2,1)S(1)} %pad_maximum_fusion.refs_5_), channel_id=1, source_target_pairs={{0,1},{1,0},{2,3},{3,2},{4,5},{5,4},{6,7},{7,6},{8,9},{9,8},{10,11... | collective-permute-start | bytes 110600 | tf_op jit(solution)/shard_map/ppermute | solution.py:256
  49.2 1.3 %collective-permute-done.9.refs_7_ = bf16[2,32,288]{2,1,0:T(8,128)(2,1)S(1)} collective-permute-done((bf16[2,32,288]{2,1,0:T(8,128)(2,1)S(1)}, bf16[2,32,288]{2,1,0:T(8,128)(2,1)S(1)}, u32[]{:S(2)}, u32[]{:S(2)}) %collective-permute-start.9) | collective-permute-done | bytes 36896 | tf_op jit(solution)/shard_map/ppermute | solution.py:255
  50.5 0.3 collective-permute-start.10
  50.8 0.9 %collective-permute-done.10.refs_8_ = bf16[2,32,288]{2,1,0:T(8,128)(2,1)S(1)} collective-permute-done((bf16[2,32,288]{2,1,0:T(8,128)(2,1)S(1)}, bf16[2,32,288]{2,1,0:T(8,128)(2,1)S(1)}, u32[]{:S(2)}, u32[]{:S(2)}) %collective-permute-start.10) | collective-permute-done | bytes 36896 | tf_op jit(solution)/shard_map/ppermute | solution.py:256
  51.8 2.0 %shard_map.57 = (bf16[16,32,256]{2,1,0:T(8,128)(2,1)S(1)}, f32[64,512]{1,0:T(8,128)S(1)}, bf16[224,64]{1,0:T(8,128)(2,1)S(1)}) custom-call(bf16[16,32,256]{2,1,0:T(8,128)(2,1)S(1)} %all-to-all-done.refs_0_, bf16[16,32,256]{2,1,0:T(8,128)(2,1)S(1)} %collective-permute-done.5.refs_1_, f32[2,64,512]{2,1,0:T(8,128)S(1)} %bitcast.54, ...), custom_call_target="tpu_custom_call" | custom-call | tf_op jit(solution)/shard_map/pallas_call | solution.py:218
  53.8 0.0 copy-start.2
  53.8 15.9 %all_to_all.10.refs_0_ = bf16[16,32,256]{2,1,0:T(8,128)(2,1)S(1)} all-to-all(bf16[16,32,256]{2,1,0:T(8,128)(2,1)S(1)} %get-tuple-element.22), channel_id=1, replica_groups=mesh['row'=8,'x'=2,'core'=2] {'row','x'}, dimensions={0} | all-to-all | bytes 524288 | tf_op jit(solution)/shard_map/all_to_all | solution.py:271
  69.7 0.4 fusion.2.refs_5_
  70.2 0.8 %collective-permute-start.16 = (f32[2,64,128]{2,1,0:T(8,128)S(1)}, f32[2,64,128]{2,1,0:T(8,128)S(1)}, u32[]{:S(2)}, u32[]{:S(2)}) collective-permute-start(f32[2,64,128]{2,1,0:T(8,128)S(1)} %fusion.2.refs_5_), channel_id=1, source_target_pairs={{0,2},{2,0},{1,3},{3,1},{4,6},{6,4},{5,7},{7,5},{8,10},{10,8},{9,1... | collective-permute-start | bytes 196616 | tf_op jit(solution)/shard_map/ppermute | solution.py:255
  71.0 0.2 collective-permute-start.15
  71.2 3.5 %collective-permute-done.16.refs_7_ = f32[2,64,128]{2,1,0:T(8,128)S(1)} collective-permute-done((f32[2,64,128]{2,1,0:T(8,128)S(1)}, f32[2,64,128]{2,1,0:T(8,128)S(1)}, u32[]{:S(2)}, u32[]{:S(2)}) %collective-permute-start.16) | collective-permute-done | bytes 65568 | tf_op jit(solution)/shard_map/ppermute | solution.py:255
  74.7 1.2 %collective-permute-done.17.refs_8_ = f32[2,64,128]{2,1,0:T(8,128)S(1)} collective-permute-done((f32[2,64,128]{2,1,0:T(8,128)S(1)}, f32[2,64,128]{2,1,0:T(8,128)S(1)}, u32[]{:S(2)}, u32[]{:S(2)}) %collective-permute-start.17) | collective-permute-done | bytes 65568 | tf_op jit(solution)/shard_map/ppermute | solution.py:256
  76.0 0.5 shard_map.58
  76.5 2.2 %shard_map.59 = f32[2,64,512]{2,1,0:T(8,128)} custom-call(bf16[16,32,256]{2,1,0:T(8,128)(2,1)S(1)} %all_to_all.10.refs_0_, bf16[16,32,256]{2,1,0:T(8,128)(2,1)S(1)} %collective-permute-done.14.refs_1_, f32[64,512]{1,0:T(8,128)S(1)} %get-tuple-element.23.refs_2_, f32[64,512]{1,0:T(8,128)S(1)} %get-tuple-element.25.refs_3_, ...), custom_call_target="tpu_custom_call" | custom-call | tf_op jit(solution)/shard_map/pallas_call | solution.py:218
  (32 shorter events, 0.2 us)
Async XLA Ops:
  0.0 9.8 %copy-start.3 = (bf16[2,1,4,1,32,512]{5,4,3,2,1,0:T(8,128)(2,1)S(1)}, bf16[2,1,4,1,32,512]{5,4,3,2,1,0:T(8,128)(2,1)}, u32[]{:S(2)}) copy-start(bf16[2,1,4,1,32,512]{5,4,3,2,1,0:T(8,128)(2,1)} %param.7) | copy-start | bytes 786436
  2.7 8.3 %collective-permute-start.3 = (bf16[768,128]{1,0:T(8,128)(2,1)}, bf16[768,128]{1,0:T(8,128)(2,1)S(1)}, u32[]{:S(2)}, u32[]{:S(2)}) collective-permute-start(bf16[768,128]{1,0:T(8,128)(2,1)} %get-tuple-element.18.refs_3_.refs_1_), channel_id=1, source_target_pairs={{0,2},{2,0},{1,3},{3,1},{4,6},{6,4},{5,7},{7,5},{8,10},{10,8},{9,1... | collective-permute-start | bytes 589832 | tf_op jit(solution)/shard_map/ppermute | solution.py:255
  5.7 7.5 %collective-permute-start.2 = (bf16[768,128]{1,0:T(8,128)(2,1)}, bf16[768,128]{1,0:T(8,128)(2,1)S(1)}, u32[]{:S(2)}, u32[]{:S(2)}) collective-permute-start(bf16[768,128]{1,0:T(8,128)(2,1)} %get-tuple-element.18.refs_3_.refs_1_), channel_id=1, source_target_pairs={{0,1},{1,0},{2,3},{3,2},{4,5},{5,4},{6,7},{7,6},{8,9},{9,8},{10,11... | collective-permute-start | bytes 589832 | tf_op jit(solution)/shard_map/ppermute | solution.py:256
  5.7 7.5 %collective-permute-start = (bf16[3,32,512]{2,1,0:T(8,128)(2,1)}, bf16[3,32,512]{2,1,0:T(8,128)(2,1)S(1)}, u32[]{:S(2)}, u32[]{:S(2)}) collective-permute-start(bf16[3,32,512]{2,1,0:T(8,128)(2,1)} %get-tuple-element.16), channel_id=1, source_target_pairs={{0,0},{1,4},{2,8},{3,12},{4,1},{5,5},{6,9},{7,13},{8,2},{9,6},{10,... | collective-permute-start | bytes 294920 | tf_op jit(solution)/shard_map/ppermute | solution.py:267
  7.2 5.9 %collective-permute-start.1 = (bf16[3,32,512]{2,1,0:T(8,128)(2,1)}, bf16[3,32,512]{2,1,0:T(8,128)(2,1)S(1)}, u32[]{:S(2)}, u32[]{:S(2)}) collective-permute-start(bf16[3,32,512]{2,1,0:T(8,128)(2,1)} %get-tuple-element.17), channel_id=1, source_target_pairs={{0,16},{1,20},{2,24},{3,28},{4,17},{5,21},{6,25},{7,29},{8,18},{9,... | collective-permute-start | bytes 294920 | tf_op jit(solution)/shard_map/ppermute | solution.py:267
  9.8 4.4 %copy-start = (f32[2,1,64,512]{3,2,1,0:T(8,128)S(1)}, f32[2,1,64,512]{3,2,1,0:T(8,128)}, u32[]{:S(2)}) copy-start(f32[2,1,64,512]{3,2,1,0:T(8,128)} %param.5) | copy-start | bytes 786436
  9.8 4.4 %copy-start.1 = (bf16[768,128]{1,0:T(8,128)(2,1)S(1)}, bf16[768,128]{1,0:T(8,128)(2,1)}, u32[]{:S(2)}) copy-start(bf16[768,128]{1,0:T(8,128)(2,1)} %get-tuple-element.18.refs_3_.refs_1_) | copy-start | bytes 589828
  11.0 3.3 %collective-permute-start.4 = (bf16[768,128]{1,0:T(8,128)(2,1)S(1)}, bf16[768,128]{1,0:T(8,128)(2,1)S(1)}, u32[]{:S(2)}, u32[]{:S(2)}) collective-permute-start(bf16[768,128]{1,0:T(8,128)(2,1)S(1)} %collective-permute-done.3.refs_5_.refs_3_), channel_id=1, source_target_pairs={{0,1},{1,0},{2,3},{3,2},{4,5},{5,4},{6,7},{7,6},{8,9},{9,8},{10,11... | collective-permute-start | bytes 589832 | tf_op jit(solution)/shard_map/ppermute | solution.py:256
  15.8 20.4 %all-to-all-start = ((bf16[16,32,256]{2,1,0:T(8,128)(2,1)}), bf16[16,32,256]{2,1,0:T(8,128)(2,1)S(1)}, u32[]{:S(2)}, u32[]{:S(2)}) async-start(bf16[16,32,256]{2,1,0:T(8,128)(2,1)} %get-tuple-element.19), calls=%async_computation | async-start | bytes 524288 | tf_op jit(solution)/shard_map/all_to_all | solution.py:271
  25.7 10.5 %collective-permute-start.12 = (bf16[1024,128]{1,0:T(8,128)(2,1)S(1)}, bf16[1024,128]{1,0:T(8,128)(2,1)S(1)}, u32[]{:S(2)}, u32[]{:S(2)}) collective-permute-start(bf16[1024,128]{1,0:T(8,128)(2,1)S(1)} %constant_dynamic-update-slice_fusion.refs_9_.refs_5_), channel_id=1, source_target_pairs={{0,2},{2,0},{1,3},{3,1},{4,6},{6,4},{5,7},{7,5},{8,10},{10,8},{9,1... | collective-permute-start | bytes 786440 | tf_op jit(solution)/shard_map/ppermute | solution.py:255
  27.7 23.1 %collective-permute-start.11 = (bf16[1024,128]{1,0:T(8,128)(2,1)S(1)}, bf16[1024,128]{1,0:T(8,128)(2,1)S(1)}, u32[]{:S(2)}, u32[]{:S(2)}) collective-permute-start(bf16[1024,128]{1,0:T(8,128)(2,1)S(1)} %constant_dynamic-update-slice_fusion.refs_9_.refs_5_), channel_id=1, source_target_pairs={{0,1},{1,0},{2,3},{3,2},{4,5},{5,4},{6,7},{7,6},{8,9},{9,8},{10,11... | collective-permute-start | bytes 786440 | tf_op jit(solution)/shard_map/ppermute | solution.py:256
  36.2 15.6 %collective-permute-start.13 = (bf16[1024,128]{1,0:T(8,128)(2,1)S(1)}, bf16[1024,128]{1,0:T(8,128)(2,1)S(1)}, u32[]{:S(2)}, u32[]{:S(2)}) collective-permute-start(bf16[1024,128]{1,0:T(8,128)(2,1)S(1)} %collective-permute-done.12.refs_11_.refs_7_), channel_id=1, source_target_pairs={{0,1},{1,0},{2,3},{3,2},{4,5},{5,4},{6,7},{7,6},{8,9},{9,8},{10,11... | collective-permute-start | bytes 786440 | tf_op jit(solution)/shard_map/ppermute | solution.py:256
  36.2 15.6 %collective-permute-start.5 = (bf16[16,32,256]{2,1,0:T(8,128)(2,1)S(1)}, bf16[16,32,256]{2,1,0:T(8,128)(2,1)S(1)}, u32[]{:S(2)}, u32[]{:S(2)}) collective-permute-start(bf16[16,32,256]{2,1,0:T(8,128)(2,1)S(1)} %all-to-all-done.refs_0_), channel_id=1, source_target_pairs={{0,1},{1,0},{2,3},{3,2},{4,5},{5,4},{6,7},{7,6},{8,9},{9,8},{10,11... | collective-permute-start | bytes 786440 | tf_op jit(solution)/shard_map/ppermute | solution.py:272
  36.7 3.1 %collective-permute-start.6 = (bf16[32,288]{1,0:T(8,128)(2,1)S(1)}, bf16[32,288]{1,0:T(8,128)(2,1)S(1)}, u32[]{:S(2)}, u32[]{:S(2)}) collective-permute-start(bf16[32,288]{1,0:T(8,128)(2,1)S(1)} %get-tuple-element.20), channel_id=1, source_target_pairs={{0,0},{1,4},{2,8},{3,12},{4,1},{5,5},{6,9},{7,13},{8,2},{9,6},{10,... | collective-permute-start | bytes 55304 | tf_op jit(solution)/shard_map/ppermute | solution.py:267
  37.3 4.8 %collective-permute-start.7 = (bf16[32,288]{1,0:T(8,128)(2,1)S(1)}, bf16[32,288]{1,0:T(8,128)(2,1)S(1)}, u32[]{:S(2)}, u32[]{:S(2)}) collective-permute-start(bf16[32,288]{1,0:T(8,128)(2,1)S(1)} %get-tuple-element.21), channel_id=1, source_target_pairs={{0,16},{1,20},{2,24},{3,28},{4,17},{5,21},{6,25},{7,29},{8,18},{9,... | collective-permute-start | bytes 55304 | tf_op jit(solution)/shard_map/ppermute | solution.py:267
  42.1 8.4 %collective-permute-start.9 = (bf16[2,32,288]{2,1,0:T(8,128)(2,1)S(1)}, bf16[2,32,288]{2,1,0:T(8,128)(2,1)S(1)}, u32[]{:S(2)}, u32[]{:S(2)}) collective-permute-start(bf16[2,32,288]{2,1,0:T(8,128)(2,1)S(1)} %pad_maximum_fusion.refs_5_), channel_id=1, source_target_pairs={{0,2},{2,0},{1,3},{3,1},{4,6},{6,4},{5,7},{7,5},{8,10},{10,8},{9,1... | collective-permute-start | bytes 110600 | tf_op jit(solution)/shard_map/ppermute | solution.py:255
  48.4 2.4 %collective-permute-start.8 = (bf16[2,32,288]{2,1,0:T(8,128)(2,1)S(1)}, bf16[2,32,288]{2,1,0:T(8,128)(2,1)S(1)}, u32[]{:S(2)}, u32[]{:S(2)}) collective-permute-start(bf16[2,32,288]{2,1,0:T(8,128)(2,1)S(1)} %pad_maximum_fusion.refs_5_), channel_id=1, source_target_pairs={{0,1},{1,0},{2,3},{3,2},{4,5},{5,4},{6,7},{7,6},{8,9},{9,8},{10,11... | collective-permute-start | bytes 110600 | tf_op jit(solution)/shard_map/ppermute | solution.py:256
  50.5 1.2 %collective-permute-start.10 = (bf16[2,32,288]{2,1,0:T(8,128)(2,1)S(1)}, bf16[2,32,288]{2,1,0:T(8,128)(2,1)S(1)}, u32[]{:S(2)}, u32[]{:S(2)}) collective-permute-start(bf16[2,32,288]{2,1,0:T(8,128)(2,1)S(1)} %collective-permute-done.9.refs_7_), channel_id=1, source_target_pairs={{0,1},{1,0},{2,3},{3,2},{4,5},{5,4},{6,7},{7,6},{8,9},{9,8},{10,11... | collective-permute-start | bytes 110600 | tf_op jit(solution)/shard_map/ppermute | solution.py:256
  53.8 15.9 %copy-start.2 = (f32[2,1,512,128]{3,2,1,0:T(8,128)S(1)}, f32[2,1,512,128]{3,2,1,0:T(8,128)}, u32[]{:S(2)}) copy-start(f32[2,1,512,128]{3,2,1,0:T(8,128)} %param.6) | copy-start | bytes 1572868
  69.7 6.8 %collective-permute-start.14 = (bf16[16,32,256]{2,1,0:T(8,128)(2,1)S(1)}, bf16[16,32,256]{2,1,0:T(8,128)(2,1)S(1)}, u32[]{:S(2)}, u32[]{:S(2)}) collective-permute-start(bf16[16,32,256]{2,1,0:T(8,128)(2,1)S(1)} %all_to_all.10.refs_0_), channel_id=1, source_target_pairs={{0,1},{1,0},{2,3},{3,2},{4,5},{5,4},{6,7},{7,6},{8,9},{9,8},{10,11... | collective-permute-start | bytes 786440 | tf_op jit(solution)/shard_map/ppermute | solution.py:272
  70.2 4.6 %collective-permute-start.16 = (f32[2,64,128]{2,1,0:T(8,128)S(1)}, f32[2,64,128]{2,1,0:T(8,128)S(1)}, u32[]{:S(2)}, u32[]{:S(2)}) collective-permute-start(f32[2,64,128]{2,1,0:T(8,128)S(1)} %fusion.2.refs_5_), channel_id=1, source_target_pairs={{0,2},{2,0},{1,3},{3,1},{4,6},{6,4},{5,7},{7,5},{8,10},{10,8},{9,1... | collective-permute-start | bytes 196616 | tf_op jit(solution)/shard_map/ppermute | solution.py:255
  71.0 3.7 %collective-permute-start.15 = (f32[2,64,128]{2,1,0:T(8,128)S(1)}, f32[2,64,128]{2,1,0:T(8,128)S(1)}, u32[]{:S(2)}, u32[]{:S(2)}) collective-permute-start(f32[2,64,128]{2,1,0:T(8,128)S(1)} %fusion.2.refs_5_), channel_id=1, source_target_pairs={{0,1},{1,0},{2,3},{3,2},{4,5},{5,4},{6,7},{7,6},{8,9},{9,8},{10,11... | collective-permute-start | bytes 196616 | tf_op jit(solution)/shard_map/ppermute | solution.py:256
  74.7 1.3 %collective-permute-start.17 = (f32[2,64,128]{2,1,0:T(8,128)S(1)}, f32[2,64,128]{2,1,0:T(8,128)S(1)}, u32[]{:S(2)}, u32[]{:S(2)}) collective-permute-start(f32[2,64,128]{2,1,0:T(8,128)S(1)} %collective-permute-done.16.refs_7_), channel_id=1, source_target_pairs={{0,1},{1,0},{2,3},{3,2},{4,5},{5,4},{6,7},{7,6},{8,9},{9,8},{10,11... | collective-permute-start | bytes 196616 | tf_op jit(solution)/shard_map/ppermute | solution.py:256

commit v5 on v4

--- a/solution.py
+++ b/solution.py
@@ -184,32 +184,39 @@
     own_ref[...] = q_ref[row][r_cols:, :]
 
 
+def gathered_z(ref, at, r_cols):
+    parts = [jnp.concatenate([ref[c, start : start + r_cols, :] for c in range(ref.shape[0])], axis=1).astype(F32)
+             for start in (at, at + r_cols)]
+    return parts[0] + parts[1]
+
+
 def early_kernel(dims, *refs):
-    n_row, n_col, _, rank, _, _ = dims
+    n_row, n_col, r_cols, rank, _, _ = dims
     own_ref = refs[0]
-    nears, zs = refs[1 : 1 + n_col], refs[1 + n_col : 1 + 2 * n_col]
-    y_ref, z_out_ref, near_ref, z_ref = refs[1 + 2 * n_col :]
+    nears, nexts = refs[1 : 1 + n_col], refs[1 + n_col : 1 + 2 * n_col]
+    y_ref, near_ref, next_ref = refs[1 + 2 * n_col :]
     order = y_ref.shape[1]
+    at = order + 2 * n_col * TURNS * rank
     join(near_ref, nears)
-    join(z_ref, zs)
+    join(next_ref, nexts)
     minus = lax.dot_general(own_ref[...], gathered_u(near_ref, order, rank, n_row - 1), TN, preferred_element_type=F32)
-    z = jnp.concatenate([z_ref[c, 0] for c in range(n_col)], axis=1)
-    y_ref[...] = z + split_mm(minus, gathered_inverse(near_ref, order))
-    z_out_ref[...] = jnp.concatenate([z_ref[c, 1] for c in range(n_col)], axis=1)
+    y_ref[...] = gathered_z(next_ref, at, r_cols) + split_mm(minus, gathered_inverse(near_ref, order))
 
 
 def last_kernel(dims, *refs):
     n_row, n_col, r_cols, rank, _, _ = dims
-    same_ref, other_ref, minus_ref, z_ref, early_ref = refs[:5]
-    y_ref, g_ref, q_ref, next_ref = refs[5 + n_col :]
+    same_ref, other_ref, minus_ref, early_ref = refs[:4]
+    y_ref, g_ref, q_ref, next_ref = refs[4 + n_col :]
     order = minus_ref.shape[1]
+    rows = n_col * TURNS * rank
     y_ref[0] = early_ref[...]
-    join(next_ref, refs[5 : 5 + n_col])
+    join(next_ref, refs[4 : 4 + n_col])
     solve(dims, same_ref, other_ref, g_ref, q_ref, None)
     own = q_ref[lax.axis_index("row")][r_cols:, :]
-    u = gathered_u(next_ref, order + n_col * TURNS * rank, rank, n_row - 1)
+    u = gathered_u(next_ref, order + rows, rank, n_row - 1)
     minus = minus_ref[...] + lax.dot_general(own, u, TN, preferred_element_type=F32)
-    y_ref[1] = z_ref[...] + split_mm(minus, gathered_inverse(next_ref, order))
+    z = gathered_z(next_ref, order + 2 * rows + 2 * r_cols, r_cols)
+    y_ref[1] = z + split_mm(minus, gathered_inverse(next_ref, order))
 
 
 def call(kernel, outs, *args, scratch=(), scalars=0, far=False, limit=24 * 2**20):
@@ -278,7 +285,7 @@
     messages = shape((n_row * n_x, rank, width), BF)
     far_shape = shape((rank, width + rank), BF)
     near_scratch = pltpu.VMEM((n_col, order + u_rows, lanes), BF)
-    next_scratch = pltpu.VMEM((n_col, order + 2 * u_rows, lanes), BF)
+    next_scratch = pltpu.VMEM((n_col, order + 2 * u_rows + 4 * r_cols, lanes), BF)
     solve_scratch = [
         pltpu.VMEM((2, n_row * n_x, rank, width), BF),
         pltpu.VMEM((n_row, width + rank, r_cols), BF),
@@ -298,18 +305,22 @@
     )
     near = gather(near)
     v_a, v_b = turn_rows([v_a, v_b])
-    later_u = u_here[1].reshape(slots, TURNS * rank, order)
-    nxt = gather(jnp.concatenate([inv_here[1].astype(BF)] + [
-        later_u[a, :, m * lanes : (m + 1) * lanes] for a in range(slots) for m in range(n_col)], axis=0))
-    z = gather(lax.dot_general(rhs_here, inv_here, (((2,), (1,)), ((0,), (0,))), precision=lax.Precision.HIGHEST,
-                               preferred_element_type=F32))
-
     msg, far_a, far_b = call(
         kernel(first_kernel), [messages, far_shape, far_shape],
         rhs_here, v_a, v_b, *near, scratch=[near_scratch],
     )
 
+    rhs_late, inv_late, later_u, msg, far_a, far_b = lax.optimization_barrier(
+        (rhs_here, inv_here, u_here[1], msg, far_a, far_b))
     far = gather(jnp.stack(turn_rows([far_a, far_b])))
+    z = lax.dot_general(rhs_late, inv_late, (((2,), (1,)), ((0,), (0,))), precision=lax.Precision.HIGHEST,
+                        preferred_element_type=F32)
+    z_high = lax.reduce_precision(z, 8, 7)
+    z_low = z - z_high
+    later_u = later_u.reshape(slots, TURNS * rank, order)
+    nxt = gather(jnp.concatenate([inv_late[1].astype(BF)] + [
+        later_u[a, :, m * lanes : (m + 1) * lanes] for a in range(slots) for m in range(n_col)] + [
+        part[a].astype(BF) for a in range(slots) for part in (z_high, z_low)], axis=0))
     same, other = spread(msg)
 
     msg, minus, own = call(
@@ -319,12 +330,12 @@
         scratch=solve_scratch + [pltpu.VMEM((n_col, TURNS, rank, width + rank), BF), next_scratch],
     )
     same, other = spread(msg)
-    early, z_last = call(
-        kernel(early_kernel), [shape((r_cols, order), F32)] * 2, own, *near, *z,
-        scratch=[near_scratch, pltpu.VMEM((n_col, slots, r_cols, lanes), F32)])
+    (early,) = call(
+        kernel(early_kernel), [shape((r_cols, order), F32)], own, *near, *nxt,
+        scratch=[near_scratch, next_scratch])
     (y,) = call(
         kernel(last_kernel), [shape((slots, r_cols, order), F32)],
-        same, other, minus, z_last, early, *nxt, scratch=solve_scratch + [next_scratch],
+        same, other, minus, early, *nxt, scratch=solve_scratch + [next_scratch],
     )
     return y[:, None]
 

time: 79.1 us -> 82.1 us (1.038)
  waiting for transfers between devices: 18.9 us -> 22.7 us
    ppermute x4, waiting for transfers between devices: 2.36 us -> 5.09 us  [turn_rows(): got.append(lax.ppermute(parts[s], everywhere, pairs))]
    ppermute x8 -> x6, starting transfers between devices: 3.57 us -> 1.15 us  [gather(): pieces += [moved, lax.ppermute(moved, 'core', swap)]]
    ppermute x4 -> x3, waiting for transfers between devices: 13.3 us -> 15.7 us  [gather(): moved = lax.ppermute(part, 'x', [(i, (i + s) % n_x) for i in range(n_x)])]
    ppermute x8 -> x6, waiting for transfers between devices: 3.24 us -> 0.96 us  [gather(): pieces += [moved, lax.ppermute(moved, 'core', swap)]]
    all_to_all x1, starting transfers between devices: 9.89 us -> 11.8 us  [spread(): lax.all_to_all(m, ('row', 'x'), split_axis=0, concat_axis=0, tiled=True)]
    ppermute x2, waiting for transfers between devices: 0.01 us -> 1.02 us  [spread(): return (same, lax.ppermute(same, 'core', swap))]
    ppermute x4 -> x3, starting transfers between devices: 12.1 us -> 11.4 us  [gather(): moved = lax.ppermute(part, 'x', [(i, (i + s) % n_x) for i in range(n_x)])]
  transfers between devices with their start and end apart: 19 -> 16, of which waited for: 7 -> 7; matrix products, arithmetic and copies ran while one was open for 2% -> 1% of each run, Pallas kernels for 1% -> 1%
where the time goes in v5:
time: 82.1 us; the launch traced here: 81.8 us
  starting transfers between devices  32.6 us (40%)
  waiting for transfers between devices  22.7 us (28%)
  blocking collectives  15.7 us (19%)
  Pallas kernels  9 us (11%)
  local copies, waits for them, and re-layouts  1.09 us (1%)
    all_to_all x1, blocking collectives, spread(): lax.all_to_all(m, ('row', 'x'), split_axis=0, concat_axis=0, tiled=True)  15.7 us
    ppermute x3, waiting for transfers between devices, gather(): moved = lax.ppermute(part, 'x', [(i, (i + s) % n_x) for i in range(n_x)])  15.7 us
    all_to_all x1, starting transfers between devices, spread(): lax.all_to_all(m, ('row', 'x'), split_axis=0, concat_axis=0, tiled=True)  11.8 us
    ppermute x3, starting transfers between devices, gather(): moved = lax.ppermute(part, 'x', [(i, (i + s) % n_x) for i in range(n_x)])  11.4 us
    pallas_call x5, Pallas kernels, call(): pl.pallas_call(kernel, out_shape=outs, in_specs=[pl.BlockSpec(memory_spac...  9 us
    ppermute x4, starting transfers between devices, turn_rows(): got.append(lax.ppermute(parts[s], everywhere, pairs))  7.64 us
    ppermute x4, waiting for transfers between devices, turn_rows(): got.append(lax.ppermute(parts[s], everywhere, pairs))  5.09 us
  transfers between devices with their start and end apart: 16, of which 7 were waited for; matrix products, arithmetic and copies ran while one was open for 1% of the time, Pallas kernels for 1%

profile of v5, /device:TPU:0, one launch (start us, length us, event | category | flops | bytes accessed | tf_op | source)
XLA Modules:
  0.0 81.8 jit_solution(18372386876267425471)
XLA Ops:
  0.0 2.7 %shard_map.55 = (bf16[3,32,512]{2,1,0:T(8,128)(2,1)}, bf16[3,32,512]{2,1,0:T(8,128)(2,1)}, bf16[768,128]{1,0:T(8,128)(2,1)}) custom-call(s32[2,1,1,4]{3,2,1,0:T(1,128)} %bitcast.86, f32[2,512,128]{2,1,0:T(8,128)} %bitcast.71, bf16[2,2,2,32,512]{4,3,2,1,0:T(8,128)(2,1)} %bitcast.74, bf16[2,2,2,32,512]{4,3,2,1,0:T(8,128)(2,1)} %bitcast.83), custom_call_target="tpu_custom_call" | custom-call | tf_op jit(solution)/shard_map/pallas_call | solution.py:225
  2.7 0.0 copy-start
  2.7 3.0 %collective-permute-start.3 = (bf16[768,128]{1,0:T(8,128)(2,1)}, bf16[768,128]{1,0:T(8,128)(2,1)S(1)}, u32[]{:S(2)}, u32[]{:S(2)}) collective-permute-start(bf16[768,128]{1,0:T(8,128)(2,1)} %get-tuple-element.22.refs_3_.refs_1_), channel_id=1, source_target_pairs={{0,2},{2,0},{1,3},{3,1},{4,6},{6,4},{5,7},{7,5},{8,10},{10,8},{9,1... | collective-permute-start | bytes 589832 | tf_op jit(solution)/shard_map/ppermute | solution.py:262
  5.7 0.0 collective-permute-start.2
  5.7 5.1 %collective-permute-done.3.refs_5_.refs_3_ = bf16[768,128]{1,0:T(8,128)(2,1)S(1)} collective-permute-done((bf16[768,128]{1,0:T(8,128)(2,1)}, bf16[768,128]{1,0:T(8,128)(2,1)S(1)}, u32[]{:S(2)}, u32[]{:S(2)}) %collective-permute-start.3) | collective-permute-done | bytes 196640 | tf_op jit(solution)/shard_map/ppermute | solution.py:262
  10.8 0.0 collective-permute-start.4
  10.8 1.5 %collective-permute-start = (bf16[3,32,512]{2,1,0:T(8,128)(2,1)}, bf16[3,32,512]{2,1,0:T(8,128)(2,1)S(1)}, u32[]{:S(2)}, u32[]{:S(2)}) collective-permute-start(bf16[3,32,512]{2,1,0:T(8,128)(2,1)} %get-tuple-element.20), channel_id=1, source_target_pairs={{0,0},{1,4},{2,8},{3,12},{4,1},{5,5},{6,9},{7,13},{8,2},{9,6},{10,... | collective-permute-start | bytes 294920 | tf_op jit(solution)/shard_map/ppermute | solution.py:274
  12.4 2.8 %collective-permute-start.1 = (bf16[3,32,512]{2,1,0:T(8,128)(2,1)}, bf16[3,32,512]{2,1,0:T(8,128)(2,1)S(1)}, u32[]{:S(2)}, u32[]{:S(2)}) collective-permute-start(bf16[3,32,512]{2,1,0:T(8,128)(2,1)} %get-tuple-element.21), channel_id=1, source_target_pairs={{0,16},{1,20},{2,24},{3,28},{4,17},{5,21},{6,25},{7,29},{8,18},{9,... | collective-permute-start | bytes 294920 | tf_op jit(solution)/shard_map/ppermute | solution.py:274
  15.2 0.0 collective-permute-done.refs_1_.refs_3_
  15.2 2.9 %collective-permute-done.1.refs_2_.refs_4_ = bf16[3,32,512]{2,1,0:T(8,128)(2,1)S(1)} collective-permute-done((bf16[3,32,512]{2,1,0:T(8,128)(2,1)}, bf16[3,32,512]{2,1,0:T(8,128)(2,1)S(1)}, u32[]{:S(2)}, u32[]{:S(2)}) %collective-permute-start.1) | collective-permute-done | bytes 98336 | tf_op jit(solution)/shard_map/ppermute | solution.py:274
  18.2 0.9 %copy-done.1 = bf16[768,128]{1,0:T(8,128)(2,1)S(1)} copy-done((bf16[768,128]{1,0:T(8,128)(2,1)S(1)}, bf16[768,128]{1,0:T(8,128)(2,1)}, u32[]{:S(2)}) %copy-start.1) | copy-done | bytes 196632
  19.1 1.5 %shard_map.56 = (bf16[16,32,256]{2,1,0:T(8,128)(2,1)}, bf16[32,288]{1,0:T(8,128)(2,1)S(1)}, bf16[32,288]{1,0:T(8,128)(2,1)S(1)}) custom-call(f32[2,64,512]{2,1,0:T(8,128)S(1)} %bitcast.68, bf16[3,32,512]{2,1,0:T(8,128)(2,1)S(1)} %collective-permute-done.refs_1_.refs_3_, bf16[3,32,512]{2,1,0:T(8,128)(2,1)S(1)} %collective-permute-done.1.refs_2_.refs_4_, ...), custom_call_target="tpu_custom_call" | custom-call | tf_op jit(solution)/shard_map/pallas_call | solution.py:225
  20.6 11.8 %all-to-all-start = ((bf16[16,32,256]{2,1,0:T(8,128)(2,1)}), bf16[16,32,256]{2,1,0:T(8,128)(2,1)S(1)}, u32[]{:S(2)}, u32[]{:S(2)}) async-start(bf16[16,32,256]{2,1,0:T(8,128)(2,1)} %get-tuple-element.26), calls=%async_computation | async-start | bytes 524288 | tf_op jit(solution)/shard_map/all_to_all | solution.py:278
  32.5 0.5 fusion.2
  33.1 2.0 %collective-permute-start.12 = (bf16[1280,128]{1,0:T(8,128)(2,1)S(1)}, bf16[1280,128]{1,0:T(8,128)(2,1)S(1)}, u32[]{:S(2)}, u32[]{:S(2)}) collective-permute-start(bf16[1280,128]{1,0:T(8,128)(2,1)S(1)} %constant_dynamic-update-slice_fusion.refs_9_.refs_5_.refs_4_), channel_id=1, source_target_pairs={{0,2},{2,0},{1,3},{3,1},{4,6},{6,4},{5,7},{7,5},{8,10},{10,8},{9,1... | collective-permute-start | bytes 983048 | tf_op jit(solution)/shard_map/ppermute | solution.py:262
  35.1 0.0 collective-permute-start.11
  35.1 9.3 %collective-permute-done.12.refs_11_.refs_7_.refs_6_ = bf16[1280,128]{1,0:T(8,128)(2,1)S(1)} collective-permute-done((bf16[1280,128]{1,0:T(8,128)(2,1)S(1)}, bf16[1280,128]{1,0:T(8,128)(2,1)S(1)}, u32[]{:S(2)}, u32[]{:S(2)}) %collective-permute-start.12) | collective-permute-done | bytes 327712 | tf_op jit(solution)/shard_map/ppermute | solution.py:262
  44.4 0.0 collective-permute-start.13
  44.4 0.5 collective-permute-start.5
  44.9 0.7 collective-permute-start.6
  45.6 2.6 %collective-permute-start.7 = (bf16[32,288]{1,0:T(8,128)(2,1)S(1)}, bf16[32,288]{1,0:T(8,128)(2,1)S(1)}, u32[]{:S(2)}, u32[]{:S(2)}) collective-permute-start(bf16[32,288]{1,0:T(8,128)(2,1)S(1)} %get-tuple-element.28), channel_id=1, source_target_pairs={{0,16},{1,20},{2,24},{3,28},{4,17},{5,21},{6,25},{7,29},{8,18},{9,... | collective-permute-start | bytes 55304 | tf_op jit(solution)/shard_map/ppermute | solution.py:274
  48.2 2.2 %collective-permute-done.7 = bf16[32,288]{1,0:T(8,128)(2,1)S(1)} collective-permute-done((bf16[32,288]{1,0:T(8,128)(2,1)S(1)}, bf16[32,288]{1,0:T(8,128)(2,1)S(1)}, u32[]{:S(2)}, u32[]{:S(2)}) %collective-permute-start.7) | collective-permute-done | bytes 18464 | tf_op jit(solution)/shard_map/ppermute | solution.py:274
  50.4 6.4 %collective-permute-start.9 = (bf16[2,32,288]{2,1,0:T(8,128)(2,1)S(1)}, bf16[2,32,288]{2,1,0:T(8,128)(2,1)S(1)}, u32[]{:S(2)}, u32[]{:S(2)}) collective-permute-start(bf16[2,32,288]{2,1,0:T(8,128)(2,1)S(1)} %pad_maximum_fusion.refs_5_), channel_id=1, source_target_pairs={{0,2},{2,0},{1,3},{3,1},{4,6},{6,4},{5,7},{7,5},{8,10},{10,8},{9,1... | collective-permute-start | bytes 110600 | tf_op jit(solution)/shard_map/ppermute | solution.py:262
  56.8 0.9 %collective-permute-start.8 = (bf16[2,32,288]{2,1,0:T(8,128)(2,1)S(1)}, bf16[2,32,288]{2,1,0:T(8,128)(2,1)S(1)}, u32[]{:S(2)}, u32[]{:S(2)}) collective-permute-start(bf16[2,32,288]{2,1,0:T(8,128)(2,1)S(1)} %pad_maximum_fusion.refs_5_), channel_id=1, source_target_pairs={{0,1},{1,0},{2,3},{3,2},{4,5},{5,4},{6,7},{7,6},{8,9},{9,8},{10,11... | collective-permute-start | bytes 110600 | tf_op jit(solution)/shard_map/ppermute | solution.py:263
  57.7 1.3 %collective-permute-done.9.refs_7_ = bf16[2,32,288]{2,1,0:T(8,128)(2,1)S(1)} collective-permute-done((bf16[2,32,288]{2,1,0:T(8,128)(2,1)S(1)}, bf16[2,32,288]{2,1,0:T(8,128)(2,1)S(1)}, u32[]{:S(2)}, u32[]{:S(2)}) %collective-permute-start.9) | collective-permute-done | bytes 36896 | tf_op jit(solution)/shard_map/ppermute | solution.py:262
  58.9 0.3 collective-permute-start.10
  59.2 1.0 %collective-permute-done.10.refs_8_ = bf16[2,32,288]{2,1,0:T(8,128)(2,1)S(1)} collective-permute-done((bf16[2,32,288]{2,1,0:T(8,128)(2,1)S(1)}, bf16[2,32,288]{2,1,0:T(8,128)(2,1)S(1)}, u32[]{:S(2)}, u32[]{:S(2)}) %collective-permute-start.10) | collective-permute-done | bytes 36896 | tf_op jit(solution)/shard_map/ppermute | solution.py:263
  60.2 2.1 %shard_map.57 = (bf16[16,32,256]{2,1,0:T(8,128)(2,1)S(1)}, f32[64,512]{1,0:T(8,128)S(1)}, bf16[224,64]{1,0:T(8,128)(2,1)S(1)}) custom-call(bf16[16,32,256]{2,1,0:T(8,128)(2,1)S(1)} %all-to-all-done.refs_0_, bf16[16,32,256]{2,1,0:T(8,128)(2,1)S(1)} %collective-permute-done.5.refs_1_, f32[2,64,512]{2,1,0:T(8,128)S(1)} %bitcast.70, ...), custom_call_target="tpu_custom_call" | custom-call | tf_op jit(solution)/shard_map/pallas_call | solution.py:225
  62.3 15.7 %all_to_all.10.refs_0_ = bf16[16,32,256]{2,1,0:T(8,128)(2,1)S(1)} all-to-all(bf16[16,32,256]{2,1,0:T(8,128)(2,1)S(1)} %get-tuple-element.32), channel_id=1, replica_groups=mesh['row'=8,'x'=2,'core'=2] {'row','x'}, dimensions={0} | all-to-all | bytes 524288 | tf_op jit(solution)/shard_map/all_to_all | solution.py:278
  78.0 0.5 shard_map.58.refs_3_
  78.5 1.0 %collective-permute-done.14.refs_1_ = bf16[16,32,256]{2,1,0:T(8,128)(2,1)S(1)} collective-permute-done((bf16[16,32,256]{2,1,0:T(8,128)(2,1)S(1)}, bf16[16,32,256]{2,1,0:T(8,128)(2,1)S(1)}, u32[]{:S(2)}, u32[]{:S(2)}) %collective-permute-start.14) | collective-permute-done | bytes 262176 | tf_op jit(solution)/shard_map/ppermute | solution.py:279
  79.5 2.2 %shard_map.59 = f32[2,64,512]{2,1,0:T(8,128)} custom-call(bf16[16,32,256]{2,1,0:T(8,128)(2,1)S(1)} %all_to_all.10.refs_0_, bf16[16,32,256]{2,1,0:T(8,128)(2,1)S(1)} %collective-permute-done.14.refs_1_, f32[64,512]{1,0:T(8,128)S(1)} %get-tuple-element.33.refs_2_, f32[64,512]{1,0:T(8,128)S(1)} %shard_map.58.refs_3_, ...), custom_call_target="tpu_custom_call" | custom-call | tf_op jit(solution)/shard_map/pallas_call | solution.py:225
  (32 shorter events, 0.2 us)
Async XLA Ops:
  0.0 15.2 %copy-start.4 = (bf16[2,1,4,1,32,512]{5,4,3,2,1,0:T(8,128)(2,1)S(1)}, bf16[2,1,4,1,32,512]{5,4,3,2,1,0:T(8,128)(2,1)}, u32[]{:S(2)}) copy-start(bf16[2,1,4,1,32,512]{5,4,3,2,1,0:T(8,128)(2,1)} %param.7) | copy-start | bytes 786436
  2.7 15.5 %copy-start = (f32[2,1,64,512]{3,2,1,0:T(8,128)S(1)}, f32[2,1,64,512]{3,2,1,0:T(8,128)}, u32[]{:S(2)}) copy-start(f32[2,1,64,512]{3,2,1,0:T(8,128)} %param.5) | copy-start | bytes 786436
  2.7 8.1 %collective-permute-start.3 = (bf16[768,128]{1,0:T(8,128)(2,1)}, bf16[768,128]{1,0:T(8,128)(2,1)S(1)}, u32[]{:S(2)}, u32[]{:S(2)}) collective-permute-start(bf16[768,128]{1,0:T(8,128)(2,1)} %get-tuple-element.22.refs_3_.refs_1_), channel_id=1, source_target_pairs={{0,2},{2,0},{1,3},{3,1},{4,6},{6,4},{5,7},{7,5},{8,10},{10,8},{9,1... | collective-permute-start | bytes 589832 | tf_op jit(solution)/shard_map/ppermute | solution.py:262
  5.7 12.4 %collective-permute-start.2 = (bf16[768,128]{1,0:T(8,128)(2,1)}, bf16[768,128]{1,0:T(8,128)(2,1)S(1)}, u32[]{:S(2)}, u32[]{:S(2)}) collective-permute-start(bf16[768,128]{1,0:T(8,128)(2,1)} %get-tuple-element.22.refs_3_.refs_1_), channel_id=1, source_target_pairs={{0,1},{1,0},{2,3},{3,2},{4,5},{5,4},{6,7},{7,6},{8,9},{9,8},{10,11... | collective-permute-start | bytes 589832 | tf_op jit(solution)/shard_map/ppermute | solution.py:263
  10.8 7.3 %collective-permute-start.4 = (bf16[768,128]{1,0:T(8,128)(2,1)S(1)}, bf16[768,128]{1,0:T(8,128)(2,1)S(1)}, u32[]{:S(2)}, u32[]{:S(2)}) collective-permute-start(bf16[768,128]{1,0:T(8,128)(2,1)S(1)} %collective-permute-done.3.refs_5_.refs_3_), channel_id=1, source_target_pairs={{0,1},{1,0},{2,3},{3,2},{4,5},{5,4},{6,7},{7,6},{8,9},{9,8},{10,11... | collective-permute-start | bytes 589832 | tf_op jit(solution)/shard_map/ppermute | solution.py:263
  10.8 4.4 %collective-permute-start = (bf16[3,32,512]{2,1,0:T(8,128)(2,1)}, bf16[3,32,512]{2,1,0:T(8,128)(2,1)S(1)}, u32[]{:S(2)}, u32[]{:S(2)}) collective-permute-start(bf16[3,32,512]{2,1,0:T(8,128)(2,1)} %get-tuple-element.20), channel_id=1, source_target_pairs={{0,0},{1,4},{2,8},{3,12},{4,1},{5,5},{6,9},{7,13},{8,2},{9,6},{10,... | collective-permute-start | bytes 294920 | tf_op jit(solution)/shard_map/ppermute | solution.py:274
  12.4 5.8 %collective-permute-start.1 = (bf16[3,32,512]{2,1,0:T(8,128)(2,1)}, bf16[3,32,512]{2,1,0:T(8,128)(2,1)S(1)}, u32[]{:S(2)}, u32[]{:S(2)}) collective-permute-start(bf16[3,32,512]{2,1,0:T(8,128)(2,1)} %get-tuple-element.21), channel_id=1, source_target_pairs={{0,16},{1,20},{2,24},{3,28},{4,17},{5,21},{6,25},{7,29},{8,18},{9,... | collective-permute-start | bytes 294920 | tf_op jit(solution)/shard_map/ppermute | solution.py:274
  18.2 0.9 %copy-start.1 = (bf16[768,128]{1,0:T(8,128)(2,1)S(1)}, bf16[768,128]{1,0:T(8,128)(2,1)}, u32[]{:S(2)}) copy-start(bf16[768,128]{1,0:T(8,128)(2,1)} %get-tuple-element.22.refs_3_.refs_1_) | copy-start | bytes 589828
  20.6 11.8 %copy-start.3 = (f32[2,1,512,128]{3,2,1,0:T(8,128)S(1)}, f32[2,1,512,128]{3,2,1,0:T(8,128)}, u32[]{:S(2)}) copy-start(f32[2,1,512,128]{3,2,1,0:T(8,128)} %param.6) | copy-start | bytes 1572868
  20.6 23.8 %all-to-all-start = ((bf16[16,32,256]{2,1,0:T(8,128)(2,1)}), bf16[16,32,256]{2,1,0:T(8,128)(2,1)S(1)}, u32[]{:S(2)}, u32[]{:S(2)}) async-start(bf16[16,32,256]{2,1,0:T(8,128)(2,1)} %get-tuple-element.26), calls=%async_computation | async-start | bytes 524288 | tf_op jit(solution)/shard_map/all_to_all | solution.py:278
  33.1 11.3 %collective-permute-start.12 = (bf16[1280,128]{1,0:T(8,128)(2,1)S(1)}, bf16[1280,128]{1,0:T(8,128)(2,1)S(1)}, u32[]{:S(2)}, u32[]{:S(2)}) collective-permute-start(bf16[1280,128]{1,0:T(8,128)(2,1)S(1)} %constant_dynamic-update-slice_fusion.refs_9_.refs_5_.refs_4_), channel_id=1, source_target_pairs={{0,2},{2,0},{1,3},{3,1},{4,6},{6,4},{5,7},{7,5},{8,10},{10,8},{9,1... | collective-permute-start | bytes 983048 | tf_op jit(solution)/shard_map/ppermute | solution.py:262
  35.1 25.1 %collective-permute-start.11 = (bf16[1280,128]{1,0:T(8,128)(2,1)S(1)}, bf16[1280,128]{1,0:T(8,128)(2,1)S(1)}, u32[]{:S(2)}, u32[]{:S(2)}) collective-permute-start(bf16[1280,128]{1,0:T(8,128)(2,1)S(1)} %constant_dynamic-update-slice_fusion.refs_9_.refs_5_.refs_4_), channel_id=1, source_target_pairs={{0,1},{1,0},{2,3},{3,2},{4,5},{5,4},{6,7},{7,6},{8,9},{9,8},{10,11... | collective-permute-start | bytes 983048 | tf_op jit(solution)/shard_map/ppermute | solution.py:263
  44.4 15.8 %collective-permute-start.13 = (bf16[1280,128]{1,0:T(8,128)(2,1)S(1)}, bf16[1280,128]{1,0:T(8,128)(2,1)S(1)}, u32[]{:S(2)}, u32[]{:S(2)}) collective-permute-start(bf16[1280,128]{1,0:T(8,128)(2,1)S(1)} %collective-permute-done.12.refs_11_.refs_7_.refs_6_), channel_id=1, source_target_pairs={{0,1},{1,0},{2,3},{3,2},{4,5},{5,4},{6,7},{7,6},{8,9},{9,8},{10,11... | collective-permute-start | bytes 983048 | tf_op jit(solution)/shard_map/ppermute | solution.py:263
  44.4 15.8 %collective-permute-start.5 = (bf16[16,32,256]{2,1,0:T(8,128)(2,1)S(1)}, bf16[16,32,256]{2,1,0:T(8,128)(2,1)S(1)}, u32[]{:S(2)}, u32[]{:S(2)}) collective-permute-start(bf16[16,32,256]{2,1,0:T(8,128)(2,1)S(1)} %all-to-all-done.refs_0_), channel_id=1, source_target_pairs={{0,1},{1,0},{2,3},{3,2},{4,5},{5,4},{6,7},{7,6},{8,9},{9,8},{10,11... | collective-permute-start | bytes 786440 | tf_op jit(solution)/shard_map/ppermute | solution.py:279
  44.9 3.3 %collective-permute-start.6 = (bf16[32,288]{1,0:T(8,128)(2,1)S(1)}, bf16[32,288]{1,0:T(8,128)(2,1)S(1)}, u32[]{:S(2)}, u32[]{:S(2)}) collective-permute-start(bf16[32,288]{1,0:T(8,128)(2,1)S(1)} %get-tuple-element.27), channel_id=1, source_target_pairs={{0,0},{1,4},{2,8},{3,12},{4,1},{5,5},{6,9},{7,13},{8,2},{9,6},{10,... | collective-permute-start | bytes 55304 | tf_op jit(solution)/shard_map/ppermute | solution.py:274
  45.6 4.8 %collective-permute-start.7 = (bf16[32,288]{1,0:T(8,128)(2,1)S(1)}, bf16[32,288]{1,0:T(8,128)(2,1)S(1)}, u32[]{:S(2)}, u32[]{:S(2)}) collective-permute-start(bf16[32,288]{1,0:T(8,128)(2,1)S(1)} %get-tuple-element.28), channel_id=1, source_target_pairs={{0,16},{1,20},{2,24},{3,28},{4,17},{5,21},{6,25},{7,29},{8,18},{9,... | collective-permute-start | bytes 55304 | tf_op jit(solution)/shard_map/ppermute | solution.py:274
  50.4 8.6 %collective-permute-start.9 = (bf16[2,32,288]{2,1,0:T(8,128)(2,1)S(1)}, bf16[2,32,288]{2,1,0:T(8,128)(2,1)S(1)}, u32[]{:S(2)}, u32[]{:S(2)}) collective-permute-start(bf16[2,32,288]{2,1,0:T(8,128)(2,1)S(1)} %pad_maximum_fusion.refs_5_), channel_id=1, source_target_pairs={{0,2},{2,0},{1,3},{3,1},{4,6},{6,4},{5,7},{7,5},{8,10},{10,8},{9,1... | collective-permute-start | bytes 110600 | tf_op jit(solution)/shard_map/ppermute | solution.py:262
  56.8 2.4 %collective-permute-start.8 = (bf16[2,32,288]{2,1,0:T(8,128)(2,1)S(1)}, bf16[2,32,288]{2,1,0:T(8,128)(2,1)S(1)}, u32[]{:S(2)}, u32[]{:S(2)}) collective-permute-start(bf16[2,32,288]{2,1,0:T(8,128)(2,1)S(1)} %pad_maximum_fusion.refs_5_), channel_id=1, source_target_pairs={{0,1},{1,0},{2,3},{3,2},{4,5},{5,4},{6,7},{7,6},{8,9},{9,8},{10,11... | collective-permute-start | bytes 110600 | tf_op jit(solution)/shard_map/ppermute | solution.py:263
  58.9 1.2 %collective-permute-start.10 = (bf16[2,32,288]{2,1,0:T(8,128)(2,1)S(1)}, bf16[2,32,288]{2,1,0:T(8,128)(2,1)S(1)}, u32[]{:S(2)}, u32[]{:S(2)}) collective-permute-start(bf16[2,32,288]{2,1,0:T(8,128)(2,1)S(1)} %collective-permute-done.9.refs_7_), channel_id=1, source_target_pairs={{0,1},{1,0},{2,3},{3,2},{4,5},{5,4},{6,7},{7,6},{8,9},{9,8},{10,11... | collective-permute-start | bytes 110600 | tf_op jit(solution)/shard_map/ppermute | solution.py:263
  62.2 15.7 %copy-start.2 = (bf16[768,128]{1,0:T(8,128)(2,1)S(1)}, bf16[768,128]{1,0:T(8,128)(2,1)}, u32[]{:S(2)}) copy-start(bf16[768,128]{1,0:T(8,128)(2,1)} %get-tuple-element.22.refs_3_.refs_1_) | copy-start | bytes 589828
  78.0 1.5 %collective-permute-start.14 = (bf16[16,32,256]{2,1,0:T(8,128)(2,1)S(1)}, bf16[16,32,256]{2,1,0:T(8,128)(2,1)S(1)}, u32[]{:S(2)}, u32[]{:S(2)}) collective-permute-start(bf16[16,32,256]{2,1,0:T(8,128)(2,1)S(1)} %all_to_all.10.refs_0_), channel_id=1, source_target_pairs={{0,1},{1,0},{2,3},{3,2},{4,5},{5,4},{6,7},{7,6},{8,9},{9,8},{10,11... | collective-permute-start | bytes 786440 | tf_op jit(solution)/shard_map/ppermute | solution.py:279

commit v6 on v4

--- a/solution.py
+++ b/solution.py
@@ -54,29 +54,26 @@
     return jnp.concatenate([ref[source, at + m * rows + start : at + m * rows + stop, :] for m in range(count)], axis=1)
 
 
-def prep_kernel(dims, ranks_ref, inv_hbm, u_hbm, v_hbm, send_a_ref, send_b_ref, near_ref, inv_ref, u_ref, v_ref, sems):
+def near_kernel(dims, inv_ref, u_ref, near_ref):
     _, _, _, rank, _, _ = dims
+    order = inv_ref.shape[1]
+    near_ref[:order, :] = inv_ref[0].astype(BF)
+    put_columns(near_ref, order, TURNS * rank, u_ref[0, 0].reshape(TURNS * rank, order))
+
+
+def mask_kernel(dims, ranks_ref, v_ref, send_a_ref, send_b_ref, later_a_ref, later_b_ref):
     _, _, turn = place()
-    order = inv_ref.shape[0]
-    copies = [
-        pltpu.make_async_copy(inv_hbm.at[0], inv_ref, sems.at[0]),
-        pltpu.make_async_copy(u_hbm.at[0, 0], u_ref, sems.at[1]),
-        pltpu.make_async_copy(v_hbm, v_ref, sems.at[2]),
-    ]
-    for copy in copies:
-        copy.start()
-    copies[0].wait()
-    copies[1].wait()
-    near_ref[:order, :] = inv_ref[...].astype(BF)
-    put_columns(near_ref, order, TURNS * rank, u_ref[...].reshape(TURNS * rank, order))
-    copies[2].wait()
     rank_rows = lax.broadcasted_iota(jnp.int32, v_ref.shape[3:], 0)
-    for s, send_ref in enumerate((send_a_ref, send_b_ref)):
+
+    def masked(i, k, t):
+        v = v_ref[i, k, t]
+        return jnp.where(rank_rows < ranks_ref[i, 0, 0, k * TURNS + t], v, jnp.zeros_like(v))
+
+    for s, (send_ref, later_ref) in enumerate(((send_a_ref, later_a_ref), (send_b_ref, later_b_ref))):
         t = lax.rem(turn + s, TURNS)
-        for n, (i, k) in enumerate(((0, 0), (1, 0), (1, 1))):
-            keep = rank_rows < ranks_ref[i, 0, 0, k * TURNS + t]
-            v = v_ref[i, k, t]
-            send_ref[n] = jnp.where(keep, v, jnp.zeros_like(v))
+        send_ref[0] = masked(0, 0, t)
+        send_ref[1] = masked(1, 0, t)
+        later_ref[...] = masked(1, 1, t)
 
 
 def gathered_inverse(ref, order):
@@ -92,24 +89,25 @@
 
 def first_kernel(dims, *refs):
     n_row, _, _, rank, width, half = dims
-    rhs_ref, v_a_ref, v_b_ref = refs[:3]
+    rhs_ref, v_a_ref, v_b_ref, later_a_ref, later_b_ref = refs[:5]
     msg_ref, far_a_ref, far_b_ref, near_ref = refs[-4:]
     row, col, turn = place()
     order = rhs_ref.shape[2]
-    join(near_ref, refs[3:-4])
+    join(near_ref, refs[5:-4])
     inv = gathered_inverse(near_ref, order)
     z = split_mm(rhs_ref[0], inv)
     w = mm(gathered_u(near_ref, order, rank, n_row - 1), inv)
     x = jnp.concatenate([z.astype(BF), w.astype(BF)], axis=0)
     tiles = []
     for v_ref in (v_a_ref, v_b_ref):
-        v = v_ref[:2].reshape(2 * rank, order)
+        v = v_ref[...].reshape(2 * rank, order)
         tiles.append(lax.dot_general(v, x, NT, preferred_element_type=F32).astype(BF))
     straight = turn == 0
     low = jnp.where(straight, tiles[0][:rank, :width], tiles[1][:rank, :width])
     high = jnp.where(straight, tiles[1][:rank, :width], tiles[0][:rank, :width])
-    far_a_ref[...] = tiles[0][rank:]
-    far_b_ref[...] = tiles[1][rank:]
+    for n, (far_ref, later_ref) in enumerate(((far_a_ref, later_a_ref), (far_b_ref, later_b_ref))):
+        far_ref[:, order : order + width + rank] = tiles[n][rank:]
+        far_ref[:, :order] = later_ref[...]
     msg = pack(low, high, col > row, half)
     for d in range(msg_ref.shape[0]):
         msg_ref[d] = msg
@@ -174,7 +172,7 @@
     z = split_mm(rhs_ref[1] - total, inv)
     minus_ref[...] = -total
     x = jnp.concatenate([z.astype(BF), w.astype(BF)], axis=0)
-    tiles = [lax.dot_general(v_ref[2], x, NT, preferred_element_type=F32).astype(BF) for v_ref in (v_a_ref, v_b_ref)]
+    tiles = [lax.dot_general(v_ref[:, :order], x, NT, preferred_element_type=F32).astype(BF) for v_ref in (v_a_ref, v_b_ref)]
     straight = turn == 0
     low = jnp.where(straight, tiles[0], tiles[1])
     high = jnp.where(straight, tiles[1], tiles[0])
@@ -212,16 +210,15 @@
     y_ref[1] = z_ref[...] + split_mm(minus, gathered_inverse(next_ref, order))
 
 
-def call(kernel, outs, *args, scratch=(), scalars=0, far=False, limit=24 * 2**20):
+def call(kernel, outs, *args, scratch=(), scalars=0):
     vmem = pl.BlockSpec(memory_space=pltpu.VMEM)
-    place_in = pl.BlockSpec(memory_space=pltpu.HBM) if far else vmem
     return pl.pallas_call(
         kernel,
         out_shape=outs,
-        in_specs=[pl.BlockSpec(memory_space=pltpu.SMEM)] * scalars + [place_in] * (len(args) - scalars),
+        in_specs=[pl.BlockSpec(memory_space=pltpu.SMEM)] * scalars + [vmem] * (len(args) - scalars),
         out_specs=[vmem] * len(outs),
         scratch_shapes=list(scratch),
-        compiler_params=pltpu.CompilerParams(vmem_limit_bytes=limit),
+        compiler_params=pltpu.CompilerParams(vmem_limit_bytes=24 * 2**20),
     )(*args)
 
 
@@ -276,7 +273,7 @@
 
     u_rows = n_col * TURNS * rank
     messages = shape((n_row * n_x, rank, width), BF)
-    far_shape = shape((rank, width + rank), BF)
+    far_shape = shape((rank, order + width + rank), BF)
     near_scratch = pltpu.VMEM((n_col, order + u_rows, lanes), BF)
     next_scratch = pltpu.VMEM((n_col, order + 2 * u_rows, lanes), BF)
     solve_scratch = [
@@ -284,38 +281,34 @@
         pltpu.VMEM((n_row, width + rank, r_cols), BF),
     ]
 
-    v_send = shape((3, rank, order), BF)
-    v_a, v_b, near = call(
-        kernel(prep_kernel),
-        [v_send, v_send, shape((order + u_rows, lanes), BF)],
-        ranks, inv_here, u_here, v_here, scalars=1, far=True, limit=67043328 - 450 * 1024,
-        scratch=[
-            pltpu.VMEM((order, lanes), F32),
-            pltpu.VMEM((TURNS, rank, order), BF),
-            pltpu.VMEM((slots, slots, TURNS, rank, order), BF),
-            pltpu.SemaphoreType.DMA((3,)),
-        ],
+    (near,) = call(kernel(near_kernel), [shape((order + u_rows, lanes), BF)], inv_here, u_here)
+    v_a, v_b, later_a, later_b = call(
+        kernel(mask_kernel),
+        [shape((2, rank, order), BF)] * 2 + [shape((rank, order), BF)] * 2,
+        ranks, v_here, scalars=1,
     )
     near = gather(near)
     v_a, v_b = turn_rows([v_a, v_b])
     later_u = u_here[1].reshape(slots, TURNS * rank, order)
     nxt = gather(jnp.concatenate([inv_here[1].astype(BF)] + [
         later_u[a, :, m * lanes : (m + 1) * lanes] for a in range(slots) for m in range(n_col)], axis=0))
-    z = gather(lax.dot_general(rhs_here, inv_here, (((2,), (1,)), ((0,), (0,))), precision=lax.Precision.HIGHEST,
-                               preferred_element_type=F32))
 
     msg, far_a, far_b = call(
         kernel(first_kernel), [messages, far_shape, far_shape],
-        rhs_here, v_a, v_b, *near, scratch=[near_scratch],
-    )
-
-    far = gather(jnp.stack(turn_rows([far_a, far_b])))
+        rhs_here, v_a, v_b, later_a, later_b, *near, scratch=[near_scratch],
+    )
+
+    rhs_late, inv_late, msg, far_a, far_b = lax.optimization_barrier((rhs_here, inv_here, msg, far_a, far_b))
+    later_a, later_b = turn_rows([far_a, far_b])
+    far = gather(jnp.stack([later_a, later_b])[:, :, order:])
     same, other = spread(msg)
+    z = gather(lax.dot_general(rhs_late, inv_late, (((2,), (1,)), ((0,), (0,))), precision=lax.Precision.HIGHEST,
+                               preferred_element_type=F32))
 
     msg, minus, own = call(
         kernel(middle_kernel),
         [messages, shape((r_cols, order), F32), shape((width + rank - r_cols, r_cols), BF)],
-        same, other, rhs_here, v_a, v_b, *far, *nxt,
+        same, other, rhs_here, later_a, later_b, *far, *nxt,
         scratch=solve_scratch + [pltpu.VMEM((n_col, TURNS, rank, width + rank), BF), next_scratch],
     )
     same, other = spread(msg)

time: 79.1 us -> 77.9 us (0.985)
  Pallas kernels: 8.92 us -> 6.89 us
  starting transfers between devices: 33.3 us -> 31.5 us
  local copies, waits for them, and re-layouts: 1.13 us -> 2.79 us
  waiting for transfers between devices: 18.9 us -> 20.4 us
    pallas_call x5 -> x6, Pallas kernels: 8.92 us -> 6.89 us  [call(): pl.pallas_call(kernel, out_shape=outs, in_specs=[pl.BlockSpec(memory_spac...]
    unnamed x16 -> x20, local copies, waits for them, and re-layouts: 1.11 us -> 2.77 us
    all_to_all x1, starting transfers between devices: 9.89 us -> 8.42 us  [spread(): lax.all_to_all(m, ('row', 'x'), split_axis=0, concat_axis=0, tiled=True)]
    ppermute x4, waiting for transfers between devices: 13.3 us -> 14.3 us  [gather(): moved = lax.ppermute(part, 'x', [(i, (i + s) % n_x) for i in range(n_x)])]
    ppermute x4, starting transfers between devices: 7.21 us -> 6.4 us  [turn_rows(): got.append(lax.ppermute(parts[s], everywhere, pairs))]
  transfers between devices with their start and end apart: 19 -> 19, of which waited for: 7 -> 8; matrix products, arithmetic and copies ran while one was open for 2% -> 1% of each run, Pallas kernels for 1% -> 1%
where the time goes in v6:
time: 77.9 us; the launch traced here: 77.6 us
  starting transfers between devices  31.5 us (40%)
  waiting for transfers between devices  20.4 us (26%)
  blocking collectives  15.4 us (20%)
  Pallas kernels  6.89 us (9%)
  local copies, waits for them, and re-layouts  2.79 us (4%)
    all_to_all x1, blocking collectives, spread(): lax.all_to_all(m, ('row', 'x'), split_axis=0, concat_axis=0, tiled=True)  15.4 us
    ppermute x4, waiting for transfers between devices, gather(): moved = lax.ppermute(part, 'x', [(i, (i + s) % n_x) for i in range(n_x)])  14.3 us
    ppermute x4, starting transfers between devices, gather(): moved = lax.ppermute(part, 'x', [(i, (i + s) % n_x) for i in range(n_x)])  12.4 us
    all_to_all x1, starting transfers between devices, spread(): lax.all_to_all(m, ('row', 'x'), split_axis=0, concat_axis=0, tiled=True)  8.42 us
    pallas_call x6, Pallas kernels, call(): pl.pallas_call(kernel, out_shape=outs, in_specs=[pl.BlockSpec(memory_spac...  6.89 us
    ppermute x4, starting transfers between devices, turn_rows(): got.append(lax.ppermute(parts[s], everywhere, pairs))  6.4 us
    ppermute x8, starting transfers between devices, gather(): pieces += [moved, lax.ppermute(moved, 'core', swap)]  3.72 us
    ppermute x8, waiting for transfers between devices, gather(): pieces += [moved, lax.ppermute(moved, 'core', swap)]  3.41 us
  transfers between devices with their start and end apart: 19, of which 8 were waited for; matrix products, arithmetic and copies ran while one was open for 1% of the time, Pallas kernels for 1%

profile of v6, /device:TPU:0, one launch (start us, length us, event | category | flops | bytes accessed | tf_op | source)
XLA Modules:
  0.0 77.6 jit_solution(17165247500376368157)
XLA Ops:
  0.0 1.0 %copy-done = f32[2,1,512,128]{3,2,1,0:T(8,128)S(1)} copy-done((f32[2,1,512,128]{3,2,1,0:T(8,128)S(1)}, f32[2,1,512,128]{3,2,1,0:T(8,128)}, u32[]{:S(2)}) %copy-start) | copy-done | bytes 524312
  1.0 0.9 %copy-done.3 = bf16[2,1,4,1,32,512]{5,4,3,2,1,0:T(8,128)(2,1)S(1)} copy-done((bf16[2,1,4,1,32,512]{5,4,3,2,1,0:T(8,128)(2,1)S(1)}, bf16[2,1,4,1,32,512]{5,4,3,2,1,0:T(8,128)(2,1)}, u32[]{:S(2)}) %copy-start.3) | copy-done | bytes 262168
  2.0 3.0 %collective-permute-start.3 = (bf16[768,128]{1,0:T(8,128)(2,1)S(1)}, bf16[768,128]{1,0:T(8,128)(2,1)S(1)}, u32[]{:S(2)}, u32[]{:S(2)}) collective-permute-start(bf16[768,128]{1,0:T(8,128)(2,1)S(1)} %shard_map.56.refs_5_.refs_1_), channel_id=1, source_target_pairs={{0,2},{2,0},{1,3},{3,1},{4,6},{6,4},{5,7},{7,5},{8,10},{10,8},{9,1... | collective-permute-start | bytes 589832 | tf_op jit(solution)/shard_map/ppermute | solution.py:252
  5.1 0.7 copy-done.5
  5.7 0.6 shard_map.55
  6.3 0.7 collective-permute-start
  7.0 2.7 %collective-permute-start.1 = (bf16[2,32,512]{2,1,0:T(8,128)(2,1)S(1)}, bf16[2,32,512]{2,1,0:T(8,128)(2,1)S(1)}, u32[]{:S(2)}, u32[]{:S(2)}) collective-permute-start(bf16[2,32,512]{2,1,0:T(8,128)(2,1)S(1)} %get-tuple-element.23), channel_id=1, source_target_pairs={{0,16},{1,20},{2,24},{3,28},{4,17},{5,21},{6,25},{7,29},{8,18},{9,... | collective-permute-start | bytes 196616 | tf_op jit(solution)/shard_map/ppermute | solution.py:264
  9.8 0.2 collective-permute-done.3.refs_7_.refs_3_
  10.0 2.8 %collective-permute-start.4 = (bf16[768,128]{1,0:T(8,128)(2,1)S(1)}, bf16[768,128]{1,0:T(8,128)(2,1)S(1)}, u32[]{:S(2)}, u32[]{:S(2)}) collective-permute-start(bf16[768,128]{1,0:T(8,128)(2,1)S(1)} %collective-permute-done.3.refs_7_.refs_3_), channel_id=1, source_target_pairs={{0,1},{1,0},{2,3},{3,2},{4,5},{5,4},{6,7},{7,6},{8,9},{9,8},{10,11... | collective-permute-start | bytes 589832 | tf_op jit(solution)/shard_map/ppermute | solution.py:253
  12.8 1.0 %collective-permute-done.4.refs_8_.refs_4_ = bf16[768,128]{1,0:T(8,128)(2,1)S(1)} collective-permute-done((bf16[768,128]{1,0:T(8,128)(2,1)S(1)}, bf16[768,128]{1,0:T(8,128)(2,1)S(1)}, u32[]{:S(2)}, u32[]{:S(2)}) %collective-permute-start.4) | collective-permute-done | bytes 196640 | tf_op jit(solution)/shard_map/ppermute | solution.py:253
  13.9 1.5 %shard_map.57 = (bf16[16,32,256]{2,1,0:T(8,128)(2,1)}, bf16[32,800]{1,0:T(8,128)(2,1)S(1)}, bf16[32,800]{1,0:T(8,128)(2,1)S(1)}) custom-call(f32[2,64,512]{2,1,0:T(8,128)S(1)} %bitcast.53, bf16[2,32,512]{2,1,0:T(8,128)(2,1)S(1)} %collective-permute-done.refs_1_, bf16[2,32,512]{2,1,0:T(8,128)(2,1)S(1)} %collective-permute-done.1.refs_2_, ...), custom_call_target="tpu_custom_call" | custom-call | tf_op jit(solution)/shard_map/pallas_call | solution.py:215
  15.4 8.4 %all-to-all-start = ((bf16[16,32,256]{2,1,0:T(8,128)(2,1)}), bf16[16,32,256]{2,1,0:T(8,128)(2,1)S(1)}, u32[]{:S(2)}, u32[]{:S(2)}) async-start(bf16[16,32,256]{2,1,0:T(8,128)(2,1)} %get-tuple-element.29), calls=%async_computation | async-start | bytes 524288 | tf_op jit(solution)/shard_map/all_to_all | solution.py:268
  23.9 2.0 %collective-permute-start.12 = (bf16[1024,128]{1,0:T(8,128)(2,1)S(1)}, bf16[1024,128]{1,0:T(8,128)(2,1)S(1)}, u32[]{:S(2)}, u32[]{:S(2)}) collective-permute-start(bf16[1024,128]{1,0:T(8,128)(2,1)S(1)} %constant_dynamic-update-slice_fusion.refs_9_.refs_5_), channel_id=1, source_target_pairs={{0,2},{2,0},{1,3},{3,1},{4,6},{6,4},{5,7},{7,5},{8,10},{10,8},{9,1... | collective-permute-start | bytes 786440 | tf_op jit(solution)/shard_map/ppermute | solution.py:252
  25.9 8.6 %collective-permute-done.12.refs_11_.refs_7_ = bf16[1024,128]{1,0:T(8,128)(2,1)S(1)} collective-permute-done((bf16[1024,128]{1,0:T(8,128)(2,1)S(1)}, bf16[1024,128]{1,0:T(8,128)(2,1)S(1)}, u32[]{:S(2)}, u32[]{:S(2)}) %collective-permute-start.12) | collective-permute-done | bytes 262176 | tf_op jit(solution)/shard_map/ppermute | solution.py:252
  34.5 0.5 collective-permute-start.5
  35.0 0.7 collective-permute-start.6
  35.7 2.4 %collective-permute-start.7 = (bf16[32,800]{1,0:T(8,128)(2,1)S(1)}, bf16[32,800]{1,0:T(8,128)(2,1)S(1)}, u32[]{:S(2)}, u32[]{:S(2)}) collective-permute-start(bf16[32,800]{1,0:T(8,128)(2,1)S(1)} %get-tuple-element.31), channel_id=1, source_target_pairs={{0,16},{1,20},{2,24},{3,28},{4,17},{5,21},{6,25},{7,29},{8,18},{9,... | collective-permute-start | bytes 153608 | tf_op jit(solution)/shard_map/ppermute | solution.py:264
  38.1 2.7 %collective-permute-done.7.refs_4_ = bf16[32,800]{1,0:T(8,128)(2,1)S(1)} collective-permute-done((bf16[32,800]{1,0:T(8,128)(2,1)S(1)}, bf16[32,800]{1,0:T(8,128)(2,1)S(1)}, u32[]{:S(2)}, u32[]{:S(2)}) %collective-permute-start.7) | collective-permute-done | bytes 51232 | tf_op jit(solution)/shard_map/ppermute | solution.py:264
  40.8 6.6 %collective-permute-start.9 = (bf16[2,32,288]{2,1,0:T(8,128)(2,1)S(1)}, bf16[2,32,288]{2,1,0:T(8,128)(2,1)S(1)}, u32[]{:S(2)}, u32[]{:S(2)}) collective-permute-start(bf16[2,32,288]{2,1,0:T(8,128)(2,1)S(1)} %pad_maximum_fusion.refs_5_), channel_id=1, source_target_pairs={{0,2},{2,0},{1,3},{3,1},{4,6},{6,4},{5,7},{7,5},{8,10},{10,8},{9,1... | collective-permute-start | bytes 110600 | tf_op jit(solution)/shard_map/ppermute | solution.py:252
  47.4 0.5 collective-permute-start.8
  47.9 2.0 %collective-permute-done.9.refs_7_ = bf16[2,32,288]{2,1,0:T(8,128)(2,1)S(1)} collective-permute-done((bf16[2,32,288]{2,1,0:T(8,128)(2,1)S(1)}, bf16[2,32,288]{2,1,0:T(8,128)(2,1)S(1)}, u32[]{:S(2)}, u32[]{:S(2)}) %collective-permute-start.9) | collective-permute-done | bytes 36896 | tf_op jit(solution)/shard_map/ppermute | solution.py:252
  49.9 0.1 collective-permute-start.10
  50.0 1.1 %collective-permute-done.10.refs_8_ = bf16[2,32,288]{2,1,0:T(8,128)(2,1)S(1)} collective-permute-done((bf16[2,32,288]{2,1,0:T(8,128)(2,1)S(1)}, bf16[2,32,288]{2,1,0:T(8,128)(2,1)S(1)}, u32[]{:S(2)}, u32[]{:S(2)}) %collective-permute-start.10) | collective-permute-done | bytes 36896 | tf_op jit(solution)/shard_map/ppermute | solution.py:253
  51.1 2.0 %shard_map.58 = (bf16[16,32,256]{2,1,0:T(8,128)(2,1)S(1)}, f32[64,512]{1,0:T(8,128)S(1)}, bf16[224,64]{1,0:T(8,128)(2,1)S(1)}) custom-call(bf16[16,32,256]{2,1,0:T(8,128)(2,1)S(1)} %all-to-all-done.refs_0_, bf16[16,32,256]{2,1,0:T(8,128)(2,1)S(1)} %collective-permute-done.5.refs_1_, f32[2,64,512]{2,1,0:T(8,128)S(1)} %bitcast.54, ...), custom_call_target="tpu_custom_call" | custom-call | tf_op jit(solution)/shard_map/pallas_call | solution.py:215
  53.2 15.4 %all_to_all.10.refs_0_ = bf16[16,32,256]{2,1,0:T(8,128)(2,1)S(1)} all-to-all(bf16[16,32,256]{2,1,0:T(8,128)(2,1)S(1)} %get-tuple-element.32), channel_id=1, replica_groups=mesh['row'=8,'x'=2,'core'=2] {'row','x'}, dimensions={0} | all-to-all | bytes 524288 | tf_op jit(solution)/shard_map/all_to_all | solution.py:268
  68.6 0.4 fusion.2.refs_5_
  69.0 0.8 %collective-permute-start.16 = (f32[2,64,128]{2,1,0:T(8,128)S(1)}, f32[2,64,128]{2,1,0:T(8,128)S(1)}, u32[]{:S(2)}, u32[]{:S(2)}) collective-permute-start(f32[2,64,128]{2,1,0:T(8,128)S(1)} %fusion.2.refs_5_), channel_id=1, source_target_pairs={{0,2},{2,0},{1,3},{3,1},{4,6},{6,4},{5,7},{7,5},{8,10},{10,8},{9,1... | collective-permute-start | bytes 196616 | tf_op jit(solution)/shard_map/ppermute | solution.py:252
  69.9 0.2 collective-permute-start.15
  70.1 3.5 %collective-permute-done.16.refs_7_ = f32[2,64,128]{2,1,0:T(8,128)S(1)} collective-permute-done((f32[2,64,128]{2,1,0:T(8,128)S(1)}, f32[2,64,128]{2,1,0:T(8,128)S(1)}, u32[]{:S(2)}, u32[]{:S(2)}) %collective-permute-start.16) | collective-permute-done | bytes 65568 | tf_op jit(solution)/shard_map/ppermute | solution.py:252
  73.6 1.2 %collective-permute-done.17.refs_8_ = f32[2,64,128]{2,1,0:T(8,128)S(1)} collective-permute-done((f32[2,64,128]{2,1,0:T(8,128)S(1)}, f32[2,64,128]{2,1,0:T(8,128)S(1)}, u32[]{:S(2)}, u32[]{:S(2)}) %collective-permute-start.17) | collective-permute-done | bytes 65568 | tf_op jit(solution)/shard_map/ppermute | solution.py:253
  74.9 0.5 shard_map.59
  75.4 2.2 %shard_map.60 = f32[2,64,512]{2,1,0:T(8,128)} custom-call(bf16[16,32,256]{2,1,0:T(8,128)(2,1)S(1)} %all_to_all.10.refs_0_, bf16[16,32,256]{2,1,0:T(8,128)(2,1)S(1)} %collective-permute-done.14.refs_1_, f32[64,512]{1,0:T(8,128)S(1)} %get-tuple-element.33.refs_2_, f32[64,512]{1,0:T(8,128)S(1)} %get-tuple-element.37.refs_3_, ...), custom_call_target="tpu_custom_call" | custom-call | tf_op jit(solution)/shard_map/pallas_call | solution.py:215
  (37 shorter events, 0.2 us)
Async XLA Ops:
  0.0 1.0 %copy-start = (f32[2,1,512,128]{3,2,1,0:T(8,128)S(1)}, f32[2,1,512,128]{3,2,1,0:T(8,128)}, u32[]{:S(2)}) copy-start(f32[2,1,512,128]{3,2,1,0:T(8,128)} %param.6) | copy-start | bytes 1572868
  1.0 0.9 %copy-start.3 = (bf16[2,1,4,1,32,512]{5,4,3,2,1,0:T(8,128)(2,1)S(1)}, bf16[2,1,4,1,32,512]{5,4,3,2,1,0:T(8,128)(2,1)}, u32[]{:S(2)}) copy-start(bf16[2,1,4,1,32,512]{5,4,3,2,1,0:T(8,128)(2,1)} %param.7) | copy-start | bytes 786436
  2.0 3.1 %copy-start.4 = (bf16[2,1,4,1,32,512]{5,4,3,2,1,0:T(8,128)(2,1)S(1)}, bf16[2,1,4,1,32,512]{5,4,3,2,1,0:T(8,128)(2,1)}, u32[]{:S(2)}) copy-start(bf16[2,1,4,1,32,512]{5,4,3,2,1,0:T(8,128)(2,1)} %param.8) | copy-start | bytes 786436
  2.0 7.7 %copy-start.1 = (f32[2,1,512,128]{3,2,1,0:T(8,128)S(1)}, f32[2,1,512,128]{3,2,1,0:T(8,128)}, u32[]{:S(2)}) copy-start(f32[2,1,512,128]{3,2,1,0:T(8,128)} %param.6) | copy-start | bytes 1572868
  2.0 7.9 %collective-permute-start.3 = (bf16[768,128]{1,0:T(8,128)(2,1)S(1)}, bf16[768,128]{1,0:T(8,128)(2,1)S(1)}, u32[]{:S(2)}, u32[]{:S(2)}) collective-permute-start(bf16[768,128]{1,0:T(8,128)(2,1)S(1)} %shard_map.56.refs_5_.refs_1_), channel_id=1, source_target_pairs={{0,2},{2,0},{1,3},{3,1},{4,6},{6,4},{5,7},{7,5},{8,10},{10,8},{9,1... | collective-permute-start | bytes 589832 | tf_op jit(solution)/shard_map/ppermute | solution.py:252
  5.1 7.8 %collective-permute-start.2 = (bf16[768,128]{1,0:T(8,128)(2,1)S(1)}, bf16[768,128]{1,0:T(8,128)(2,1)S(1)}, u32[]{:S(2)}, u32[]{:S(2)}) collective-permute-start(bf16[768,128]{1,0:T(8,128)(2,1)S(1)} %shard_map.56.refs_5_.refs_1_), channel_id=1, source_target_pairs={{0,1},{1,0},{2,3},{3,2},{4,5},{5,4},{6,7},{7,6},{8,9},{9,8},{10,11... | collective-permute-start | bytes 589832 | tf_op jit(solution)/shard_map/ppermute | solution.py:253
  5.1 0.7 copy-start.5
  6.3 6.5 %collective-permute-start = (bf16[2,32,512]{2,1,0:T(8,128)(2,1)S(1)}, bf16[2,32,512]{2,1,0:T(8,128)(2,1)S(1)}, u32[]{:S(2)}, u32[]{:S(2)}) collective-permute-start(bf16[2,32,512]{2,1,0:T(8,128)(2,1)S(1)} %get-tuple-element.22), channel_id=1, source_target_pairs={{0,0},{1,4},{2,8},{3,12},{4,1},{5,5},{6,9},{7,13},{8,2},{9,6},{10,... | collective-permute-start | bytes 196616 | tf_op jit(solution)/shard_map/ppermute | solution.py:264
  7.0 5.8 %collective-permute-start.1 = (bf16[2,32,512]{2,1,0:T(8,128)(2,1)S(1)}, bf16[2,32,512]{2,1,0:T(8,128)(2,1)S(1)}, u32[]{:S(2)}, u32[]{:S(2)}) collective-permute-start(bf16[2,32,512]{2,1,0:T(8,128)(2,1)S(1)} %get-tuple-element.23), channel_id=1, source_target_pairs={{0,16},{1,20},{2,24},{3,28},{4,17},{5,21},{6,25},{7,29},{8,18},{9,... | collective-permute-start | bytes 196616 | tf_op jit(solution)/shard_map/ppermute | solution.py:264
  9.7 4.2 %copy-start.2 = (f32[2,1,64,512]{3,2,1,0:T(8,128)S(1)}, f32[2,1,64,512]{3,2,1,0:T(8,128)}, u32[]{:S(2)}) copy-start(f32[2,1,64,512]{3,2,1,0:T(8,128)} %param.5) | copy-start | bytes 786436
  10.0 3.9 %collective-permute-start.4 = (bf16[768,128]{1,0:T(8,128)(2,1)S(1)}, bf16[768,128]{1,0:T(8,128)(2,1)S(1)}, u32[]{:S(2)}, u32[]{:S(2)}) collective-permute-start(bf16[768,128]{1,0:T(8,128)(2,1)S(1)} %collective-permute-done.3.refs_7_.refs_3_), channel_id=1, source_target_pairs={{0,1},{1,0},{2,3},{3,2},{4,5},{5,4},{6,7},{7,6},{8,9},{9,8},{10,11... | collective-permute-start | bytes 589832 | tf_op jit(solution)/shard_map/ppermute | solution.py:253
  15.4 19.1 %all-to-all-start = ((bf16[16,32,256]{2,1,0:T(8,128)(2,1)}), bf16[16,32,256]{2,1,0:T(8,128)(2,1)S(1)}, u32[]{:S(2)}, u32[]{:S(2)}) async-start(bf16[16,32,256]{2,1,0:T(8,128)(2,1)} %get-tuple-element.29), calls=%async_computation | async-start | bytes 524288 | tf_op jit(solution)/shard_map/all_to_all | solution.py:268
  23.9 10.6 %collective-permute-start.12 = (bf16[1024,128]{1,0:T(8,128)(2,1)S(1)}, bf16[1024,128]{1,0:T(8,128)(2,1)S(1)}, u32[]{:S(2)}, u32[]{:S(2)}) collective-permute-start(bf16[1024,128]{1,0:T(8,128)(2,1)S(1)} %constant_dynamic-update-slice_fusion.refs_9_.refs_5_), channel_id=1, source_target_pairs={{0,2},{2,0},{1,3},{3,1},{4,6},{6,4},{5,7},{7,5},{8,10},{10,8},{9,1... | collective-permute-start | bytes 786440 | tf_op jit(solution)/shard_map/ppermute | solution.py:252
  25.9 24.1 %collective-permute-start.11 = (bf16[1024,128]{1,0:T(8,128)(2,1)S(1)}, bf16[1024,128]{1,0:T(8,128)(2,1)S(1)}, u32[]{:S(2)}, u32[]{:S(2)}) collective-permute-start(bf16[1024,128]{1,0:T(8,128)(2,1)S(1)} %constant_dynamic-update-slice_fusion.refs_9_.refs_5_), channel_id=1, source_target_pairs={{0,1},{1,0},{2,3},{3,2},{4,5},{5,4},{6,7},{7,6},{8,9},{9,8},{10,11... | collective-permute-start | bytes 786440 | tf_op jit(solution)/shard_map/ppermute | solution.py:253
  34.5 16.6 %collective-permute-start.13 = (bf16[1024,128]{1,0:T(8,128)(2,1)S(1)}, bf16[1024,128]{1,0:T(8,128)(2,1)S(1)}, u32[]{:S(2)}, u32[]{:S(2)}) collective-permute-start(bf16[1024,128]{1,0:T(8,128)(2,1)S(1)} %collective-permute-done.12.refs_11_.refs_7_), channel_id=1, source_target_pairs={{0,1},{1,0},{2,3},{3,2},{4,5},{5,4},{6,7},{7,6},{8,9},{9,8},{10,11... | collective-permute-start | bytes 786440 | tf_op jit(solution)/shard_map/ppermute | solution.py:253
  34.5 16.6 %collective-permute-start.5 = (bf16[16,32,256]{2,1,0:T(8,128)(2,1)S(1)}, bf16[16,32,256]{2,1,0:T(8,128)(2,1)S(1)}, u32[]{:S(2)}, u32[]{:S(2)}) collective-permute-start(bf16[16,32,256]{2,1,0:T(8,128)(2,1)S(1)} %all-to-all-done.refs_0_), channel_id=1, source_target_pairs={{0,1},{1,0},{2,3},{3,2},{4,5},{5,4},{6,7},{7,6},{8,9},{9,8},{10,11... | collective-permute-start | bytes 786440 | tf_op jit(solution)/shard_map/ppermute | solution.py:269
  35.0 3.1 %collective-permute-start.6 = (bf16[32,800]{1,0:T(8,128)(2,1)S(1)}, bf16[32,800]{1,0:T(8,128)(2,1)S(1)}, u32[]{:S(2)}, u32[]{:S(2)}) collective-permute-start(bf16[32,800]{1,0:T(8,128)(2,1)S(1)} %get-tuple-element.30), channel_id=1, source_target_pairs={{0,0},{1,4},{2,8},{3,12},{4,1},{5,5},{6,9},{7,13},{8,2},{9,6},{10,... | collective-permute-start | bytes 153608 | tf_op jit(solution)/shard_map/ppermute | solution.py:264
  35.7 5.1 %collective-permute-start.7 = (bf16[32,800]{1,0:T(8,128)(2,1)S(1)}, bf16[32,800]{1,0:T(8,128)(2,1)S(1)}, u32[]{:S(2)}, u32[]{:S(2)}) collective-permute-start(bf16[32,800]{1,0:T(8,128)(2,1)S(1)} %get-tuple-element.31), channel_id=1, source_target_pairs={{0,16},{1,20},{2,24},{3,28},{4,17},{5,21},{6,25},{7,29},{8,18},{9,... | collective-permute-start | bytes 153608 | tf_op jit(solution)/shard_map/ppermute | solution.py:264
  40.8 9.1 %collective-permute-start.9 = (bf16[2,32,288]{2,1,0:T(8,128)(2,1)S(1)}, bf16[2,32,288]{2,1,0:T(8,128)(2,1)S(1)}, u32[]{:S(2)}, u32[]{:S(2)}) collective-permute-start(bf16[2,32,288]{2,1,0:T(8,128)(2,1)S(1)} %pad_maximum_fusion.refs_5_), channel_id=1, source_target_pairs={{0,2},{2,0},{1,3},{3,1},{4,6},{6,4},{5,7},{7,5},{8,10},{10,8},{9,1... | collective-permute-start | bytes 110600 | tf_op jit(solution)/shard_map/ppermute | solution.py:252
  47.4 2.6 %collective-permute-start.8 = (bf16[2,32,288]{2,1,0:T(8,128)(2,1)S(1)}, bf16[2,32,288]{2,1,0:T(8,128)(2,1)S(1)}, u32[]{:S(2)}, u32[]{:S(2)}) collective-permute-start(bf16[2,32,288]{2,1,0:T(8,128)(2,1)S(1)} %pad_maximum_fusion.refs_5_), channel_id=1, source_target_pairs={{0,1},{1,0},{2,3},{3,2},{4,5},{5,4},{6,7},{7,6},{8,9},{9,8},{10,11... | collective-permute-start | bytes 110600 | tf_op jit(solution)/shard_map/ppermute | solution.py:253
  49.9 1.2 %collective-permute-start.10 = (bf16[2,32,288]{2,1,0:T(8,128)(2,1)S(1)}, bf16[2,32,288]{2,1,0:T(8,128)(2,1)S(1)}, u32[]{:S(2)}, u32[]{:S(2)}) collective-permute-start(bf16[2,32,288]{2,1,0:T(8,128)(2,1)S(1)} %collective-permute-done.9.refs_7_), channel_id=1, source_target_pairs={{0,1},{1,0},{2,3},{3,2},{4,5},{5,4},{6,7},{7,6},{8,9},{9,8},{10,11... | collective-permute-start | bytes 110600 | tf_op jit(solution)/shard_map/ppermute | solution.py:253
  68.6 6.8 %collective-permute-start.14 = (bf16[16,32,256]{2,1,0:T(8,128)(2,1)S(1)}, bf16[16,32,256]{2,1,0:T(8,128)(2,1)S(1)}, u32[]{:S(2)}, u32[]{:S(2)}) collective-permute-start(bf16[16,32,256]{2,1,0:T(8,128)(2,1)S(1)} %all_to_all.10.refs_0_), channel_id=1, source_target_pairs={{0,1},{1,0},{2,3},{3,2},{4,5},{5,4},{6,7},{7,6},{8,9},{9,8},{10,11... | collective-permute-start | bytes 786440 | tf_op jit(solution)/shard_map/ppermute | solution.py:269
  69.0 4.6 %collective-permute-start.16 = (f32[2,64,128]{2,1,0:T(8,128)S(1)}, f32[2,64,128]{2,1,0:T(8,128)S(1)}, u32[]{:S(2)}, u32[]{:S(2)}) collective-permute-start(f32[2,64,128]{2,1,0:T(8,128)S(1)} %fusion.2.refs_5_), channel_id=1, source_target_pairs={{0,2},{2,0},{1,3},{3,1},{4,6},{6,4},{5,7},{7,5},{8,10},{10,8},{9,1... | collective-permute-start | bytes 196616 | tf_op jit(solution)/shard_map/ppermute | solution.py:252
  69.9 3.7 %collective-permute-start.15 = (f32[2,64,128]{2,1,0:T(8,128)S(1)}, f32[2,64,128]{2,1,0:T(8,128)S(1)}, u32[]{:S(2)}, u32[]{:S(2)}) collective-permute-start(f32[2,64,128]{2,1,0:T(8,128)S(1)} %fusion.2.refs_5_), channel_id=1, source_target_pairs={{0,1},{1,0},{2,3},{3,2},{4,5},{5,4},{6,7},{7,6},{8,9},{9,8},{10,11... | collective-permute-start | bytes 196616 | tf_op jit(solution)/shard_map/ppermute | solution.py:253
  73.6 1.3 %collective-permute-start.17 = (f32[2,64,128]{2,1,0:T(8,128)S(1)}, f32[2,64,128]{2,1,0:T(8,128)S(1)}, u32[]{:S(2)}, u32[]{:S(2)}) collective-permute-start(f32[2,64,128]{2,1,0:T(8,128)S(1)} %collective-permute-done.16.refs_7_), channel_id=1, source_target_pairs={{0,1},{1,0},{2,3},{3,2},{4,5},{5,4},{6,7},{7,6},{8,9},{9,8},{10,11... | collective-permute-start | bytes 196616 | tf_op jit(solution)/shard_map/ppermute | solution.py:253

commit v7 on v6

--- a/solution.py
+++ b/solution.py
@@ -67,7 +67,8 @@
 
     def masked(i, k, t):
         v = v_ref[i, k, t]
-        return jnp.where(rank_rows < ranks_ref[i, 0, 0, k * TURNS + t], v, jnp.zeros_like(v))
+        ranks = [ranks_ref[i, 0, :, k * TURNS + n : k * TURNS + n + 1] for n in range(TURNS)]
+        return jnp.where(rank_rows < jnp.where(t == 0, *ranks), v, jnp.zeros_like(v))
 
     for s, (send_ref, later_ref) in enumerate(((send_a_ref, later_a_ref), (send_b_ref, later_b_ref))):
         t = lax.rem(turn + s, TURNS)
@@ -210,12 +211,12 @@
     y_ref[1] = z_ref[...] + split_mm(minus, gathered_inverse(next_ref, order))
 
 
-def call(kernel, outs, *args, scratch=(), scalars=0):
+def call(kernel, outs, *args, scratch=()):
     vmem = pl.BlockSpec(memory_space=pltpu.VMEM)
     return pl.pallas_call(
         kernel,
         out_shape=outs,
-        in_specs=[pl.BlockSpec(memory_space=pltpu.SMEM)] * scalars + [vmem] * (len(args) - scalars),
+        in_specs=[vmem] * len(args),
         out_specs=[vmem] * len(outs),
         scratch_shapes=list(scratch),
         compiler_params=pltpu.CompilerParams(vmem_limit_bytes=24 * 2**20),
@@ -285,7 +286,7 @@
     v_a, v_b, later_a, later_b = call(
         kernel(mask_kernel),
         [shape((2, rank, order), BF)] * 2 + [shape((rank, order), BF)] * 2,
-        ranks, v_here, scalars=1,
+        ranks, v_here,
     )
     near = gather(near)
     v_a, v_b = turn_rows([v_a, v_b])

time: 77.9 us -> 77.5 us (level)
  no operation moved by 1% of the time
where the time goes in v7:
time: 77.5 us; the launch traced here: 77.1 us
  starting transfers between devices  31 us (40%)
  waiting for transfers between devices  20.8 us (27%)
  blocking collectives  15.4 us (20%)
  Pallas kernels  6.45 us (8%)
  local copies, waits for them, and re-layouts  2.79 us (4%)
    all_to_all x1, blocking collectives, spread(): lax.all_to_all(m, ('row', 'x'), split_axis=0, concat_axis=0, tiled=True)  15.4 us
    ppermute x4, waiting for transfers between devices, gather(): moved = lax.ppermute(part, 'x', [(i, (i + s) % n_x) for i in range(n_x)])  14.7 us
    ppermute x4, starting transfers between devices, gather(): moved = lax.ppermute(part, 'x', [(i, (i + s) % n_x) for i in range(n_x)])  12.4 us
    all_to_all x1, starting transfers between devices, spread(): lax.all_to_all(m, ('row', 'x'), split_axis=0, concat_axis=0, tiled=True)  8.42 us
    pallas_call x6, Pallas kernels, call(): pl.pallas_call(kernel, out_shape=outs, in_specs=[vmem] * len(args), out_s...  6.45 us
    ppermute x4, starting transfers between devices, turn_rows(): got.append(lax.ppermute(parts[s], everywhere, pairs))  6.4 us
    ppermute x8, waiting for transfers between devices, gather(): pieces += [moved, lax.ppermute(moved, 'core', swap)]  3.41 us
    ppermute x8, starting transfers between devices, gather(): pieces += [moved, lax.ppermute(moved, 'core', swap)]  3.28 us
  transfers between devices with their start and end apart: 19, of which 8 were waited for; matrix products, arithmetic and copies ran while one was open for 1% of the time, Pallas kernels for 1%

profile of v7, /device:TPU:0, one launch (start us, length us, event | category | flops | bytes accessed | tf_op | source)
XLA Modules:
  0.0 77.1 jit_solution(9753698540544348316)
XLA Ops:
  0.0 1.0 %copy-done = f32[2,1,512,128]{3,2,1,0:T(8,128)S(1)} copy-done((f32[2,1,512,128]{3,2,1,0:T(8,128)S(1)}, f32[2,1,512,128]{3,2,1,0:T(8,128)}, u32[]{:S(2)}) %copy-start) | copy-done | bytes 524312
  1.0 0.9 %copy-done.3 = bf16[2,1,4,1,32,512]{5,4,3,2,1,0:T(8,128)(2,1)S(1)} copy-done((bf16[2,1,4,1,32,512]{5,4,3,2,1,0:T(8,128)(2,1)S(1)}, bf16[2,1,4,1,32,512]{5,4,3,2,1,0:T(8,128)(2,1)}, u32[]{:S(2)}) %copy-start.3) | copy-done | bytes 262168
  2.0 3.0 %collective-permute-start.3 = (bf16[768,128]{1,0:T(8,128)(2,1)S(1)}, bf16[768,128]{1,0:T(8,128)(2,1)S(1)}, u32[]{:S(2)}, u32[]{:S(2)}) collective-permute-start(bf16[768,128]{1,0:T(8,128)(2,1)S(1)} %shard_map.56.refs_5_.refs_1_), channel_id=1, source_target_pairs={{0,2},{2,0},{1,3},{3,1},{4,6},{6,4},{5,7},{7,5},{8,10},{10,8},{9,1... | collective-permute-start | bytes 589832 | tf_op jit(solution)/shard_map/ppermute | solution.py:253
  5.1 0.7 copy-done.5
  5.7 0.2 shard_map.55
  5.9 0.7 collective-permute-start
  6.6 2.7 %collective-permute-start.1 = (bf16[2,32,512]{2,1,0:T(8,128)(2,1)S(1)}, bf16[2,32,512]{2,1,0:T(8,128)(2,1)S(1)}, u32[]{:S(2)}, u32[]{:S(2)}) collective-permute-start(bf16[2,32,512]{2,1,0:T(8,128)(2,1)S(1)} %get-tuple-element.23), channel_id=1, source_target_pairs={{0,16},{1,20},{2,24},{3,28},{4,17},{5,21},{6,25},{7,29},{8,18},{9,... | collective-permute-start | bytes 196616 | tf_op jit(solution)/shard_map/ppermute | solution.py:265
  9.4 0.6 collective-permute-done.3.refs_7_.refs_3_
  10.0 2.4 %collective-permute-start.4 = (bf16[768,128]{1,0:T(8,128)(2,1)S(1)}, bf16[768,128]{1,0:T(8,128)(2,1)S(1)}, u32[]{:S(2)}, u32[]{:S(2)}) collective-permute-start(bf16[768,128]{1,0:T(8,128)(2,1)S(1)} %collective-permute-done.3.refs_7_.refs_3_), channel_id=1, source_target_pairs={{0,1},{1,0},{2,3},{3,2},{4,5},{5,4},{6,7},{7,6},{8,9},{9,8},{10,11... | collective-permute-start | bytes 589832 | tf_op jit(solution)/shard_map/ppermute | solution.py:254
  12.4 1.0 %collective-permute-done.4.refs_8_.refs_4_ = bf16[768,128]{1,0:T(8,128)(2,1)S(1)} collective-permute-done((bf16[768,128]{1,0:T(8,128)(2,1)S(1)}, bf16[768,128]{1,0:T(8,128)(2,1)S(1)}, u32[]{:S(2)}, u32[]{:S(2)}) %collective-permute-start.4) | collective-permute-done | bytes 196640 | tf_op jit(solution)/shard_map/ppermute | solution.py:254
  13.4 1.5 %shard_map.57 = (bf16[16,32,256]{2,1,0:T(8,128)(2,1)}, bf16[32,800]{1,0:T(8,128)(2,1)S(1)}, bf16[32,800]{1,0:T(8,128)(2,1)S(1)}) custom-call(f32[2,64,512]{2,1,0:T(8,128)S(1)} %bitcast.53, bf16[2,32,512]{2,1,0:T(8,128)(2,1)S(1)} %collective-permute-done.refs_1_, bf16[2,32,512]{2,1,0:T(8,128)(2,1)S(1)} %collective-permute-done.1.refs_2_, ...), custom_call_target="tpu_custom_call" | custom-call | tf_op jit(solution)/shard_map/pallas_call | solution.py:216
  15.0 8.4 %all-to-all-start = ((bf16[16,32,256]{2,1,0:T(8,128)(2,1)}), bf16[16,32,256]{2,1,0:T(8,128)(2,1)S(1)}, u32[]{:S(2)}, u32[]{:S(2)}) async-start(bf16[16,32,256]{2,1,0:T(8,128)(2,1)} %get-tuple-element.29), calls=%async_computation | async-start | bytes 524288 | tf_op jit(solution)/shard_map/all_to_all | solution.py:269
  23.4 2.0 %collective-permute-start.12 = (bf16[1024,128]{1,0:T(8,128)(2,1)S(1)}, bf16[1024,128]{1,0:T(8,128)(2,1)S(1)}, u32[]{:S(2)}, u32[]{:S(2)}) collective-permute-start(bf16[1024,128]{1,0:T(8,128)(2,1)S(1)} %constant_dynamic-update-slice_fusion.refs_9_.refs_5_), channel_id=1, source_target_pairs={{0,2},{2,0},{1,3},{3,1},{4,6},{6,4},{5,7},{7,5},{8,10},{10,8},{9,1... | collective-permute-start | bytes 786440 | tf_op jit(solution)/shard_map/ppermute | solution.py:253
  25.4 8.6 %collective-permute-done.12.refs_11_.refs_7_ = bf16[1024,128]{1,0:T(8,128)(2,1)S(1)} collective-permute-done((bf16[1024,128]{1,0:T(8,128)(2,1)S(1)}, bf16[1024,128]{1,0:T(8,128)(2,1)S(1)}, u32[]{:S(2)}, u32[]{:S(2)}) %collective-permute-start.12) | collective-permute-done | bytes 262176 | tf_op jit(solution)/shard_map/ppermute | solution.py:253
  34.1 0.5 collective-permute-start.5
  34.6 0.7 collective-permute-start.6
  35.2 2.4 %collective-permute-start.7 = (bf16[32,800]{1,0:T(8,128)(2,1)S(1)}, bf16[32,800]{1,0:T(8,128)(2,1)S(1)}, u32[]{:S(2)}, u32[]{:S(2)}) collective-permute-start(bf16[32,800]{1,0:T(8,128)(2,1)S(1)} %get-tuple-element.31), channel_id=1, source_target_pairs={{0,16},{1,20},{2,24},{3,28},{4,17},{5,21},{6,25},{7,29},{8,18},{9,... | collective-permute-start | bytes 153608 | tf_op jit(solution)/shard_map/ppermute | solution.py:265
  37.7 2.7 %collective-permute-done.7.refs_4_ = bf16[32,800]{1,0:T(8,128)(2,1)S(1)} collective-permute-done((bf16[32,800]{1,0:T(8,128)(2,1)S(1)}, bf16[32,800]{1,0:T(8,128)(2,1)S(1)}, u32[]{:S(2)}, u32[]{:S(2)}) %collective-permute-start.7) | collective-permute-done | bytes 51232 | tf_op jit(solution)/shard_map/ppermute | solution.py:265
  40.4 6.6 %collective-permute-start.9 = (bf16[2,32,288]{2,1,0:T(8,128)(2,1)S(1)}, bf16[2,32,288]{2,1,0:T(8,128)(2,1)S(1)}, u32[]{:S(2)}, u32[]{:S(2)}) collective-permute-start(bf16[2,32,288]{2,1,0:T(8,128)(2,1)S(1)} %pad_maximum_fusion.refs_5_), channel_id=1, source_target_pairs={{0,2},{2,0},{1,3},{3,1},{4,6},{6,4},{5,7},{7,5},{8,10},{10,8},{9,1... | collective-permute-start | bytes 110600 | tf_op jit(solution)/shard_map/ppermute | solution.py:253
  47.0 0.5 collective-permute-start.8
  47.5 2.0 %collective-permute-done.9.refs_7_ = bf16[2,32,288]{2,1,0:T(8,128)(2,1)S(1)} collective-permute-done((bf16[2,32,288]{2,1,0:T(8,128)(2,1)S(1)}, bf16[2,32,288]{2,1,0:T(8,128)(2,1)S(1)}, u32[]{:S(2)}, u32[]{:S(2)}) %collective-permute-start.9) | collective-permute-done | bytes 36896 | tf_op jit(solution)/shard_map/ppermute | solution.py:253
  49.4 0.1 collective-permute-start.10
  49.6 1.1 %collective-permute-done.10.refs_8_ = bf16[2,32,288]{2,1,0:T(8,128)(2,1)S(1)} collective-permute-done((bf16[2,32,288]{2,1,0:T(8,128)(2,1)S(1)}, bf16[2,32,288]{2,1,0:T(8,128)(2,1)S(1)}, u32[]{:S(2)}, u32[]{:S(2)}) %collective-permute-start.10) | collective-permute-done | bytes 36896 | tf_op jit(solution)/shard_map/ppermute | solution.py:254
  50.7 2.0 %shard_map.58 = (bf16[16,32,256]{2,1,0:T(8,128)(2,1)S(1)}, f32[64,512]{1,0:T(8,128)S(1)}, bf16[224,64]{1,0:T(8,128)(2,1)S(1)}) custom-call(bf16[16,32,256]{2,1,0:T(8,128)(2,1)S(1)} %all-to-all-done.refs_0_, bf16[16,32,256]{2,1,0:T(8,128)(2,1)S(1)} %collective-permute-done.5.refs_1_, f32[2,64,512]{2,1,0:T(8,128)S(1)} %bitcast.54, ...), custom_call_target="tpu_custom_call" | custom-call | tf_op jit(solution)/shard_map/pallas_call | solution.py:216
  52.7 15.4 %all_to_all.10.refs_0_ = bf16[16,32,256]{2,1,0:T(8,128)(2,1)S(1)} all-to-all(bf16[16,32,256]{2,1,0:T(8,128)(2,1)S(1)} %get-tuple-element.32), channel_id=1, replica_groups=mesh['row'=8,'x'=2,'core'=2] {'row','x'}, dimensions={0} | all-to-all | bytes 524288 | tf_op jit(solution)/shard_map/all_to_all | solution.py:269
  68.2 0.4 fusion.2.refs_5_
  68.6 0.8 %collective-permute-start.16 = (f32[2,64,128]{2,1,0:T(8,128)S(1)}, f32[2,64,128]{2,1,0:T(8,128)S(1)}, u32[]{:S(2)}, u32[]{:S(2)}) collective-permute-start(f32[2,64,128]{2,1,0:T(8,128)S(1)} %fusion.2.refs_5_), channel_id=1, source_target_pairs={{0,2},{2,0},{1,3},{3,1},{4,6},{6,4},{5,7},{7,5},{8,10},{10,8},{9,1... | collective-permute-start | bytes 196616 | tf_op jit(solution)/shard_map/ppermute | solution.py:253
  69.4 0.2 collective-permute-start.15
  69.7 3.5 %collective-permute-done.16.refs_7_ = f32[2,64,128]{2,1,0:T(8,128)S(1)} collective-permute-done((f32[2,64,128]{2,1,0:T(8,128)S(1)}, f32[2,64,128]{2,1,0:T(8,128)S(1)}, u32[]{:S(2)}, u32[]{:S(2)}) %collective-permute-start.16) | collective-permute-done | bytes 65568 | tf_op jit(solution)/shard_map/ppermute | solution.py:253
  73.2 1.2 %collective-permute-done.17.refs_8_ = f32[2,64,128]{2,1,0:T(8,128)S(1)} collective-permute-done((f32[2,64,128]{2,1,0:T(8,128)S(1)}, f32[2,64,128]{2,1,0:T(8,128)S(1)}, u32[]{:S(2)}, u32[]{:S(2)}) %collective-permute-start.17) | collective-permute-done | bytes 65568 | tf_op jit(solution)/shard_map/ppermute | solution.py:254
  74.4 0.5 shard_map.59
  74.9 2.2 %shard_map.60 = f32[2,64,512]{2,1,0:T(8,128)} custom-call(bf16[16,32,256]{2,1,0:T(8,128)(2,1)S(1)} %all_to_all.10.refs_0_, bf16[16,32,256]{2,1,0:T(8,128)(2,1)S(1)} %collective-permute-done.14.refs_1_, f32[64,512]{1,0:T(8,128)S(1)} %get-tuple-element.33.refs_2_, f32[64,512]{1,0:T(8,128)S(1)} %get-tuple-element.37.refs_3_, ...), custom_call_target="tpu_custom_call" | custom-call | tf_op jit(solution)/shard_map/pallas_call | solution.py:216
  (37 shorter events, 0.2 us)
Async XLA Ops:
  0.0 1.0 %copy-start = (f32[2,1,512,128]{3,2,1,0:T(8,128)S(1)}, f32[2,1,512,128]{3,2,1,0:T(8,128)}, u32[]{:S(2)}) copy-start(f32[2,1,512,128]{3,2,1,0:T(8,128)} %param.6) | copy-start | bytes 1572868
  1.0 0.9 %copy-start.3 = (bf16[2,1,4,1,32,512]{5,4,3,2,1,0:T(8,128)(2,1)S(1)}, bf16[2,1,4,1,32,512]{5,4,3,2,1,0:T(8,128)(2,1)}, u32[]{:S(2)}) copy-start(bf16[2,1,4,1,32,512]{5,4,3,2,1,0:T(8,128)(2,1)} %param.7) | copy-start | bytes 786436
  2.0 3.1 %copy-start.4 = (bf16[2,1,4,1,32,512]{5,4,3,2,1,0:T(8,128)(2,1)S(1)}, bf16[2,1,4,1,32,512]{5,4,3,2,1,0:T(8,128)(2,1)}, u32[]{:S(2)}) copy-start(bf16[2,1,4,1,32,512]{5,4,3,2,1,0:T(8,128)(2,1)} %param.8) | copy-start | bytes 786436
  2.0 7.2 %copy-start.1 = (f32[2,1,512,128]{3,2,1,0:T(8,128)S(1)}, f32[2,1,512,128]{3,2,1,0:T(8,128)}, u32[]{:S(2)}) copy-start(f32[2,1,512,128]{3,2,1,0:T(8,128)} %param.6) | copy-start | bytes 1572868
  2.0 7.9 %collective-permute-start.3 = (bf16[768,128]{1,0:T(8,128)(2,1)S(1)}, bf16[768,128]{1,0:T(8,128)(2,1)S(1)}, u32[]{:S(2)}, u32[]{:S(2)}) collective-permute-start(bf16[768,128]{1,0:T(8,128)(2,1)S(1)} %shard_map.56.refs_5_.refs_1_), channel_id=1, source_target_pairs={{0,2},{2,0},{1,3},{3,1},{4,6},{6,4},{5,7},{7,5},{8,10},{10,8},{9,1... | collective-permute-start | bytes 589832 | tf_op jit(solution)/shard_map/ppermute | solution.py:253
  5.1 7.3 %collective-permute-start.2 = (bf16[768,128]{1,0:T(8,128)(2,1)S(1)}, bf16[768,128]{1,0:T(8,128)(2,1)S(1)}, u32[]{:S(2)}, u32[]{:S(2)}) collective-permute-start(bf16[768,128]{1,0:T(8,128)(2,1)S(1)} %shard_map.56.refs_5_.refs_1_), channel_id=1, source_target_pairs={{0,1},{1,0},{2,3},{3,2},{4,5},{5,4},{6,7},{7,6},{8,9},{9,8},{10,11... | collective-permute-start | bytes 589832 | tf_op jit(solution)/shard_map/ppermute | solution.py:254
  5.1 0.7 copy-start.5
  5.9 6.5 %collective-permute-start = (bf16[2,32,512]{2,1,0:T(8,128)(2,1)S(1)}, bf16[2,32,512]{2,1,0:T(8,128)(2,1)S(1)}, u32[]{:S(2)}, u32[]{:S(2)}) collective-permute-start(bf16[2,32,512]{2,1,0:T(8,128)(2,1)S(1)} %get-tuple-element.22), channel_id=1, source_target_pairs={{0,0},{1,4},{2,8},{3,12},{4,1},{5,5},{6,9},{7,13},{8,2},{9,6},{10,... | collective-permute-start | bytes 196616 | tf_op jit(solution)/shard_map/ppermute | solution.py:265
  6.6 5.8 %collective-permute-start.1 = (bf16[2,32,512]{2,1,0:T(8,128)(2,1)S(1)}, bf16[2,32,512]{2,1,0:T(8,128)(2,1)S(1)}, u32[]{:S(2)}, u32[]{:S(2)}) collective-permute-start(bf16[2,32,512]{2,1,0:T(8,128)(2,1)S(1)} %get-tuple-element.23), channel_id=1, source_target_pairs={{0,16},{1,20},{2,24},{3,28},{4,17},{5,21},{6,25},{7,29},{8,18},{9,... | collective-permute-start | bytes 196616 | tf_op jit(solution)/shard_map/ppermute | solution.py:265
  9.2 4.2 %copy-start.2 = (f32[2,1,64,512]{3,2,1,0:T(8,128)S(1)}, f32[2,1,64,512]{3,2,1,0:T(8,128)}, u32[]{:S(2)}) copy-start(f32[2,1,64,512]{3,2,1,0:T(8,128)} %param.5) | copy-start | bytes 786436
  10.0 3.5 %collective-permute-start.4 = (bf16[768,128]{1,0:T(8,128)(2,1)S(1)}, bf16[768,128]{1,0:T(8,128)(2,1)S(1)}, u32[]{:S(2)}, u32[]{:S(2)}) collective-permute-start(bf16[768,128]{1,0:T(8,128)(2,1)S(1)} %collective-permute-done.3.refs_7_.refs_3_), channel_id=1, source_target_pairs={{0,1},{1,0},{2,3},{3,2},{4,5},{5,4},{6,7},{7,6},{8,9},{9,8},{10,11... | collective-permute-start | bytes 589832 | tf_op jit(solution)/shard_map/ppermute | solution.py:254
  15.0 19.1 %all-to-all-start = ((bf16[16,32,256]{2,1,0:T(8,128)(2,1)}), bf16[16,32,256]{2,1,0:T(8,128)(2,1)S(1)}, u32[]{:S(2)}, u32[]{:S(2)}) async-start(bf16[16,32,256]{2,1,0:T(8,128)(2,1)} %get-tuple-element.29), calls=%async_computation | async-start | bytes 524288 | tf_op jit(solution)/shard_map/all_to_all | solution.py:269
  23.4 10.6 %collective-permute-start.12 = (bf16[1024,128]{1,0:T(8,128)(2,1)S(1)}, bf16[1024,128]{1,0:T(8,128)(2,1)S(1)}, u32[]{:S(2)}, u32[]{:S(2)}) collective-permute-start(bf16[1024,128]{1,0:T(8,128)(2,1)S(1)} %constant_dynamic-update-slice_fusion.refs_9_.refs_5_), channel_id=1, source_target_pairs={{0,2},{2,0},{1,3},{3,1},{4,6},{6,4},{5,7},{7,5},{8,10},{10,8},{9,1... | collective-permute-start | bytes 786440 | tf_op jit(solution)/shard_map/ppermute | solution.py:253
  25.4 24.1 %collective-permute-start.11 = (bf16[1024,128]{1,0:T(8,128)(2,1)S(1)}, bf16[1024,128]{1,0:T(8,128)(2,1)S(1)}, u32[]{:S(2)}, u32[]{:S(2)}) collective-permute-start(bf16[1024,128]{1,0:T(8,128)(2,1)S(1)} %constant_dynamic-update-slice_fusion.refs_9_.refs_5_), channel_id=1, source_target_pairs={{0,1},{1,0},{2,3},{3,2},{4,5},{5,4},{6,7},{7,6},{8,9},{9,8},{10,11... | collective-permute-start | bytes 786440 | tf_op jit(solution)/shard_map/ppermute | solution.py:254
  34.1 16.6 %collective-permute-start.13 = (bf16[1024,128]{1,0:T(8,128)(2,1)S(1)}, bf16[1024,128]{1,0:T(8,128)(2,1)S(1)}, u32[]{:S(2)}, u32[]{:S(2)}) collective-permute-start(bf16[1024,128]{1,0:T(8,128)(2,1)S(1)} %collective-permute-done.12.refs_11_.refs_7_), channel_id=1, source_target_pairs={{0,1},{1,0},{2,3},{3,2},{4,5},{5,4},{6,7},{7,6},{8,9},{9,8},{10,11... | collective-permute-start | bytes 786440 | tf_op jit(solution)/shard_map/ppermute | solution.py:254
  34.1 16.6 %collective-permute-start.5 = (bf16[16,32,256]{2,1,0:T(8,128)(2,1)S(1)}, bf16[16,32,256]{2,1,0:T(8,128)(2,1)S(1)}, u32[]{:S(2)}, u32[]{:S(2)}) collective-permute-start(bf16[16,32,256]{2,1,0:T(8,128)(2,1)S(1)} %all-to-all-done.refs_0_), channel_id=1, source_target_pairs={{0,1},{1,0},{2,3},{3,2},{4,5},{5,4},{6,7},{7,6},{8,9},{9,8},{10,11... | collective-permute-start | bytes 786440 | tf_op jit(solution)/shard_map/ppermute | solution.py:270
  34.6 3.1 %collective-permute-start.6 = (bf16[32,800]{1,0:T(8,128)(2,1)S(1)}, bf16[32,800]{1,0:T(8,128)(2,1)S(1)}, u32[]{:S(2)}, u32[]{:S(2)}) collective-permute-start(bf16[32,800]{1,0:T(8,128)(2,1)S(1)} %get-tuple-element.30), channel_id=1, source_target_pairs={{0,0},{1,4},{2,8},{3,12},{4,1},{5,5},{6,9},{7,13},{8,2},{9,6},{10,... | collective-permute-start | bytes 153608 | tf_op jit(solution)/shard_map/ppermute | solution.py:265
  35.2 5.1 %collective-permute-start.7 = (bf16[32,800]{1,0:T(8,128)(2,1)S(1)}, bf16[32,800]{1,0:T(8,128)(2,1)S(1)}, u32[]{:S(2)}, u32[]{:S(2)}) collective-permute-start(bf16[32,800]{1,0:T(8,128)(2,1)S(1)} %get-tuple-element.31), channel_id=1, source_target_pairs={{0,16},{1,20},{2,24},{3,28},{4,17},{5,21},{6,25},{7,29},{8,18},{9,... | collective-permute-start | bytes 153608 | tf_op jit(solution)/shard_map/ppermute | solution.py:265
  40.4 9.1 %collective-permute-start.9 = (bf16[2,32,288]{2,1,0:T(8,128)(2,1)S(1)}, bf16[2,32,288]{2,1,0:T(8,128)(2,1)S(1)}, u32[]{:S(2)}, u32[]{:S(2)}) collective-permute-start(bf16[2,32,288]{2,1,0:T(8,128)(2,1)S(1)} %pad_maximum_fusion.refs_5_), channel_id=1, source_target_pairs={{0,2},{2,0},{1,3},{3,1},{4,6},{6,4},{5,7},{7,5},{8,10},{10,8},{9,1... | collective-permute-start | bytes 110600 | tf_op jit(solution)/shard_map/ppermute | solution.py:253
  47.0 2.6 %collective-permute-start.8 = (bf16[2,32,288]{2,1,0:T(8,128)(2,1)S(1)}, bf16[2,32,288]{2,1,0:T(8,128)(2,1)S(1)}, u32[]{:S(2)}, u32[]{:S(2)}) collective-permute-start(bf16[2,32,288]{2,1,0:T(8,128)(2,1)S(1)} %pad_maximum_fusion.refs_5_), channel_id=1, source_target_pairs={{0,1},{1,0},{2,3},{3,2},{4,5},{5,4},{6,7},{7,6},{8,9},{9,8},{10,11... | collective-permute-start | bytes 110600 | tf_op jit(solution)/shard_map/ppermute | solution.py:254
  49.4 1.2 %collective-permute-start.10 = (bf16[2,32,288]{2,1,0:T(8,128)(2,1)S(1)}, bf16[2,32,288]{2,1,0:T(8,128)(2,1)S(1)}, u32[]{:S(2)}, u32[]{:S(2)}) collective-permute-start(bf16[2,32,288]{2,1,0:T(8,128)(2,1)S(1)} %collective-permute-done.9.refs_7_), channel_id=1, source_target_pairs={{0,1},{1,0},{2,3},{3,2},{4,5},{5,4},{6,7},{7,6},{8,9},{9,8},{10,11... | collective-permute-start | bytes 110600 | tf_op jit(solution)/shard_map/ppermute | solution.py:254
  68.2 6.8 %collective-permute-start.14 = (bf16[16,32,256]{2,1,0:T(8,128)(2,1)S(1)}, bf16[16,32,256]{2,1,0:T(8,128)(2,1)S(1)}, u32[]{:S(2)}, u32[]{:S(2)}) collective-permute-start(bf16[16,32,256]{2,1,0:T(8,128)(2,1)S(1)} %all_to_all.10.refs_0_), channel_id=1, source_target_pairs={{0,1},{1,0},{2,3},{3,2},{4,5},{5,4},{6,7},{7,6},{8,9},{9,8},{10,11... | collective-permute-start | bytes 786440 | tf_op jit(solution)/shard_map/ppermute | solution.py:270
  68.6 4.6 %collective-permute-start.16 = (f32[2,64,128]{2,1,0:T(8,128)S(1)}, f32[2,64,128]{2,1,0:T(8,128)S(1)}, u32[]{:S(2)}, u32[]{:S(2)}) collective-permute-start(f32[2,64,128]{2,1,0:T(8,128)S(1)} %fusion.2.refs_5_), channel_id=1, source_target_pairs={{0,2},{2,0},{1,3},{3,1},{4,6},{6,4},{5,7},{7,5},{8,10},{10,8},{9,1... | collective-permute-start | bytes 196616 | tf_op jit(solution)/shard_map/ppermute | solution.py:253
  69.4 3.7 %collective-permute-start.15 = (f32[2,64,128]{2,1,0:T(8,128)S(1)}, f32[2,64,128]{2,1,0:T(8,128)S(1)}, u32[]{:S(2)}, u32[]{:S(2)}) collective-permute-start(f32[2,64,128]{2,1,0:T(8,128)S(1)} %fusion.2.refs_5_), channel_id=1, source_target_pairs={{0,1},{1,0},{2,3},{3,2},{4,5},{5,4},{6,7},{7,6},{8,9},{9,8},{10,11... | collective-permute-start | bytes 196616 | tf_op jit(solution)/shard_map/ppermute | solution.py:254
  73.2 1.3 %collective-permute-start.17 = (f32[2,64,128]{2,1,0:T(8,128)S(1)}, f32[2,64,128]{2,1,0:T(8,128)S(1)}, u32[]{:S(2)}, u32[]{:S(2)}) collective-permute-start(f32[2,64,128]{2,1,0:T(8,128)S(1)} %collective-permute-done.16.refs_7_), channel_id=1, source_target_pairs={{0,1},{1,0},{2,3},{3,2},{4,5},{5,4},{6,7},{7,6},{8,9},{9,8},{10,11... | collective-permute-start | bytes 196616 | tf_op jit(solution)/shard_map/ppermute | solution.py:254

commit v8 on v6

--- a/solution.py
+++ b/solution.py
@@ -54,15 +54,25 @@
     return jnp.concatenate([ref[source, at + m * rows + start : at + m * rows + stop, :] for m in range(count)], axis=1)
 
 
-def near_kernel(dims, inv_ref, u_ref, near_ref):
+def prep_kernel(dims, ranks_hbm, inv_hbm, u_hbm, v_hbm, near_ref, send_a_ref, send_b_ref, later_a_ref, later_b_ref,
+                ranks_ref, inv_ref, u_ref, v_ref, sems):
     _, _, _, rank, _, _ = dims
-    order = inv_ref.shape[1]
-    near_ref[:order, :] = inv_ref[0].astype(BF)
-    put_columns(near_ref, order, TURNS * rank, u_ref[0, 0].reshape(TURNS * rank, order))
-
-
-def mask_kernel(dims, ranks_ref, v_ref, send_a_ref, send_b_ref, later_a_ref, later_b_ref):
     _, _, turn = place()
+    order = inv_ref.shape[0]
+    copies = [
+        pltpu.make_async_copy(inv_hbm.at[0], inv_ref, sems.at[0]),
+        pltpu.make_async_copy(u_hbm.at[0, 0], u_ref, sems.at[1]),
+        pltpu.make_async_copy(v_hbm, v_ref, sems.at[2]),
+        pltpu.make_async_copy(ranks_hbm, ranks_ref, sems.at[3]),
+    ]
+    for copy in copies:
+        copy.start()
+    copies[0].wait()
+    copies[1].wait()
+    near_ref[:order, :] = inv_ref[...].astype(BF)
+    put_columns(near_ref, order, TURNS * rank, u_ref[...].reshape(TURNS * rank, order))
+    copies[2].wait()
+    copies[3].wait()
     rank_rows = lax.broadcasted_iota(jnp.int32, v_ref.shape[3:], 0)
 
     def masked(i, k, t):
@@ -210,13 +220,12 @@
     y_ref[1] = z_ref[...] + split_mm(minus, gathered_inverse(next_ref, order))
 
 
-def call(kernel, outs, *args, scratch=(), scalars=0):
-    vmem = pl.BlockSpec(memory_space=pltpu.VMEM)
+def call(kernel, outs, *args, scratch=(), space=pltpu.VMEM):
     return pl.pallas_call(
         kernel,
         out_shape=outs,
-        in_specs=[pl.BlockSpec(memory_space=pltpu.SMEM)] * scalars + [vmem] * (len(args) - scalars),
-        out_specs=[vmem] * len(outs),
+        in_specs=[pl.BlockSpec(memory_space=space)] * len(args),
+        out_specs=[pl.BlockSpec(memory_space=pltpu.VMEM)] * len(outs),
         scratch_shapes=list(scratch),
         compiler_params=pltpu.CompilerParams(vmem_limit_bytes=24 * 2**20),
     )(*args)
@@ -281,11 +290,18 @@
         pltpu.VMEM((n_row, width + rank, r_cols), BF),
     ]
 
-    (near,) = call(kernel(near_kernel), [shape((order + u_rows, lanes), BF)], inv_here, u_here)
-    v_a, v_b, later_a, later_b = call(
-        kernel(mask_kernel),
-        [shape((2, rank, order), BF)] * 2 + [shape((rank, order), BF)] * 2,
-        ranks, v_here, scalars=1,
+    in_hbm = [pltpu.with_memory_space_constraint(x, pltpu.HBM) for x in (ranks, inv_here, u_here, v_here)]
+    near, v_a, v_b, later_a, later_b = call(
+        kernel(prep_kernel),
+        [shape((order + u_rows, lanes), BF)] + [shape((2, rank, order), BF)] * 2 + [shape((rank, order), BF)] * 2,
+        *in_hbm, space=pltpu.HBM,
+        scratch=[
+            pltpu.SMEM(ranks.shape, jnp.int32),
+            pltpu.VMEM((order, lanes), F32),
+            pltpu.VMEM((TURNS, rank, order), BF),
+            pltpu.VMEM((slots, slots, TURNS, rank, order), BF),
+            pltpu.SemaphoreType.DMA((4,)),
+        ],
     )
     near = gather(near)
     v_a, v_b = turn_rows([v_a, v_b])

time: 77.9 us -> 75.8 us (0.973)
  local copies, waits for them, and re-layouts: 2.79 us -> 0.12 us
  starting transfers between devices: 31.5 us -> 30.2 us
  waiting for transfers between devices: 20.4 us -> 21.7 us
    unnamed x20 -> x14, local copies, waits for them, and re-layouts: 2.77 us -> 0.1 us
    ppermute x8, starting transfers between devices: 3.72 us -> 2.43 us  [gather(): pieces += [moved, lax.ppermute(moved, 'core', swap)]]
    ppermute x4, waiting for transfers between devices: 14.3 us -> 15.5 us  [gather(): moved = lax.ppermute(part, 'x', [(i, (i + s) % n_x) for i in range(n_x)])]
    pallas_call x6 -> x5, Pallas kernels: 6.89 us -> 7.48 us  [call(): pl.pallas_call(kernel, out_shape=outs, in_specs=[pl.BlockSpec(memory_spac...]
where the time goes in v8:
time: 75.8 us; the launch traced here: 75.5 us
  starting transfers between devices  30.2 us (40%)
  waiting for transfers between devices  21.7 us (29%)
  blocking collectives  15.4 us (20%)
  Pallas kernels  7.48 us (10%)
    ppermute x4, waiting for transfers between devices, gather(): moved = lax.ppermute(part, 'x', [(i, (i + s) % n_x) for i in range(n_x)])  15.5 us
    all_to_all x1, blocking collectives, spread(): lax.all_to_all(m, ('row', 'x'), split_axis=0, concat_axis=0, tiled=True)  15.4 us
    ppermute x4, starting transfers between devices, gather(): moved = lax.ppermute(part, 'x', [(i, (i + s) % n_x) for i in range(n_x)])  12.4 us
    all_to_all x1, starting transfers between devices, spread(): lax.all_to_all(m, ('row', 'x'), split_axis=0, concat_axis=0, tiled=True)  8.42 us
    pallas_call x5, Pallas kernels, call(): pl.pallas_call(kernel, out_shape=outs, in_specs=[pl.BlockSpec(memory_spac...  7.48 us
    ppermute x4, starting transfers between devices, turn_rows(): got.append(lax.ppermute(parts[s], everywhere, pairs))  6.39 us
    ppermute x8, waiting for transfers between devices, gather(): pieces += [moved, lax.ppermute(moved, 'core', swap)]  3.41 us
    ppermute x4, waiting for transfers between devices, turn_rows(): got.append(lax.ppermute(parts[s], everywhere, pairs))  2.72 us
  transfers between devices with their start and end apart: 19, of which 8 were waited for; matrix products, arithmetic and copies ran while one was open for 1% of the time, Pallas kernels for 1%

profile of v8, /device:TPU:0, one launch (start us, length us, event | category | flops | bytes accessed | tf_op | source)
XLA Modules:
  0.0 75.5 jit_solution(8487047730398561538)
XLA Ops:
  0.0 1.2 %shard_map.55 = (bf16[768,128]{1,0:T(8,128)(2,1)S(1)}, bf16[2,32,512]{2,1,0:T(8,128)(2,1)S(1)}, bf16[2,32,512]{2,1,0:T(8,128)(2,1)S(1)}, bf16[32,512]{1,0:T(8,128)(2,1)S(1)}, bf16[32,512]{1,0:T(8,128)(2,1)S(1)}) custom-call(s32[2,1,1,4]{3,2,1,0:T(1,128)} %bitcast.68, f32[2,512,128]{2,1,0:T(8,128)} %bitcast.56, bf16[2,2,2,32,512]{4,3,2,1,0:T(8,128)(2,1)} %bitcast.58, ...), custom_call_target="tpu_custom_call" | custom-call | tf_op jit(solution)/shard_map/pallas_call | solution.py:224
  1.2 3.0 %collective-permute-start.3 = (bf16[768,128]{1,0:T(8,128)(2,1)S(1)}, bf16[768,128]{1,0:T(8,128)(2,1)S(1)}, u32[]{:S(2)}, u32[]{:S(2)}) collective-permute-start(bf16[768,128]{1,0:T(8,128)(2,1)S(1)} %get-tuple-element.27.refs_5_.refs_1_), channel_id=1, source_target_pairs={{0,2},{2,0},{1,3},{3,1},{4,6},{6,4},{5,7},{7,5},{8,10},{10,8},{9,1... | collective-permute-start | bytes 589832 | tf_op jit(solution)/shard_map/ppermute | solution.py:261
  4.3 0.7 collective-permute-start
  4.9 2.7 %collective-permute-start.1 = (bf16[2,32,512]{2,1,0:T(8,128)(2,1)S(1)}, bf16[2,32,512]{2,1,0:T(8,128)(2,1)S(1)}, u32[]{:S(2)}, u32[]{:S(2)}) collective-permute-start(bf16[2,32,512]{2,1,0:T(8,128)(2,1)S(1)} %get-tuple-element.24), channel_id=1, source_target_pairs={{0,16},{1,20},{2,24},{3,28},{4,17},{5,21},{6,25},{7,29},{8,18},{9,... | collective-permute-start | bytes 196616 | tf_op jit(solution)/shard_map/ppermute | solution.py:273
  7.6 0.0 copy-start
  7.7 1.4 %collective-permute-done.3.refs_7_.refs_3_ = bf16[768,128]{1,0:T(8,128)(2,1)S(1)} collective-permute-done((bf16[768,128]{1,0:T(8,128)(2,1)S(1)}, bf16[768,128]{1,0:T(8,128)(2,1)S(1)}, u32[]{:S(2)}, u32[]{:S(2)}) %collective-permute-start.3) | collective-permute-done | bytes 196640 | tf_op jit(solution)/shard_map/ppermute | solution.py:261
  9.1 1.6 %collective-permute-start.4 = (bf16[768,128]{1,0:T(8,128)(2,1)S(1)}, bf16[768,128]{1,0:T(8,128)(2,1)S(1)}, u32[]{:S(2)}, u32[]{:S(2)}) collective-permute-start(bf16[768,128]{1,0:T(8,128)(2,1)S(1)} %collective-permute-done.3.refs_7_.refs_3_), channel_id=1, source_target_pairs={{0,1},{1,0},{2,3},{3,2},{4,5},{5,4},{6,7},{7,6},{8,9},{9,8},{10,11... | collective-permute-start | bytes 589832 | tf_op jit(solution)/shard_map/ppermute | solution.py:262
  10.7 1.0 %collective-permute-done.4.refs_8_.refs_4_ = bf16[768,128]{1,0:T(8,128)(2,1)S(1)} collective-permute-done((bf16[768,128]{1,0:T(8,128)(2,1)S(1)}, bf16[768,128]{1,0:T(8,128)(2,1)S(1)}, u32[]{:S(2)}, u32[]{:S(2)}) %collective-permute-start.4) | collective-permute-done | bytes 196640 | tf_op jit(solution)/shard_map/ppermute | solution.py:262
  11.8 1.5 %shard_map.56 = (bf16[16,32,256]{2,1,0:T(8,128)(2,1)}, bf16[32,800]{1,0:T(8,128)(2,1)S(1)}, bf16[32,800]{1,0:T(8,128)(2,1)S(1)}) custom-call(f32[2,64,512]{2,1,0:T(8,128)S(1)} %bitcast.51, bf16[2,32,512]{2,1,0:T(8,128)(2,1)S(1)} %collective-permute-done.refs_1_, bf16[2,32,512]{2,1,0:T(8,128)(2,1)S(1)} %collective-permute-done.1.refs_2_, ...), custom_call_target="tpu_custom_call" | custom-call | tf_op jit(solution)/shard_map/pallas_call | solution.py:224
  13.3 8.4 %all-to-all-start = ((bf16[16,32,256]{2,1,0:T(8,128)(2,1)}), bf16[16,32,256]{2,1,0:T(8,128)(2,1)S(1)}, u32[]{:S(2)}, u32[]{:S(2)}) async-start(bf16[16,32,256]{2,1,0:T(8,128)(2,1)} %get-tuple-element.31), calls=%async_computation | async-start | bytes 524288 | tf_op jit(solution)/shard_map/all_to_all | solution.py:277
  21.8 2.0 %collective-permute-start.12 = (bf16[1024,128]{1,0:T(8,128)(2,1)S(1)}, bf16[1024,128]{1,0:T(8,128)(2,1)S(1)}, u32[]{:S(2)}, u32[]{:S(2)}) collective-permute-start(bf16[1024,128]{1,0:T(8,128)(2,1)S(1)} %constant_dynamic-update-slice_fusion.refs_9_.refs_5_), channel_id=1, source_target_pairs={{0,2},{2,0},{1,3},{3,1},{4,6},{6,4},{5,7},{7,5},{8,10},{10,8},{9,1... | collective-permute-start | bytes 786440 | tf_op jit(solution)/shard_map/ppermute | solution.py:261
  23.8 0.0 collective-permute-start.11
  23.8 8.6 %collective-permute-done.12.refs_11_.refs_7_ = bf16[1024,128]{1,0:T(8,128)(2,1)S(1)} collective-permute-done((bf16[1024,128]{1,0:T(8,128)(2,1)S(1)}, bf16[1024,128]{1,0:T(8,128)(2,1)S(1)}, u32[]{:S(2)}, u32[]{:S(2)}) %collective-permute-start.12) | collective-permute-done | bytes 262176 | tf_op jit(solution)/shard_map/ppermute | solution.py:261
  32.4 0.5 collective-permute-start.5
  32.9 0.7 collective-permute-start.6
  33.6 2.4 %collective-permute-start.7 = (bf16[32,800]{1,0:T(8,128)(2,1)S(1)}, bf16[32,800]{1,0:T(8,128)(2,1)S(1)}, u32[]{:S(2)}, u32[]{:S(2)}) collective-permute-start(bf16[32,800]{1,0:T(8,128)(2,1)S(1)} %get-tuple-element.33), channel_id=1, source_target_pairs={{0,16},{1,20},{2,24},{3,28},{4,17},{5,21},{6,25},{7,29},{8,18},{9,... | collective-permute-start | bytes 153608 | tf_op jit(solution)/shard_map/ppermute | solution.py:273
  36.0 0.0 collective-permute-done.6.refs_3_
  36.0 2.7 %collective-permute-done.7.refs_4_ = bf16[32,800]{1,0:T(8,128)(2,1)S(1)} collective-permute-done((bf16[32,800]{1,0:T(8,128)(2,1)S(1)}, bf16[32,800]{1,0:T(8,128)(2,1)S(1)}, u32[]{:S(2)}, u32[]{:S(2)}) %collective-permute-start.7) | collective-permute-done | bytes 51232 | tf_op jit(solution)/shard_map/ppermute | solution.py:273
  38.7 6.6 %collective-permute-start.9 = (bf16[2,32,288]{2,1,0:T(8,128)(2,1)S(1)}, bf16[2,32,288]{2,1,0:T(8,128)(2,1)S(1)}, u32[]{:S(2)}, u32[]{:S(2)}) collective-permute-start(bf16[2,32,288]{2,1,0:T(8,128)(2,1)S(1)} %pad_maximum_fusion.refs_5_), channel_id=1, source_target_pairs={{0,2},{2,0},{1,3},{3,1},{4,6},{6,4},{5,7},{7,5},{8,10},{10,8},{9,1... | collective-permute-start | bytes 110600 | tf_op jit(solution)/shard_map/ppermute | solution.py:261
  45.3 0.5 collective-permute-start.8
  45.8 2.0 %collective-permute-done.9.refs_7_ = bf16[2,32,288]{2,1,0:T(8,128)(2,1)S(1)} collective-permute-done((bf16[2,32,288]{2,1,0:T(8,128)(2,1)S(1)}, bf16[2,32,288]{2,1,0:T(8,128)(2,1)S(1)}, u32[]{:S(2)}, u32[]{:S(2)}) %collective-permute-start.9) | collective-permute-done | bytes 36896 | tf_op jit(solution)/shard_map/ppermute | solution.py:261
  47.8 0.1 collective-permute-start.10
  47.9 1.1 %collective-permute-done.10.refs_8_ = bf16[2,32,288]{2,1,0:T(8,128)(2,1)S(1)} collective-permute-done((bf16[2,32,288]{2,1,0:T(8,128)(2,1)S(1)}, bf16[2,32,288]{2,1,0:T(8,128)(2,1)S(1)}, u32[]{:S(2)}, u32[]{:S(2)}) %collective-permute-start.10) | collective-permute-done | bytes 36896 | tf_op jit(solution)/shard_map/ppermute | solution.py:262
  49.0 2.0 %shard_map.57 = (bf16[16,32,256]{2,1,0:T(8,128)(2,1)S(1)}, f32[64,512]{1,0:T(8,128)S(1)}, bf16[224,64]{1,0:T(8,128)(2,1)S(1)}) custom-call(bf16[16,32,256]{2,1,0:T(8,128)(2,1)S(1)} %all-to-all-done.refs_0_, bf16[16,32,256]{2,1,0:T(8,128)(2,1)S(1)} %collective-permute-done.5.refs_1_, f32[2,64,512]{2,1,0:T(8,128)S(1)} %bitcast.52, ...), custom_call_target="tpu_custom_call" | custom-call | tf_op jit(solution)/shard_map/pallas_call | solution.py:224
  51.1 15.4 %all_to_all.10.refs_0_ = bf16[16,32,256]{2,1,0:T(8,128)(2,1)S(1)} all-to-all(bf16[16,32,256]{2,1,0:T(8,128)(2,1)S(1)} %get-tuple-element.34), channel_id=1, replica_groups=mesh['row'=8,'x'=2,'core'=2] {'row','x'}, dimensions={0} | all-to-all | bytes 524288 | tf_op jit(solution)/shard_map/all_to_all | solution.py:277
  66.5 0.4 fusion.2.refs_5_
  66.9 0.8 %collective-permute-start.16 = (f32[2,64,128]{2,1,0:T(8,128)S(1)}, f32[2,64,128]{2,1,0:T(8,128)S(1)}, u32[]{:S(2)}, u32[]{:S(2)}) collective-permute-start(f32[2,64,128]{2,1,0:T(8,128)S(1)} %fusion.2.refs_5_), channel_id=1, source_target_pairs={{0,2},{2,0},{1,3},{3,1},{4,6},{6,4},{5,7},{7,5},{8,10},{10,8},{9,1... | collective-permute-start | bytes 196616 | tf_op jit(solution)/shard_map/ppermute | solution.py:261
  67.8 0.2 collective-permute-start.15
  68.0 3.5 %collective-permute-done.16.refs_7_ = f32[2,64,128]{2,1,0:T(8,128)S(1)} collective-permute-done((f32[2,64,128]{2,1,0:T(8,128)S(1)}, f32[2,64,128]{2,1,0:T(8,128)S(1)}, u32[]{:S(2)}, u32[]{:S(2)}) %collective-permute-start.16) | collective-permute-done | bytes 65568 | tf_op jit(solution)/shard_map/ppermute | solution.py:261
  71.5 1.2 %collective-permute-done.17.refs_8_ = f32[2,64,128]{2,1,0:T(8,128)S(1)} collective-permute-done((f32[2,64,128]{2,1,0:T(8,128)S(1)}, f32[2,64,128]{2,1,0:T(8,128)S(1)}, u32[]{:S(2)}, u32[]{:S(2)}) %collective-permute-start.17) | collective-permute-done | bytes 65568 | tf_op jit(solution)/shard_map/ppermute | solution.py:262
  72.8 0.5 shard_map.58
  73.3 2.2 %shard_map.59 = f32[2,64,512]{2,1,0:T(8,128)} custom-call(bf16[16,32,256]{2,1,0:T(8,128)(2,1)S(1)} %all_to_all.10.refs_0_, bf16[16,32,256]{2,1,0:T(8,128)(2,1)S(1)} %collective-permute-done.14.refs_1_, f32[64,512]{1,0:T(8,128)S(1)} %get-tuple-element.35.refs_2_, f32[64,512]{1,0:T(8,128)S(1)} %get-tuple-element.39.refs_3_, ...), custom_call_target="tpu_custom_call" | custom-call | tf_op jit(solution)/shard_map/pallas_call | solution.py:224
  (30 shorter events, 0.2 us)
Async XLA Ops:
  0.0 7.6 %copy-start.2 = (bf16[2,1,4,1,32,512]{5,4,3,2,1,0:T(8,128)(2,1)S(1)}, bf16[2,1,4,1,32,512]{5,4,3,2,1,0:T(8,128)(2,1)}, u32[]{:S(2)}) copy-start(bf16[2,1,4,1,32,512]{5,4,3,2,1,0:T(8,128)(2,1)} %param.7) | copy-start | bytes 786436
  0.0 7.6 %copy-start.1 = (f32[2,1,512,128]{3,2,1,0:T(8,128)S(1)}, f32[2,1,512,128]{3,2,1,0:T(8,128)}, u32[]{:S(2)}) copy-start(f32[2,1,512,128]{3,2,1,0:T(8,128)} %param.6) | copy-start | bytes 1572868
  1.2 7.9 %collective-permute-start.3 = (bf16[768,128]{1,0:T(8,128)(2,1)S(1)}, bf16[768,128]{1,0:T(8,128)(2,1)S(1)}, u32[]{:S(2)}, u32[]{:S(2)}) collective-permute-start(bf16[768,128]{1,0:T(8,128)(2,1)S(1)} %get-tuple-element.27.refs_5_.refs_1_), channel_id=1, source_target_pairs={{0,2},{2,0},{1,3},{3,1},{4,6},{6,4},{5,7},{7,5},{8,10},{10,8},{9,1... | collective-permute-start | bytes 589832 | tf_op jit(solution)/shard_map/ppermute | solution.py:261
  4.2 6.5 %collective-permute-start.2 = (bf16[768,128]{1,0:T(8,128)(2,1)S(1)}, bf16[768,128]{1,0:T(8,128)(2,1)S(1)}, u32[]{:S(2)}, u32[]{:S(2)}) collective-permute-start(bf16[768,128]{1,0:T(8,128)(2,1)S(1)} %get-tuple-element.27.refs_5_.refs_1_), channel_id=1, source_target_pairs={{0,1},{1,0},{2,3},{3,2},{4,5},{5,4},{6,7},{7,6},{8,9},{9,8},{10,11... | collective-permute-start | bytes 589832 | tf_op jit(solution)/shard_map/ppermute | solution.py:262
  4.3 6.5 %collective-permute-start = (bf16[2,32,512]{2,1,0:T(8,128)(2,1)S(1)}, bf16[2,32,512]{2,1,0:T(8,128)(2,1)S(1)}, u32[]{:S(2)}, u32[]{:S(2)}) collective-permute-start(bf16[2,32,512]{2,1,0:T(8,128)(2,1)S(1)} %get-tuple-element.23), channel_id=1, source_target_pairs={{0,0},{1,4},{2,8},{3,12},{4,1},{5,5},{6,9},{7,13},{8,2},{9,6},{10,... | collective-permute-start | bytes 196616 | tf_op jit(solution)/shard_map/ppermute | solution.py:273
  4.9 5.8 %collective-permute-start.1 = (bf16[2,32,512]{2,1,0:T(8,128)(2,1)S(1)}, bf16[2,32,512]{2,1,0:T(8,128)(2,1)S(1)}, u32[]{:S(2)}, u32[]{:S(2)}) collective-permute-start(bf16[2,32,512]{2,1,0:T(8,128)(2,1)S(1)} %get-tuple-element.24), channel_id=1, source_target_pairs={{0,16},{1,20},{2,24},{3,28},{4,17},{5,21},{6,25},{7,29},{8,18},{9,... | collective-permute-start | bytes 196616 | tf_op jit(solution)/shard_map/ppermute | solution.py:273
  7.6 4.2 %copy-start = (f32[2,1,64,512]{3,2,1,0:T(8,128)S(1)}, f32[2,1,64,512]{3,2,1,0:T(8,128)}, u32[]{:S(2)}) copy-start(f32[2,1,64,512]{3,2,1,0:T(8,128)} %param.5) | copy-start | bytes 786436
  9.1 2.6 %collective-permute-start.4 = (bf16[768,128]{1,0:T(8,128)(2,1)S(1)}, bf16[768,128]{1,0:T(8,128)(2,1)S(1)}, u32[]{:S(2)}, u32[]{:S(2)}) collective-permute-start(bf16[768,128]{1,0:T(8,128)(2,1)S(1)} %collective-permute-done.3.refs_7_.refs_3_), channel_id=1, source_target_pairs={{0,1},{1,0},{2,3},{3,2},{4,5},{5,4},{6,7},{7,6},{8,9},{9,8},{10,11... | collective-permute-start | bytes 589832 | tf_op jit(solution)/shard_map/ppermute | solution.py:262
  13.3 19.1 %all-to-all-start = ((bf16[16,32,256]{2,1,0:T(8,128)(2,1)}), bf16[16,32,256]{2,1,0:T(8,128)(2,1)S(1)}, u32[]{:S(2)}, u32[]{:S(2)}) async-start(bf16[16,32,256]{2,1,0:T(8,128)(2,1)} %get-tuple-element.31), calls=%async_computation | async-start | bytes 524288 | tf_op jit(solution)/shard_map/all_to_all | solution.py:277
  21.8 10.6 %collective-permute-start.12 = (bf16[1024,128]{1,0:T(8,128)(2,1)S(1)}, bf16[1024,128]{1,0:T(8,128)(2,1)S(1)}, u32[]{:S(2)}, u32[]{:S(2)}) collective-permute-start(bf16[1024,128]{1,0:T(8,128)(2,1)S(1)} %constant_dynamic-update-slice_fusion.refs_9_.refs_5_), channel_id=1, source_target_pairs={{0,2},{2,0},{1,3},{3,1},{4,6},{6,4},{5,7},{7,5},{8,10},{10,8},{9,1... | collective-permute-start | bytes 786440 | tf_op jit(solution)/shard_map/ppermute | solution.py:261
  23.8 24.1 %collective-permute-start.11 = (bf16[1024,128]{1,0:T(8,128)(2,1)S(1)}, bf16[1024,128]{1,0:T(8,128)(2,1)S(1)}, u32[]{:S(2)}, u32[]{:S(2)}) collective-permute-start(bf16[1024,128]{1,0:T(8,128)(2,1)S(1)} %constant_dynamic-update-slice_fusion.refs_9_.refs_5_), channel_id=1, source_target_pairs={{0,1},{1,0},{2,3},{3,2},{4,5},{5,4},{6,7},{7,6},{8,9},{9,8},{10,11... | collective-permute-start | bytes 786440 | tf_op jit(solution)/shard_map/ppermute | solution.py:262
  32.4 16.6 %collective-permute-start.13 = (bf16[1024,128]{1,0:T(8,128)(2,1)S(1)}, bf16[1024,128]{1,0:T(8,128)(2,1)S(1)}, u32[]{:S(2)}, u32[]{:S(2)}) collective-permute-start(bf16[1024,128]{1,0:T(8,128)(2,1)S(1)} %collective-permute-done.12.refs_11_.refs_7_), channel_id=1, source_target_pairs={{0,1},{1,0},{2,3},{3,2},{4,5},{5,4},{6,7},{7,6},{8,9},{9,8},{10,11... | collective-permute-start | bytes 786440 | tf_op jit(solution)/shard_map/ppermute | solution.py:262
  32.4 16.6 %collective-permute-start.5 = (bf16[16,32,256]{2,1,0:T(8,128)(2,1)S(1)}, bf16[16,32,256]{2,1,0:T(8,128)(2,1)S(1)}, u32[]{:S(2)}, u32[]{:S(2)}) collective-permute-start(bf16[16,32,256]{2,1,0:T(8,128)(2,1)S(1)} %all-to-all-done.refs_0_), channel_id=1, source_target_pairs={{0,1},{1,0},{2,3},{3,2},{4,5},{5,4},{6,7},{7,6},{8,9},{9,8},{10,11... | collective-permute-start | bytes 786440 | tf_op jit(solution)/shard_map/ppermute | solution.py:278
  32.9 3.1 %collective-permute-start.6 = (bf16[32,800]{1,0:T(8,128)(2,1)S(1)}, bf16[32,800]{1,0:T(8,128)(2,1)S(1)}, u32[]{:S(2)}, u32[]{:S(2)}) collective-permute-start(bf16[32,800]{1,0:T(8,128)(2,1)S(1)} %get-tuple-element.32), channel_id=1, source_target_pairs={{0,0},{1,4},{2,8},{3,12},{4,1},{5,5},{6,9},{7,13},{8,2},{9,6},{10,... | collective-permute-start | bytes 153608 | tf_op jit(solution)/shard_map/ppermute | solution.py:273
  33.6 5.1 %collective-permute-start.7 = (bf16[32,800]{1,0:T(8,128)(2,1)S(1)}, bf16[32,800]{1,0:T(8,128)(2,1)S(1)}, u32[]{:S(2)}, u32[]{:S(2)}) collective-permute-start(bf16[32,800]{1,0:T(8,128)(2,1)S(1)} %get-tuple-element.33), channel_id=1, source_target_pairs={{0,16},{1,20},{2,24},{3,28},{4,17},{5,21},{6,25},{7,29},{8,18},{9,... | collective-permute-start | bytes 153608 | tf_op jit(solution)/shard_map/ppermute | solution.py:273
  38.7 9.1 %collective-permute-start.9 = (bf16[2,32,288]{2,1,0:T(8,128)(2,1)S(1)}, bf16[2,32,288]{2,1,0:T(8,128)(2,1)S(1)}, u32[]{:S(2)}, u32[]{:S(2)}) collective-permute-start(bf16[2,32,288]{2,1,0:T(8,128)(2,1)S(1)} %pad_maximum_fusion.refs_5_), channel_id=1, source_target_pairs={{0,2},{2,0},{1,3},{3,1},{4,6},{6,4},{5,7},{7,5},{8,10},{10,8},{9,1... | collective-permute-start | bytes 110600 | tf_op jit(solution)/shard_map/ppermute | solution.py:261
  45.3 2.6 %collective-permute-start.8 = (bf16[2,32,288]{2,1,0:T(8,128)(2,1)S(1)}, bf16[2,32,288]{2,1,0:T(8,128)(2,1)S(1)}, u32[]{:S(2)}, u32[]{:S(2)}) collective-permute-start(bf16[2,32,288]{2,1,0:T(8,128)(2,1)S(1)} %pad_maximum_fusion.refs_5_), channel_id=1, source_target_pairs={{0,1},{1,0},{2,3},{3,2},{4,5},{5,4},{6,7},{7,6},{8,9},{9,8},{10,11... | collective-permute-start | bytes 110600 | tf_op jit(solution)/shard_map/ppermute | solution.py:262
  47.8 1.2 %collective-permute-start.10 = (bf16[2,32,288]{2,1,0:T(8,128)(2,1)S(1)}, bf16[2,32,288]{2,1,0:T(8,128)(2,1)S(1)}, u32[]{:S(2)}, u32[]{:S(2)}) collective-permute-start(bf16[2,32,288]{2,1,0:T(8,128)(2,1)S(1)} %collective-permute-done.9.refs_7_), channel_id=1, source_target_pairs={{0,1},{1,0},{2,3},{3,2},{4,5},{5,4},{6,7},{7,6},{8,9},{9,8},{10,11... | collective-permute-start | bytes 110600 | tf_op jit(solution)/shard_map/ppermute | solution.py:262
  66.5 6.8 %collective-permute-start.14 = (bf16[16,32,256]{2,1,0:T(8,128)(2,1)S(1)}, bf16[16,32,256]{2,1,0:T(8,128)(2,1)S(1)}, u32[]{:S(2)}, u32[]{:S(2)}) collective-permute-start(bf16[16,32,256]{2,1,0:T(8,128)(2,1)S(1)} %all_to_all.10.refs_0_), channel_id=1, source_target_pairs={{0,1},{1,0},{2,3},{3,2},{4,5},{5,4},{6,7},{7,6},{8,9},{9,8},{10,11... | collective-permute-start | bytes 786440 | tf_op jit(solution)/shard_map/ppermute | solution.py:278
  66.9 4.6 %collective-permute-start.16 = (f32[2,64,128]{2,1,0:T(8,128)S(1)}, f32[2,64,128]{2,1,0:T(8,128)S(1)}, u32[]{:S(2)}, u32[]{:S(2)}) collective-permute-start(f32[2,64,128]{2,1,0:T(8,128)S(1)} %fusion.2.refs_5_), channel_id=1, source_target_pairs={{0,2},{2,0},{1,3},{3,1},{4,6},{6,4},{5,7},{7,5},{8,10},{10,8},{9,1... | collective-permute-start | bytes 196616 | tf_op jit(solution)/shard_map/ppermute | solution.py:261
  67.8 3.7 %collective-permute-start.15 = (f32[2,64,128]{2,1,0:T(8,128)S(1)}, f32[2,64,128]{2,1,0:T(8,128)S(1)}, u32[]{:S(2)}, u32[]{:S(2)}) collective-permute-start(f32[2,64,128]{2,1,0:T(8,128)S(1)} %fusion.2.refs_5_), channel_id=1, source_target_pairs={{0,1},{1,0},{2,3},{3,2},{4,5},{5,4},{6,7},{7,6},{8,9},{9,8},{10,11... | collective-permute-start | bytes 196616 | tf_op jit(solution)/shard_map/ppermute | solution.py:262
  71.5 1.3 %collective-permute-start.17 = (f32[2,64,128]{2,1,0:T(8,128)S(1)}, f32[2,64,128]{2,1,0:T(8,128)S(1)}, u32[]{:S(2)}, u32[]{:S(2)}) collective-permute-start(f32[2,64,128]{2,1,0:T(8,128)S(1)} %collective-permute-done.16.refs_7_), channel_id=1, source_target_pairs={{0,1},{1,0},{2,3},{3,2},{4,5},{5,4},{6,7},{7,6},{8,9},{9,8},{10,11... | collective-permute-start | bytes 196616 | tf_op jit(solution)/shard_map/ppermute | solution.py:262

commit v9 on v8

--- a/solution.py
+++ b/solution.py
@@ -133,16 +133,17 @@
         q_ref[k, :r_cols, :] = eye
 
 
-def solve(dims, same_ref, other_ref, g_ref, q_ref, extra):
+def solve(dims, same_ref, other_ref, g_ref, q_ref, c_ref, extra):
     n_row, n_col, r_cols, rank, width, half = dims
     core = lax.axis_index("core")
     g_ref[core] = same_ref[...]
     g_ref[1 - core] = other_ref[...]
     start_solve(q_ref, n_row, r_cols)
-    extras = []
-    for k in range(n_row):
+    c_ref[...] = jnp.zeros(c_ref.shape, BF)
+
+    def blocks(k):
+        w = half if k <= n_col - 2 else width
         parts = []
-        w = half if k <= n_col - 2 else width
         for i in range(k + 1, n_row):
             c, t = i % n_col, i // n_col
             at = half if t == 0 else 0
@@ -151,15 +152,37 @@
             if k == n_row - 1:
                 w = width + rank
             parts.append(extra(k)[:, :w])
-        if not parts:
-            break
-        a = parts[0] if len(parts) == 1 else jnp.concatenate(parts, axis=0)
-        new = mm(a, q_ref[k, :w, :])
-        for i in range(k + 1, n_row):
-            at = (i - k - 1) * rank
-            q_ref[i, r_cols + k * rank : r_cols + (k + 1) * rank, :] = (-new[at : at + rank]).astype(BF)
+        return (jnp.concatenate(parts, axis=0) if parts else None), w
+
+    carried = []
+    for k in range(0, n_row, 2):
+        first, w = blocks(k)
+        second, w_next = blocks(k + 1)
+        if second is None:
+            carried.append(None)
+            continue
+        at = r_cols + k * rank
+        c_ref[k // 2, at : at + rank, :w] = -first[:rank]
+        carried.append(mm(second, c_ref[k // 2, :w_next, :w]).astype(BF))
+
+    extras = []
+    for k in range(0, n_row, 2):
+        first, w = blocks(k)
+        second, w_next = blocks(k + 1)
+        at = r_cols + k * rank
+        q = q_ref[k, :w, :]
+        new = mm(first, q)
         if extra is not None:
             extras.append(new[(n_row - 1 - k) * rank :].astype(BF))
+        if second is not None:
+            later = mm(second, q_ref[k + 1, :w_next, :]) + mm(carried[k // 2], q)
+            if extra is not None:
+                extras.append(later[(n_row - 2 - k) * rank :].astype(BF))
+        q_ref[k + 1, at : at + rank, :] = (-new[:rank]).astype(BF)
+        for i in range(k + 2, n_row):
+            row = (i - k - 1) * rank
+            pair = jnp.concatenate([new[row : row + rank], later[row - rank : row]], axis=0)
+            q_ref[i, at : at + 2 * rank, :] = (-pair).astype(BF)
     return extras
 
 
@@ -167,7 +190,7 @@
     n_row, n_col, r_cols, rank, _, half = dims
     same_ref, other_ref, rhs_ref, v_a_ref, v_b_ref = refs[:5]
     fars, nexts = refs[5 : 5 + n_col], refs[5 + n_col : 5 + 2 * n_col]
-    msg_ref, minus_ref, own_ref, g_ref, q_ref, far_ref, next_ref = refs[5 + 2 * n_col :]
+    msg_ref, minus_ref, own_ref, g_ref, q_ref, c_ref, far_ref, next_ref = refs[5 + 2 * n_col :]
     row, col, turn = place()
     order = rhs_ref.shape[2]
     rows = n_col * TURNS * rank
@@ -175,7 +198,7 @@
     join(far_ref, fars)
     inv = gathered_inverse(next_ref, order)
     w = mm(gathered_u(next_ref, order + rows, rank, n_row - 2), inv)
-    p = solve(dims, same_ref, other_ref, g_ref, q_ref,
+    p = solve(dims, same_ref, other_ref, g_ref, q_ref, c_ref,
               lambda k: far_ref[k % n_col, lax.rem(turn - k // n_col + TURNS, TURNS)])
     total = lax.dot_general(jnp.concatenate(p, axis=0), gathered_u(next_ref, order, rank, n_row), TN,
                             preferred_element_type=F32)
@@ -195,29 +218,26 @@
 def early_kernel(dims, *refs):
     n_row, n_col, _, rank, _, _ = dims
     own_ref = refs[0]
-    nears, zs = refs[1 : 1 + n_col], refs[1 + n_col : 1 + 2 * n_col]
-    y_ref, z_out_ref, near_ref, z_ref = refs[1 + 2 * n_col :]
+    nears, zs, nexts = (refs[1 + n * n_col : 1 + (n + 1) * n_col] for n in range(3))
+    y_ref, z_out_ref, inv_ref, u_ref, near_ref, z_ref, next_ref = refs[1 + 3 * n_col :]
     order = y_ref.shape[1]
     join(near_ref, nears)
     join(z_ref, zs)
+    join(next_ref, nexts)
     minus = lax.dot_general(own_ref[...], gathered_u(near_ref, order, rank, n_row - 1), TN, preferred_element_type=F32)
     z = jnp.concatenate([z_ref[c, 0] for c in range(n_col)], axis=1)
     y_ref[...] = z + split_mm(minus, gathered_inverse(near_ref, order))
     z_out_ref[...] = jnp.concatenate([z_ref[c, 1] for c in range(n_col)], axis=1)
-
-
-def last_kernel(dims, *refs):
-    n_row, n_col, r_cols, rank, _, _ = dims
-    same_ref, other_ref, minus_ref, z_ref, early_ref = refs[:5]
-    y_ref, g_ref, q_ref, next_ref = refs[5 + n_col :]
-    order = minus_ref.shape[1]
+    inv_ref[...] = gathered_inverse(next_ref, order)
+    u_ref[...] = gathered_u(next_ref, order + n_col * TURNS * rank, rank, n_row - 1)
+
+
+def last_kernel(dims, same_ref, other_ref, minus_ref, z_ref, early_ref, inv_ref, u_ref, y_ref, g_ref, q_ref, c_ref):
     y_ref[0] = early_ref[...]
-    join(next_ref, refs[5 : 5 + n_col])
-    solve(dims, same_ref, other_ref, g_ref, q_ref, None)
-    own = q_ref[lax.axis_index("row")][r_cols:, :]
-    u = gathered_u(next_ref, order + n_col * TURNS * rank, rank, n_row - 1)
-    minus = minus_ref[...] + lax.dot_general(own, u, TN, preferred_element_type=F32)
-    y_ref[1] = z_ref[...] + split_mm(minus, gathered_inverse(next_ref, order))
+    solve(dims, same_ref, other_ref, g_ref, q_ref, c_ref, None)
+    own = q_ref[lax.axis_index("row")][dims[2] :, :]
+    minus = minus_ref[...] + lax.dot_general(own, u_ref[...], TN, preferred_element_type=F32)
+    y_ref[1] = z_ref[...] + split_mm(minus, inv_ref[...])
 
 
 def call(kernel, outs, *args, scratch=(), space=pltpu.VMEM):
@@ -288,6 +308,7 @@
     solve_scratch = [
         pltpu.VMEM((2, n_row * n_x, rank, width), BF),
         pltpu.VMEM((n_row, width + rank, r_cols), BF),
+        pltpu.VMEM((n_row // 2, width + rank, width), BF),
     ]
 
     in_hbm = [pltpu.with_memory_space_constraint(x, pltpu.HBM) for x in (ranks, inv_here, u_here, v_here)]
@@ -328,12 +349,14 @@
         scratch=solve_scratch + [pltpu.VMEM((n_col, TURNS, rank, width + rank), BF), next_scratch],
     )
     same, other = spread(msg)
-    early, z_last = call(
-        kernel(early_kernel), [shape((r_cols, order), F32)] * 2, own, *near, *z,
-        scratch=[near_scratch, pltpu.VMEM((n_col, slots, r_cols, lanes), F32)])
+    early, z_last, inv_last, u_last = call(
+        kernel(early_kernel),
+        [shape((r_cols, order), F32)] * 2 + [shape((order, order), BF), shape(((n_row - 1) * rank, order), BF)],
+        own, *near, *z, *nxt,
+        scratch=[near_scratch, pltpu.VMEM((n_col, slots, r_cols, lanes), F32), next_scratch])
     (y,) = call(
         kernel(last_kernel), [shape((slots, r_cols, order), F32)],
-        same, other, minus, z_last, early, *nxt, scratch=solve_scratch + [next_scratch],
+        same, other, minus, z_last, early, inv_last, u_last, scratch=solve_scratch,
     )
     return y[:, None]
 

time: 75.8 us -> 75.6 us (level)
  no operation moved by 1% of the time
where the time goes in v9:
time: 75.6 us; the launch traced here: 75.3 us
  starting transfers between devices  30.2 us (40%)
  waiting for transfers between devices  21.7 us (29%)
  blocking collectives  15.4 us (20%)
  Pallas kernels  7.26 us (10%)
    ppermute x4, waiting for transfers between devices, gather(): moved = lax.ppermute(part, 'x', [(i, (i + s) % n_x) for i in range(n_x)])  15.5 us
    all_to_all x1, blocking collectives, spread(): lax.all_to_all(m, ('row', 'x'), split_axis=0, concat_axis=0, tiled=True)  15.4 us
    ppermute x4, starting transfers between devices, gather(): moved = lax.ppermute(part, 'x', [(i, (i + s) % n_x) for i in range(n_x)])  12.4 us
    all_to_all x1, starting transfers between devices, spread(): lax.all_to_all(m, ('row', 'x'), split_axis=0, concat_axis=0, tiled=True)  8.42 us
    pallas_call x5, Pallas kernels, call(): pl.pallas_call(kernel, out_shape=outs, in_specs=[pl.BlockSpec(memory_spac...  7.26 us
    ppermute x4, starting transfers between devices, turn_rows(): got.append(lax.ppermute(parts[s], everywhere, pairs))  6.39 us
    ppermute x8, waiting for transfers between devices, gather(): pieces += [moved, lax.ppermute(moved, 'core', swap)]  3.41 us
    ppermute x4, waiting for transfers between devices, turn_rows(): got.append(lax.ppermute(parts[s], everywhere, pairs))  2.72 us
  transfers between devices with their start and end apart: 19, of which 8 were waited for; matrix products, arithmetic and copies ran while one was open for 1% of the time, Pallas kernels for 1%

profile of v9, /device:TPU:0, one launch (start us, length us, event | category | flops | bytes accessed | tf_op | source)
XLA Modules:
  0.0 75.3 jit_solution(18231178388394955581)
XLA Ops:
  0.0 1.2 %shard_map.55 = (bf16[768,128]{1,0:T(8,128)(2,1)S(1)}, bf16[2,32,512]{2,1,0:T(8,128)(2,1)S(1)}, bf16[2,32,512]{2,1,0:T(8,128)(2,1)S(1)}, bf16[32,512]{1,0:T(8,128)(2,1)S(1)}, bf16[32,512]{1,0:T(8,128)(2,1)S(1)}) custom-call(s32[2,1,1,4]{3,2,1,0:T(1,128)} %bitcast.68, f32[2,512,128]{2,1,0:T(8,128)} %bitcast.56, bf16[2,2,2,32,512]{4,3,2,1,0:T(8,128)(2,1)} %bitcast.58, ...), custom_call_target="tpu_custom_call" | custom-call | tf_op jit(solution)/shard_map/pallas_call | solution.py:244
  1.2 3.0 %collective-permute-start.3 = (bf16[768,128]{1,0:T(8,128)(2,1)S(1)}, bf16[768,128]{1,0:T(8,128)(2,1)S(1)}, u32[]{:S(2)}, u32[]{:S(2)}) collective-permute-start(bf16[768,128]{1,0:T(8,128)(2,1)S(1)} %get-tuple-element.29.refs_5_.refs_1_), channel_id=1, source_target_pairs={{0,2},{2,0},{1,3},{3,1},{4,6},{6,4},{5,7},{7,5},{8,10},{10,8},{9,1... | collective-permute-start | bytes 589832 | tf_op jit(solution)/shard_map/ppermute | solution.py:281
  4.3 0.7 collective-permute-start
  4.9 2.7 %collective-permute-start.1 = (bf16[2,32,512]{2,1,0:T(8,128)(2,1)S(1)}, bf16[2,32,512]{2,1,0:T(8,128)(2,1)S(1)}, u32[]{:S(2)}, u32[]{:S(2)}) collective-permute-start(bf16[2,32,512]{2,1,0:T(8,128)(2,1)S(1)} %get-tuple-element.26), channel_id=1, source_target_pairs={{0,16},{1,20},{2,24},{3,28},{4,17},{5,21},{6,25},{7,29},{8,18},{9,... | collective-permute-start | bytes 196616 | tf_op jit(solution)/shard_map/ppermute | solution.py:293
  7.6 0.0 copy-start
  7.7 1.4 %collective-permute-done.3.refs_7_.refs_3_ = bf16[768,128]{1,0:T(8,128)(2,1)S(1)} collective-permute-done((bf16[768,128]{1,0:T(8,128)(2,1)S(1)}, bf16[768,128]{1,0:T(8,128)(2,1)S(1)}, u32[]{:S(2)}, u32[]{:S(2)}) %collective-permute-start.3) | collective-permute-done | bytes 196640 | tf_op jit(solution)/shard_map/ppermute | solution.py:281
  9.1 1.6 %collective-permute-start.4 = (bf16[768,128]{1,0:T(8,128)(2,1)S(1)}, bf16[768,128]{1,0:T(8,128)(2,1)S(1)}, u32[]{:S(2)}, u32[]{:S(2)}) collective-permute-start(bf16[768,128]{1,0:T(8,128)(2,1)S(1)} %collective-permute-done.3.refs_7_.refs_3_), channel_id=1, source_target_pairs={{0,1},{1,0},{2,3},{3,2},{4,5},{5,4},{6,7},{7,6},{8,9},{9,8},{10,11... | collective-permute-start | bytes 589832 | tf_op jit(solution)/shard_map/ppermute | solution.py:282
  10.7 1.0 %collective-permute-done.4.refs_8_.refs_4_ = bf16[768,128]{1,0:T(8,128)(2,1)S(1)} collective-permute-done((bf16[768,128]{1,0:T(8,128)(2,1)S(1)}, bf16[768,128]{1,0:T(8,128)(2,1)S(1)}, u32[]{:S(2)}, u32[]{:S(2)}) %collective-permute-start.4) | collective-permute-done | bytes 196640 | tf_op jit(solution)/shard_map/ppermute | solution.py:282
  11.8 1.5 %shard_map.56 = (bf16[16,32,256]{2,1,0:T(8,128)(2,1)}, bf16[32,800]{1,0:T(8,128)(2,1)S(1)}, bf16[32,800]{1,0:T(8,128)(2,1)S(1)}) custom-call(f32[2,64,512]{2,1,0:T(8,128)S(1)} %bitcast.51, bf16[2,32,512]{2,1,0:T(8,128)(2,1)S(1)} %collective-permute-done.refs_1_, bf16[2,32,512]{2,1,0:T(8,128)(2,1)S(1)} %collective-permute-done.1.refs_2_, ...), custom_call_target="tpu_custom_call" | custom-call | tf_op jit(solution)/shard_map/pallas_call | solution.py:244
  13.3 8.4 %all-to-all-start = ((bf16[16,32,256]{2,1,0:T(8,128)(2,1)}), bf16[16,32,256]{2,1,0:T(8,128)(2,1)S(1)}, u32[]{:S(2)}, u32[]{:S(2)}) async-start(bf16[16,32,256]{2,1,0:T(8,128)(2,1)} %get-tuple-element.33), calls=%async_computation | async-start | bytes 524288 | tf_op jit(solution)/shard_map/all_to_all | solution.py:297
  21.8 2.0 %collective-permute-start.12 = (bf16[1024,128]{1,0:T(8,128)(2,1)S(1)}, bf16[1024,128]{1,0:T(8,128)(2,1)S(1)}, u32[]{:S(2)}, u32[]{:S(2)}) collective-permute-start(bf16[1024,128]{1,0:T(8,128)(2,1)S(1)} %constant_dynamic-update-slice_fusion.refs_9_), channel_id=1, source_target_pairs={{0,2},{2,0},{1,3},{3,1},{4,6},{6,4},{5,7},{7,5},{8,10},{10,8},{9,1... | collective-permute-start | bytes 786440 | tf_op jit(solution)/shard_map/ppermute | solution.py:281
  23.8 0.0 collective-permute-start.11
  23.8 8.6 %collective-permute-done.12.refs_11_ = bf16[1024,128]{1,0:T(8,128)(2,1)S(1)} collective-permute-done((bf16[1024,128]{1,0:T(8,128)(2,1)S(1)}, bf16[1024,128]{1,0:T(8,128)(2,1)S(1)}, u32[]{:S(2)}, u32[]{:S(2)}) %collective-permute-start.12) | collective-permute-done | bytes 262176 | tf_op jit(solution)/shard_map/ppermute | solution.py:281
  32.4 0.5 collective-permute-start.5
  32.9 0.7 collective-permute-start.6
  33.6 2.4 %collective-permute-start.7 = (bf16[32,800]{1,0:T(8,128)(2,1)S(1)}, bf16[32,800]{1,0:T(8,128)(2,1)S(1)}, u32[]{:S(2)}, u32[]{:S(2)}) collective-permute-start(bf16[32,800]{1,0:T(8,128)(2,1)S(1)} %get-tuple-element.35), channel_id=1, source_target_pairs={{0,16},{1,20},{2,24},{3,28},{4,17},{5,21},{6,25},{7,29},{8,18},{9,... | collective-permute-start | bytes 153608 | tf_op jit(solution)/shard_map/ppermute | solution.py:293
  36.0 0.0 collective-permute-done.6.refs_3_
  36.0 2.7 %collective-permute-done.7.refs_4_ = bf16[32,800]{1,0:T(8,128)(2,1)S(1)} collective-permute-done((bf16[32,800]{1,0:T(8,128)(2,1)S(1)}, bf16[32,800]{1,0:T(8,128)(2,1)S(1)}, u32[]{:S(2)}, u32[]{:S(2)}) %collective-permute-start.7) | collective-permute-done | bytes 51232 | tf_op jit(solution)/shard_map/ppermute | solution.py:293
  38.7 6.6 %collective-permute-start.9 = (bf16[2,32,288]{2,1,0:T(8,128)(2,1)S(1)}, bf16[2,32,288]{2,1,0:T(8,128)(2,1)S(1)}, u32[]{:S(2)}, u32[]{:S(2)}) collective-permute-start(bf16[2,32,288]{2,1,0:T(8,128)(2,1)S(1)} %pad_maximum_fusion.refs_5_), channel_id=1, source_target_pairs={{0,2},{2,0},{1,3},{3,1},{4,6},{6,4},{5,7},{7,5},{8,10},{10,8},{9,1... | collective-permute-start | bytes 110600 | tf_op jit(solution)/shard_map/ppermute | solution.py:281
  45.3 0.5 collective-permute-start.8
  45.8 2.0 %collective-permute-done.9.refs_7_ = bf16[2,32,288]{2,1,0:T(8,128)(2,1)S(1)} collective-permute-done((bf16[2,32,288]{2,1,0:T(8,128)(2,1)S(1)}, bf16[2,32,288]{2,1,0:T(8,128)(2,1)S(1)}, u32[]{:S(2)}, u32[]{:S(2)}) %collective-permute-start.9) | collective-permute-done | bytes 36896 | tf_op jit(solution)/shard_map/ppermute | solution.py:281
  47.8 0.1 collective-permute-start.10
  47.9 1.1 %collective-permute-done.10.refs_8_ = bf16[2,32,288]{2,1,0:T(8,128)(2,1)S(1)} collective-permute-done((bf16[2,32,288]{2,1,0:T(8,128)(2,1)S(1)}, bf16[2,32,288]{2,1,0:T(8,128)(2,1)S(1)}, u32[]{:S(2)}, u32[]{:S(2)}) %collective-permute-start.10) | collective-permute-done | bytes 36896 | tf_op jit(solution)/shard_map/ppermute | solution.py:282
  49.0 1.8 %shard_map.57 = (bf16[16,32,256]{2,1,0:T(8,128)(2,1)S(1)}, f32[64,512]{1,0:T(8,128)S(1)}, bf16[224,64]{1,0:T(8,128)(2,1)S(1)}) custom-call(bf16[16,32,256]{2,1,0:T(8,128)(2,1)S(1)} %all-to-all-done.refs_0_, bf16[16,32,256]{2,1,0:T(8,128)(2,1)S(1)} %collective-permute-done.5.refs_1_, f32[2,64,512]{2,1,0:T(8,128)S(1)} %bitcast.52, ...), custom_call_target="tpu_custom_call" | custom-call | tf_op jit(solution)/shard_map/pallas_call | solution.py:244
  50.9 15.4 %all_to_all.10.same_ref = bf16[16,32,256]{2,1,0:T(8,128)(2,1)S(1)} all-to-all(bf16[16,32,256]{2,1,0:T(8,128)(2,1)S(1)} %get-tuple-element.36), channel_id=1, replica_groups=mesh['row'=8,'x'=2,'core'=2] {'row','x'}, dimensions={0} | all-to-all | bytes 524288 | tf_op jit(solution)/shard_map/all_to_all | solution.py:297
  66.3 0.4 fusion.2.refs_5_
  66.7 0.8 %collective-permute-start.16 = (f32[2,64,128]{2,1,0:T(8,128)S(1)}, f32[2,64,128]{2,1,0:T(8,128)S(1)}, u32[]{:S(2)}, u32[]{:S(2)}) collective-permute-start(f32[2,64,128]{2,1,0:T(8,128)S(1)} %fusion.2.refs_5_), channel_id=1, source_target_pairs={{0,2},{2,0},{1,3},{3,1},{4,6},{6,4},{5,7},{7,5},{8,10},{10,8},{9,1... | collective-permute-start | bytes 196616 | tf_op jit(solution)/shard_map/ppermute | solution.py:281
  67.6 0.2 collective-permute-start.15
  67.8 3.5 %collective-permute-done.16.refs_7_ = f32[2,64,128]{2,1,0:T(8,128)S(1)} collective-permute-done((f32[2,64,128]{2,1,0:T(8,128)S(1)}, f32[2,64,128]{2,1,0:T(8,128)S(1)}, u32[]{:S(2)}, u32[]{:S(2)}) %collective-permute-start.16) | collective-permute-done | bytes 65568 | tf_op jit(solution)/shard_map/ppermute | solution.py:281
  71.3 1.2 %collective-permute-done.17.refs_8_ = f32[2,64,128]{2,1,0:T(8,128)S(1)} collective-permute-done((f32[2,64,128]{2,1,0:T(8,128)S(1)}, f32[2,64,128]{2,1,0:T(8,128)S(1)}, u32[]{:S(2)}, u32[]{:S(2)}) %collective-permute-start.17) | collective-permute-done | bytes 65568 | tf_op jit(solution)/shard_map/ppermute | solution.py:282
  72.6 0.6 shard_map.58
  73.2 2.1 %shard_map.59 = f32[2,64,512]{2,1,0:T(8,128)} custom-call(bf16[16,32,256]{2,1,0:T(8,128)(2,1)S(1)} %all_to_all.10.same_ref, bf16[16,32,256]{2,1,0:T(8,128)(2,1)S(1)} %collective-permute-done.14.other_ref, f32[64,512]{1,0:T(8,128)S(1)} %get-tuple-element.37.minus_ref, f32[64,512]{1,0:T(8,128)S(1)} %get-tuple-element.41.z_ref, ...), custom_call_target="tpu_custom_call" | custom-call | tf_op jit(solution)/shard_map/pallas_call | solution.py:244
  (30 shorter events, 0.2 us)
Async XLA Ops:
  0.0 7.6 %copy-start.2 = (bf16[2,1,4,1,32,512]{5,4,3,2,1,0:T(8,128)(2,1)S(1)}, bf16[2,1,4,1,32,512]{5,4,3,2,1,0:T(8,128)(2,1)}, u32[]{:S(2)}) copy-start(bf16[2,1,4,1,32,512]{5,4,3,2,1,0:T(8,128)(2,1)} %param.7) | copy-start | bytes 786436
  0.0 7.6 %copy-start.1 = (f32[2,1,512,128]{3,2,1,0:T(8,128)S(1)}, f32[2,1,512,128]{3,2,1,0:T(8,128)}, u32[]{:S(2)}) copy-start(f32[2,1,512,128]{3,2,1,0:T(8,128)} %param.6) | copy-start | bytes 1572868
  1.2 7.9 %collective-permute-start.3 = (bf16[768,128]{1,0:T(8,128)(2,1)S(1)}, bf16[768,128]{1,0:T(8,128)(2,1)S(1)}, u32[]{:S(2)}, u32[]{:S(2)}) collective-permute-start(bf16[768,128]{1,0:T(8,128)(2,1)S(1)} %get-tuple-element.29.refs_5_.refs_1_), channel_id=1, source_target_pairs={{0,2},{2,0},{1,3},{3,1},{4,6},{6,4},{5,7},{7,5},{8,10},{10,8},{9,1... | collective-permute-start | bytes 589832 | tf_op jit(solution)/shard_map/ppermute | solution.py:281
  4.2 6.5 %collective-permute-start.2 = (bf16[768,128]{1,0:T(8,128)(2,1)S(1)}, bf16[768,128]{1,0:T(8,128)(2,1)S(1)}, u32[]{:S(2)}, u32[]{:S(2)}) collective-permute-start(bf16[768,128]{1,0:T(8,128)(2,1)S(1)} %get-tuple-element.29.refs_5_.refs_1_), channel_id=1, source_target_pairs={{0,1},{1,0},{2,3},{3,2},{4,5},{5,4},{6,7},{7,6},{8,9},{9,8},{10,11... | collective-permute-start | bytes 589832 | tf_op jit(solution)/shard_map/ppermute | solution.py:282
  4.3 6.5 %collective-permute-start = (bf16[2,32,512]{2,1,0:T(8,128)(2,1)S(1)}, bf16[2,32,512]{2,1,0:T(8,128)(2,1)S(1)}, u32[]{:S(2)}, u32[]{:S(2)}) collective-permute-start(bf16[2,32,512]{2,1,0:T(8,128)(2,1)S(1)} %get-tuple-element.25), channel_id=1, source_target_pairs={{0,0},{1,4},{2,8},{3,12},{4,1},{5,5},{6,9},{7,13},{8,2},{9,6},{10,... | collective-permute-start | bytes 196616 | tf_op jit(solution)/shard_map/ppermute | solution.py:293
  4.9 5.8 %collective-permute-start.1 = (bf16[2,32,512]{2,1,0:T(8,128)(2,1)S(1)}, bf16[2,32,512]{2,1,0:T(8,128)(2,1)S(1)}, u32[]{:S(2)}, u32[]{:S(2)}) collective-permute-start(bf16[2,32,512]{2,1,0:T(8,128)(2,1)S(1)} %get-tuple-element.26), channel_id=1, source_target_pairs={{0,16},{1,20},{2,24},{3,28},{4,17},{5,21},{6,25},{7,29},{8,18},{9,... | collective-permute-start | bytes 196616 | tf_op jit(solution)/shard_map/ppermute | solution.py:293
  7.6 4.2 %copy-start = (f32[2,1,64,512]{3,2,1,0:T(8,128)S(1)}, f32[2,1,64,512]{3,2,1,0:T(8,128)}, u32[]{:S(2)}) copy-start(f32[2,1,64,512]{3,2,1,0:T(8,128)} %param.5) | copy-start | bytes 786436
  9.1 2.6 %collective-permute-start.4 = (bf16[768,128]{1,0:T(8,128)(2,1)S(1)}, bf16[768,128]{1,0:T(8,128)(2,1)S(1)}, u32[]{:S(2)}, u32[]{:S(2)}) collective-permute-start(bf16[768,128]{1,0:T(8,128)(2,1)S(1)} %collective-permute-done.3.refs_7_.refs_3_), channel_id=1, source_target_pairs={{0,1},{1,0},{2,3},{3,2},{4,5},{5,4},{6,7},{7,6},{8,9},{9,8},{10,11... | collective-permute-start | bytes 589832 | tf_op jit(solution)/shard_map/ppermute | solution.py:282
  13.3 19.1 %all-to-all-start = ((bf16[16,32,256]{2,1,0:T(8,128)(2,1)}), bf16[16,32,256]{2,1,0:T(8,128)(2,1)S(1)}, u32[]{:S(2)}, u32[]{:S(2)}) async-start(bf16[16,32,256]{2,1,0:T(8,128)(2,1)} %get-tuple-element.33), calls=%async_computation | async-start | bytes 524288 | tf_op jit(solution)/shard_map/all_to_all | solution.py:297
  21.8 10.6 %collective-permute-start.12 = (bf16[1024,128]{1,0:T(8,128)(2,1)S(1)}, bf16[1024,128]{1,0:T(8,128)(2,1)S(1)}, u32[]{:S(2)}, u32[]{:S(2)}) collective-permute-start(bf16[1024,128]{1,0:T(8,128)(2,1)S(1)} %constant_dynamic-update-slice_fusion.refs_9_), channel_id=1, source_target_pairs={{0,2},{2,0},{1,3},{3,1},{4,6},{6,4},{5,7},{7,5},{8,10},{10,8},{9,1... | collective-permute-start | bytes 786440 | tf_op jit(solution)/shard_map/ppermute | solution.py:281
  23.8 24.1 %collective-permute-start.11 = (bf16[1024,128]{1,0:T(8,128)(2,1)S(1)}, bf16[1024,128]{1,0:T(8,128)(2,1)S(1)}, u32[]{:S(2)}, u32[]{:S(2)}) collective-permute-start(bf16[1024,128]{1,0:T(8,128)(2,1)S(1)} %constant_dynamic-update-slice_fusion.refs_9_), channel_id=1, source_target_pairs={{0,1},{1,0},{2,3},{3,2},{4,5},{5,4},{6,7},{7,6},{8,9},{9,8},{10,11... | collective-permute-start | bytes 786440 | tf_op jit(solution)/shard_map/ppermute | solution.py:282
  32.4 16.6 %collective-permute-start.13 = (bf16[1024,128]{1,0:T(8,128)(2,1)S(1)}, bf16[1024,128]{1,0:T(8,128)(2,1)S(1)}, u32[]{:S(2)}, u32[]{:S(2)}) collective-permute-start(bf16[1024,128]{1,0:T(8,128)(2,1)S(1)} %collective-permute-done.12.refs_11_), channel_id=1, source_target_pairs={{0,1},{1,0},{2,3},{3,2},{4,5},{5,4},{6,7},{7,6},{8,9},{9,8},{10,11... | collective-permute-start | bytes 786440 | tf_op jit(solution)/shard_map/ppermute | solution.py:282
  32.4 16.6 %collective-permute-start.5 = (bf16[16,32,256]{2,1,0:T(8,128)(2,1)S(1)}, bf16[16,32,256]{2,1,0:T(8,128)(2,1)S(1)}, u32[]{:S(2)}, u32[]{:S(2)}) collective-permute-start(bf16[16,32,256]{2,1,0:T(8,128)(2,1)S(1)} %all-to-all-done.refs_0_), channel_id=1, source_target_pairs={{0,1},{1,0},{2,3},{3,2},{4,5},{5,4},{6,7},{7,6},{8,9},{9,8},{10,11... | collective-permute-start | bytes 786440 | tf_op jit(solution)/shard_map/ppermute | solution.py:298
  32.9 3.1 %collective-permute-start.6 = (bf16[32,800]{1,0:T(8,128)(2,1)S(1)}, bf16[32,800]{1,0:T(8,128)(2,1)S(1)}, u32[]{:S(2)}, u32[]{:S(2)}) collective-permute-start(bf16[32,800]{1,0:T(8,128)(2,1)S(1)} %get-tuple-element.34), channel_id=1, source_target_pairs={{0,0},{1,4},{2,8},{3,12},{4,1},{5,5},{6,9},{7,13},{8,2},{9,6},{10,... | collective-permute-start | bytes 153608 | tf_op jit(solution)/shard_map/ppermute | solution.py:293
  33.6 5.1 %collective-permute-start.7 = (bf16[32,800]{1,0:T(8,128)(2,1)S(1)}, bf16[32,800]{1,0:T(8,128)(2,1)S(1)}, u32[]{:S(2)}, u32[]{:S(2)}) collective-permute-start(bf16[32,800]{1,0:T(8,128)(2,1)S(1)} %get-tuple-element.35), channel_id=1, source_target_pairs={{0,16},{1,20},{2,24},{3,28},{4,17},{5,21},{6,25},{7,29},{8,18},{9,... | collective-permute-start | bytes 153608 | tf_op jit(solution)/shard_map/ppermute | solution.py:293
  38.7 9.1 %collective-permute-start.9 = (bf16[2,32,288]{2,1,0:T(8,128)(2,1)S(1)}, bf16[2,32,288]{2,1,0:T(8,128)(2,1)S(1)}, u32[]{:S(2)}, u32[]{:S(2)}) collective-permute-start(bf16[2,32,288]{2,1,0:T(8,128)(2,1)S(1)} %pad_maximum_fusion.refs_5_), channel_id=1, source_target_pairs={{0,2},{2,0},{1,3},{3,1},{4,6},{6,4},{5,7},{7,5},{8,10},{10,8},{9,1... | collective-permute-start | bytes 110600 | tf_op jit(solution)/shard_map/ppermute | solution.py:281
  45.3 2.6 %collective-permute-start.8 = (bf16[2,32,288]{2,1,0:T(8,128)(2,1)S(1)}, bf16[2,32,288]{2,1,0:T(8,128)(2,1)S(1)}, u32[]{:S(2)}, u32[]{:S(2)}) collective-permute-start(bf16[2,32,288]{2,1,0:T(8,128)(2,1)S(1)} %pad_maximum_fusion.refs_5_), channel_id=1, source_target_pairs={{0,1},{1,0},{2,3},{3,2},{4,5},{5,4},{6,7},{7,6},{8,9},{9,8},{10,11... | collective-permute-start | bytes 110600 | tf_op jit(solution)/shard_map/ppermute | solution.py:282
  47.8 1.2 %collective-permute-start.10 = (bf16[2,32,288]{2,1,0:T(8,128)(2,1)S(1)}, bf16[2,32,288]{2,1,0:T(8,128)(2,1)S(1)}, u32[]{:S(2)}, u32[]{:S(2)}) collective-permute-start(bf16[2,32,288]{2,1,0:T(8,128)(2,1)S(1)} %collective-permute-done.9.refs_7_), channel_id=1, source_target_pairs={{0,1},{1,0},{2,3},{3,2},{4,5},{5,4},{6,7},{7,6},{8,9},{9,8},{10,11... | collective-permute-start | bytes 110600 | tf_op jit(solution)/shard_map/ppermute | solution.py:282
  66.3 6.9 %collective-permute-start.14 = (bf16[16,32,256]{2,1,0:T(8,128)(2,1)S(1)}, bf16[16,32,256]{2,1,0:T(8,128)(2,1)S(1)}, u32[]{:S(2)}, u32[]{:S(2)}) collective-permute-start(bf16[16,32,256]{2,1,0:T(8,128)(2,1)S(1)} %all_to_all.10.same_ref), channel_id=1, source_target_pairs={{0,1},{1,0},{2,3},{3,2},{4,5},{5,4},{6,7},{7,6},{8,9},{9,8},{10,11... | collective-permute-start | bytes 786440 | tf_op jit(solution)/shard_map/ppermute | solution.py:298
  66.7 4.6 %collective-permute-start.16 = (f32[2,64,128]{2,1,0:T(8,128)S(1)}, f32[2,64,128]{2,1,0:T(8,128)S(1)}, u32[]{:S(2)}, u32[]{:S(2)}) collective-permute-start(f32[2,64,128]{2,1,0:T(8,128)S(1)} %fusion.2.refs_5_), channel_id=1, source_target_pairs={{0,2},{2,0},{1,3},{3,1},{4,6},{6,4},{5,7},{7,5},{8,10},{10,8},{9,1... | collective-permute-start | bytes 196616 | tf_op jit(solution)/shard_map/ppermute | solution.py:281
  67.6 3.7 %collective-permute-start.15 = (f32[2,64,128]{2,1,0:T(8,128)S(1)}, f32[2,64,128]{2,1,0:T(8,128)S(1)}, u32[]{:S(2)}, u32[]{:S(2)}) collective-permute-start(f32[2,64,128]{2,1,0:T(8,128)S(1)} %fusion.2.refs_5_), channel_id=1, source_target_pairs={{0,1},{1,0},{2,3},{3,2},{4,5},{5,4},{6,7},{7,6},{8,9},{9,8},{10,11... | collective-permute-start | bytes 196616 | tf_op jit(solution)/shard_map/ppermute | solution.py:282
  71.3 1.3 %collective-permute-start.17 = (f32[2,64,128]{2,1,0:T(8,128)S(1)}, f32[2,64,128]{2,1,0:T(8,128)S(1)}, u32[]{:S(2)}, u32[]{:S(2)}) collective-permute-start(f32[2,64,128]{2,1,0:T(8,128)S(1)} %collective-permute-done.16.refs_7_), channel_id=1, source_target_pairs={{0,1},{1,0},{2,3},{3,2},{4,5},{5,4},{6,7},{7,6},{8,9},{9,8},{10,11... | collective-permute-start | bytes 196616 | tf_op jit(solution)/shard_map/ppermute | solution.py:282

commit v10 on v9

--- a/solution.py
+++ b/solution.py
@@ -186,30 +186,47 @@
     return extras
 
 
-def middle_kernel(dims, *refs):
-    n_row, n_col, r_cols, rank, _, half = dims
-    same_ref, other_ref, rhs_ref, v_a_ref, v_b_ref = refs[:5]
-    fars, nexts = refs[5 : 5 + n_col], refs[5 + n_col : 5 + 2 * n_col]
-    msg_ref, minus_ref, own_ref, g_ref, q_ref, c_ref, far_ref, next_ref = refs[5 + 2 * n_col :]
-    row, col, turn = place()
-    order = rhs_ref.shape[2]
+def ready_kernel(dims, *refs):
+    n_row, n_col, r_cols, rank, _, _ = dims
+    v_a_ref, v_b_ref = refs[:2]
+    fars, nexts = refs[2 : 2 + n_col], refs[2 + n_col : 2 + 2 * n_col]
+    far_ref, inv_ref, u_low_ref, u_ref, m_ref, next_ref = refs[2 + 2 * n_col :]
+    _, _, turn = place()
+    order = inv_ref.shape[1]
     rows = n_col * TURNS * rank
     join(next_ref, nexts)
     join(far_ref, fars)
     inv = gathered_inverse(next_ref, order)
-    w = mm(gathered_u(next_ref, order + rows, rank, n_row - 2), inv)
+    inv_ref[...] = inv
+    u_low_ref[...] = gathered_u(next_ref, order, rank, n_row)
+    u = gathered_u(next_ref, order + rows, rank, n_row - 1)
+    u_ref[...] = u
+    w = mm(u[: (n_row - 2) * rank], inv)
+    x = jnp.concatenate([jnp.zeros((r_cols, order), BF), w.astype(BF)], axis=0)
+    tiles = [lax.dot_general(v_ref[:, :order], x, NT, preferred_element_type=F32).astype(BF)
+             for v_ref in (v_a_ref, v_b_ref)]
+    straight = turn == 0
+    m_ref[0] = jnp.where(straight, tiles[0], tiles[1])
+    m_ref[1] = jnp.where(straight, tiles[1], tiles[0])
+
+
+def middle_kernel(dims, same_ref, other_ref, rhs_ref, v_a_ref, v_b_ref, far_ref, inv_ref, u_low_ref, m_ref,
+                  msg_ref, minus_ref, own_ref, g_ref, q_ref, c_ref):
+    _, n_col, r_cols, _, _, half = dims
+    row, col, turn = place()
+    order = rhs_ref.shape[2]
     p = solve(dims, same_ref, other_ref, g_ref, q_ref, c_ref,
               lambda k: far_ref[k % n_col, lax.rem(turn - k // n_col + TURNS, TURNS)])
-    total = lax.dot_general(jnp.concatenate(p, axis=0), gathered_u(next_ref, order, rank, n_row), TN,
-                            preferred_element_type=F32)
-    z = split_mm(rhs_ref[1] - total, inv)
+    total = lax.dot_general(jnp.concatenate(p, axis=0), u_low_ref[...], TN, preferred_element_type=F32)
+    z = split_mm(rhs_ref[1] - total, inv_ref[...])
     minus_ref[...] = -total
-    x = jnp.concatenate([z.astype(BF), w.astype(BF)], axis=0)
-    tiles = [lax.dot_general(v_ref[:, :order], x, NT, preferred_element_type=F32).astype(BF) for v_ref in (v_a_ref, v_b_ref)]
+    x = jnp.concatenate([z.astype(BF), jnp.zeros((half - r_cols, order), BF)], axis=0)
+    tiles = [lax.dot_general(v_ref[:, :order], x, NT, preferred_element_type=F32).astype(BF)
+             for v_ref in (v_a_ref, v_b_ref)]
     straight = turn == 0
-    low = jnp.where(straight, tiles[0], tiles[1])
-    high = jnp.where(straight, tiles[1], tiles[0])
-    msg = pack(low, high, col > row, half)
+    low = m_ref[0, :, :half] + jnp.where(straight, tiles[0], tiles[1])
+    high = m_ref[1, :, :half] + jnp.where(straight, tiles[1], tiles[0])
+    msg = jnp.concatenate([high, jnp.where(col > row, low, m_ref[1, :, half:])], axis=1)
     for d in range(msg_ref.shape[0]):
         msg_ref[d] = msg
     own_ref[...] = q_ref[row][r_cols:, :]
@@ -218,18 +235,15 @@
 def early_kernel(dims, *refs):
     n_row, n_col, _, rank, _, _ = dims
     own_ref = refs[0]
-    nears, zs, nexts = (refs[1 + n * n_col : 1 + (n + 1) * n_col] for n in range(3))
-    y_ref, z_out_ref, inv_ref, u_ref, near_ref, z_ref, next_ref = refs[1 + 3 * n_col :]
+    nears, zs = refs[1 : 1 + n_col], refs[1 + n_col : 1 + 2 * n_col]
+    y_ref, z_out_ref, near_ref, z_ref = refs[1 + 2 * n_col :]
     order = y_ref.shape[1]
     join(near_ref, nears)
     join(z_ref, zs)
-    join(next_ref, nexts)
     minus = lax.dot_general(own_ref[...], gathered_u(near_ref, order, rank, n_row - 1), TN, preferred_element_type=F32)
     z = jnp.concatenate([z_ref[c, 0] for c in range(n_col)], axis=1)
     y_ref[...] = z + split_mm(minus, gathered_inverse(near_ref, order))
     z_out_ref[...] = jnp.concatenate([z_ref[c, 1] for c in range(n_col)], axis=1)
-    inv_ref[...] = gathered_inverse(next_ref, order)
-    u_ref[...] = gathered_u(next_ref, order + n_col * TURNS * rank, rank, n_row - 1)
 
 
 def last_kernel(dims, same_ref, other_ref, minus_ref, z_ref, early_ref, inv_ref, u_ref, y_ref, g_ref, q_ref, c_ref):
@@ -342,21 +356,29 @@
     z = gather(lax.dot_general(rhs_late, inv_late, (((2,), (1,)), ((0,), (0,))), precision=lax.Precision.HIGHEST,
                                preferred_element_type=F32))
 
+    far, inv_next, u_low, u_next, m_next = call(
+        kernel(ready_kernel),
+        [
+            shape((n_col, TURNS, rank, width + rank), BF),
+            shape((order, order), BF),
+            shape((n_row * rank, order), BF),
+            shape(((n_row - 1) * rank, order), BF),
+            shape((TURNS, rank, width), BF),
+        ],
+        later_a, later_b, *far, *nxt, scratch=[next_scratch],
+    )
     msg, minus, own = call(
         kernel(middle_kernel),
         [messages, shape((r_cols, order), F32), shape((width + rank - r_cols, r_cols), BF)],
-        same, other, rhs_here, later_a, later_b, *far, *nxt,
-        scratch=solve_scratch + [pltpu.VMEM((n_col, TURNS, rank, width + rank), BF), next_scratch],
+        same, other, rhs_here, later_a, later_b, far, inv_next, u_low, m_next, scratch=solve_scratch,
     )
     same, other = spread(msg)
-    early, z_last, inv_last, u_last = call(
-        kernel(early_kernel),
-        [shape((r_cols, order), F32)] * 2 + [shape((order, order), BF), shape(((n_row - 1) * rank, order), BF)],
-        own, *near, *z, *nxt,
-        scratch=[near_scratch, pltpu.VMEM((n_col, slots, r_cols, lanes), F32), next_scratch])
+    early, z_last = call(
+        kernel(early_kernel), [shape((r_cols, order), F32)] * 2, own, *near, *z,
+        scratch=[near_scratch, pltpu.VMEM((n_col, slots, r_cols, lanes), F32)])
     (y,) = call(
         kernel(last_kernel), [shape((slots, r_cols, order), F32)],
-        same, other, minus, z_last, early, inv_last, u_last, scratch=solve_scratch,
+        same, other, minus, z_last, early, inv_next, u_next, scratch=solve_scratch,
     )
     return y[:, None]
 

time: 75.6 us -> 75.8 us (level)
    pallas_call x5 -> x6, Pallas kernels: 7.26 us -> 7.49 us  [call(): pl.pallas_call(kernel, out_shape=outs, in_specs=[pl.BlockSpec(memory_spac...]
  transfers between devices with their start and end apart: 19 -> 19, of which waited for: 8 -> 8; matrix products, arithmetic and copies ran while one was open for 1% -> 1% of each run, Pallas kernels for 1% -> 2%
where the time goes in v10:
time: 75.8 us; the launch traced here: 75.5 us
  starting transfers between devices  30.2 us (40%)
  waiting for transfers between devices  21.7 us (29%)
  blocking collectives  15.4 us (20%)
  Pallas kernels  7.49 us (10%)
    ppermute x4, waiting for transfers between devices, gather(): moved = lax.ppermute(part, 'x', [(i, (i + s) % n_x) for i in range(n_x)])  15.5 us
    all_to_all x1, blocking collectives, spread(): lax.all_to_all(m, ('row', 'x'), split_axis=0, concat_axis=0, tiled=True)  15.4 us
    ppermute x4, starting transfers between devices, gather(): moved = lax.ppermute(part, 'x', [(i, (i + s) % n_x) for i in range(n_x)])  12.4 us
    all_to_all x1, starting transfers between devices, spread(): lax.all_to_all(m, ('row', 'x'), split_axis=0, concat_axis=0, tiled=True)  8.42 us
    pallas_call x6, Pallas kernels, call(): pl.pallas_call(kernel, out_shape=outs, in_specs=[pl.BlockSpec(memory_spac...  7.49 us
    ppermute x4, starting transfers between devices, turn_rows(): got.append(lax.ppermute(parts[s], everywhere, pairs))  6.39 us
    ppermute x8, waiting for transfers between devices, gather(): pieces += [moved, lax.ppermute(moved, 'core', swap)]  3.41 us
    ppermute x4, waiting for transfers between devices, turn_rows(): got.append(lax.ppermute(parts[s], everywhere, pairs))  2.72 us
  transfers between devices with their start and end apart: 19, of which 8 were waited for; matrix products, arithmetic and copies ran while one was open for 1% of the time, Pallas kernels for 2%

profile of v10, /device:TPU:0, one launch (start us, length us, event | category | flops | bytes accessed | tf_op | source)
XLA Modules:
  0.0 75.5 jit_solution(16640712219667782688)
XLA Ops:
  0.0 1.2 %shard_map.55 = (bf16[768,128]{1,0:T(8,128)(2,1)S(1)}, bf16[2,32,512]{2,1,0:T(8,128)(2,1)S(1)}, bf16[2,32,512]{2,1,0:T(8,128)(2,1)S(1)}, bf16[32,512]{1,0:T(8,128)(2,1)S(1)}, bf16[32,512]{1,0:T(8,128)(2,1)S(1)}) custom-call(s32[2,1,1,4]{3,2,1,0:T(1,128)} %bitcast.68, f32[2,512,128]{2,1,0:T(8,128)} %bitcast.56, bf16[2,2,2,32,512]{4,3,2,1,0:T(8,128)(2,1)} %bitcast.58, ...), custom_call_target="tpu_custom_call" | custom-call | tf_op jit(solution)/shard_map/pallas_call | solution.py:258
  1.2 3.0 %collective-permute-start.3 = (bf16[768,128]{1,0:T(8,128)(2,1)S(1)}, bf16[768,128]{1,0:T(8,128)(2,1)S(1)}, u32[]{:S(2)}, u32[]{:S(2)}) collective-permute-start(bf16[768,128]{1,0:T(8,128)(2,1)S(1)} %get-tuple-element.32.refs_5_.refs_1_), channel_id=1, source_target_pairs={{0,2},{2,0},{1,3},{3,1},{4,6},{6,4},{5,7},{7,5},{8,10},{10,8},{9,1... | collective-permute-start | bytes 589832 | tf_op jit(solution)/shard_map/ppermute | solution.py:295
  4.3 0.7 collective-permute-start
  4.9 2.7 %collective-permute-start.1 = (bf16[2,32,512]{2,1,0:T(8,128)(2,1)S(1)}, bf16[2,32,512]{2,1,0:T(8,128)(2,1)S(1)}, u32[]{:S(2)}, u32[]{:S(2)}) collective-permute-start(bf16[2,32,512]{2,1,0:T(8,128)(2,1)S(1)} %get-tuple-element.29), channel_id=1, source_target_pairs={{0,16},{1,20},{2,24},{3,28},{4,17},{5,21},{6,25},{7,29},{8,18},{9,... | collective-permute-start | bytes 196616 | tf_op jit(solution)/shard_map/ppermute | solution.py:307
  7.6 0.0 copy-start
  7.7 1.4 %collective-permute-done.3.refs_7_.refs_3_ = bf16[768,128]{1,0:T(8,128)(2,1)S(1)} collective-permute-done((bf16[768,128]{1,0:T(8,128)(2,1)S(1)}, bf16[768,128]{1,0:T(8,128)(2,1)S(1)}, u32[]{:S(2)}, u32[]{:S(2)}) %collective-permute-start.3) | collective-permute-done | bytes 196640 | tf_op jit(solution)/shard_map/ppermute | solution.py:295
  9.1 1.6 %collective-permute-start.4 = (bf16[768,128]{1,0:T(8,128)(2,1)S(1)}, bf16[768,128]{1,0:T(8,128)(2,1)S(1)}, u32[]{:S(2)}, u32[]{:S(2)}) collective-permute-start(bf16[768,128]{1,0:T(8,128)(2,1)S(1)} %collective-permute-done.3.refs_7_.refs_3_), channel_id=1, source_target_pairs={{0,1},{1,0},{2,3},{3,2},{4,5},{5,4},{6,7},{7,6},{8,9},{9,8},{10,11... | collective-permute-start | bytes 589832 | tf_op jit(solution)/shard_map/ppermute | solution.py:296
  10.7 1.0 %collective-permute-done.4.refs_8_.refs_4_ = bf16[768,128]{1,0:T(8,128)(2,1)S(1)} collective-permute-done((bf16[768,128]{1,0:T(8,128)(2,1)S(1)}, bf16[768,128]{1,0:T(8,128)(2,1)S(1)}, u32[]{:S(2)}, u32[]{:S(2)}) %collective-permute-start.4) | collective-permute-done | bytes 196640 | tf_op jit(solution)/shard_map/ppermute | solution.py:296
  11.8 1.5 %shard_map.56 = (bf16[16,32,256]{2,1,0:T(8,128)(2,1)}, bf16[32,800]{1,0:T(8,128)(2,1)S(1)}, bf16[32,800]{1,0:T(8,128)(2,1)S(1)}) custom-call(f32[2,64,512]{2,1,0:T(8,128)S(1)} %bitcast.51, bf16[2,32,512]{2,1,0:T(8,128)(2,1)S(1)} %collective-permute-done.refs_1_, bf16[2,32,512]{2,1,0:T(8,128)(2,1)S(1)} %collective-permute-done.1.refs_2_, ...), custom_call_target="tpu_custom_call" | custom-call | tf_op jit(solution)/shard_map/pallas_call | solution.py:258
  13.3 8.4 %all-to-all-start = ((bf16[16,32,256]{2,1,0:T(8,128)(2,1)}), bf16[16,32,256]{2,1,0:T(8,128)(2,1)S(1)}, u32[]{:S(2)}, u32[]{:S(2)}) async-start(bf16[16,32,256]{2,1,0:T(8,128)(2,1)} %get-tuple-element.36), calls=%async_computation | async-start | bytes 524288 | tf_op jit(solution)/shard_map/all_to_all | solution.py:311
  21.8 2.0 %collective-permute-start.12 = (bf16[1024,128]{1,0:T(8,128)(2,1)S(1)}, bf16[1024,128]{1,0:T(8,128)(2,1)S(1)}, u32[]{:S(2)}, u32[]{:S(2)}) collective-permute-start(bf16[1024,128]{1,0:T(8,128)(2,1)S(1)} %constant_dynamic-update-slice_fusion.refs_6_), channel_id=1, source_target_pairs={{0,2},{2,0},{1,3},{3,1},{4,6},{6,4},{5,7},{7,5},{8,10},{10,8},{9,1... | collective-permute-start | bytes 786440 | tf_op jit(solution)/shard_map/ppermute | solution.py:295
  23.8 8.6 %collective-permute-done.12.refs_8_ = bf16[1024,128]{1,0:T(8,128)(2,1)S(1)} collective-permute-done((bf16[1024,128]{1,0:T(8,128)(2,1)S(1)}, bf16[1024,128]{1,0:T(8,128)(2,1)S(1)}, u32[]{:S(2)}, u32[]{:S(2)}) %collective-permute-start.12) | collective-permute-done | bytes 262176 | tf_op jit(solution)/shard_map/ppermute | solution.py:295
  32.4 0.5 collective-permute-start.5
  32.9 0.7 collective-permute-start.6
  33.6 2.4 %collective-permute-start.7 = (bf16[32,800]{1,0:T(8,128)(2,1)S(1)}, bf16[32,800]{1,0:T(8,128)(2,1)S(1)}, u32[]{:S(2)}, u32[]{:S(2)}) collective-permute-start(bf16[32,800]{1,0:T(8,128)(2,1)S(1)} %get-tuple-element.38), channel_id=1, source_target_pairs={{0,16},{1,20},{2,24},{3,28},{4,17},{5,21},{6,25},{7,29},{8,18},{9,... | collective-permute-start | bytes 153608 | tf_op jit(solution)/shard_map/ppermute | solution.py:307
  36.0 2.7 %collective-permute-done.7.refs_1_.v_b_ref = bf16[32,800]{1,0:T(8,128)(2,1)S(1)} collective-permute-done((bf16[32,800]{1,0:T(8,128)(2,1)S(1)}, bf16[32,800]{1,0:T(8,128)(2,1)S(1)}, u32[]{:S(2)}, u32[]{:S(2)}) %collective-permute-start.7) | collective-permute-done | bytes 51232 | tf_op jit(solution)/shard_map/ppermute | solution.py:307
  38.7 6.6 %collective-permute-start.9 = (bf16[2,32,288]{2,1,0:T(8,128)(2,1)S(1)}, bf16[2,32,288]{2,1,0:T(8,128)(2,1)S(1)}, u32[]{:S(2)}, u32[]{:S(2)}) collective-permute-start(bf16[2,32,288]{2,1,0:T(8,128)(2,1)S(1)} %pad_maximum_fusion.refs_2_), channel_id=1, source_target_pairs={{0,2},{2,0},{1,3},{3,1},{4,6},{6,4},{5,7},{7,5},{8,10},{10,8},{9,1... | collective-permute-start | bytes 110600 | tf_op jit(solution)/shard_map/ppermute | solution.py:295
  45.3 0.5 collective-permute-start.8
  45.8 2.0 %collective-permute-done.9.refs_4_ = bf16[2,32,288]{2,1,0:T(8,128)(2,1)S(1)} collective-permute-done((bf16[2,32,288]{2,1,0:T(8,128)(2,1)S(1)}, bf16[2,32,288]{2,1,0:T(8,128)(2,1)S(1)}, u32[]{:S(2)}, u32[]{:S(2)}) %collective-permute-start.9) | collective-permute-done | bytes 36896 | tf_op jit(solution)/shard_map/ppermute | solution.py:295
  47.8 0.1 collective-permute-start.10
  47.9 1.1 %collective-permute-done.10.refs_5_ = bf16[2,32,288]{2,1,0:T(8,128)(2,1)S(1)} collective-permute-done((bf16[2,32,288]{2,1,0:T(8,128)(2,1)S(1)}, bf16[2,32,288]{2,1,0:T(8,128)(2,1)S(1)}, u32[]{:S(2)}, u32[]{:S(2)}) %collective-permute-start.10) | collective-permute-done | bytes 36896 | tf_op jit(solution)/shard_map/ppermute | solution.py:296
  49.0 0.7 shard_map.57
  49.7 0.0 collective-permute-done.5.other_ref
  49.8 1.5 %shard_map.58 = (bf16[16,32,256]{2,1,0:T(8,128)(2,1)S(1)}, f32[64,512]{1,0:T(8,128)S(1)}, bf16[224,64]{1,0:T(8,128)(2,1)S(1)}) custom-call(bf16[16,32,256]{2,1,0:T(8,128)(2,1)S(1)} %all-to-all-done.same_ref, bf16[16,32,256]{2,1,0:T(8,128)(2,1)S(1)} %collective-permute-done.5.other_ref, f32[2,64,512]{2,1,0:T(8,128)S(1)} %bitcast.52, ...), custom_call_target="tpu_custom_call" | custom-call | tf_op jit(solution)/shard_map/pallas_call | solution.py:258
  51.3 15.4 %all_to_all.10.same_ref = bf16[16,32,256]{2,1,0:T(8,128)(2,1)S(1)} all-to-all(bf16[16,32,256]{2,1,0:T(8,128)(2,1)S(1)} %get-tuple-element.43), channel_id=1, replica_groups=mesh['row'=8,'x'=2,'core'=2] {'row','x'}, dimensions={0} | all-to-all | bytes 524288 | tf_op jit(solution)/shard_map/all_to_all | solution.py:311
  66.7 0.4 fusion.2.refs_5_
  67.2 0.8 %collective-permute-start.16 = (f32[2,64,128]{2,1,0:T(8,128)S(1)}, f32[2,64,128]{2,1,0:T(8,128)S(1)}, u32[]{:S(2)}, u32[]{:S(2)}) collective-permute-start(f32[2,64,128]{2,1,0:T(8,128)S(1)} %fusion.2.refs_5_), channel_id=1, source_target_pairs={{0,2},{2,0},{1,3},{3,1},{4,6},{6,4},{5,7},{7,5},{8,10},{10,8},{9,1... | collective-permute-start | bytes 196616 | tf_op jit(solution)/shard_map/ppermute | solution.py:295
  68.0 0.2 collective-permute-start.15
  68.2 3.5 %collective-permute-done.16.refs_7_ = f32[2,64,128]{2,1,0:T(8,128)S(1)} collective-permute-done((f32[2,64,128]{2,1,0:T(8,128)S(1)}, f32[2,64,128]{2,1,0:T(8,128)S(1)}, u32[]{:S(2)}, u32[]{:S(2)}) %collective-permute-start.16) | collective-permute-done | bytes 65568 | tf_op jit(solution)/shard_map/ppermute | solution.py:295
  71.7 1.2 %collective-permute-done.17.refs_8_ = f32[2,64,128]{2,1,0:T(8,128)S(1)} collective-permute-done((f32[2,64,128]{2,1,0:T(8,128)S(1)}, f32[2,64,128]{2,1,0:T(8,128)S(1)}, u32[]{:S(2)}, u32[]{:S(2)}) %collective-permute-start.17) | collective-permute-done | bytes 65568 | tf_op jit(solution)/shard_map/ppermute | solution.py:296
  73.0 0.5 shard_map.59
  73.5 2.1 %shard_map.60 = f32[2,64,512]{2,1,0:T(8,128)} custom-call(bf16[16,32,256]{2,1,0:T(8,128)(2,1)S(1)} %all_to_all.10.same_ref, bf16[16,32,256]{2,1,0:T(8,128)(2,1)S(1)} %collective-permute-done.14.other_ref, f32[64,512]{1,0:T(8,128)S(1)} %get-tuple-element.44.minus_ref, f32[64,512]{1,0:T(8,128)S(1)} %get-tuple-element.48.z_ref, ...), custom_call_target="tpu_custom_call" | custom-call | tf_op jit(solution)/shard_map/pallas_call | solution.py:258
  (31 shorter events, 0.2 us)
Async XLA Ops:
  0.0 7.6 %copy-start.2 = (bf16[2,1,4,1,32,512]{5,4,3,2,1,0:T(8,128)(2,1)S(1)}, bf16[2,1,4,1,32,512]{5,4,3,2,1,0:T(8,128)(2,1)}, u32[]{:S(2)}) copy-start(bf16[2,1,4,1,32,512]{5,4,3,2,1,0:T(8,128)(2,1)} %param.7) | copy-start | bytes 786436
  0.0 7.6 %copy-start.1 = (f32[2,1,512,128]{3,2,1,0:T(8,128)S(1)}, f32[2,1,512,128]{3,2,1,0:T(8,128)}, u32[]{:S(2)}) copy-start(f32[2,1,512,128]{3,2,1,0:T(8,128)} %param.6) | copy-start | bytes 1572868
  1.2 7.9 %collective-permute-start.3 = (bf16[768,128]{1,0:T(8,128)(2,1)S(1)}, bf16[768,128]{1,0:T(8,128)(2,1)S(1)}, u32[]{:S(2)}, u32[]{:S(2)}) collective-permute-start(bf16[768,128]{1,0:T(8,128)(2,1)S(1)} %get-tuple-element.32.refs_5_.refs_1_), channel_id=1, source_target_pairs={{0,2},{2,0},{1,3},{3,1},{4,6},{6,4},{5,7},{7,5},{8,10},{10,8},{9,1... | collective-permute-start | bytes 589832 | tf_op jit(solution)/shard_map/ppermute | solution.py:295
  4.2 6.5 %collective-permute-start.2 = (bf16[768,128]{1,0:T(8,128)(2,1)S(1)}, bf16[768,128]{1,0:T(8,128)(2,1)S(1)}, u32[]{:S(2)}, u32[]{:S(2)}) collective-permute-start(bf16[768,128]{1,0:T(8,128)(2,1)S(1)} %get-tuple-element.32.refs_5_.refs_1_), channel_id=1, source_target_pairs={{0,1},{1,0},{2,3},{3,2},{4,5},{5,4},{6,7},{7,6},{8,9},{9,8},{10,11... | collective-permute-start | bytes 589832 | tf_op jit(solution)/shard_map/ppermute | solution.py:296
  4.3 6.5 %collective-permute-start = (bf16[2,32,512]{2,1,0:T(8,128)(2,1)S(1)}, bf16[2,32,512]{2,1,0:T(8,128)(2,1)S(1)}, u32[]{:S(2)}, u32[]{:S(2)}) collective-permute-start(bf16[2,32,512]{2,1,0:T(8,128)(2,1)S(1)} %get-tuple-element.28), channel_id=1, source_target_pairs={{0,0},{1,4},{2,8},{3,12},{4,1},{5,5},{6,9},{7,13},{8,2},{9,6},{10,... | collective-permute-start | bytes 196616 | tf_op jit(solution)/shard_map/ppermute | solution.py:307
  4.9 5.8 %collective-permute-start.1 = (bf16[2,32,512]{2,1,0:T(8,128)(2,1)S(1)}, bf16[2,32,512]{2,1,0:T(8,128)(2,1)S(1)}, u32[]{:S(2)}, u32[]{:S(2)}) collective-permute-start(bf16[2,32,512]{2,1,0:T(8,128)(2,1)S(1)} %get-tuple-element.29), channel_id=1, source_target_pairs={{0,16},{1,20},{2,24},{3,28},{4,17},{5,21},{6,25},{7,29},{8,18},{9,... | collective-permute-start | bytes 196616 | tf_op jit(solution)/shard_map/ppermute | solution.py:307
  7.6 4.2 %copy-start = (f32[2,1,64,512]{3,2,1,0:T(8,128)S(1)}, f32[2,1,64,512]{3,2,1,0:T(8,128)}, u32[]{:S(2)}) copy-start(f32[2,1,64,512]{3,2,1,0:T(8,128)} %param.5) | copy-start | bytes 786436
  9.1 2.6 %collective-permute-start.4 = (bf16[768,128]{1,0:T(8,128)(2,1)S(1)}, bf16[768,128]{1,0:T(8,128)(2,1)S(1)}, u32[]{:S(2)}, u32[]{:S(2)}) collective-permute-start(bf16[768,128]{1,0:T(8,128)(2,1)S(1)} %collective-permute-done.3.refs_7_.refs_3_), channel_id=1, source_target_pairs={{0,1},{1,0},{2,3},{3,2},{4,5},{5,4},{6,7},{7,6},{8,9},{9,8},{10,11... | collective-permute-start | bytes 589832 | tf_op jit(solution)/shard_map/ppermute | solution.py:296
  13.3 19.1 %all-to-all-start = ((bf16[16,32,256]{2,1,0:T(8,128)(2,1)}), bf16[16,32,256]{2,1,0:T(8,128)(2,1)S(1)}, u32[]{:S(2)}, u32[]{:S(2)}) async-start(bf16[16,32,256]{2,1,0:T(8,128)(2,1)} %get-tuple-element.36), calls=%async_computation | async-start | bytes 524288 | tf_op jit(solution)/shard_map/all_to_all | solution.py:311
  21.8 10.6 %collective-permute-start.12 = (bf16[1024,128]{1,0:T(8,128)(2,1)S(1)}, bf16[1024,128]{1,0:T(8,128)(2,1)S(1)}, u32[]{:S(2)}, u32[]{:S(2)}) collective-permute-start(bf16[1024,128]{1,0:T(8,128)(2,1)S(1)} %constant_dynamic-update-slice_fusion.refs_6_), channel_id=1, source_target_pairs={{0,2},{2,0},{1,3},{3,1},{4,6},{6,4},{5,7},{7,5},{8,10},{10,8},{9,1... | collective-permute-start | bytes 786440 | tf_op jit(solution)/shard_map/ppermute | solution.py:295
  23.8 24.1 %collective-permute-start.11 = (bf16[1024,128]{1,0:T(8,128)(2,1)S(1)}, bf16[1024,128]{1,0:T(8,128)(2,1)S(1)}, u32[]{:S(2)}, u32[]{:S(2)}) collective-permute-start(bf16[1024,128]{1,0:T(8,128)(2,1)S(1)} %constant_dynamic-update-slice_fusion.refs_6_), channel_id=1, source_target_pairs={{0,1},{1,0},{2,3},{3,2},{4,5},{5,4},{6,7},{7,6},{8,9},{9,8},{10,11... | collective-permute-start | bytes 786440 | tf_op jit(solution)/shard_map/ppermute | solution.py:296
  32.4 16.6 %collective-permute-start.13 = (bf16[1024,128]{1,0:T(8,128)(2,1)S(1)}, bf16[1024,128]{1,0:T(8,128)(2,1)S(1)}, u32[]{:S(2)}, u32[]{:S(2)}) collective-permute-start(bf16[1024,128]{1,0:T(8,128)(2,1)S(1)} %collective-permute-done.12.refs_8_), channel_id=1, source_target_pairs={{0,1},{1,0},{2,3},{3,2},{4,5},{5,4},{6,7},{7,6},{8,9},{9,8},{10,11... | collective-permute-start | bytes 786440 | tf_op jit(solution)/shard_map/ppermute | solution.py:296
  32.4 17.4 %collective-permute-start.5 = (bf16[16,32,256]{2,1,0:T(8,128)(2,1)S(1)}, bf16[16,32,256]{2,1,0:T(8,128)(2,1)S(1)}, u32[]{:S(2)}, u32[]{:S(2)}) collective-permute-start(bf16[16,32,256]{2,1,0:T(8,128)(2,1)S(1)} %all-to-all-done.same_ref), channel_id=1, source_target_pairs={{0,1},{1,0},{2,3},{3,2},{4,5},{5,4},{6,7},{7,6},{8,9},{9,8},{10,11... | collective-permute-start | bytes 786440 | tf_op jit(solution)/shard_map/ppermute | solution.py:312
  32.9 3.1 %collective-permute-start.6 = (bf16[32,800]{1,0:T(8,128)(2,1)S(1)}, bf16[32,800]{1,0:T(8,128)(2,1)S(1)}, u32[]{:S(2)}, u32[]{:S(2)}) collective-permute-start(bf16[32,800]{1,0:T(8,128)(2,1)S(1)} %get-tuple-element.37), channel_id=1, source_target_pairs={{0,0},{1,4},{2,8},{3,12},{4,1},{5,5},{6,9},{7,13},{8,2},{9,6},{10,... | collective-permute-start | bytes 153608 | tf_op jit(solution)/shard_map/ppermute | solution.py:307
  33.6 5.1 %collective-permute-start.7 = (bf16[32,800]{1,0:T(8,128)(2,1)S(1)}, bf16[32,800]{1,0:T(8,128)(2,1)S(1)}, u32[]{:S(2)}, u32[]{:S(2)}) collective-permute-start(bf16[32,800]{1,0:T(8,128)(2,1)S(1)} %get-tuple-element.38), channel_id=1, source_target_pairs={{0,16},{1,20},{2,24},{3,28},{4,17},{5,21},{6,25},{7,29},{8,18},{9,... | collective-permute-start | bytes 153608 | tf_op jit(solution)/shard_map/ppermute | solution.py:307
  38.7 9.1 %collective-permute-start.9 = (bf16[2,32,288]{2,1,0:T(8,128)(2,1)S(1)}, bf16[2,32,288]{2,1,0:T(8,128)(2,1)S(1)}, u32[]{:S(2)}, u32[]{:S(2)}) collective-permute-start(bf16[2,32,288]{2,1,0:T(8,128)(2,1)S(1)} %pad_maximum_fusion.refs_2_), channel_id=1, source_target_pairs={{0,2},{2,0},{1,3},{3,1},{4,6},{6,4},{5,7},{7,5},{8,10},{10,8},{9,1... | collective-permute-start | bytes 110600 | tf_op jit(solution)/shard_map/ppermute | solution.py:295
  45.3 2.6 %collective-permute-start.8 = (bf16[2,32,288]{2,1,0:T(8,128)(2,1)S(1)}, bf16[2,32,288]{2,1,0:T(8,128)(2,1)S(1)}, u32[]{:S(2)}, u32[]{:S(2)}) collective-permute-start(bf16[2,32,288]{2,1,0:T(8,128)(2,1)S(1)} %pad_maximum_fusion.refs_2_), channel_id=1, source_target_pairs={{0,1},{1,0},{2,3},{3,2},{4,5},{5,4},{6,7},{7,6},{8,9},{9,8},{10,11... | collective-permute-start | bytes 110600 | tf_op jit(solution)/shard_map/ppermute | solution.py:296
  47.8 1.2 %collective-permute-start.10 = (bf16[2,32,288]{2,1,0:T(8,128)(2,1)S(1)}, bf16[2,32,288]{2,1,0:T(8,128)(2,1)S(1)}, u32[]{:S(2)}, u32[]{:S(2)}) collective-permute-start(bf16[2,32,288]{2,1,0:T(8,128)(2,1)S(1)} %collective-permute-done.9.refs_4_), channel_id=1, source_target_pairs={{0,1},{1,0},{2,3},{3,2},{4,5},{5,4},{6,7},{7,6},{8,9},{9,8},{10,11... | collective-permute-start | bytes 110600 | tf_op jit(solution)/shard_map/ppermute | solution.py:296
  66.7 6.8 %collective-permute-start.14 = (bf16[16,32,256]{2,1,0:T(8,128)(2,1)S(1)}, bf16[16,32,256]{2,1,0:T(8,128)(2,1)S(1)}, u32[]{:S(2)}, u32[]{:S(2)}) collective-permute-start(bf16[16,32,256]{2,1,0:T(8,128)(2,1)S(1)} %all_to_all.10.same_ref), channel_id=1, source_target_pairs={{0,1},{1,0},{2,3},{3,2},{4,5},{5,4},{6,7},{7,6},{8,9},{9,8},{10,11... | collective-permute-start | bytes 786440 | tf_op jit(solution)/shard_map/ppermute | solution.py:312
  67.2 4.6 %collective-permute-start.16 = (f32[2,64,128]{2,1,0:T(8,128)S(1)}, f32[2,64,128]{2,1,0:T(8,128)S(1)}, u32[]{:S(2)}, u32[]{:S(2)}) collective-permute-start(f32[2,64,128]{2,1,0:T(8,128)S(1)} %fusion.2.refs_5_), channel_id=1, source_target_pairs={{0,2},{2,0},{1,3},{3,1},{4,6},{6,4},{5,7},{7,5},{8,10},{10,8},{9,1... | collective-permute-start | bytes 196616 | tf_op jit(solution)/shard_map/ppermute | solution.py:295
  68.0 3.7 %collective-permute-start.15 = (f32[2,64,128]{2,1,0:T(8,128)S(1)}, f32[2,64,128]{2,1,0:T(8,128)S(1)}, u32[]{:S(2)}, u32[]{:S(2)}) collective-permute-start(f32[2,64,128]{2,1,0:T(8,128)S(1)} %fusion.2.refs_5_), channel_id=1, source_target_pairs={{0,1},{1,0},{2,3},{3,2},{4,5},{5,4},{6,7},{7,6},{8,9},{9,8},{10,11... | collective-permute-start | bytes 196616 | tf_op jit(solution)/shard_map/ppermute | solution.py:296
  71.7 1.3 %collective-permute-start.17 = (f32[2,64,128]{2,1,0:T(8,128)S(1)}, f32[2,64,128]{2,1,0:T(8,128)S(1)}, u32[]{:S(2)}, u32[]{:S(2)}) collective-permute-start(f32[2,64,128]{2,1,0:T(8,128)S(1)} %collective-permute-done.16.refs_7_), channel_id=1, source_target_pairs={{0,1},{1,0},{2,3},{3,2},{4,5},{5,4},{6,7},{7,6},{8,9},{9,8},{10,11... | collective-permute-start | bytes 196616 | tf_op jit(solution)/shard_map/ppermute | solution.py:296

commit v11 on v10

--- a/solution.py
+++ b/solution.py
@@ -97,17 +97,24 @@
          for j in range(blocks)], axis=0)
 
 
-def first_kernel(dims, *refs):
-    n_row, _, _, rank, width, half = dims
-    rhs_ref, v_a_ref, v_b_ref, later_a_ref, later_b_ref = refs[:5]
-    msg_ref, far_a_ref, far_b_ref, near_ref = refs[-4:]
+def rows_kernel(dims, rhs_ref, *refs):
+    n_row, n_col, r_cols, rank, _, _ = dims
+    x_ref, inv_ref, u_ref, near_ref = refs[n_col:]
+    order = rhs_ref.shape[2]
+    join(near_ref, refs[:n_col])
+    inv = gathered_inverse(near_ref, order)
+    u = gathered_u(near_ref, order, rank, n_row - 1)
+    inv_ref[...] = inv
+    u_ref[...] = u
+    x_ref[:r_cols, :] = split_mm(rhs_ref[0], inv).astype(BF)
+    x_ref[r_cols:, :] = mm(u, inv).astype(BF)
+
+
+def first_kernel(dims, x_ref, v_a_ref, v_b_ref, later_a_ref, later_b_ref, msg_ref, far_a_ref, far_b_ref):
+    _, _, _, rank, width, half = dims
     row, col, turn = place()
-    order = rhs_ref.shape[2]
-    join(near_ref, refs[5:-4])
-    inv = gathered_inverse(near_ref, order)
-    z = split_mm(rhs_ref[0], inv)
-    w = mm(gathered_u(near_ref, order, rank, n_row - 1), inv)
-    x = jnp.concatenate([z.astype(BF), w.astype(BF)], axis=0)
+    order = x_ref.shape[1]
+    x = x_ref[...]
     tiles = []
     for v_ref in (v_a_ref, v_b_ref):
         v = v_ref[...].reshape(2 * rank, order)
@@ -233,33 +240,36 @@
 
 
 def early_kernel(dims, *refs):
-    n_row, n_col, _, rank, _, _ = dims
-    own_ref = refs[0]
-    nears, zs = refs[1 : 1 + n_col], refs[1 + n_col : 1 + 2 * n_col]
-    y_ref, z_out_ref, near_ref, z_ref = refs[1 + 2 * n_col :]
-    order = y_ref.shape[1]
-    join(near_ref, nears)
-    join(z_ref, zs)
-    minus = lax.dot_general(own_ref[...], gathered_u(near_ref, order, rank, n_row - 1), TN, preferred_element_type=F32)
+    _, n_col, _, _, _, _ = dims
+    own_ref, inv_ref, u_ref = refs[:3]
+    y_ref, z_out_ref, z_ref = refs[3 + n_col :]
+    join(z_ref, refs[3 : 3 + n_col])
+    minus = lax.dot_general(own_ref[...], u_ref[...], TN, preferred_element_type=F32)
     z = jnp.concatenate([z_ref[c, 0] for c in range(n_col)], axis=1)
-    y_ref[...] = z + split_mm(minus, gathered_inverse(near_ref, order))
+    y_ref[...] = z + split_mm(minus, inv_ref[...])
     z_out_ref[...] = jnp.concatenate([z_ref[c, 1] for c in range(n_col)], axis=1)
 
 
-def last_kernel(dims, same_ref, other_ref, minus_ref, z_ref, early_ref, inv_ref, u_ref, y_ref, g_ref, q_ref, c_ref):
-    y_ref[0] = early_ref[...]
+def last_kernel(dims, same_ref, other_ref, minus_ref, z_ref, early_ref, inv_ref, u_ref, y_hbm,
+                g_ref, q_ref, c_ref, late_ref, sems):
+    first_out = pltpu.make_async_copy(early_ref, y_hbm.at[0], sems.at[0])
+    first_out.start()
     solve(dims, same_ref, other_ref, g_ref, q_ref, c_ref, None)
     own = q_ref[lax.axis_index("row")][dims[2] :, :]
     minus = minus_ref[...] + lax.dot_general(own, u_ref[...], TN, preferred_element_type=F32)
-    y_ref[1] = z_ref[...] + split_mm(minus, inv_ref[...])
-
-
-def call(kernel, outs, *args, scratch=(), space=pltpu.VMEM):
+    late_ref[...] = z_ref[...] + split_mm(minus, inv_ref[...])
+    second_out = pltpu.make_async_copy(late_ref, y_hbm.at[1], sems.at[1])
+    second_out.start()
+    first_out.wait()
+    second_out.wait()
+
+
+def call(kernel, outs, *args, scratch=(), space=pltpu.VMEM, out_space=pltpu.VMEM):
     return pl.pallas_call(
         kernel,
         out_shape=outs,
         in_specs=[pl.BlockSpec(memory_space=space)] * len(args),
-        out_specs=[pl.BlockSpec(memory_space=pltpu.VMEM)] * len(outs),
+        out_specs=[pl.BlockSpec(memory_space=out_space)] * len(outs),
         scratch_shapes=list(scratch),
         compiler_params=pltpu.CompilerParams(vmem_limit_bytes=24 * 2**20),
     )(*args)
@@ -344,9 +354,14 @@
     nxt = gather(jnp.concatenate([inv_here[1].astype(BF)] + [
         later_u[a, :, m * lanes : (m + 1) * lanes] for a in range(slots) for m in range(n_col)], axis=0))
 
+    x_rows, inv_near, u_near = call(
+        kernel(rows_kernel),
+        [shape((width + rank, order), BF), shape((order, order), BF), shape(((n_row - 1) * rank, order), BF)],
+        rhs_here, *near, scratch=[near_scratch],
+    )
     msg, far_a, far_b = call(
         kernel(first_kernel), [messages, far_shape, far_shape],
-        rhs_here, v_a, v_b, later_a, later_b, *near, scratch=[near_scratch],
+        x_rows, v_a, v_b, later_a, later_b,
     )
 
     rhs_late, inv_late, msg, far_a, far_b = lax.optimization_barrier((rhs_here, inv_here, msg, far_a, far_b))
@@ -374,11 +389,12 @@
     )
     same, other = spread(msg)
     early, z_last = call(
-        kernel(early_kernel), [shape((r_cols, order), F32)] * 2, own, *near, *z,
-        scratch=[near_scratch, pltpu.VMEM((n_col, slots, r_cols, lanes), F32)])
+        kernel(early_kernel), [shape((r_cols, order), F32)] * 2, own, inv_near, u_near, *z,
+        scratch=[pltpu.VMEM((n_col, slots, r_cols, lanes), F32)])
     (y,) = call(
         kernel(last_kernel), [shape((slots, r_cols, order), F32)],
-        same, other, minus, z_last, early, inv_next, u_next, scratch=solve_scratch,
+        same, other, minus, z_last, early, inv_next, u_next, out_space=pltpu.HBM,
+        scratch=solve_scratch + [pltpu.VMEM((r_cols, order), F32), pltpu.SemaphoreType.DMA((2,))],
     )
     return y[:, None]
 

time: 75.8 us -> 75.2 us (level)
    pallas_call x6 -> x7, Pallas kernels: 7.49 us -> 7.46 us  [call(): pl.pallas_call(kernel, out_shape=outs, in_specs=[pl.BlockSpec(memory_spac...]
where the time goes in v11:
time: 75.2 us; the launch traced here: 74.9 us
  starting transfers between devices  29.6 us (39%)
  waiting for transfers between devices  21.7 us (29%)
  blocking collectives  15.4 us (20%)
  Pallas kernels  7.46 us (10%)
    ppermute x4, waiting for transfers between devices, gather(): moved = lax.ppermute(part, 'x', [(i, (i + s) % n_x) for i in range(n_x)])  15.5 us
    all_to_all x1, blocking collectives, spread(): lax.all_to_all(m, ('row', 'x'), split_axis=0, concat_axis=0, tiled=True)  15.4 us
    ppermute x4, starting transfers between devices, gather(): moved = lax.ppermute(part, 'x', [(i, (i + s) % n_x) for i in range(n_x)])  12.4 us
    all_to_all x1, starting transfers between devices, spread(): lax.all_to_all(m, ('row', 'x'), split_axis=0, concat_axis=0, tiled=True)  7.8 us
    pallas_call x7, Pallas kernels, call(): pl.pallas_call(kernel, out_shape=outs, in_specs=[pl.BlockSpec(memory_spac...  7.46 us
    ppermute x4, starting transfers between devices, turn_rows(): got.append(lax.ppermute(parts[s], everywhere, pairs))  6.39 us
    ppermute x8, waiting for transfers between devices, gather(): pieces += [moved, lax.ppermute(moved, 'core', swap)]  3.43 us
    ppermute x4, waiting for transfers between devices, turn_rows(): got.append(lax.ppermute(parts[s], everywhere, pairs))  2.72 us
  transfers between devices with their start and end apart: 19, of which 8 were waited for; matrix products, arithmetic and copies ran while one was open for 1% of the time, Pallas kernels for 2%

profile of v11, /device:TPU:0, one launch (start us, length us, event | category | flops | bytes accessed | tf_op | source)
XLA Modules:
  0.0 74.9 jit_solution(15141368531791357089)
XLA Ops:
  0.0 1.2 %shard_map.55 = (bf16[768,128]{1,0:T(8,128)(2,1)S(1)}, bf16[2,32,512]{2,1,0:T(8,128)(2,1)S(1)}, bf16[2,32,512]{2,1,0:T(8,128)(2,1)S(1)}, bf16[32,512]{1,0:T(8,128)(2,1)S(1)}, bf16[32,512]{1,0:T(8,128)(2,1)S(1)}) custom-call(s32[2,1,1,4]{3,2,1,0:T(1,128)} %bitcast.68, f32[2,512,128]{2,1,0:T(8,128)} %bitcast.56, bf16[2,2,2,32,512]{4,3,2,1,0:T(8,128)(2,1)} %bitcast.58, ...), custom_call_target="tpu_custom_call" | custom-call | tf_op jit(solution)/shard_map/pallas_call | solution.py:268
  1.2 3.0 %collective-permute-start.1 = (bf16[768,128]{1,0:T(8,128)(2,1)S(1)}, bf16[768,128]{1,0:T(8,128)(2,1)S(1)}, u32[]{:S(2)}, u32[]{:S(2)}) collective-permute-start(bf16[768,128]{1,0:T(8,128)(2,1)S(1)} %get-tuple-element.31.refs_0_), channel_id=1, source_target_pairs={{0,2},{2,0},{1,3},{3,1},{4,6},{6,4},{5,7},{7,5},{8,10},{10,8},{9,1... | collective-permute-start | bytes 589832 | tf_op jit(solution)/shard_map/ppermute | solution.py:305
  4.3 0.7 collective-permute-start.3
  4.9 2.7 %collective-permute-start.4 = (bf16[2,32,512]{2,1,0:T(8,128)(2,1)S(1)}, bf16[2,32,512]{2,1,0:T(8,128)(2,1)S(1)}, u32[]{:S(2)}, u32[]{:S(2)}) collective-permute-start(bf16[2,32,512]{2,1,0:T(8,128)(2,1)S(1)} %get-tuple-element.34), channel_id=1, source_target_pairs={{0,16},{1,20},{2,24},{3,28},{4,17},{5,21},{6,25},{7,29},{8,18},{9,... | collective-permute-start | bytes 196616 | tf_op jit(solution)/shard_map/ppermute | solution.py:317
  7.6 0.0 copy-start
  7.7 1.4 %collective-permute-done.1.refs_2_ = bf16[768,128]{1,0:T(8,128)(2,1)S(1)} collective-permute-done((bf16[768,128]{1,0:T(8,128)(2,1)S(1)}, bf16[768,128]{1,0:T(8,128)(2,1)S(1)}, u32[]{:S(2)}, u32[]{:S(2)}) %collective-permute-start.1) | collective-permute-done | bytes 196640 | tf_op jit(solution)/shard_map/ppermute | solution.py:305
  9.1 1.6 %collective-permute-start.2 = (bf16[768,128]{1,0:T(8,128)(2,1)S(1)}, bf16[768,128]{1,0:T(8,128)(2,1)S(1)}, u32[]{:S(2)}, u32[]{:S(2)}) collective-permute-start(bf16[768,128]{1,0:T(8,128)(2,1)S(1)} %collective-permute-done.1.refs_2_), channel_id=1, source_target_pairs={{0,1},{1,0},{2,3},{3,2},{4,5},{5,4},{6,7},{7,6},{8,9},{9,8},{10,11... | collective-permute-start | bytes 589832 | tf_op jit(solution)/shard_map/ppermute | solution.py:306
  10.7 1.1 %collective-permute-done.2.refs_3_ = bf16[768,128]{1,0:T(8,128)(2,1)S(1)} collective-permute-done((bf16[768,128]{1,0:T(8,128)(2,1)S(1)}, bf16[768,128]{1,0:T(8,128)(2,1)S(1)}, u32[]{:S(2)}, u32[]{:S(2)}) %collective-permute-start.2) | collective-permute-done | bytes 196640 | tf_op jit(solution)/shard_map/ppermute | solution.py:306
  11.8 0.6 shard_map.56
  12.4 1.0 %shard_map.57 = (bf16[16,32,256]{2,1,0:T(8,128)(2,1)}, bf16[32,800]{1,0:T(8,128)(2,1)S(1)}, bf16[32,800]{1,0:T(8,128)(2,1)S(1)}) custom-call(bf16[288,512]{1,0:T(8,128)(2,1)S(1)} %get-tuple-element.32.x_ref, bf16[2,32,512]{2,1,0:T(8,128)(2,1)S(1)} %collective-permute-done.3.v_a_ref, bf16[2,32,512]{2,1,0:T(8,128)(2,1)S(1)} %collective-permute-done.4.v_b_ref, ...), custom_call_target="tpu_custom_call" | custom-call | tf_op jit(solution)/shard_map/pallas_call | solution.py:268
  13.4 7.8 %all-to-all-start = ((bf16[16,32,256]{2,1,0:T(8,128)(2,1)}), bf16[16,32,256]{2,1,0:T(8,128)(2,1)S(1)}, u32[]{:S(2)}, u32[]{:S(2)}) async-start(bf16[16,32,256]{2,1,0:T(8,128)(2,1)} %get-tuple-element.40), calls=%async_computation | async-start | bytes 524288 | tf_op jit(solution)/shard_map/all_to_all | solution.py:321
  21.2 2.0 %collective-permute-start.12 = (bf16[1024,128]{1,0:T(8,128)(2,1)S(1)}, bf16[1024,128]{1,0:T(8,128)(2,1)S(1)}, u32[]{:S(2)}, u32[]{:S(2)}) collective-permute-start(bf16[1024,128]{1,0:T(8,128)(2,1)S(1)} %constant_dynamic-update-slice_fusion.refs_6_), channel_id=1, source_target_pairs={{0,2},{2,0},{1,3},{3,1},{4,6},{6,4},{5,7},{7,5},{8,10},{10,8},{9,1... | collective-permute-start | bytes 786440 | tf_op jit(solution)/shard_map/ppermute | solution.py:305
  23.2 8.6 %collective-permute-done.12.refs_8_ = bf16[1024,128]{1,0:T(8,128)(2,1)S(1)} collective-permute-done((bf16[1024,128]{1,0:T(8,128)(2,1)S(1)}, bf16[1024,128]{1,0:T(8,128)(2,1)S(1)}, u32[]{:S(2)}, u32[]{:S(2)}) %collective-permute-start.12) | collective-permute-done | bytes 262176 | tf_op jit(solution)/shard_map/ppermute | solution.py:305
  31.9 0.5 collective-permute-start.5
  32.4 0.7 collective-permute-start.6
  33.0 2.4 %collective-permute-start.7 = (bf16[32,800]{1,0:T(8,128)(2,1)S(1)}, bf16[32,800]{1,0:T(8,128)(2,1)S(1)}, u32[]{:S(2)}, u32[]{:S(2)}) collective-permute-start(bf16[32,800]{1,0:T(8,128)(2,1)S(1)} %get-tuple-element.42), channel_id=1, source_target_pairs={{0,16},{1,20},{2,24},{3,28},{4,17},{5,21},{6,25},{7,29},{8,18},{9,... | collective-permute-start | bytes 153608 | tf_op jit(solution)/shard_map/ppermute | solution.py:317
  35.5 2.7 %collective-permute-done.7.refs_1_.v_b_ref = bf16[32,800]{1,0:T(8,128)(2,1)S(1)} collective-permute-done((bf16[32,800]{1,0:T(8,128)(2,1)S(1)}, bf16[32,800]{1,0:T(8,128)(2,1)S(1)}, u32[]{:S(2)}, u32[]{:S(2)}) %collective-permute-start.7) | collective-permute-done | bytes 51232 | tf_op jit(solution)/shard_map/ppermute | solution.py:317
  38.2 6.6 %collective-permute-start.9 = (bf16[2,32,288]{2,1,0:T(8,128)(2,1)S(1)}, bf16[2,32,288]{2,1,0:T(8,128)(2,1)S(1)}, u32[]{:S(2)}, u32[]{:S(2)}) collective-permute-start(bf16[2,32,288]{2,1,0:T(8,128)(2,1)S(1)} %pad_maximum_fusion.refs_2_), channel_id=1, source_target_pairs={{0,2},{2,0},{1,3},{3,1},{4,6},{6,4},{5,7},{7,5},{8,10},{10,8},{9,1... | collective-permute-start | bytes 110600 | tf_op jit(solution)/shard_map/ppermute | solution.py:305
  44.8 0.5 collective-permute-start.8
  45.3 2.0 %collective-permute-done.9.refs_4_ = bf16[2,32,288]{2,1,0:T(8,128)(2,1)S(1)} collective-permute-done((bf16[2,32,288]{2,1,0:T(8,128)(2,1)S(1)}, bf16[2,32,288]{2,1,0:T(8,128)(2,1)S(1)}, u32[]{:S(2)}, u32[]{:S(2)}) %collective-permute-start.9) | collective-permute-done | bytes 36896 | tf_op jit(solution)/shard_map/ppermute | solution.py:305
  47.2 0.1 collective-permute-start.10
  47.4 1.1 %collective-permute-done.10.refs_5_ = bf16[2,32,288]{2,1,0:T(8,128)(2,1)S(1)} collective-permute-done((bf16[2,32,288]{2,1,0:T(8,128)(2,1)S(1)}, bf16[2,32,288]{2,1,0:T(8,128)(2,1)S(1)}, u32[]{:S(2)}, u32[]{:S(2)}) %collective-permute-start.10) | collective-permute-done | bytes 36896 | tf_op jit(solution)/shard_map/ppermute | solution.py:306
  48.5 0.7 shard_map.58
  49.2 1.5 %shard_map.59 = (bf16[16,32,256]{2,1,0:T(8,128)(2,1)S(1)}, f32[64,512]{1,0:T(8,128)S(1)}, bf16[224,64]{1,0:T(8,128)(2,1)S(1)}) custom-call(bf16[16,32,256]{2,1,0:T(8,128)(2,1)S(1)} %all-to-all-done.same_ref, bf16[16,32,256]{2,1,0:T(8,128)(2,1)S(1)} %collective-permute-done.5.other_ref, f32[2,64,512]{2,1,0:T(8,128)S(1)} %bitcast.52, ...), custom_call_target="tpu_custom_call" | custom-call | tf_op jit(solution)/shard_map/pallas_call | solution.py:268
  50.7 15.4 %all_to_all.10.same_ref = bf16[16,32,256]{2,1,0:T(8,128)(2,1)S(1)} all-to-all(bf16[16,32,256]{2,1,0:T(8,128)(2,1)S(1)} %get-tuple-element.47), channel_id=1, replica_groups=mesh['row'=8,'x'=2,'core'=2] {'row','x'}, dimensions={0} | all-to-all | bytes 524288 | tf_op jit(solution)/shard_map/all_to_all | solution.py:321
  66.2 0.4 fusion.2.refs_3_
  66.6 0.8 %collective-permute-start.16 = (f32[2,64,128]{2,1,0:T(8,128)S(1)}, f32[2,64,128]{2,1,0:T(8,128)S(1)}, u32[]{:S(2)}, u32[]{:S(2)}) collective-permute-start(f32[2,64,128]{2,1,0:T(8,128)S(1)} %fusion.2.refs_3_), channel_id=1, source_target_pairs={{0,2},{2,0},{1,3},{3,1},{4,6},{6,4},{5,7},{7,5},{8,10},{10,8},{9,1... | collective-permute-start | bytes 196616 | tf_op jit(solution)/shard_map/ppermute | solution.py:305
  67.4 0.2 collective-permute-start.15
  67.7 3.5 %collective-permute-done.16.refs_5_ = f32[2,64,128]{2,1,0:T(8,128)S(1)} collective-permute-done((f32[2,64,128]{2,1,0:T(8,128)S(1)}, f32[2,64,128]{2,1,0:T(8,128)S(1)}, u32[]{:S(2)}, u32[]{:S(2)}) %collective-permute-start.16) | collective-permute-done | bytes 65568 | tf_op jit(solution)/shard_map/ppermute | solution.py:305
  71.2 1.2 %collective-permute-done.17.refs_6_ = f32[2,64,128]{2,1,0:T(8,128)S(1)} collective-permute-done((f32[2,64,128]{2,1,0:T(8,128)S(1)}, f32[2,64,128]{2,1,0:T(8,128)S(1)}, u32[]{:S(2)}, u32[]{:S(2)}) %collective-permute-start.17) | collective-permute-done | bytes 65568 | tf_op jit(solution)/shard_map/ppermute | solution.py:306
  72.4 0.4 shard_map.60
  72.9 2.0 %shard_map.61 = f32[2,64,512]{2,1,0:T(8,128)} custom-call(bf16[16,32,256]{2,1,0:T(8,128)(2,1)S(1)} %all_to_all.10.same_ref, bf16[16,32,256]{2,1,0:T(8,128)(2,1)S(1)} %collective-permute-done.14.other_ref, f32[64,512]{1,0:T(8,128)S(1)} %get-tuple-element.48.minus_ref, f32[64,512]{1,0:T(8,128)S(1)} %get-tuple-element.54.z_ref, ...), custom_call_target="tpu_custom_call" | custom-call | tf_op jit(solution)/shard_map/pallas_call | solution.py:268
  (32 shorter events, 0.2 us)
Async XLA Ops:
  0.0 7.6 %copy-start.2 = (bf16[2,1,4,1,32,512]{5,4,3,2,1,0:T(8,128)(2,1)S(1)}, bf16[2,1,4,1,32,512]{5,4,3,2,1,0:T(8,128)(2,1)}, u32[]{:S(2)}) copy-start(bf16[2,1,4,1,32,512]{5,4,3,2,1,0:T(8,128)(2,1)} %param.7) | copy-start | bytes 786436
  0.0 7.6 %copy-start.1 = (f32[2,1,512,128]{3,2,1,0:T(8,128)S(1)}, f32[2,1,512,128]{3,2,1,0:T(8,128)}, u32[]{:S(2)}) copy-start(f32[2,1,512,128]{3,2,1,0:T(8,128)} %param.6) | copy-start | bytes 1572868
  1.2 7.9 %collective-permute-start.1 = (bf16[768,128]{1,0:T(8,128)(2,1)S(1)}, bf16[768,128]{1,0:T(8,128)(2,1)S(1)}, u32[]{:S(2)}, u32[]{:S(2)}) collective-permute-start(bf16[768,128]{1,0:T(8,128)(2,1)S(1)} %get-tuple-element.31.refs_0_), channel_id=1, source_target_pairs={{0,2},{2,0},{1,3},{3,1},{4,6},{6,4},{5,7},{7,5},{8,10},{10,8},{9,1... | collective-permute-start | bytes 589832 | tf_op jit(solution)/shard_map/ppermute | solution.py:305
  4.2 6.5 %collective-permute-start = (bf16[768,128]{1,0:T(8,128)(2,1)S(1)}, bf16[768,128]{1,0:T(8,128)(2,1)S(1)}, u32[]{:S(2)}, u32[]{:S(2)}) collective-permute-start(bf16[768,128]{1,0:T(8,128)(2,1)S(1)} %get-tuple-element.31.refs_0_), channel_id=1, source_target_pairs={{0,1},{1,0},{2,3},{3,2},{4,5},{5,4},{6,7},{7,6},{8,9},{9,8},{10,11... | collective-permute-start | bytes 589832 | tf_op jit(solution)/shard_map/ppermute | solution.py:306
  4.3 8.1 %collective-permute-start.3 = (bf16[2,32,512]{2,1,0:T(8,128)(2,1)S(1)}, bf16[2,32,512]{2,1,0:T(8,128)(2,1)S(1)}, u32[]{:S(2)}, u32[]{:S(2)}) collective-permute-start(bf16[2,32,512]{2,1,0:T(8,128)(2,1)S(1)} %get-tuple-element.33), channel_id=1, source_target_pairs={{0,0},{1,4},{2,8},{3,12},{4,1},{5,5},{6,9},{7,13},{8,2},{9,6},{10,... | collective-permute-start | bytes 196616 | tf_op jit(solution)/shard_map/ppermute | solution.py:317
  4.9 7.5 %collective-permute-start.4 = (bf16[2,32,512]{2,1,0:T(8,128)(2,1)S(1)}, bf16[2,32,512]{2,1,0:T(8,128)(2,1)S(1)}, u32[]{:S(2)}, u32[]{:S(2)}) collective-permute-start(bf16[2,32,512]{2,1,0:T(8,128)(2,1)S(1)} %get-tuple-element.34), channel_id=1, source_target_pairs={{0,16},{1,20},{2,24},{3,28},{4,17},{5,21},{6,25},{7,29},{8,18},{9,... | collective-permute-start | bytes 196616 | tf_op jit(solution)/shard_map/ppermute | solution.py:317
  7.6 4.2 %copy-start = (f32[2,1,64,512]{3,2,1,0:T(8,128)S(1)}, f32[2,1,64,512]{3,2,1,0:T(8,128)}, u32[]{:S(2)}) copy-start(f32[2,1,64,512]{3,2,1,0:T(8,128)} %param.5) | copy-start | bytes 786436
  9.1 2.6 %collective-permute-start.2 = (bf16[768,128]{1,0:T(8,128)(2,1)S(1)}, bf16[768,128]{1,0:T(8,128)(2,1)S(1)}, u32[]{:S(2)}, u32[]{:S(2)}) collective-permute-start(bf16[768,128]{1,0:T(8,128)(2,1)S(1)} %collective-permute-done.1.refs_2_), channel_id=1, source_target_pairs={{0,1},{1,0},{2,3},{3,2},{4,5},{5,4},{6,7},{7,6},{8,9},{9,8},{10,11... | collective-permute-start | bytes 589832 | tf_op jit(solution)/shard_map/ppermute | solution.py:306
  13.4 18.5 %all-to-all-start = ((bf16[16,32,256]{2,1,0:T(8,128)(2,1)}), bf16[16,32,256]{2,1,0:T(8,128)(2,1)S(1)}, u32[]{:S(2)}, u32[]{:S(2)}) async-start(bf16[16,32,256]{2,1,0:T(8,128)(2,1)} %get-tuple-element.40), calls=%async_computation | async-start | bytes 524288 | tf_op jit(solution)/shard_map/all_to_all | solution.py:321
  21.2 10.6 %collective-permute-start.12 = (bf16[1024,128]{1,0:T(8,128)(2,1)S(1)}, bf16[1024,128]{1,0:T(8,128)(2,1)S(1)}, u32[]{:S(2)}, u32[]{:S(2)}) collective-permute-start(bf16[1024,128]{1,0:T(8,128)(2,1)S(1)} %constant_dynamic-update-slice_fusion.refs_6_), channel_id=1, source_target_pairs={{0,2},{2,0},{1,3},{3,1},{4,6},{6,4},{5,7},{7,5},{8,10},{10,8},{9,1... | collective-permute-start | bytes 786440 | tf_op jit(solution)/shard_map/ppermute | solution.py:305
  23.2 24.1 %collective-permute-start.11 = (bf16[1024,128]{1,0:T(8,128)(2,1)S(1)}, bf16[1024,128]{1,0:T(8,128)(2,1)S(1)}, u32[]{:S(2)}, u32[]{:S(2)}) collective-permute-start(bf16[1024,128]{1,0:T(8,128)(2,1)S(1)} %constant_dynamic-update-slice_fusion.refs_6_), channel_id=1, source_target_pairs={{0,1},{1,0},{2,3},{3,2},{4,5},{5,4},{6,7},{7,6},{8,9},{9,8},{10,11... | collective-permute-start | bytes 786440 | tf_op jit(solution)/shard_map/ppermute | solution.py:306
  31.8 16.6 %collective-permute-start.13 = (bf16[1024,128]{1,0:T(8,128)(2,1)S(1)}, bf16[1024,128]{1,0:T(8,128)(2,1)S(1)}, u32[]{:S(2)}, u32[]{:S(2)}) collective-permute-start(bf16[1024,128]{1,0:T(8,128)(2,1)S(1)} %collective-permute-done.12.refs_8_), channel_id=1, source_target_pairs={{0,1},{1,0},{2,3},{3,2},{4,5},{5,4},{6,7},{7,6},{8,9},{9,8},{10,11... | collective-permute-start | bytes 786440 | tf_op jit(solution)/shard_map/ppermute | solution.py:306
  31.9 17.4 %collective-permute-start.5 = (bf16[16,32,256]{2,1,0:T(8,128)(2,1)S(1)}, bf16[16,32,256]{2,1,0:T(8,128)(2,1)S(1)}, u32[]{:S(2)}, u32[]{:S(2)}) collective-permute-start(bf16[16,32,256]{2,1,0:T(8,128)(2,1)S(1)} %all-to-all-done.same_ref), channel_id=1, source_target_pairs={{0,1},{1,0},{2,3},{3,2},{4,5},{5,4},{6,7},{7,6},{8,9},{9,8},{10,11... | collective-permute-start | bytes 786440 | tf_op jit(solution)/shard_map/ppermute | solution.py:322
  32.4 3.1 %collective-permute-start.6 = (bf16[32,800]{1,0:T(8,128)(2,1)S(1)}, bf16[32,800]{1,0:T(8,128)(2,1)S(1)}, u32[]{:S(2)}, u32[]{:S(2)}) collective-permute-start(bf16[32,800]{1,0:T(8,128)(2,1)S(1)} %get-tuple-element.41), channel_id=1, source_target_pairs={{0,0},{1,4},{2,8},{3,12},{4,1},{5,5},{6,9},{7,13},{8,2},{9,6},{10,... | collective-permute-start | bytes 153608 | tf_op jit(solution)/shard_map/ppermute | solution.py:317
  33.0 5.1 %collective-permute-start.7 = (bf16[32,800]{1,0:T(8,128)(2,1)S(1)}, bf16[32,800]{1,0:T(8,128)(2,1)S(1)}, u32[]{:S(2)}, u32[]{:S(2)}) collective-permute-start(bf16[32,800]{1,0:T(8,128)(2,1)S(1)} %get-tuple-element.42), channel_id=1, source_target_pairs={{0,16},{1,20},{2,24},{3,28},{4,17},{5,21},{6,25},{7,29},{8,18},{9,... | collective-permute-start | bytes 153608 | tf_op jit(solution)/shard_map/ppermute | solution.py:317
  38.2 9.1 %collective-permute-start.9 = (bf16[2,32,288]{2,1,0:T(8,128)(2,1)S(1)}, bf16[2,32,288]{2,1,0:T(8,128)(2,1)S(1)}, u32[]{:S(2)}, u32[]{:S(2)}) collective-permute-start(bf16[2,32,288]{2,1,0:T(8,128)(2,1)S(1)} %pad_maximum_fusion.refs_2_), channel_id=1, source_target_pairs={{0,2},{2,0},{1,3},{3,1},{4,6},{6,4},{5,7},{7,5},{8,10},{10,8},{9,1... | collective-permute-start | bytes 110600 | tf_op jit(solution)/shard_map/ppermute | solution.py:305
  44.8 2.6 %collective-permute-start.8 = (bf16[2,32,288]{2,1,0:T(8,128)(2,1)S(1)}, bf16[2,32,288]{2,1,0:T(8,128)(2,1)S(1)}, u32[]{:S(2)}, u32[]{:S(2)}) collective-permute-start(bf16[2,32,288]{2,1,0:T(8,128)(2,1)S(1)} %pad_maximum_fusion.refs_2_), channel_id=1, source_target_pairs={{0,1},{1,0},{2,3},{3,2},{4,5},{5,4},{6,7},{7,6},{8,9},{9,8},{10,11... | collective-permute-start | bytes 110600 | tf_op jit(solution)/shard_map/ppermute | solution.py:306
  47.2 1.2 %collective-permute-start.10 = (bf16[2,32,288]{2,1,0:T(8,128)(2,1)S(1)}, bf16[2,32,288]{2,1,0:T(8,128)(2,1)S(1)}, u32[]{:S(2)}, u32[]{:S(2)}) collective-permute-start(bf16[2,32,288]{2,1,0:T(8,128)(2,1)S(1)} %collective-permute-done.9.refs_4_), channel_id=1, source_target_pairs={{0,1},{1,0},{2,3},{3,2},{4,5},{5,4},{6,7},{7,6},{8,9},{9,8},{10,11... | collective-permute-start | bytes 110600 | tf_op jit(solution)/shard_map/ppermute | solution.py:306
  66.2 6.7 %collective-permute-start.14 = (bf16[16,32,256]{2,1,0:T(8,128)(2,1)S(1)}, bf16[16,32,256]{2,1,0:T(8,128)(2,1)S(1)}, u32[]{:S(2)}, u32[]{:S(2)}) collective-permute-start(bf16[16,32,256]{2,1,0:T(8,128)(2,1)S(1)} %all_to_all.10.same_ref), channel_id=1, source_target_pairs={{0,1},{1,0},{2,3},{3,2},{4,5},{5,4},{6,7},{7,6},{8,9},{9,8},{10,11... | collective-permute-start | bytes 786440 | tf_op jit(solution)/shard_map/ppermute | solution.py:322
  66.6 4.6 %collective-permute-start.16 = (f32[2,64,128]{2,1,0:T(8,128)S(1)}, f32[2,64,128]{2,1,0:T(8,128)S(1)}, u32[]{:S(2)}, u32[]{:S(2)}) collective-permute-start(f32[2,64,128]{2,1,0:T(8,128)S(1)} %fusion.2.refs_3_), channel_id=1, source_target_pairs={{0,2},{2,0},{1,3},{3,1},{4,6},{6,4},{5,7},{7,5},{8,10},{10,8},{9,1... | collective-permute-start | bytes 196616 | tf_op jit(solution)/shard_map/ppermute | solution.py:305
  67.4 3.7 %collective-permute-start.15 = (f32[2,64,128]{2,1,0:T(8,128)S(1)}, f32[2,64,128]{2,1,0:T(8,128)S(1)}, u32[]{:S(2)}, u32[]{:S(2)}) collective-permute-start(f32[2,64,128]{2,1,0:T(8,128)S(1)} %fusion.2.refs_3_), channel_id=1, source_target_pairs={{0,1},{1,0},{2,3},{3,2},{4,5},{5,4},{6,7},{7,6},{8,9},{9,8},{10,11... | collective-permute-start | bytes 196616 | tf_op jit(solution)/shard_map/ppermute | solution.py:306
  71.2 1.3 %collective-permute-start.17 = (f32[2,64,128]{2,1,0:T(8,128)S(1)}, f32[2,64,128]{2,1,0:T(8,128)S(1)}, u32[]{:S(2)}, u32[]{:S(2)}) collective-permute-start(f32[2,64,128]{2,1,0:T(8,128)S(1)} %collective-permute-done.16.refs_5_), channel_id=1, source_target_pairs={{0,1},{1,0},{2,3},{3,2},{4,5},{5,4},{6,7},{7,6},{8,9},{9,8},{10,11... | collective-permute-start | bytes 196616 | tf_op jit(solution)/shard_map/ppermute | solution.py:306
